TPU v7x, 32 devices: a whole 2x2x4 slice. The times are simulated.
32 devices in a mesh: dp: 4 (over y, x), row: 2 (over core), col: 4 (over z).
Axes of the slice: x: 2, y: 2, z: 4, core: 2. Of those that a mesh axis runs over, the one named last changes fastest.
Arguments:
- block_input: bfloat16 [8192, 1536], P(('dp', 'row', 'col')), may hold values from -6 to 6
- segment_ids: int32 [8192], P(('dp', 'row', 'col')), may hold values from 0 to 6, as said below
- norm_gain: float32 [1536], replicated, may hold values from 0.1 to 1.9
- proj_zx: bfloat16 [1536, 2, 3072], P(('dp', 'row'), None, 'col'), may hold values from -0.15625 to 0.15625
- proj_bc: bfloat16 [1536, 256], P(('dp', 'row')), may hold values from -0.15625 to 0.15625
- proj_dt: bfloat16 [1536, 48], P(('dp', 'row'), 'col'), may hold values from -0.15625 to 0.15625
- conv_inner: float32 [4, 3072], P(None, 'col'), may hold values from -3 to 3
- conv_inner_bias: float32 [3072], P('col'), may hold values from -3 to 3
- conv_shared: float32 [4, 256], replicated, may hold values from -3 to 3
- conv_shared_bias: float32 [256], replicated, may hold values from -3 to 3
- step_bias: float32 [48], P('col'), may hold values from -6.9 to -2.3
- rate_log: float32 [48], P('col'), may hold values from 0 to 2.77
- skip_gain: float32 [48], P('col'), may hold values from 0.5 to 2
- gated_gain: float32 [3072], P('col'), may hold values from 0.1 to 1.9
- proj_out: bfloat16 [3072, 1536], P('col', ('dp', 'row')), may hold values from -0.109375 to 0.109375
- cotangent: bfloat16 [8192, 1536], P(('dp', 'row', 'col')), may hold values from -6 to 6
Outputs:
- block_output: bfloat16 [8192, 1536], P(('dp', 'row', 'col'))
- grad_input: bfloat16 [8192, 1536], P(('dp', 'row', 'col'))
- grad_norm_gain: float32 [1536], replicated
- grad_proj_zx: float32 [1536, 2, 3072], P(('dp', 'row'), None, 'col')
- grad_proj_bc: float32 [1536, 256], P(('dp', 'row'))
- grad_proj_dt: float32 [1536, 48], P(('dp', 'row'), 'col')
- grad_conv_inner: float32 [4, 3072], P(None, 'col')
- grad_conv_inner_bias: float32 [3072], P('col')
- grad_conv_shared: float32 [4, 256], replicated
- grad_conv_shared_bias: float32 [256], replicated
- grad_step_bias: float32 [48], P('col')
- grad_rate_log: float32 [48], P('col')
- grad_skip_gain: float32 [48], P('col')
- grad_gated_gain: float32 [3072], P('col')
- grad_proj_out: float32 [3072, 1536], P('col', ('dp', 'row'))
Inputs may be any that keep to these rules, and one draw needn't show every extreme that they name: `segment_ids`: within each aligned sequence of 2048 tokens the ids start at 0 on its first token, never fall, and rise by one at exactly six document starts: three in the first quarter of the sequence (never its first token) and three in its last quarter; so every sequence holds seven documents and its middle half lies in one of them.
All inputs are finite; a program needn't handle non-finite values.
Results may differ from a plain program's by a relative error of at most 0.011.
Values may be sent and summed in bfloat16 or wider, within the bound.
A program may use at most 256 MiB of HBM per device.

v0:
```python
from functools import partial

import jax
import jax.numpy as jnp
from jax import lax
from jax.sharding import PartitionSpec as P

SPAN = 256
DI = 3072


EPS = 1e-05
HIGH = lax.Precision.HIGHEST


def from_behind(value, axis, by):
    devices = lax.axis_size(axis)
    pairs = [(i, i + by) for i in range(devices) if 0 <= i + by < devices]
    return lax.ppermute(value, axis, pairs)


def delayed(values, delay_steps, filler):
    padding = jnp.full((delay_steps,) + values.shape[1:], filler, values.dtype)
    return jnp.concatenate([padding, values[:-delay_steps]], axis=0)


def causal_conv(values, kernel, offset, segment):
    kernel_size = kernel.shape[0]
    running = kernel[kernel_size - 1][None, :] * values + offset[None, :]
    for delay_steps in range(1, kernel_size):
        linked = (delayed(segment, delay_steps, -1) == segment).astype(jnp.float32)
        running = (
            running
            + kernel[kernel_size - 1 - delay_steps][None, :]
            * delayed(values, delay_steps, 0.0)
            * linked[:, None]
        )
    return running


def block_update(carried, previous, cumulative, step_block, x_block, b_block, seg_block):
    closing = seg_block[-1]
    leaving = (
        jnp.exp(cumulative[-1][None, :] - cumulative)
        * (seg_block == closing).astype(jnp.float32)[:, None]
        * step_block
    )
    retained = jnp.exp(cumulative[-1]) * (closing == previous).astype(jnp.float32)
    carried = carried * retained[:, None, None] + jnp.einsum(
        "sh,shp,sn->hpn", leaving, x_block, b_block, precision=HIGH
    )
    return (carried, closing)


def span_scan(
    heads_in, step_size, log_decay, b_matrix, c_matrix, segment, block_len, start_state, start_prev
):
    seq_len, head_count, head_dim = heads_in.shape
    blocks_count = seq_len // block_len

    def span_reshaped(tensor):
        return tensor.reshape((blocks_count, block_len) + tensor.shape[1:])

    def span_advance(carry, block):
        carried, previous = carry
        x_block, step_block, log_block, b_block, c_block, seg_block = block
        cumulative = jnp.cumsum(log_block, axis=0)
        position = jnp.arange(block_len)
        linked = (position[:, None] >= position[None, :]) & (
            seg_block[:, None] == seg_block[None, :]
        )
        linked_float = linked.astype(jnp.float32)
        spread = cumulative.T[:, :, None] - cumulative.T[:, None, :]
        decays = jnp.exp(jnp.where(linked[None], spread, 0.0)) * linked_float[None]
        scores = jnp.dot(c_block, b_block.T, precision=HIGH)
        mixing = decays * scores[None] * step_block.T[:, None, :]
        output = jnp.einsum("hts,shp->thp", mixing, x_block, precision=HIGH)
        entering = jnp.exp(cumulative) * (seg_block == previous).astype(jnp.float32)[:, None]
        output = (
            output
            + jnp.einsum("tn,hpn->thp", c_block, carried, precision=HIGH) * entering[:, :, None]
        )
        return (
            block_update(carried, previous, cumulative, step_block, x_block, b_block, seg_block),
            output,
        )

    blocks = tuple(
        (
            span_reshaped(member)
            for member in (heads_in, step_size, log_decay, b_matrix, c_matrix, segment)
        )
    )
    _, outputs = lax.scan(jax.checkpoint(span_advance), (start_state, start_prev), blocks)
    return outputs.reshape(seq_len, head_count, head_dim)


def closing_scan(
    heads_in, step_size, log_decay, b_matrix, segment, block_len, start_state, start_prev
):
    seq_len = heads_in.shape[0]
    blocks_count = seq_len // block_len

    def closing_reshaped(tensor):
        return tensor.reshape((blocks_count, block_len) + tensor.shape[1:])

    def closing_advance(carry, block):
        carried, previous = carry
        x_block, step_block, log_block, b_block, seg_block = block
        cumulative = jnp.cumsum(log_block, axis=0)
        return (
            block_update(carried, previous, cumulative, step_block, x_block, b_block, seg_block),
            None,
        )

    blocks = tuple(
        (closing_reshaped(member) for member in (heads_in, step_size, log_decay, b_matrix, segment))
    )
    (final_state, _), _ = lax.scan(closing_advance, (start_state, start_prev), blocks)
    return final_state


def prepared(
    inner_ext,
    shared_ext,
    step_part,
    conv_inner,
    conv_inner_bias,
    conv_shared,
    conv_shared_bias,
    step_bias,
    rate_log,
    seg_ext,
):
    rim = conv_inner.shape[0] - 1
    seq_len = step_part.shape[0]
    head_count = step_part.shape[1]
    head_dim = inner_ext.shape[1] // head_count
    inner = jax.nn.silu(causal_conv(inner_ext, conv_inner, conv_inner_bias, seg_ext))[rim:]
    shared = jax.nn.silu(causal_conv(shared_ext, conv_shared, conv_shared_bias, seg_ext))[rim:]
    step_size = jax.nn.softplus(step_part + step_bias[None, :])
    log_decay = -jnp.exp(rate_log)[None, :] * step_size
    heads_in = inner.reshape(seq_len, head_count, head_dim)
    return (heads_in, shared, step_size, log_decay, seg_ext[rim:], seg_ext[rim - 1])


def state_only(
    inner_ext,
    shared_ext,
    step_part,
    conv_inner,
    conv_inner_bias,
    conv_shared,
    conv_shared_bias,
    step_bias,
    rate_log,
    seg_ext,
):
    heads_in, shared, step_size, log_decay, segment, start_prev = prepared(
        inner_ext,
        shared_ext,
        step_part,
        conv_inner,
        conv_inner_bias,
        conv_shared,
        conv_shared_bias,
        step_bias,
        rate_log,
        seg_ext,
    )
    state_dim = shared.shape[1] // 2
    start_state = jnp.zeros((heads_in.shape[1], heads_in.shape[2], state_dim), jnp.float32)
    return closing_scan(
        heads_in,
        step_size,
        log_decay,
        shared[:, :state_dim],
        segment,
        SPAN,
        start_state,
        start_prev,
    )


def mixer_local(
    gate_part,
    inner_ext,
    shared_ext,
    step_part,
    conv_inner,
    conv_inner_bias,
    conv_shared,
    conv_shared_bias,
    step_bias,
    rate_log,
    skip_gain,
    start_state,
    seg_ext,
):
    heads_in, shared, step_size, log_decay, segment, start_prev = prepared(
        inner_ext,
        shared_ext,
        step_part,
        conv_inner,
        conv_inner_bias,
        conv_shared,
        conv_shared_bias,
        step_bias,
        rate_log,
        seg_ext,
    )
    seq_len, head_count, head_dim = heads_in.shape
    state_dim = shared.shape[1] // 2
    mixed = span_scan(
        heads_in,
        step_size,
        log_decay,
        shared[:, :state_dim],
        shared[:, state_dim:],
        segment,
        SPAN,
        start_state,
        start_prev,
    )
    mixed = mixed + skip_gain[None, :, None] * heads_in
    return mixed.reshape(seq_len, head_count * head_dim) * jax.nn.silu(gate_part)


def rim_add(values, border):
    width = border.shape[0]
    return jnp.concatenate([values[:-width], values[-width:] + border], axis=0)


def contract_rows(left, right):
    return lax.dot_general(
        left, right, (((0,), (0,)), ((), ())), preferred_element_type=jnp.float32
    )


def contract_cols(left, right):
    return lax.dot_general(
        left, right, (((1,), (1,)), ((), ())), preferred_element_type=jnp.float32
    )


def reduce_output_grads(part_out):
    return lax.psum_scatter(part_out, ("dp", "row"), scatter_dimension=1, tiled=True)


def per_device(
    block_input,
    segment_ids,
    norm_gain,
    proj_zx,
    proj_bc,
    proj_dt,
    conv_inner,
    conv_inner_bias,
    conv_shared,
    conv_shared_bias,
    step_bias,
    rate_log,
    skip_gain,
    gated_gain,
    proj_out,
    cotangent,
):
    model_dim = block_input.shape[1]
    group_inner = proj_zx.shape[2]
    shared_cols = proj_bc.shape[1]
    rim = conv_inner.shape[0] - 1
    wide = block_input.astype(jnp.float32)
    scale = lax.rsqrt(jnp.mean(wide * wide, axis=1, keepdims=True) + EPS)
    normed_local = (wide * scale * norm_gain[None, :]).astype(jnp.bfloat16)
    normed, segment, cot_seq = (
        lax.all_gather(normed_local, "col", axis=0, tiled=True),
        lax.all_gather(segment_ids, "col", axis=0, tiled=True),
        lax.all_gather(cotangent, "col", axis=0, tiled=True),
    )
    pieces = (
        lax.all_gather(proj_zx, ("dp", "row"), axis=0, tiled=True),
        lax.all_gather(proj_bc, ("dp", "row"), axis=0, tiled=True),
        lax.all_gather(proj_dt, ("dp", "row"), axis=0, tiled=True),
    )
    row_count = pieces[0].shape[0]
    both_raw = jnp.dot(
        normed, pieces[0].reshape(row_count, 2 * group_inner), preferred_element_type=jnp.float32
    )
    shared_raw = jnp.dot(normed, pieces[1], preferred_element_type=jnp.float32)
    step_raw = jnp.dot(normed, pieces[2], preferred_element_type=jnp.float32)
    both = lax.optimization_barrier(both_raw.astype(jnp.bfloat16))
    shared_in = lax.optimization_barrier(shared_raw.astype(jnp.bfloat16))
    both_wide = both.astype(jnp.float32)
    shared_wide = shared_in.astype(jnp.float32)
    gate_part = both_wide[:, :group_inner]
    inner_part = both_wide[:, group_inner:]
    inner_zero = jnp.concatenate([jnp.zeros((rim, group_inner), jnp.float32), inner_part], axis=0)
    shared_zero = jnp.concatenate([jnp.zeros((rim, shared_cols), jnp.float32), shared_wide], axis=0)
    seg_zero = jnp.concatenate([jnp.zeros((rim,), jnp.int32), segment], axis=0)
    final_state, pull_state = jax.vjp(
        partial(state_only, seg_ext=seg_zero),
        inner_zero,
        shared_zero,
        step_raw,
        conv_inner,
        conv_inner_bias,
        conv_shared,
        conv_shared_bias,
        step_bias,
        rate_log,
    )
    start_state, inner_tail, shared_tail, seg_tail_float = from_behind(
        (final_state, inner_part[-rim:], shared_wide[-rim:], segment[-rim:].astype(jnp.float32)),
        "row",
        1,
    )
    seg_tail = seg_tail_float.astype(jnp.int32)
    inner_ext = jnp.concatenate([inner_tail, inner_part], axis=0)
    shared_ext = jnp.concatenate([shared_tail, shared_wide], axis=0)
    seg_ext = jnp.concatenate([seg_tail, segment], axis=0)
    gated, pullback = jax.vjp(
        partial(mixer_local, seg_ext=seg_ext),
        gate_part,
        inner_ext,
        shared_ext,
        step_raw,
        conv_inner,
        conv_inner_bias,
        conv_shared,
        conv_shared_bias,
        step_bias,
        rate_log,
        skip_gain,
        start_state,
    )
    squares = lax.psum(jnp.sum(gated * gated, axis=1), "col")
    rescale = lax.rsqrt(squares / DI + EPS)[:, None]
    gated_normed = (gated * rescale * gated_gain[None, :]).astype(jnp.bfloat16)
    out_full = lax.all_gather(proj_out, ("dp", "row"), axis=1, tiled=True)
    projected = lax.psum_scatter(
        jnp.dot(gated_normed, out_full, preferred_element_type=jnp.float32),
        "col",
        scatter_dimension=0,
        tiled=True,
    )
    block_output = (wide + projected).astype(jnp.bfloat16)
    grad_out_part = contract_rows(gated_normed, cot_seq)
    back = contract_cols(cot_seq, out_full)
    weighted = back * gated_gain[None, :]
    inner_sum = lax.psum(jnp.sum(weighted * gated, axis=1), "col")[:, None]
    gain_out_part = jnp.sum(back * gated * rescale, axis=0)
    grad_gated = rescale * weighted - gated * (rescale**3 * inner_sum / DI)
    (
        grad_gate,
        grad_inner_ext,
        grad_shared_ext,
        grad_step,
        part_conv_inner,
        part_conv_inner_bias,
        part_conv_shared,
        part_conv_shared_bias,
        part_step_bias,
        part_rate_log,
        part_skip_gain,
        grad_start,
    ) = pullback(grad_gated)
    grad_final, inner_border, shared_border = from_behind(
        (grad_start, grad_inner_ext[:rim], grad_shared_ext[:rim]), "row", -1
    )
    (
        extra_inner,
        extra_shared,
        extra_step,
        extra_conv_inner,
        extra_conv_inner_bias,
        extra_conv_shared,
        extra_conv_shared_bias,
        extra_step_bias,
        extra_rate_log,
    ) = pull_state(grad_final)
    grad_inner = rim_add(grad_inner_ext[rim:] + extra_inner[rim:], inner_border)
    grad_shared = rim_add(grad_shared_ext[rim:] + extra_shared[rim:], shared_border)
    grad_step = grad_step + extra_step
    part_conv_inner = part_conv_inner + extra_conv_inner
    part_conv_inner_bias = part_conv_inner_bias + extra_conv_inner_bias
    part_conv_shared = part_conv_shared + extra_conv_shared
    part_conv_shared_bias = part_conv_shared_bias + extra_conv_shared_bias
    part_step_bias = part_step_bias + extra_step_bias
    part_rate_log = part_rate_log + extra_rate_log
    grad_both = jnp.concatenate([grad_gate, grad_inner], axis=1).astype(jnp.bfloat16)
    shared_back = grad_shared.astype(jnp.bfloat16)
    step_back = grad_step.astype(jnp.bfloat16)
    part_zx = contract_rows(normed, grad_both).reshape(model_dim, 2, group_inner)
    part_bc = contract_rows(normed, shared_back)
    part_dt = contract_rows(normed, step_back)
    pieces = lax.all_gather((proj_zx, proj_bc, proj_dt), ("dp", "row"), axis=0, tiled=True)
    row_count = pieces[0].shape[0]
    partial_terms = (
        contract_cols(grad_both, pieces[0].reshape(row_count, 2 * group_inner))
        + contract_cols(shared_back, pieces[1])
        + contract_cols(step_back, pieces[2])
    )
    grad_normed = lax.psum_scatter(partial_terms, "col", scatter_dimension=0, tiled=True)
    gain_in_part = jnp.sum(grad_normed * wide * scale, axis=0)
    pushed = grad_normed * norm_gain[None, :]
    grad_wide = scale * pushed - wide * scale**3 * jnp.mean(pushed * wide, axis=1, keepdims=True)
    grad_input = (cotangent.astype(jnp.float32) + grad_wide).astype(jnp.bfloat16)
    grad_proj_zx, bc_rows, grad_proj_dt = (
        lax.psum_scatter(part_zx, ("dp", "row"), scatter_dimension=0, tiled=True),
        lax.psum_scatter(part_bc, ("dp", "row"), scatter_dimension=0, tiled=True),
        lax.psum_scatter(part_dt, ("dp", "row"), scatter_dimension=0, tiled=True),
    )
    grad_proj_out = reduce_output_grads(grad_out_part)
    (
        grad_conv_inner,
        grad_conv_inner_bias,
        grad_step_bias,
        grad_rate_log,
        grad_skip_gain,
        grad_gated_gain,
        conv_shared_rows,
        conv_shared_bias_rows,
        gain_in_rows,
    ) = lax.psum(
        (
            part_conv_inner,
            part_conv_inner_bias,
            part_step_bias,
            part_rate_log,
            part_skip_gain,
            gain_out_part,
            part_conv_shared,
            part_conv_shared_bias,
            gain_in_part,
        ),
        ("dp", "row"),
    )
    grad_proj_bc, grad_conv_shared, grad_conv_shared_bias, grad_norm_gain = lax.psum(
        (bc_rows, conv_shared_rows, conv_shared_bias_rows, gain_in_rows), "col"
    )
    return (
        block_output,
        grad_input,
        grad_norm_gain,
        grad_proj_zx,
        grad_proj_bc,
        grad_proj_dt,
        grad_conv_inner,
        grad_conv_inner_bias,
        grad_conv_shared,
        grad_conv_shared_bias,
        grad_step_bias,
        grad_rate_log,
        grad_skip_gain,
        grad_gated_gain,
        grad_proj_out,
    )


def solution(mesh):
    in_specs = (
        P(("dp", "row", "col"), None),
        P(("dp", "row", "col")),
        P(),
        P(("dp", "row"), None, "col"),
        P(("dp", "row"), None),
        P(("dp", "row"), "col"),
        P(None, "col"),
        P("col"),
        P(),
        P(),
        P("col"),
        P("col"),
        P("col"),
        P("col"),
        P("col", ("dp", "row")),
        P(("dp", "row", "col"), None),
    )
    out_specs = (
        P(("dp", "row", "col"), None),
        P(("dp", "row", "col"), None),
        P(),
        P(("dp", "row"), None, "col"),
        P(("dp", "row"), None),
        P(("dp", "row"), "col"),
        P(None, "col"),
        P("col"),
        P(),
        P(),
        P("col"),
        P("col"),
        P("col"),
        P("col"),
        P("col", ("dp", "row")),
    )
    return jax.shard_map(
        per_device, mesh=mesh, in_specs=in_specs, out_specs=out_specs, check_vma=False
    )
```

profile of v0, /device:TPU:0, one launch (start us, length us, event | category | flops | bytes accessed | tf_op | source)
XLA Modules:
  0.0 1511.7 jit_solution(12572392298847303606)
XLA Ops:
  13.7 12.7 all-gather.1
  28.5 10.4 all_gather.28
  39.0 9.2 all-gather
  49.5 28.9 %all-gather.7.cloned.1.call-done = bf16[1024,1536]{1,0:T(8,128)(2,1)} async-done(((bf16[256,1536]{1,0:T(8,128)(2,1)}), bf16[1024,1536]{1,0:T(8,128)(2,1)}) %all-gather.7.cloned.1.call-update) | async-done | bytes 3145744 | tf_op jit(solution)/shard_map/all_gather | solution.py:276
  90.6 27.2 %all-gather.9.cloned.1.call-done = bf16[1536,2,768]{2,1,0:T(2,128)(2,1)} async-done(((bf16[192,2,768]{2,1,0:T(2,128)(2,1)}), bf16[1536,2,768]{2,1,0:T(2,128)(2,1)}) %all-gather.9.cloned.1.call-update) | async-done | bytes 4718608 | tf_op jit(solution)/shard_map/all_gather | solution.py:281
  121.2 5.3 convolution_convert_fusion
  153.3 61.7 %while.100 = (s32[]{:T(128)}, f32[12,64,128]{2,1,0:T(8,128)}, s32[]{:T(128)}, f32[4,256,12]{1,2,0:T(8,128)S(1)}, f32[4,256,1]{1,2,0:T(1,128)}, /*index=5*/f32[4,...) while((s32[]{:T(128)}, f32[12,64,128]{2,1,0:T(8,128)}, ...), condition=%wide.region_4.6_spmd.clone, body=%wide.region_1.5_spmd.clone.sunk | while | flops 303179328 | bytes 5977654 | solution.py:119
  217.0 6.2 add_divide_fusion
  241.3 140.2 %while.99 = (s32[]{:T(128)}, f32[12,64,128]{2,1,0:T(8,128)S(1)}, s32[]{:T(128)}, f32[4,256,12,64]{1,0,3,2:T(4,128)}, f32[4,12,64,128]{3,2,1,0:T(8,128)}, /*index...) while((s32[]{:T(128)}, f32[12,64,128]{2,1,0:T(8,128)S(1)}, ...), condition=%wide.region_8.10_spmd.clone, body=%wide.region_5.9_spmd.clone.sunk | while | flops 1314010112 | bytes 11125435 | solution.py:94
  253.6 17.9 %dynamic_update_slice.185 = f32[4,256,12,64]{1,0,3,2:T(4,128)} dynamic-update-slice(f32[4,256,12,64]{1,0,3,2:T(4,128)} %get-tuple-element.2287, f32[1,256,12,64]{1,0,3,2:T(1,128)S(1)} %copy.412, s32[]{:T(128)} %get-tuple-element.2284, s32[]{:T(128)} %constant.224.clone.1..sunk.1, s32[]{:T(128)} %constant.224.clone.1..sunk.1, s32[]{:T(128)} %constant.224.clone.1..sunk.1) | dynamic-update-slice | bytes 1572868 | tf_op jit(solution)/shard_map/jvp()/while/body/jit(dynamic_update_index_in_dim)/dynamic_update_slice | solution.py:119
  288.7 17.9 %dynamic_update_slice.185 = f32[4,256,12,64]{1,0,3,2:T(4,128)} dynamic-update-slice(f32[4,256,12,64]{1,0,3,2:T(4,128)} %get-tuple-element.2287, f32[1,256,12,64]{1,0,3,2:T(1,128)S(1)} %copy.412, s32[]{:T(128)} %get-tuple-element.2284, s32[]{:T(128)} %constant.224.clone.1..sunk.1, s32[]{:T(128)} %constant.224.clone.1..sunk.1, s32[]{:T(128)} %constant.224.clone.1..sunk.1) | dynamic-update-slice | bytes 1572868 | tf_op jit(solution)/shard_map/jvp()/while/body/jit(dynamic_update_index_in_dim)/dynamic_update_slice | solution.py:119
  323.7 17.9 %dynamic_update_slice.185 = f32[4,256,12,64]{1,0,3,2:T(4,128)} dynamic-update-slice(f32[4,256,12,64]{1,0,3,2:T(4,128)} %get-tuple-element.2287, f32[1,256,12,64]{1,0,3,2:T(1,128)S(1)} %copy.412, s32[]{:T(128)} %get-tuple-element.2284, s32[]{:T(128)} %constant.224.clone.1..sunk.1, s32[]{:T(128)} %constant.224.clone.1..sunk.1, s32[]{:T(128)} %constant.224.clone.1..sunk.1) | dynamic-update-slice | bytes 1572868 | tf_op jit(solution)/shard_map/jvp()/while/body/jit(dynamic_update_index_in_dim)/dynamic_update_slice | solution.py:119
  358.7 17.9 %dynamic_update_slice.185 = f32[4,256,12,64]{1,0,3,2:T(4,128)} dynamic-update-slice(f32[4,256,12,64]{1,0,3,2:T(4,128)} %get-tuple-element.2287, f32[1,256,12,64]{1,0,3,2:T(1,128)S(1)} %copy.412, s32[]{:T(128)} %get-tuple-element.2284, s32[]{:T(128)} %constant.224.clone.1..sunk.1, s32[]{:T(128)} %constant.224.clone.1..sunk.1, s32[]{:T(128)} %constant.224.clone.1..sunk.1) | dynamic-update-slice | bytes 1572868 | tf_op jit(solution)/shard_map/jvp()/while/body/jit(dynamic_update_index_in_dim)/dynamic_update_slice | solution.py:119
  389.6 5.5 multiply_reduce_fusion.16
  395.1 11.6 psum.105
  406.8 8.5 multiply_reduce_fusion.13
  415.3 8.3 psum.106
  423.6 8.0 multiply_reduce_fusion.14
  442.1 248.1 %while.101 = (s32[]{:T(128)}, f32[12,64,128]{2,1,0:T(8,128)}, f32[4,256,12,64]{1,0,3,2:T(4,128)}, f32[4,256,12]{1,0,2:T(4,128)}, f32[4,256,12]{1,0,2:T(4,128)}, ...) while((s32[]{:T(128)}, f32[12,64,128]{2,1,0:T(8,128)}, ...), condition=%wide.region_26.28_spmd.clone, body=%wide.region_14.27_spmd.clone.sunk | while | flops 3038993408 | bytes 29344420 | solution.py:94
  461.6 5.2 fusion.315
  482.4 17.9 %dynamic_update_slice.196 = f32[4,256,12,64]{1,0,3,2:T(4,128)} dynamic-update-slice(f32[4,256,12,64]{1,0,3,2:T(4,128)} %get-tuple-element.2338, f32[1,256,12,64]{1,0,3,2:T(1,128)S(1)} %copy.425, s32[]{:T(128)S(6)} %sub.343, s32[]{:T(128)} %constant.224.clone.1..sunk.3, s32[]{:T(128)} %constant.224.clone.1..sunk.3, s32[]{:T(128)} %constant.224.clone.1..sunk.3) | dynamic-update-slice | bytes 1572868 | tf_op jit(solution)/shard_map/transpose(jvp())/while/body/jit(dynamic_update_index_in_dim)/dynamic_update_slice | solution.py:119
  523.8 5.2 fusion.315
  544.5 17.9 %dynamic_update_slice.196 = f32[4,256,12,64]{1,0,3,2:T(4,128)} dynamic-update-slice(f32[4,256,12,64]{1,0,3,2:T(4,128)} %get-tuple-element.2338, f32[1,256,12,64]{1,0,3,2:T(1,128)S(1)} %copy.425, s32[]{:T(128)S(6)} %sub.343, s32[]{:T(128)} %constant.224.clone.1..sunk.3, s32[]{:T(128)} %constant.224.clone.1..sunk.3, s32[]{:T(128)} %constant.224.clone.1..sunk.3) | dynamic-update-slice | bytes 1572868 | tf_op jit(solution)/shard_map/transpose(jvp())/while/body/jit(dynamic_update_index_in_dim)/dynamic_update_slice | solution.py:119
  586.0 5.2 fusion.315
  606.7 17.9 %dynamic_update_slice.196 = f32[4,256,12,64]{1,0,3,2:T(4,128)} dynamic-update-slice(f32[4,256,12,64]{1,0,3,2:T(4,128)} %get-tuple-element.2338, f32[1,256,12,64]{1,0,3,2:T(1,128)S(1)} %copy.425, s32[]{:T(128)S(6)} %sub.343, s32[]{:T(128)} %constant.224.clone.1..sunk.3, s32[]{:T(128)} %constant.224.clone.1..sunk.3, s32[]{:T(128)} %constant.224.clone.1..sunk.3) | dynamic-update-slice | bytes 1572868 | tf_op jit(solution)/shard_map/transpose(jvp())/while/body/jit(dynamic_update_index_in_dim)/dynamic_update_slice | solution.py:119
  648.2 5.2 fusion.315
  668.9 17.9 %dynamic_update_slice.196 = f32[4,256,12,64]{1,0,3,2:T(4,128)} dynamic-update-slice(f32[4,256,12,64]{1,0,3,2:T(4,128)} %get-tuple-element.2338, f32[1,256,12,64]{1,0,3,2:T(1,128)S(1)} %copy.425, s32[]{:T(128)S(6)} %sub.343, s32[]{:T(128)} %constant.224.clone.1..sunk.3, s32[]{:T(128)} %constant.224.clone.1..sunk.3, s32[]{:T(128)} %constant.224.clone.1..sunk.3) | dynamic-update-slice | bytes 1572868 | tf_op jit(solution)/shard_map/transpose(jvp())/while/body/jit(dynamic_update_index_in_dim)/dynamic_update_slice | solution.py:119
  716.7 187.6 %while.98 = (s32[]{:T(128)}, f32[12,64,128]{2,1,0:T(8,128)S(1)}, f32[4,256,12,64]{1,0,3,2:T(4,128)}, f32[4,256,12]{2,1,0:T(8,128)}, f32[4,256,12]{1,0,2:T(4,128)...) while((s32[]{:T(128)}, f32[12,64,128]{2,1,0:T(8,128)S(1)}, ...), condition=%wide.region_32.34_spmd, body=%wide.region_27.33_spmd.sunk | while | flops 605279296 | bytes 15451689 | solution.py:119
  745.7 17.9 %dynamic_update_slice.182 = f32[4,256,12,64]{1,0,3,2:T(4,128)} dynamic-update-slice(f32[4,256,12,64]{1,0,3,2:T(4,128)} %get-tuple-element.2400, f32[1,256,12,64]{1,0,3,2:T(1,128)S(1)} %copy.399, s32[]{:T(128)S(6)} %sub.329, s32[]{:T(128)} %constant.224.clone.1..sunk, s32[]{:T(128)} %constant.224.clone.1..sunk, s32[]{:T(128)} %constant.224.clone.1..sunk) | dynamic-update-slice | bytes 1572868 | tf_op jit(solution)/shard_map/transpose(jvp())/while/body/jit(dynamic_update_index_in_dim)/dynamic_update_slice | solution.py:119
  792.6 17.9 %dynamic_update_slice.182 = f32[4,256,12,64]{1,0,3,2:T(4,128)} dynamic-update-slice(f32[4,256,12,64]{1,0,3,2:T(4,128)} %get-tuple-element.2400, f32[1,256,12,64]{1,0,3,2:T(1,128)S(1)} %copy.399, s32[]{:T(128)S(6)} %sub.329, s32[]{:T(128)} %constant.224.clone.1..sunk, s32[]{:T(128)} %constant.224.clone.1..sunk, s32[]{:T(128)} %constant.224.clone.1..sunk) | dynamic-update-slice | bytes 1572868 | tf_op jit(solution)/shard_map/transpose(jvp())/while/body/jit(dynamic_update_index_in_dim)/dynamic_update_slice | solution.py:119
  839.5 17.9 %dynamic_update_slice.182 = f32[4,256,12,64]{1,0,3,2:T(4,128)} dynamic-update-slice(f32[4,256,12,64]{1,0,3,2:T(4,128)} %get-tuple-element.2400, f32[1,256,12,64]{1,0,3,2:T(1,128)S(1)} %copy.399, s32[]{:T(128)S(6)} %sub.329, s32[]{:T(128)} %constant.224.clone.1..sunk, s32[]{:T(128)} %constant.224.clone.1..sunk, s32[]{:T(128)} %constant.224.clone.1..sunk) | dynamic-update-slice | bytes 1572868 | tf_op jit(solution)/shard_map/transpose(jvp())/while/body/jit(dynamic_update_index_in_dim)/dynamic_update_slice | solution.py:119
  886.4 17.9 %dynamic_update_slice.182 = f32[4,256,12,64]{1,0,3,2:T(4,128)} dynamic-update-slice(f32[4,256,12,64]{1,0,3,2:T(4,128)} %get-tuple-element.2400, f32[1,256,12,64]{1,0,3,2:T(1,128)S(1)} %copy.399, s32[]{:T(128)S(6)} %sub.329, s32[]{:T(128)} %constant.224.clone.1..sunk, s32[]{:T(128)} %constant.224.clone.1..sunk, s32[]{:T(128)} %constant.224.clone.1..sunk) | dynamic-update-slice | bytes 1572868 | tf_op jit(solution)/shard_map/transpose(jvp())/while/body/jit(dynamic_update_index_in_dim)/dynamic_update_slice | solution.py:119
  923.8 9.2 multiply_reduce_fusion.8
  936.0 5.9 slice_multiply_fusion.5
  943.1 8.0 fusion.171
  967.9 5.5 fusion.118
  979.3 9.5 fusion.132
  988.8 14.9 copy.232
  1005.6 7.1 fusion.133
  1018.3 6.3 fusion.169
  1025.5 6.8 fusion.168
  1041.2 139.6 %all-reduce.66.cloned.1.call-done = f32[1536,2,768]{2,1,0:T(2,128)} async-done(((f32[1536,2,768]{2,1,0:T(2,128)}), f32[1536,2,768]{2,1,0:T(2,128)}) %all-reduce.66.cloned.1.call-update) | async-done | bytes 9437200
  1183.5 110.5 %reduce-scatter.10.cloned.1.call-done = f32[256,1536]{1,0:T(8,128)} async-done(((f32[1024,1536]{1,0:T(8,128)}), f32[256,1536]{1,0:T(8,128)}) %reduce-scatter.10.cloned.1.call-update) | async-done | bytes 1572880 | tf_op jit(solution)/shard_map/reduce_scatter | solution.py:403
  1295.9 25.4 %all-reduce.59 = (f32[1536]{0:T(1024)S(1)}, f32[4,768]{1,0:T(4,128)}, f32[768]{0:T(1024)}, f32[4,256]{1,0:T(4,128)S(1)}, f32[256]{0:T(256)S(1)}, /*index=5*/f32[...) all-reduce(f32[1536]{0:T(1024)S(1)} %get-tuple-element.1399, ...), channel_id=1, replica_groups=mesh['dp'=4,'row'=2,'col'=4] {'dp','row'}, use_global_device_ids=true, to_apply=%region_36.38 | all-reduce | flops 7460 | bytes 59680 | tf_op jit(solution)/shard_map/psum | solution.py:424
  1321.4 21.3 %all-reduce.60 = (f32[1536]{0:T(1024)}, f32[4,256]{1,0:T(4,128)}, f32[256]{0:T(256)}) all-reduce(f32[1536]{0:T(1024)S(1)} %get-tuple-element.1537, f32[4,256]{1,0:T(4,128)S(1)} %get-tuple-element.1540, f32[256]{0:T(256)S(1)} %get-tuple-element.1541), channel_id=1, replica_groups=mesh['dp'=4,'row'=2,'col'=4] {'col'}, use_global_device_ids=true, to_apply=%region_37.39 | all-reduce | flops 2816 | bytes 22528 | tf_op jit(solution)/shard_map/psum | solution.py:438
  1342.7 65.4 %reduce-scatter.8.cloned.1.call-done = f32[256,1536]{1,0:T(8,128)} async-done(((f32[1024,1536]{1,0:T(8,128)}), f32[256,1536]{1,0:T(8,128)}) %reduce-scatter.8.cloned.1.call-update) | async-done | bytes 1572880 | tf_op jit(solution)/shard_map/reduce_scatter | solution.py:340
  1411.3 34.6 %all-reduce.64.cloned.1.call-done = f32[192,256]{1,0:T(8,128)} async-done(((f32[192,256]{1,0:T(8,128)}), f32[192,256]{1,0:T(8,128)}) %all-reduce.64.cloned.1.call-update) | async-done | bytes 196624 | tf_op jit(solution)/shard_map/psum | solution.py:438
  1445.8 57.5 %reduce-scatter.14.cloned.1.call-done = f32[768,192]{0,1:T(8,128)} async-done(((f32[768,1536]{0,1:T(8,128)}), f32[768,192]{0,1:T(8,128)}) %reduce-scatter.14.cloned.1.call-update) | async-done | bytes 589840 | tf_op jit(solution)/shard_map/reduce_scatter | solution.py:247
  (1121 shorter events, 572.4 us)
Async XLA Ops:
  7.2 41.1 %copy-start.158 = (f32[12]{0:T(128)S(1)}, f32[12]{0:T(128)}, u32[]{:S(2)}) copy-start(f32[12]{0:T(128)} %param.36) | copy-start | bytes 148
  7.2 41.1 %copy-start.157 = (f32[12]{0:T(128)S(1)}, f32[12]{0:T(128)}, u32[]{:S(2)}) copy-start(f32[12]{0:T(128)} %param.37) | copy-start | bytes 148
  7.3 71.2 %all-gather.7.cloned.1.call-start = ((), (), s32[]{:S(2)}) async-start(), calls=%async_computation.5 | async-start | bytes 3932160 | tf_op jit(solution)/shard_map/all_gather | solution.py:276
  12.1 105.7 %all-gather.9.cloned.1.call-start = ((), (), s32[]{:S(2)}) async-start(), calls=%async_computation.6 | async-start | bytes 5308416 | tf_op jit(solution)/shard_map/all_gather | solution.py:281
  12.9 393.9 %all-gather.11.cloned.1.call-start = ((), (), s32[]{:S(2)}) async-start(), calls=%async_computation.7 | async-start | bytes 2654208 | tf_op jit(solution)/shard_map/all_gather | solution.py:339
  13.6 393.2 %all-gather.13.cloned.1.call-start = ((), (), s32[]{:S(2)}) async-start(), calls=%async_computation.9 | async-start | bytes 3932160 | tf_op jit(solution)/shard_map/all_gather | solution.py:278
  26.4 22.1 %collective-permute-start.1 = (f32[3]{0:T(128)S(1)}, f32[3]{0:T(128)S(1)}, u32[]{:S(2)}, u32[]{:S(2)}) collective-permute-start(f32[3]{0:T(128)S(1)} %slice_convert_fusion.2), channel_id=1, source_target_pairs={{0,4},{1,5},{2,6},{3,7},{8,12},{9,13},{10,14},{11,15},{16,20},{17,... | collective-permute-start | bytes 44 | tf_op jit(solution)/shard_map/ppermute | solution.py:19
  27.7 996.9 %reduce-scatter.12.cloned.1.call-start = ((), (), s32[]{:S(2)}) async-start(), calls=%async_computation.11 | async-start | bytes 1769472 | tf_op jit(solution)/shard_map/reduce_scatter | solution.py:410
  28.4 188.5 %copy-start.98 = (f32[768]{0:T(1024)}, f32[768]{0:T(1024)S(1)}, u32[]{:S(2)}) copy-start(f32[768]{0:T(1024)S(1)} %get-tuple-element.1410) | copy-start | bytes 9220
  28.5 188.5 %copy-start.101 = (f32[768]{0:T(1024)}, f32[768]{0:T(1024)S(1)}, u32[]{:S(2)}) copy-start(f32[768]{0:T(1024)S(1)} %get-tuple-element.1408) | copy-start | bytes 9220
  28.5 188.5 %copy-start.103 = (f32[768]{0:T(1024)}, f32[768]{0:T(1024)S(1)}, u32[]{:S(2)}) copy-start(f32[768]{0:T(1024)S(1)} %get-tuple-element.1407) | copy-start | bytes 9220
  28.5 188.5 %copy-start.107 = (f32[768]{0:T(1024)}, f32[768]{0:T(1024)S(1)}, u32[]{:S(2)}) copy-start(f32[768]{0:T(1024)S(1)} %get-tuple-element.1409) | copy-start | bytes 9220
  38.9 42.6 %copy-start.53 = (bf16[1536,256]{1,0:T(8,128)(2,1)}, bf16[1536,256]{1,0:T(8,128)(2,1)S(1)}, u32[]{:S(2)}) copy-start(bf16[1536,256]{1,0:T(8,128)(2,1)S(1)} %all_gather.28) | copy-start | bytes 2359300
  38.9 50.3 %copy-start.111 = (f32[1,256]{1,0:T(1,128)}, f32[1,256]{1,0:T(1,128)S(1)}, u32[]{:S(2)}) copy-start(f32[1,256]{1,0:T(1,128)S(1)} %get-tuple-element.1696) | copy-start | bytes 3076
  38.9 50.3 %copy-start.113 = (f32[1,256]{1,0:T(1,128)}, f32[1,256]{1,0:T(1,128)S(1)}, u32[]{:S(2)}) copy-start(f32[1,256]{1,0:T(1,128)S(1)} %get-tuple-element.1698) | copy-start | bytes 3076
  38.9 50.3 %copy-start.115 = (f32[1,256]{1,0:T(1,128)}, f32[1,256]{1,0:T(1,128)S(1)}, u32[]{:S(2)}) copy-start(f32[1,256]{1,0:T(1,128)S(1)} %get-tuple-element.1695) | copy-start | bytes 3076
  38.9 50.3 %copy-start.127 = (f32[1,256]{1,0:T(1,128)}, f32[1,256]{1,0:T(1,128)S(1)}, u32[]{:S(2)}) copy-start(f32[1,256]{1,0:T(1,128)S(1)} %get-tuple-element.1697) | copy-start | bytes 3076
  48.3 34.7 %copy-start.71 = (bf16[1536,12]{0,1:T(8,128)(2,1)}, bf16[1536,12]{0,1:T(8,128)(2,1)S(1)}, u32[]{:S(2)}) copy-start(bf16[1536,12]{0,1:T(8,128)(2,1)S(1)} %reshape.824) | copy-start | bytes 110596
  48.5 375.1 %copy-start.109 = (f32[768]{0:T(1024)}, f32[768]{0:T(1024)S(1)}, u32[]{:S(2)}) copy-start(f32[768]{0:T(1024)S(1)} %mul.1402) | copy-start | bytes 9220
  49.4 91.0 %copy-start.83 = (f32[1027]{0:T(1024)}, f32[1027]{0:T(1024)S(1)}, u32[]{:S(2)}) copy-start(f32[1027]{0:T(1024)S(1)} %get-tuple-element.1688) | copy-start | bytes 12328
  49.4 91.0 %copy-start.85 = (f32[1027]{0:T(1024)}, f32[1027]{0:T(1024)S(1)}, u32[]{:S(2)}) copy-start(f32[1027]{0:T(1024)S(1)} %get-tuple-element.1686) | copy-start | bytes 12328
  49.4 91.0 %copy-start.87 = (f32[1027]{0:T(1024)}, f32[1027]{0:T(1024)S(1)}, u32[]{:S(2)}) copy-start(f32[1027]{0:T(1024)S(1)} %get-tuple-element.1687) | copy-start | bytes 12328
  49.5 167.5 %copy-start.77 = (f32[1027]{0:T(1024)}, f32[1027]{0:T(1024)S(1)}, u32[]{:S(2)}) copy-start(f32[1027]{0:T(1024)S(1)} %get-tuple-element.1683) | copy-start | bytes 12328
  49.5 167.5 %copy-start.79 = (f32[1027]{0:T(1024)}, f32[1027]{0:T(1024)S(1)}, u32[]{:S(2)}) copy-start(f32[1027]{0:T(1024)S(1)} %get-tuple-element.1681) | copy-start | bytes 12328
  49.5 167.5 %copy-start.81 = (f32[1027]{0:T(1024)}, f32[1027]{0:T(1024)S(1)}, u32[]{:S(2)}) copy-start(f32[1027]{0:T(1024)S(1)} %get-tuple-element.1682) | copy-start | bytes 12328
  81.5 3.4 collective-permute-start.3
  90.6 38.2 %copy-start.44 = (f32[1027,256]{1,0:T(8,128)}, f32[1027,256]{1,0:T(8,128)S(1)}, u32[]{:S(2)}) copy-start(f32[1027,256]{1,0:T(8,128)S(1)} %get-tuple-element.1596) | copy-start | bytes 3154948
  126.5 7.1 collective-permute-start.2
  133.6 83.4 %copy-start.74 = (f32[3,768]{1,0:T(4,128)}, f32[3,768]{1,0:T(4,128)S(1)}, u32[]{:S(2)}) copy-start(f32[3,768]{1,0:T(4,128)S(1)} %collective-permute-done.2) | copy-start | bytes 27652
  215.1 22.4 %collective-permute-start = (f32[12,64,128]{2,1,0:T(8,128)}, f32[12,64,128]{2,1,0:T(8,128)S(1)}, u32[]{:S(2)}, u32[]{:S(2)}) collective-permute-start(f32[12,64,128]{2,1,0:T(8,128)} %get-tuple-element.907), channel_id=1, source_target_pairs={{0,4},{1,5},{2,6},{3,7},{8,12},{9,13},{10,14},{11,15},{16,20},{17,... | collective-permute-start | bytes 1179656 | tf_op jit(solution)/shard_map/ppermute | solution.py:19
  690.3 21.8 %collective-permute-start.4 = (f32[12,64,128]{2,1,0:T(8,128)}, f32[12,64,128]{2,1,0:T(8,128)S(1)}, u32[]{:S(2)}, u32[]{:S(2)}) collective-permute-start(f32[12,64,128]{2,1,0:T(8,128)} %get-tuple-element.912), channel_id=1, source_target_pairs={{4,0},{5,1},{6,2},{7,3},{12,8},{13,9},{14,10},{15,11},{20,16},{21,... | collective-permute-start | bytes 1179656 | tf_op jit(solution)/shard_map/ppermute | solution.py:19
  716.6 187.6 %copy-start.80 = (f32[1027]{0:T(1024)S(1)}, f32[1027]{0:T(1024)}, u32[]{:S(2)}) copy-start(f32[1027]{0:T(1024)} %copy-done.79) | copy-start | bytes 12328
  716.6 187.6 %copy-start.82 = (f32[1027]{0:T(1024)S(1)}, f32[1027]{0:T(1024)}, u32[]{:S(2)}) copy-start(f32[1027]{0:T(1024)} %copy-done.81) | copy-start | bytes 12328
  916.3 42.6 %collective-permute-start.6 = (f32[3,256]{1,0:T(4,128)}, f32[3,256]{1,0:T(4,128)}, u32[]{:S(2)}, u32[]{:S(2)}) collective-permute-start(f32[3,256]{1,0:T(4,128)} %slice.380), channel_id=1, source_target_pairs={{4,0},{5,1},{6,2},{7,3},{12,8},{13,9},{14,10},{15,11},{20,16},{21,... | collective-permute-start | bytes 9224 | tf_op jit(solution)/shard_map/ppermute | solution.py:19
  953.4 25.2 %collective-permute-start.5 = (f32[3,768]{1,0:T(4,128)}, f32[3,768]{1,0:T(4,128)}, u32[]{:S(2)}, u32[]{:S(2)}) collective-permute-start(f32[3,768]{1,0:T(4,128)} %slice.375), channel_id=1, source_target_pairs={{4,0},{5,1},{6,2},{7,3},{12,8},{13,9},{14,10},{15,11},{20,16},{21,... | collective-permute-start | bytes 27656 | tf_op jit(solution)/shard_map/ppermute | solution.py:19
  961.9 77.7 %reduce-scatter.16.cloned.1.call-start = ((), (), s32[]{:S(2)}) async-start(), calls=%async_computation.14 | async-start | bytes 884736
  978.5 202.3 %all-reduce.66.cloned.1.call-start = ((), (), s32[]{:S(2)}) async-start(), calls=%async_computation.15 | async-start | bytes 18874368
  1003.7 290.3 %reduce-scatter.10.cloned.1.call-start = ((), (), s32[]{:S(2)}) async-start(), calls=%async_computation.10 | async-start | bytes 7864320 | tf_op jit(solution)/shard_map/reduce_scatter | solution.py:403
  1016.4 391.7 %reduce-scatter.8.cloned.1.call-start = ((), (), s32[]{:S(2)}) async-start(), calls=%async_computation.8 | async-start | bytes 7864320 | tf_op jit(solution)/shard_map/reduce_scatter | solution.py:340
  1024.6 421.2 %all-reduce.64.cloned.1.call-start = ((), (), s32[]{:S(2)}) async-start(), calls=%async_computation.12 | async-start | bytes 393216 | tf_op jit(solution)/shard_map/psum | solution.py:438
  1025.2 478.1 %reduce-scatter.14.cloned.1.call-start = ((), (), s32[]{:S(2)}) async-start(), calls=%async_computation.13 | async-start | bytes 5308416 | tf_op jit(solution)/shard_map/reduce_scatter | solution.py:247
  1032.5 261.5 %copy-start.29 = (bf16[256,1536]{1,0:T(8,128)(2,1)S(1)}, bf16[256,1536]{1,0:T(8,128)(2,1)}, u32[]{:S(2)}) copy-start(bf16[256,1536]{1,0:T(8,128)(2,1)} %param.25) | copy-start | bytes 2359300
  1032.5 261.5 %copy-start.106 = (f32[1536]{0:T(1024)S(1)}, f32[1536]{0:T(1024)}, u32[]{:S(2)}) copy-start(f32[1536]{0:T(1024)} %param.27) | copy-start | bytes 18436
  1032.5 261.5 %copy-start.126 = (f32[256]{0:T(256)S(1)}, f32[256]{0:T(256)}, u32[]{:S(2)}) copy-start(f32[256]{0:T(256)} %copy-done.125) | copy-start | bytes 3076
  1032.6 263.4 %copy-start.149 = (f32[768]{0:T(1024)S(1)}, f32[768]{0:T(1024)}, u32[]{:S(2)}) copy-start(f32[768]{0:T(1024)} %get-tuple-element.1393) | copy-start | bytes 9220
  1032.6 375.6 %copy-start.52 = (bf16[256,1536]{1,0:T(8,128)(2,1)S(1)}, bf16[256,1536]{1,0:T(8,128)(2,1)}, u32[]{:S(2)}) copy-start(bf16[256,1536]{1,0:T(8,128)(2,1)} %param.40) | copy-start | bytes 2359300
  1032.6 375.6 %copy-start.139 = (f32[256]{0:T(256)S(1)}, f32[256]{0:T(256)}, u32[]{:S(2)}) copy-start(f32[256]{0:T(256)} %get-tuple-element.1699) | copy-start | bytes 3076
  1294.0 114.2 %copy-start.47 = (f32[256,1536]{1,0:T(8,128)S(1)}, f32[256,1536]{1,0:T(8,128)}, u32[]{:S(2)}) copy-start(f32[256,1536]{1,0:T(8,128)} %reduce-scatter.10.cloned.1.call-done) | copy-start | bytes 4718596
  (171 other events, 967.9 us)
Sparse Core Ops, SparseCore 0:
  12.2 66.1 all-gather.6
  80.3 37.4 all-gather.8
  119.7 28.8 all-gather.10
  150.0 63.4 all-gather.12
  962.0 39.0 reduce-scatter.11
  1004.6 34.9 reduce-scatter.15
  1043.1 137.6 all-reduce.65
  1183.1 110.8 reduce-scatter.9
  1296.3 111.7 reduce-scatter.7
  1410.3 35.4 all-reduce.63
  1449.8 53.4 reduce-scatter.13
where the time goes:
time: 1530 us; the launch traced here: 1510 us
  local copies, waits for them, and re-layouts  498 us (33%)
  waiting for transfers between devices  471 us (31%)
  other arithmetic  207 us (14%)
  matrix products  190 us (12%)
  blocking collectives  99 us (6%)
  loops' own time  18.3 us (1%)
  between operations  16.8 us (1%)
    dynamic_update_slice x68, local copies, waits for them, and re-layouts, closing_scan(): lax.scan(closing_advance, (start_state, start_prev), blocks)  253 us
    unnamed x13, waiting for transfers between devices  146 us
    reduce_scatter x1, waiting for transfers between devices, per_device(): lax.psum_scatter(partial_terms, 'col', scatter_dimension=0, tiled=True)  111 us
    dynamic_slice x52, local copies, waits for them, and re-layouts, closing_scan(): lax.scan(closing_advance, (start_state, start_prev), blocks)  70.4 us
    reduce_scatter x1, waiting for transfers between devices, per_device(): lax.psum_scatter(jnp.dot(gated_normed, out_full, preferred_element_type=j...  65.4 us
    reduce_scatter x1, waiting for transfers between devices, reduce_output_grads(): lax.psum_scatter(part_out, ('dp', 'row'), scatter_dimension=1, tiled=True)  57.5 us
    dot_general x12, matrix products, span_advance(): output = jnp.einsum('hts,shp->thp', mixing, x_block, precision=HIGH)  56.4 us
    unnamed x325, local copies, waits for them, and re-layouts  47.1 us
  transfers between devices with their start and end apart: 18, of which 8 were waited for; matrix products, arithmetic and copies ran while one was open for 26% of the time, Pallas kernels for 0%

commit v1 on v0

v1 whole, which is shorter than its diff:
```python
import functools
import jax, jax.numpy as jnp
from jax import lax
from jax.experimental import pallas as pl
from jax.experimental.pallas import tpu as pltpu
from jax.sharding import PartitionSpec as P

F32, BF16 = jnp.float32, jnp.bfloat16
HIGH = lax.Precision.HIGHEST
SPAN = 256
HALO = 16
EPS = 1e-5


def nn(a, b):
    return lax.dot_general(a, b, (((1,), (0,)), ((), ())), preferred_element_type=F32)


def nt(a, b):
    return lax.dot_general(a, b, (((1,), (1,)), ((), ())), preferred_element_type=F32)


def tn(a, b):
    return lax.dot_general(a, b, (((0,), (0,)), ((), ())), preferred_element_type=F32)


def iota(shape, axis):
    return lax.broadcasted_iota(jnp.int32, shape, axis)


def split_dot(a, b01):
    hi = a.astype(BF16)
    lo = (a - hi.astype(F32)).astype(BF16)
    return nn(hi, b01) + nn(lo, b01)


def sigmoid(v):
    return 1.0 / (1.0 + jnp.exp(-v))


def softplus(v):
    return jnp.maximum(v, 0.0) + jnp.log1p(jnp.exp(-jnp.abs(v)))


def chunk_links(segc, halo):
    ext = jnp.concatenate([halo[HALO - 8 :], segc], axis=0)
    length = segc.shape[0]
    return [(ext[8 - j : 8 - j + length] == segc).astype(F32) for j in range(1, 4)]


def conv_tile(cur, halo, links, taps, sl):
    v = jnp.concatenate([halo[HALO - 8 :, sl].astype(F32), cur[:, sl].astype(F32)], axis=0)
    length = cur.shape[0]
    shifted = [v[8 - j : 8 - j + length] * links[j - 1] for j in range(1, 4)]
    pre = taps[4:5, sl] + taps[3:4, sl] * v[8:]
    for j in range(1, 4):
        pre = pre + taps[3 - j : 4 - j, sl] * shifted[j - 1]
    return pre, [v[8:]] + shifted


def pick(lo, cols, h):
    return jnp.where(lo, cols[:, h : h + 1], cols[:, h + 1 : h + 2])


def forward_kernel(
    inner, inner_halo, shared, shared_halo, step_raw, segc, segc_halo, segr, taps, taps_s, heads,
    y_out, x_out, bc_out, dt_out, c_out, ct_out, dec_out, enter_out, final_out, state, total,
):
    k = pl.program_id(0)
    length, width = inner.shape
    pairs = width // 128
    state_dim = state.shape[0]

    @pl.when(k == 0)
    def _():
        state[...] = jnp.zeros_like(state)
        total[...] = jnp.zeros_like(total)

    seg = segc[...]
    seg_halo = segc_halo[...]
    links = chunk_links(seg, seg_halo)
    closing = (seg == seg[length - 1 :]).astype(F32)
    entering = (seg == seg_halo[HALO - 1 :]).astype(F32)
    kept = (seg[length - 1 :] == seg_halo[HALO - 1 :]).astype(F32)
    dt = softplus(step_raw[...] + heads[0:1])
    log_decay = -jnp.exp(heads[1:2]) * dt
    rows, cols = iota((length, length), 0), iota((length, length), 1)
    lower = (rows >= cols).astype(F32)
    c = jnp.dot(lower, log_decay, precision=HIGH, preferred_element_type=F32)
    ct = c.T
    dt_out[...] = dt
    c_out[...] = c
    ct_out[...] = ct[: ct_out.shape[0]]
    whole = c + total[0:1]
    dec_out[...] = jnp.exp(whole) * (seg == heads[7:8, 0:1].astype(jnp.int32)).astype(F32)
    total[0:1] = whole[length - 1 :]
    for half in range(2):
        sl = slice(half * state_dim, (half + 1) * state_dim)
        pre, _ = conv_tile(shared, shared_halo, links, taps_s, sl)
        bc_out[:, sl] = (pre * sigmoid(pre)).astype(BF16)
    b = bc_out[:, :state_dim]
    cc = bc_out[:, state_dim:]
    scores = jnp.where((rows >= cols) & (seg == segr[...]), nt(cc, b), 0.0)
    lo = iota((length, 128), 1) < 64
    enter_out[...] = state[...].astype(BF16)
    for p in range(pairs):
        sl = slice(p * 128, (p + 1) * 128)
        pre, _ = conv_tile(inner, inner_halo, links, taps, sl)
        xp = pre * sigmoid(pre)
        xb = xp.astype(BF16)
        x_out[:, sl] = xb
        xdt = xb.astype(F32) * pick(lo, dt, 2 * p)
        cb = pick(lo, c, 2 * p)
        acc = nn(cc, state[:, sl].astype(BF16)) * (jnp.exp(cb) * entering)
        for a in range(2):
            h = 2 * p + a
            weights = jnp.exp(jnp.minimum(c[:, h : h + 1] - ct[h : h + 1], 0.0)) * scores
            mine = lo if a == 0 else ~lo
            acc = acc + nn(weights.astype(BF16), jnp.where(mine, xdt, 0.0).astype(BF16))
        y_out[:, sl] = acc
        last = cb[length - 1 :]
        leaving = jnp.exp(last - cb) * closing * xdt
        state[:, sl] = state[:, sl] * (jnp.exp(last) * kept) + tn(b, leaving.astype(BF16))

    @pl.when(k == pl.num_programs(0) - 1)
    def _():
        final_out[...] = state[...]


def halo_index(chunk, chunks):
    return jnp.where(chunk == 0, chunks * (SPAN // HALO), chunk * (SPAN // HALO) - 1)


def run_forward(both_ext, shared_ext, step_raw, segc_ext, segr, taps, taps_s, heads):
    width = taps.shape[1]
    scols = taps_s.shape[1]
    length = segr.shape[1]
    chunks = length // SPAN
    nrow = -(-heads.shape[1] // 8) * 0 + 16
    row = lambda k: (k, 0)
    halo = lambda col: (lambda k: (halo_index(k, chunks), col))
    fixed = lambda k: (0, 0)
    S = jax.ShapeDtypeStruct
    return pl.pallas_call(
        forward_kernel,
        grid=(chunks,),
        in_specs=[
            pl.BlockSpec((SPAN, width), lambda k: (k, 1)),
            pl.BlockSpec((HALO, width), halo(1)),
            pl.BlockSpec((SPAN, scols), row),
            pl.BlockSpec((HALO, scols), halo(0)),
            pl.BlockSpec((SPAN, 128), row),
            pl.BlockSpec((SPAN, 1), row),
            pl.BlockSpec((HALO, 1), halo(0)),
            pl.BlockSpec((1, SPAN), lambda k: (0, k)),
            pl.BlockSpec(taps.shape, fixed),
            pl.BlockSpec(taps_s.shape, fixed),
            pl.BlockSpec(heads.shape, fixed),
        ],
        out_specs=[
            pl.BlockSpec((SPAN, width), row),
            pl.BlockSpec((SPAN, width), row),
            pl.BlockSpec((SPAN, scols), row),
            pl.BlockSpec((SPAN, 128), row),
            pl.BlockSpec((SPAN, 128), row),
            pl.BlockSpec((nrow, SPAN), lambda k: (0, k)),
            pl.BlockSpec((SPAN, 128), row),
            pl.BlockSpec((None, scols // 2, width), lambda k: (k, 0, 0)),
            pl.BlockSpec((scols // 2, width), fixed),
        ],
        out_shape=[
            S((length, width), F32),
            S((length, width), BF16),
            S((length, scols), BF16),
            S((length, 128), F32),
            S((length, 128), F32),
            S((nrow, length), F32),
            S((length, 128), F32),
            S((chunks, scols // 2, width), BF16),
            S((scols // 2, width), F32),
        ],
        scratch_shapes=[pltpu.VMEM((scols // 2, width), F32), pltpu.VMEM((8, 128), F32)],
        name="scan_forward",
    )(both_ext, both_ext, shared_ext, shared_ext, step_raw, segc_ext, segc_ext, segr, taps, taps_s, heads)


def row_sums(value):
    hi = value.astype(BF16)
    lo = (value - hi.astype(F32)).astype(BF16)
    ones = jnp.ones((8, value.shape[1]), BF16)
    return nt(ones, hi) + nt(ones, lo)


def gate_kernel(y, x, bc, dec, start, gate, back, taps, ssd_out, sums_out):
    length, width = x.shape
    state_dim = start.shape[0]
    cc = bc[:, state_dim:]
    lo = iota((length, 128), 1) < 64
    squares = jnp.zeros((length, 128), F32)
    inner = jnp.zeros((length, 128), F32)
    for p in range(width // 128):
        sl = slice(p * 128, (p + 1) * 128)
        corr = nn(cc, start[:, sl].astype(BF16)) * pick(lo, dec, 2 * p)
        ssd = y[:, sl] + corr + taps[6:7, sl] * x[:, sl].astype(F32)
        ssd_out[:, sl] = ssd
        g = gate[:, sl].astype(F32)
        gated = ssd * (g * sigmoid(g))
        squares = squares + gated * gated
        inner = inner + back[:, sl].astype(F32) * taps[5:6, sl] * gated
    sums_out[0:8] = row_sums(squares)
    sums_out[8:16] = row_sums(inner)


def run_gate(y, x, bc, dec, start, both_ext, back, taps):
    length, width = x.shape
    row = lambda k: (k, 0)
    fixed = lambda k: (0, 0)
    S = jax.ShapeDtypeStruct
    return pl.pallas_call(
        gate_kernel,
        grid=(length // SPAN,),
        in_specs=[
            pl.BlockSpec((SPAN, width), row),
            pl.BlockSpec((SPAN, width), row),
            pl.BlockSpec((SPAN, bc.shape[1]), row),
            pl.BlockSpec((SPAN, 128), row),
            pl.BlockSpec(start.shape, fixed),
            pl.BlockSpec((SPAN, width), row),
            pl.BlockSpec((SPAN, width), row),
            pl.BlockSpec(taps.shape, fixed),
        ],
        out_specs=[pl.BlockSpec((SPAN, width), row), pl.BlockSpec((16, SPAN), lambda k: (0, k))],
        out_shape=[S((length, width), F32), S((16, length), F32)],
        name="gate_sums",
    )(y, x, bc, dec, start, both_ext, back, taps)


def columns(row):
    return jnp.broadcast_to(row, (128, row.shape[1])).T


def back_kernel(
    full_width, ssd, x, bc, dec, gate, back, sums, taps,
    normed_out, dy_out, ggate_out, row_out, colsum_out, dstart_out,
):
    length, width = x.shape
    state_dim = dstart_out.shape[0]

    @pl.when(pl.program_id(0) == 0)
    def _():
        colsum_out[...] = jnp.zeros_like(colsum_out)
        dstart_out[...] = jnp.zeros_like(dstart_out)

    cc = bc[:, state_dim:]
    lo = iota((length, 128), 1) < 64
    rescale = columns(lax.rsqrt(sums[0:1] / full_width + EPS))
    pull = columns(sums[1:2]) * (rescale * rescale * rescale / full_width)
    rowterm = jnp.zeros((length, 128), F32)
    for p in range(width // 128):
        sl = slice(p * 128, (p + 1) * 128)
        s_ssd = ssd[:, sl]
        xp = x[:, sl].astype(F32)
        g = gate[:, sl].astype(F32)
        s = sigmoid(g)
        gated = s_ssd * (g * s)
        bk = back[:, sl].astype(F32)
        gain = taps[5:6, sl]
        normed_out[:, sl] = (gated * rescale * gain).astype(BF16)
        gg = rescale * (bk * gain) - gated * pull
        dy = gg * (g * s)
        dyb = dy.astype(BF16)
        dy_out[:, sl] = dyb
        ggate_out[:, sl] = (gg * s_ssd * s * (1.0 + g * (1.0 - s))).astype(BF16)
        colsum_out[0:1, sl] += jnp.sum(bk * gated * rescale, axis=0, keepdims=True)
        colsum_out[1:2, sl] += jnp.sum(dy * xp, axis=0, keepdims=True)
        dstart_out[:, sl] += tn(cc, (dy * pick(lo, dec, 2 * p)).astype(BF16))
        rowterm = rowterm + split_dot(dyb.astype(F32) * (s_ssd - taps[6:7, sl] * xp), head_map(p))
    row_out[...] = rowterm


def head_map(p):
    lane, head = iota((128, 128), 0), iota((128, 128), 1)
    return (head == 2 * p + lane // 64).astype(BF16)


def run_back(full_width, ssd, x, bc, dec, both_ext, back, sums, taps):
    length, width = x.shape
    row = lambda k: (k, 0)
    fixed = lambda k: (0, 0)
    S = jax.ShapeDtypeStruct
    return pl.pallas_call(
        functools.partial(back_kernel, full_width),
        grid=(length // SPAN,),
        in_specs=[
            pl.BlockSpec((SPAN, width), row),
            pl.BlockSpec((SPAN, width), row),
            pl.BlockSpec((SPAN, bc.shape[1]), row),
            pl.BlockSpec((SPAN, 128), row),
            pl.BlockSpec((SPAN, width), row),
            pl.BlockSpec((SPAN, width), row),
            pl.BlockSpec((sums.shape[0], SPAN), lambda k: (0, k)),
            pl.BlockSpec(taps.shape, fixed),
        ],
        out_specs=[
            pl.BlockSpec((SPAN, width), row),
            pl.BlockSpec((SPAN, width), row),
            pl.BlockSpec((SPAN, width), row),
            pl.BlockSpec((SPAN, 128), row),
            pl.BlockSpec((8, width), fixed),
            pl.BlockSpec((bc.shape[1] // 2, width), fixed),
        ],
        out_shape=[
            S((length, width), BF16),
            S((length, width), BF16),
            S((length, width), BF16),
            S((length, 128), F32),
            S((8, width), F32),
            S((bc.shape[1] // 2, width), F32),
        ],
        name="gated_back",
    )(ssd, x, bc, dec, both_ext, back, sums, taps)


def conv_back(dout, pre, shifts, links, taps, sl, carry, carry_links, par_out):
    length = dout.shape[0]
    s = sigmoid(pre)
    dconv = dout * (s * (1.0 + pre * (1.0 - s)))
    nxt = carry[:, sl]
    grad = taps[3:4, sl] * dconv
    above = jnp.zeros((8, dout.shape[1]), F32)
    par_out[3:4, sl] += jnp.sum(dconv * shifts[0], axis=0, keepdims=True)
    par_out[4:5, sl] += jnp.sum(dconv, axis=0, keepdims=True)
    for j in range(1, 4):
        z = dconv * links[j - 1]
        w = taps[3 - j : 4 - j, sl]
        low = jnp.concatenate([z, nxt * carry_links[:, j - 1 : j]], axis=0)
        grad = grad + w * low[j : j + length]
        high = jnp.concatenate([above * 0.0, z[0:8]], axis=0)
        above = above + w * high[j : j + 8]
        par_out[3 - j : 4 - j, sl] += jnp.sum(dconv * shifts[j], axis=0, keepdims=True)
    carry[:, sl] = dconv[0:8]
    return grad, above


def backward_kernel(
    inner, inner_halo, shared, shared_halo, step_raw, segc, segc_halo, segr, taps, taps_s, heads,
    dy, x, bc, dt_in, c_in, ct_in, dec_halo, enter, start, row_in, dend,
    ginner_out, gshared_out, gstep_out, par_out, par_s_out, par_h_out, edge_out, edge_s_out, last_out, last_s_out,
    dstate, carry, carry_s, carry_links, grads_bc,
):
    i = pl.program_id(0)
    k = pl.num_programs(0) - 1 - i
    length, width = x.shape
    state_dim = dstate.shape[0]

    @pl.when(i == 0)
    def _():
        dstate[...] = dend[...]
        carry[...] = jnp.zeros_like(carry)
        carry_s[...] = jnp.zeros_like(carry_s)
        carry_links[...] = jnp.zeros_like(carry_links)
        par_out[...] = jnp.zeros_like(par_out)
        par_s_out[...] = jnp.zeros_like(par_s_out)
        par_h_out[...] = jnp.zeros_like(par_h_out)

    seg = segc[...]
    seg_halo = segc_halo[...]
    links = chunk_links(seg, seg_halo)
    closing = (seg == seg[length - 1 :]).astype(F32)
    entering = (seg == seg_halo[HALO - 1 :]).astype(F32)
    kept = (seg[length - 1 :] == seg_halo[HALO - 1 :]).astype(F32)
    next_links = carry_links[...]
    dt = dt_in[...]
    c = c_in[...]
    ct = ct_in[...]
    first = (k == 0).astype(F32)
    reach = dec_halo[7:8] * (1.0 - first) + first
    b = bc[:, :state_dim]
    cc = bc[:, state_dim:]
    rows, cols = iota((length, length), 0), iota((length, length), 1)
    allowed = (rows <= cols) & (seg == segr[...])
    scores = jnp.where(allowed, nt(b, cc), 0.0)
    lo = iota((length, 128), 1) < 64
    lo1 = lo[0:1]
    dscores = jnp.zeros((length, length), F32)
    db = jnp.zeros((length, state_dim), F32)
    dc_mat = jnp.zeros((length, state_dim), F32)
    direct = jnp.zeros((length, 128), F32)
    matched = jnp.zeros((length, 128), F32)
    closing_term = jnp.zeros((1, 128), F32)
    for p in range(width // 128):
        sl = slice(p * 128, (p + 1) * 128)
        pre, shifts = conv_tile(inner, inner_halo, links, taps, sl)
        dyb = dy[:, sl]
        dyf = dyb.astype(F32)
        xp = x[:, sl].astype(F32)
        dtb = pick(lo, dt, 2 * p)
        xdt = xp * dtb
        cb = pick(lo, c, 2 * p)
        hm = head_map(p)
        last = cb[length - 1 :]
        entry = enter[:, sl].astype(F32) + start[:, sl] * pick(lo1, reach, 2 * p)
        entryb = entry.astype(BF16)
        ds = dstate[:, sl]
        dsb = ds.astype(BF16)
        leaving = jnp.exp(last - cb) * closing
        bds = nn(b, dsb)
        dxdt = jnp.zeros((length, 128), F32)
        for a in range(2):
            h = 2 * p + a
            mine = lo if a == 0 else ~lo
            decay = jnp.exp(jnp.minimum(ct[h : h + 1] - c[:, h : h + 1], 0.0))
            dscores = dscores + decay * nt(jnp.where(mine, xdt, 0.0).astype(BF16), dyb)
            dxdt = dxdt + nn((decay * scores).astype(BF16), jnp.where(mine, dyf, 0.0).astype(BF16))
        spread = leaving * xdt
        moved = spread * bds
        matched = matched + split_dot(xdt.astype(BF16).astype(F32) * dxdt + moved, hm)
        dxdt = dxdt + leaving * bds
        held = jnp.exp(last) * kept
        col = jnp.sum(moved, axis=0, keepdims=True) + held * jnp.sum(entry * ds, axis=0, keepdims=True)
        closing_term = closing_term + split_dot(jnp.broadcast_to(col, (8, 128)), hm)[0:1]
        direct = direct + split_dot(xp * dxdt, hm)
        edy = (jnp.exp(cb) * entering * dyf).astype(BF16)
        db = db + nt(spread.astype(BF16), dsb)
        dc_mat = dc_mat + nt(edy, entryb)
        dstate[:, sl] = ds * held + tn(cc, edy)
        dx = dtb * dxdt + taps[6:7, sl] * dyf
        grad, above = conv_back(dx, pre, shifts, links, taps, sl, carry, next_links, par_out)
        ginner_out[:, sl] = grad.astype(BF16)
        edge_out[:, sl] = above

        @pl.when(i == 0)
        def _():
            last_out[:, sl] = grad[length - 8 :]

    dsc = jnp.where(allowed, dscores, 0.0).astype(BF16)
    grads_bc[:, :state_dim] = db + nn(dsc, cc)
    grads_bc[:, state_dim:] = dc_mat + tn(dsc, b)
    for half in range(2):
        sl = slice(half * state_dim, (half + 1) * state_dim)
        pre, shifts = conv_tile(shared, shared_halo, links, taps_s, sl)
        grad, above = conv_back(grads_bc[:, sl], pre, shifts, links, taps_s, sl, carry_s, next_links, par_s_out)
        gshared_out[:, sl] = grad.astype(BF16)
        edge_s_out[:, sl] = above

        @pl.when(i == 0)
        def _():
            last_s_out[:, sl] = grad[length - 8 :]

    for j in range(3):
        carry_links[:, j : j + 1] = links[j][0:8]
    dcum = row_in[...] - matched
    upper = (rows <= cols).astype(F32)
    dlog = jnp.dot(upper, dcum, precision=HIGH, preferred_element_type=F32) + closing_term
    rate = -jnp.exp(heads[1:2])
    dstep = (direct + dlog * rate) * sigmoid(step_raw[...] + heads[0:1])
    gstep_out[...] = dstep.astype(BF16)
    par_h_out[0:1] += jnp.sum(dstep, axis=0, keepdims=True)
    par_h_out[1:2] += jnp.sum(dlog * (rate * dt), axis=0, keepdims=True)


def run_backward(
    both_ext, shared_ext, step_raw, segc_ext, segr, taps, taps_s, heads,
    dy, x, bc, dt, c, ct, dec, enter, start, rowterm, dend,
):
    length, width = x.shape
    scols = bc.shape[1]
    chunks = length // SPAN
    at = lambda i: chunks - 1 - i
    row = lambda i: (at(i), 0)
    halo = lambda col: (lambda i: (halo_index(at(i), chunks), col))
    fixed = lambda i: (0, 0)
    S = jax.ShapeDtypeStruct
    return pl.pallas_call(
        backward_kernel,
        grid=(chunks,),
        in_specs=[
            pl.BlockSpec((SPAN, width), lambda i: (at(i), 1)),
            pl.BlockSpec((HALO, width), halo(1)),
            pl.BlockSpec((SPAN, scols), row),
            pl.BlockSpec((HALO, scols), halo(0)),
            pl.BlockSpec((SPAN, 128), row),
            pl.BlockSpec((SPAN, 1), row),
            pl.BlockSpec((HALO, 1), halo(0)),
            pl.BlockSpec((1, SPAN), lambda i: (0, at(i))),
            pl.BlockSpec(taps.shape, fixed),
            pl.BlockSpec(taps_s.shape, fixed),
            pl.BlockSpec(heads.shape, fixed),
            pl.BlockSpec((SPAN, width), row),
            pl.BlockSpec((SPAN, width), row),
            pl.BlockSpec((SPAN, scols), row),
            pl.BlockSpec((SPAN, 128), row),
            pl.BlockSpec((SPAN, 128), row),
            pl.BlockSpec((ct.shape[0], SPAN), lambda i: (0, at(i))),
            pl.BlockSpec((8, 128), lambda i: (jnp.maximum(at(i) * (SPAN // 8) - 1, 0), 0)),
            pl.BlockSpec((None, scols // 2, width), lambda i: (at(i), 0, 0)),
            pl.BlockSpec(start.shape, fixed),
            pl.BlockSpec((SPAN, 128), row),
            pl.BlockSpec(dend.shape, fixed),
        ],
        out_specs=[
            pl.BlockSpec((SPAN, width), row),
            pl.BlockSpec((SPAN, scols), row),
            pl.BlockSpec((SPAN, 128), row),
            pl.BlockSpec((8, width), fixed),
            pl.BlockSpec((8, scols), fixed),
            pl.BlockSpec((8, 128), fixed),
            pl.BlockSpec((8, width), fixed),
            pl.BlockSpec((8, scols), fixed),
            pl.BlockSpec((8, width), fixed),
            pl.BlockSpec((8, scols), fixed),
        ],
        out_shape=[
            S((length, width), BF16),
            S((length, scols), BF16),
            S((length, 128), BF16),
            S((8, width), F32),
            S((8, scols), F32),
            S((8, 128), F32),
            S((8, width), F32),
            S((8, scols), F32),
            S((8, width), F32),
            S((8, scols), F32),
        ],
        scratch_shapes=[
            pltpu.VMEM((scols // 2, width), F32),
            pltpu.VMEM((8, width), F32),
            pltpu.VMEM((8, scols), F32),
            pltpu.VMEM((8, 128), F32),
            pltpu.VMEM((SPAN, scols), F32),
        ],
        name="scan_backward",
    )(both_ext, both_ext, shared_ext, shared_ext, step_raw, segc_ext, segc_ext, segr, taps, taps_s, heads,
      dy, x, bc, dt, c, ct, dec, enter, start, rowterm, dend)


def pass_on(value, axis, by):
    count = lax.axis_size(axis)
    pairs = [(i, i + by) for i in range(count) if 0 <= i + by < count]
    return lax.ppermute(value, axis, pairs)


def pack_rows(rows, width):
    used = sum(r.shape[0] for r in rows)
    return jnp.concatenate(rows + [jnp.zeros((8 - used, width), F32)], axis=0)


def per_device(
    block_input, segment_ids, norm_gain, proj_zx, proj_bc, proj_dt, conv_inner, conv_inner_bias,
    conv_shared, conv_shared_bias, step_bias, rate_log, skip_gain, gated_gain, proj_out, cotangent,
):
    model_dim = block_input.shape[1]
    width = proj_zx.shape[2]
    scols = proj_bc.shape[1]
    nheads = proj_dt.shape[1]
    full_width = float(width * lax.axis_size("col"))
    shards = ("dp", "row")
    x_all = lax.all_gather(block_input, "col", axis=0, tiled=True)
    cot_all = lax.all_gather(cotangent, "col", axis=0, tiled=True)
    seg_all = lax.all_gather(segment_ids, "col", axis=0, tiled=True)
    w_in = lax.all_gather(proj_zx.reshape(-1, 2 * width), shards, axis=0, tiled=True)
    small_own = jnp.concatenate(
        [proj_bc, proj_dt, jnp.zeros((proj_dt.shape[0], 128 - nheads), BF16)], axis=1
    )
    w_small = lax.all_gather(small_own, shards, axis=0, tiled=True)
    out_t = lax.all_gather(proj_out.T, shards, axis=0, tiled=True)

    length = x_all.shape[0]
    tail_x, tail_seg = pass_on((x_all[-HALO:], seg_all[-HALO:] + 1), "row", 1)
    x_ext = jnp.concatenate([x_all, tail_x], axis=0)
    seg_ext = jnp.concatenate([seg_all, tail_seg - 1], axis=0)
    wide = x_ext.astype(F32)
    scale = lax.rsqrt(jnp.mean(wide * wide, axis=1, keepdims=True) + EPS)
    normed_ext = (wide * scale * norm_gain[None, :]).astype(BF16)
    normed = normed_ext[:length]
    both_ext = nn(normed_ext, w_in).astype(BF16)
    small_ext = nn(normed_ext, w_small)
    shared_ext = small_ext[:, :scols].astype(BF16)
    step_ext = small_ext[:, scols:]

    head_dim = width // nheads
    taps = pack_rows(
        [conv_inner, conv_inner_bias[None], gated_gain[None], jnp.repeat(skip_gain, head_dim)[None]], width
    )
    taps_s = pack_rows([conv_shared, conv_shared_bias[None]], scols)
    fill = (0, 128 - nheads)
    heads = pack_rows([jnp.pad(step_bias, fill)[None], jnp.pad(rate_log, fill)[None], jnp.zeros((5, 128), F32)], 128)
    heads = jnp.concatenate([heads[:7], jnp.full((1, 128), seg_ext[-1], F32)], axis=0)
    common = (both_ext, shared_ext, step_ext, seg_ext[:, None], seg_all[None, :], taps, taps_s, heads)
    y, x, bc, dt, c, ct, dec, enter, final = run_forward(*common)
    start = pass_on(final, "row", 1)
    back = nn(cot_all, out_t).astype(BF16)
    ssd, sums = run_gate(y, x, bc, dec, start, both_ext, back, taps)
    sums = lax.psum(jnp.concatenate([sums[0:1], sums[8:9]], axis=0), "col")
    sums = jnp.concatenate([sums, jnp.zeros((6, length), F32)], axis=0)
    gated_normed, dy, ggate, rowterm, colsum, dstart = run_back(
        full_width, ssd, x, bc, dec, both_ext, back, sums, taps
    )
    dend = pass_on(dstart, "row", -1)
    projected = lax.psum_scatter(
        nt(gated_normed, out_t).astype(BF16), "col", scatter_dimension=0, tiled=True
    )
    block_output = (block_input.astype(F32) + projected.astype(F32)).astype(BF16)
    grad_out = lax.psum_scatter(
        tn(cot_all, gated_normed).astype(BF16), shards, scatter_dimension=0, tiled=True
    )
    ginner, gshared, gstep, par, par_s, par_h, edge, edge_s, last, last_s = run_backward(
        *common, dy, x, bc, dt, c, ct, dec, enter, start, rowterm, dend
    )
    edge, edge_s = pass_on((edge, edge_s), "row", -1)
    ginner = lax.dynamic_update_slice(ginner, (last + edge).astype(BF16), (length - 8, 0))
    gshared = lax.dynamic_update_slice(gshared, (last_s + edge_s).astype(BF16), (length - 8, 0))
    gsmall = jnp.concatenate([gshared, gstep], axis=1)
    part_normed = nt(ggate, w_in[:, :width]) + nt(ginner, w_in[:, width:]) + nt(gsmall, w_small)
    grad_normed = lax.psum_scatter(
        part_normed.astype(BF16), "col", scatter_dimension=0, tiled=True
    ).astype(F32)
    gain_part = jnp.sum(part_normed * (wide * scale)[:length], axis=0)
    gboth = jnp.concatenate([ggate, ginner], axis=1)
    gzx = lax.psum_scatter(tn(normed, gboth).astype(BF16), shards, scatter_dimension=0, tiled=True)
    gsm = lax.psum_scatter(tn(normed, gsmall), shards, scatter_dimension=0, tiled=True)
    rows_a = jnp.concatenate([par[:5], colsum[:2], jnp.zeros((1, width), F32)], axis=0)
    vec_a = jnp.concatenate([rows_a.reshape(-1), par_h[:2].reshape(-1)])
    vec_b = jnp.concatenate([par_s[:5].reshape(-1), gain_part])
    vec_a = lax.psum(vec_a, shards)
    vec_b = lax.psum(vec_b, shards)
    vec_b, grad_bc = lax.psum((vec_b, gsm[:, :scols]), "col")
    rows_a = vec_a[: 8 * width].reshape(8, width)
    par_h = vec_a[8 * width :].reshape(2, 128)[:, :nheads]
    rows_b = vec_b[: 5 * scols].reshape(5, scols)
    own = block_input.astype(F32)
    own_scale = lax.rsqrt(jnp.mean(own * own, axis=1, keepdims=True) + EPS)
    pushed = grad_normed * norm_gain[None, :]
    grad_wide = own_scale * pushed - own * own_scale**3 * jnp.mean(pushed * own, axis=1, keepdims=True)
    grad_input = (cotangent.astype(F32) + grad_wide).astype(BF16)
    return (
        block_output,
        grad_input,
        vec_b[5 * scols :],
        gzx.astype(F32).reshape(-1, 2, width),
        grad_bc,
        gsm[:, scols : scols + nheads],
        rows_a[:4],
        rows_a[4],
        rows_b[:4],
        rows_b[4],
        par_h[0],
        par_h[1],
        jnp.sum(rows_a[6].reshape(nheads, head_dim), axis=1),
        rows_a[5],
        grad_out.astype(F32).T,
    )


def solution(mesh):
    shards = ("dp", "row")
    tokens = P(("dp", "row", "col"), None)
    zx = P(shards, None, "col")
    in_specs = (
        tokens, P(("dp", "row", "col")), P(), zx, P(shards, None), P(shards, "col"), P(None, "col"), P("col"),
        P(), P(), P("col"), P("col"), P("col"), P("col"), P("col", shards), tokens,
    )
    out_specs = (
        tokens, tokens, P(), zx, P(shards, None), P(shards, "col"), P(None, "col"), P("col"),
        P(), P(), P("col"), P("col"), P("col"), P("col"), P("col", shards),
    )
    return jax.shard_map(per_device, mesh=mesh, in_specs=in_specs, out_specs=out_specs, check_vma=False)
```

time: 1530 us -> 608 us (0.40)
  local copies, waits for them, and re-layouts: 498 us -> 28.9 us
  other arithmetic: 207 us -> 16.9 us
  waiting for transfers between devices: 471 us -> 339 us
  matrix products: 190 us -> 59.6 us
  Pallas kernels: 0 us -> 60.2 us
  blocking collectives: 99 us -> 68.4 us
  loops' own time: 18.3 us -> 0 us
    dynamic_update_slice x72 -> x0, local copies, waits for them, and re-layouts: 258 us -> none  [the longest x68 253 us: closing_scan(): lax.scan(closing_advance, (start_state, start_prev), blocks)]
    unnamed x13 -> x12, waiting for transfers between devices: 146 us -> 1.87 us
    dot_general x79 -> x10, matrix products: 189 us -> 59.6 us  [the longest x4 21.7 us: nt(): lax.dot_general(a, b, (((1,), (1,)), ((), ())), preferred_element_type=F32)]
    all_gather x4 -> x5, waiting for transfers between devices: 56.1 us -> 165 us  [the longest x1 64.9 us: per_device(): cot_all = lax.all_gather(cotangent, 'col', axis=0, tiled=True)]
    reduce_scatter x4, waiting for transfers between devices: 233 us -> 132 us  [the longest x1 61 us: per_device(): lax.psum_scatter(nt(gated_normed, out_t).astype(BF16), 'col', scatter_dim...]
    dynamic_slice x56 -> x0, local copies, waits for them, and re-layouts: 75.2 us -> none  [the longest x52 70.4 us: closing_scan(): lax.scan(closing_advance, (start_state, start_prev), blocks)]
    pallas_call x0 -> x4, Pallas kernels: none -> 60.2 us  [the longest x1 30.4 us: run_backward(): pl.pallas_call(backward_kernel, grid=(chunks,), in_specs=[pl.BlockSpec((S...]
    reduce_sum x27 -> x2, other arithmetic: 56 us -> 2.2 us  [the longest x1 1.57 us: per_device(): own_scale = lax.rsqrt(jnp.mean(own * own, axis=1, keepdims=True) + EPS)]
  transfers between devices with their start and end apart: 18 -> 17, of which waited for: 8 -> 11; matrix products, arithmetic and copies ran while one was open for 26% -> 15% of each run, Pallas kernels for 0% -> 7%
where the time goes in v1:
time: 608 us; the launch traced here: 599 us
  waiting for transfers between devices  339 us (56%)
  blocking collectives  68.4 us (11%)
  Pallas kernels  60.2 us (10%)
  matrix products  59.6 us (10%)
  local copies, waits for them, and re-layouts  28.9 us (5%)
  other arithmetic  16.9 us (3%)
  between operations  15.5 us (3%)
  starting transfers between devices  10.4 us (2%)
    all_gather x1, waiting for transfers between devices, per_device(): cot_all = lax.all_gather(cotangent, 'col', axis=0, tiled=True)  64.9 us
    reduce_scatter x1, waiting for transfers between devices, per_device(): lax.psum_scatter(nt(gated_normed, out_t).astype(BF16), 'col', scatter_dim...  61 us
    reduce_scatter x1, waiting for transfers between devices, per_device(): lax.psum_scatter(tn(normed, gboth).astype(BF16), shards, scatter_dimensio...  53.8 us
    all_gather x1, waiting for transfers between devices, per_device(): x_all = lax.all_gather(block_input, 'col', axis=0, tiled=True)  44.3 us
    all_gather x1, waiting for transfers between devices, per_device(): lax.all_gather(proj_zx.reshape(-1, 2 * width), shards, axis=0, tiled=True)  36.5 us
    psum x1, waiting for transfers between devices, per_device(): vec_b, grad_bc = lax.psum((vec_b, gsm[:, :scols]), 'col')  35 us
    pallas_call x1, Pallas kernels, run_backward(): pl.pallas_call(backward_kernel, grid=(chunks,), in_specs=[pl.BlockSpec((S...  30.4 us
    psum x1, blocking collectives, per_device(): vec_b = lax.psum(vec_b, shards)  26.8 us
  transfers between devices with their start and end apart: 17, of which 11 were waited for; matrix products, arithmetic and copies ran while one was open for 15% of the time, Pallas kernels for 7%

profile of v1, /device:TPU:0, one launch (start us, length us, event | category | flops | bytes accessed | tf_op | source)
XLA Modules:
  0.0 598.5 jit_solution(7108509060602609987)
XLA Ops:
  9.0 1.6 maximum_maximum_fusion
  10.6 1.9 copy.57
  13.8 12.7 %all-gather = s32[4,1,256]{2,1,0:T(1,128)S(1)} all-gather(s32[1,1,256]{2,1,0:T(1,128)S(1)} %bitcast.51), channel_id=1, replica_groups=mesh['dp'=4,'row'=2,'col'=4] {'col'}, dimensions={0}, use_global_device_ids=true | all-gather | bytes 5120 | tf_op jit(solution)/shard_map/all_gather | solution.py:560
  26.6 1.3 collective-permute-start.1
  31.6 44.3 %all-gather.7.cloned.1.call-done = bf16[1024,1536]{1,0:T(8,128)(2,1)} async-done(((bf16[256,1536]{1,0:T(8,128)(2,1)}), bf16[1024,1536]{1,0:T(8,128)(2,1)}) %all-gather.7.cloned.1.call-update) | async-done | bytes 3145744 | tf_op jit(solution)/shard_map/all_gather | solution.py:558
  76.8 1.7 collective-permute-start
  79.6 2.6 fusion
  82.2 4.5 convert_multiply_fusion
  86.7 14.2 %all-gather.11.cloned.1.call-done = bf16[1536,384]{1,0:T(8,128)(2,1)} async-done(((bf16[192,384]{1,0:T(8,128)(2,1)}), bf16[1536,384]{1,0:T(8,128)(2,1)}) %all-gather.11.cloned.1.call-update) | async-done | bytes 1179664 | tf_op jit(solution)/shard_map/all_gather | solution.py:565
  100.9 3.1 fusion.27
  105.6 36.5 %all-gather.9.cloned.1.call-done = bf16[1536,1536]{1,0:T(8,128)(2,1)} async-done(((bf16[192,1536]{1,0:T(8,128)(2,1)}), bf16[1536,1536]{1,0:T(8,128)(2,1)}) %all-gather.9.cloned.1.call-update) | async-done | bytes 4718608 | tf_op jit(solution)/shard_map/all_gather | solution.py:561
  142.2 8.8 %convolution_convert_fusion.1.inner.inner_halo.gate = bf16[1040,1536]{1,0:T(8,128)(2,1)} fusion(bf16[1040,1536]{1,0:T(8,128)(2,1)S(1)} %get-tuple-element.136, bf16[1536,1536]{1,0:T(8,128)(2,1)} %all-gather.9.cloned.1.call-done), kind=kOutput, calls=%fused_computation.3 | convolution fusion | flops 4908933120 | bytes 11108352 | tf_op jit(solution)/shard_map/dot_general | solution.py:16
  151.0 13.7 %scan_forward.1 = (f32[1024,768]{1,0:T(8,128)}, bf16[1024,768]{1,0:T(8,128)(2,1)}, bf16[1024,256]{1,0:T(8,128)(2,1)}, f32[1024,128]{1,0:T(8,128)}, f32[1024,128]...) custom-call(bf16[1040,1536]{1,0:T(8,128)(2,1)} %convolution_convert_, ...), custom_call_target="tpu_custom_call" | custom-call | tf_op jit(solution)/shard_map/scan_forward/pallas_call | solution.py:144
  164.6 2.9 collective-permute-start.2
  167.5 5.3 all-gather.15.cloned.1.call-done
  172.8 64.9 %all-gather.13.cloned.1.call-done = bf16[1024,1536]{1,0:T(8,128)(2,1)} async-done(((bf16[256,1536]{1,0:T(8,128)(2,1)}), bf16[1024,1536]{1,0:T(8,128)(2,1)}) %all-gather.13.cloned.1.call-update) | async-done | bytes 3145744 | tf_op jit(solution)/shard_map/all_gather | solution.py:559
  237.7 6.4 %convolution_convert_fusion.4.back = bf16[1024,768]{1,0:T(8,128)(2,1)} fusion(bf16[1024,1536]{1,0:T(8,128)(2,1)} %all-gather.13.cloned.1.call-done, bf16[1536,768]{1,0:T(8,128)(2,1)} %all-gather.15.cloned.1.call-done), kind=kOutput, calls=%fused_computation.27 | convolution fusion | flops 2416705536 | bytes 7077888 | tf_op jit(solution)/shard_map/dot_general | solution.py:16
  244.1 6.9 %gate_sums.1 = (f32[1024,768]{1,0:T(8,128)}, f32[16,1024]{1,0:T(8,128)}) custom-call(f32[1024,768]{1,0:T(8,128)} %get-tuple-element.42.y, bf16[1024,768]{1,0:T(8,128)(2,1)} %get-tuple-element.43.x, bf16[1024,256]{1,0:T(8,128)(2,1)} %get-tuple-element.44.bc, f32[1024,128]{1,0:T(8,128)} %get-tuple-element.45.dec.dec_halo, ...), custom_call_target="tpu_custom_call" | custom-call | tf_op jit(solution)/shard_map/gate_sums/pallas_call | solution.py:219
  251.8 9.4 %psum.35 = f32[2,1024]{1,0:T(2,128)S(1)} all-reduce(f32[2,1024]{1,0:T(2,128)S(1)} %pad_maximum_fusion.7), channel_id=1, replica_groups=mesh['dp'=4,'row'=2,'col'=4] {'col'}, use_global_device_ids=true, to_apply=%region_1.2 | all-reduce | flops 2048 | bytes 16384 | tf_op jit(solution)/shard_map/psum | solution.py:594
  261.8 9.3 %gated_back.1 = (bf16[1024,768]{1,0:T(8,128)(2,1)}, bf16[1024,768]{1,0:T(8,128)(2,1)}, bf16[1024,768]{1,0:T(8,128)(2,1)}, f32[1024,128]{1,0:T(8,128)}, f32[8,768]{1,0:T(8,128)}, /*index=5*/f32[128,768]{1,0:T(8,128)}) custom-call(f32[1024,768]{1,0:T(8,128)} %get-tuple-element.47.ssd, bf16[1024,768]{1,0:T(8,128)(2,1)} %get-tuple-element.43.x, ...), custom_call_target="tpu_custom_call" | custom-call | tf_op jit(solution)/shard_map/gated_back/pallas_call | solution.py:291
  271.1 6.4 %fusion.5 = bf16[1536,768]{0,1:T(8,128)(2,1)} fusion(bf16[1024,768]{1,0:T(8,128)(2,1)} %get-tuple-element.49, bf16[1024,1536]{1,0:T(8,128)(2,1)} %all-gather.13.cloned.1.call-done), kind=kOutput, calls=%fused_computation.15 | convolution fusion | flops 2417098752 | bytes 7077888 | tf_op jit(solution)/shard_map/dot_general | solution.py:24
  277.5 4.3 copy.55
  281.8 1.3 collective-permute-start.3
  283.1 2.7 collective-permute-done.3.dend
  285.8 30.4 %scan_backward.1 = (bf16[1024,768]{1,0:T(8,128)(2,1)}, bf16[1024,256]{1,0:T(8,128)(2,1)}, bf16[1024,128]{1,0:T(8,128)(2,1)}, f32[8,768]{1,0:T(8,128)}, f32[8,256...) custom-call(bf16[1040,1536]{1,0:T(8,128)(2,1)} %convolution_convert_, ...), custom_call_target="tpu_custom_call" | custom-call | tf_op jit(solution)/shard_map/scan_backward/pallas_call | solution.py:474
  316.2 1.5 collective-permute-start.5
  317.7 1.8 collective-permute-done.5
  319.4 1.3 fusion.21
  320.7 4.5 fusion.6
  325.3 1.3 collective-permute-start.4
  326.7 4.9 fusion.11
  331.7 5.0 fusion.9
  336.7 5.3 fusion.1
  342.1 6.5 %convolution_convert_fusion.2 = bf16[1024,1536]{1,0:T(8,128)(2,1)} fusion(bf16[1024,768]{1,0:T(8,128)(2,1)} %get-tuple-element.49, bf16[1536,768]{1,0:T(8,128)(2,1)} %all-gather.15.cloned.1.call-done), kind=kOutput, calls=%fused_computation.9 | convolution fusion | flops 2417491968 | bytes 7077888 | tf_op jit(solution)/shard_map/dot_general | solution.py:20
  348.7 8.7 %convolution_convert_fusion = bf16[1536,1536]{1,0:T(8,128)(2,1)} fusion(bf16[1024,768]{1,0:T(8,128)(2,1)} %copy-done.19, bf16[1024,768]{1,0:T(8,128)(2,1)} %get-tuple-element.50, bf16[1040,1536]{1,0:T(8,128)(2,1)S(1)} %get-tuple-element.136), kind=kOutput, calls=%fused_computation.2 | convolution fusion | flops 4840488960 | bytes 11010048 | tf_op jit(solution)/shard_map/dot_general | solution.py:24
  359.0 26.8 %all-reduce.3 = (f32[2816]{0:T(1024)S(1)}, f32[6400]{0:T(1024)S(1)}) all-reduce(f32[2816]{0:T(1024)S(1)} %pad_maximum_fusion.6, f32[6400]{0:T(1024)S(1)} %pad_maximum_fusion.4), channel_id=1, replica_groups=mesh['dp'=4,'row'=2,'col'=4] {'dp','row'}, use_global_device_ids=true, to_apply=%region_7.8 | all-reduce | flops 9216 | bytes 73728 | tf_op jit(solution)/shard_map/psum | solution.py:626
  385.8 19.5 %psum.37 = f32[2816]{0:T(1024)S(1)} all-reduce(f32[2816]{0:T(1024)S(1)} %get-tuple-element.131), channel_id=1, replica_groups=mesh['dp'=4,'row'=2,'col'=4] {'col'}, use_global_device_ids=true, to_apply=%region_8.9 | all-reduce | flops 2816 | bytes 22528 | tf_op jit(solution)/shard_map/psum | solution.py:627
  409.5 1.1 copy.56
  410.7 1.1 copy.54
  413.4 1.6 slice.175
  415.0 17.5 %reduce-scatter.10.cloned.1.call-done = bf16[256,1536]{1,0:T(8,128)(2,1)} async-done(((bf16[1024,1536]{1,0:T(8,128)(2,1)}), bf16[256,1536]{1,0:T(8,128)(2,1)}) %reduce-scatter.10.cloned.1.call-update) | async-done | bytes 786448 | tf_op jit(solution)/shard_map/reduce_scatter | solution.py:615
  432.5 1.6 fusion.14
  434.1 61.0 %reduce-scatter.8.cloned.1.call-done = bf16[256,1536]{1,0:T(8,128)(2,1)} async-done(((bf16[1024,1536]{1,0:T(8,128)(2,1)}), bf16[256,1536]{1,0:T(8,128)(2,1)}) %reduce-scatter.8.cloned.1.call-update) | async-done | bytes 786448 | tf_op jit(solution)/shard_map/reduce_scatter | solution.py:600
  495.1 3.2 fusion.18
  498.2 53.8 %reduce-scatter.12.cloned.1.call-done = bf16[192,1536]{1,0:T(8,128)(2,1)} async-done(((bf16[1536,1536]{1,0:T(8,128)(2,1)}), bf16[192,1536]{1,0:T(8,128)(2,1)}) %reduce-scatter.12.cloned.1.call-update) | async-done | bytes 589840 | tf_op jit(solution)/shard_map/reduce_scatter | solution.py:620
  552.1 2.8 reshape.125
  554.9 35.0 %all-reduce.6.cloned.1.call-done = f32[192,256]{1,0:T(8,128)} async-done(((f32[192,256]{1,0:T(8,128)}), f32[192,256]{1,0:T(8,128)}) %all-reduce.6.cloned.1.call-update) | async-done | bytes 196624 | tf_op jit(solution)/shard_map/psum | solution.py:627
  590.0 1.6 copy.61
  (128 shorter events, 18.9 us)
Async XLA Ops:
  7.2 6.6 %copy-start.13 = (s32[256]{0:T(256)S(1)}, s32[256]{0:T(256)}, u32[]{:S(2)}) copy-start(s32[256]{0:T(256)} %param.17) | copy-start | bytes 3076
  7.2 20.9 %copy-start.11 = (f32[768]{0:T(1024)S(1)}, f32[768]{0:T(1024)}, u32[]{:S(2)}) copy-start(f32[768]{0:T(1024)} %param.23) | copy-start | bytes 9220
  7.2 20.9 %copy-start.12 = (f32[768]{0:T(1024)S(1)}, f32[768]{0:T(1024)}, u32[]{:S(2)}) copy-start(f32[768]{0:T(1024)} %param.29) | copy-start | bytes 9220
  7.2 20.9 %copy-start.15 = (f32[12]{0:T(128)S(1)}, f32[12]{0:T(128)}, u32[]{:S(2)}) copy-start(f32[12]{0:T(128)} %param.28) | copy-start | bytes 148
  7.2 21.0 %copy-start.16 = (f32[12]{0:T(128)S(1)}, f32[12]{0:T(128)}, u32[]{:S(2)}) copy-start(f32[12]{0:T(128)} %param.27) | copy-start | bytes 148
  7.2 21.0 %copy-start.17 = (f32[12]{0:T(128)S(1)}, f32[12]{0:T(128)}, u32[]{:S(2)}) copy-start(f32[12]{0:T(128)} %param.26) | copy-start | bytes 148
  7.2 21.0 %copy-start.14 = (f32[256]{0:T(256)S(1)}, f32[256]{0:T(256)}, u32[]{:S(2)}) copy-start(f32[256]{0:T(256)} %param.25) | copy-start | bytes 3076
  7.3 21.0 %copy-start.10 = (f32[4,256]{1,0:T(4,128)S(1)}, f32[4,256]{1,0:T(4,128)}, u32[]{:S(2)}) copy-start(f32[4,256]{1,0:T(4,128)} %param.24) | copy-start | bytes 12292
  7.3 21.7 %copy-start.8 = (f32[4,768]{1,0:T(4,128)S(1)}, f32[4,768]{1,0:T(4,128)}, u32[]{:S(2)}) copy-start(f32[4,768]{1,0:T(4,128)} %param.22) | copy-start | bytes 36868
  7.3 68.6 %all-gather.7.cloned.1.call-start = ((), (), s32[]{:S(2)}) async-start(), calls=%async_computation.5 | async-start | bytes 3932160 | tf_op jit(solution)/shard_map/all_gather | solution.py:558
  8.0 92.9 %all-gather.11.cloned.1.call-start = ((), (), s32[]{:S(2)}) async-start(), calls=%async_computation.7 | async-start | bytes 1327104 | tf_op jit(solution)/shard_map/all_gather | solution.py:565
  10.6 131.6 %all-gather.9.cloned.1.call-start = ((), (), s32[]{:S(2)}) async-start(), calls=%async_computation.6 | async-start | bytes 5308416 | tf_op jit(solution)/shard_map/all_gather | solution.py:561
  10.6 71.5 %copy-start.4 = (f32[1536]{0:T(1024)S(1)}, f32[1536]{0:T(1024)}, u32[]{:S(2)}) copy-start(f32[1536]{0:T(1024)} %param.18) | copy-start | bytes 18436
  12.6 160.2 %all-gather.15.cloned.1.call-start = ((), (), s32[]{:S(2)}) async-start(), calls=%async_computation.9 | async-start | bytes 2654208 | tf_op jit(solution)/shard_map/all_gather | solution.py:566
  13.2 224.5 %all-gather.13.cloned.1.call-start = ((), (), s32[]{:S(2)}) async-start(), calls=%async_computation.8 | async-start | bytes 3932160 | tf_op jit(solution)/shard_map/all_gather | solution.py:559
  13.8 395.8 %reduce-scatter.16.cloned.1.call-start = ((), (), s32[]{:S(2)}) async-start(), calls=%async_computation.15 | async-start | bytes 2654208
  26.5 60.2 %copy-start.5 = (s32[4,1,256]{2,1,0:T(1,128)}, s32[4,1,256]{2,1,0:T(1,128)S(1)}, u32[]{:S(2)}) copy-start(s32[4,1,256]{2,1,0:T(1,128)S(1)} %all-gather) | copy-start | bytes 12292
  26.6 3.0 collective-permute-start.1
  75.9 6.3 %copy-start = (bf16[1024,1536]{1,0:T(8,128)(2,1)S(1)}, bf16[1024,1536]{1,0:T(8,128)(2,1)}, u32[]{:S(2)}) copy-start(bf16[1024,1536]{1,0:T(8,128)(2,1)} %all-gather.7.cloned.1.call-done) | copy-start | bytes 9437188
  76.8 2.7 collective-permute-start
  164.6 79.4 %collective-permute-start.2 = (f32[128,768]{1,0:T(8,128)}, f32[128,768]{1,0:T(8,128)}, u32[]{:S(2)}, u32[]{:S(2)}) collective-permute-start(f32[128,768]{1,0:T(8,128)} %get-tuple-element.46), channel_id=1, source_target_pairs={{0,4},{1,5},{2,6},{3,7},{8,12},{9,13},{10,14},{11,15},{16,20},{17,... | collective-permute-start | bytes 1179656 | tf_op jit(solution)/shard_map/ppermute | solution.py:540
  281.8 130.0 %reduce-scatter.14.cloned.1.call-start = ((), (), s32[]{:S(2)}) async-start(), calls=%async_computation.13 | async-start | bytes 2654208 | tf_op jit(solution)/shard_map/reduce_scatter | solution.py:621
  281.8 4.0 collective-permute-start.3
  316.2 3.3 collective-permute-start.5
  320.7 4.6 copy-start.20
  325.3 107.2 %reduce-scatter.10.cloned.1.call-start = ((), (), s32[]{:S(2)}) async-start(), calls=%async_computation.11 | async-start | bytes 3932160 | tf_op jit(solution)/shard_map/reduce_scatter | solution.py:615
  325.3 6.3 %collective-permute-start.4 = (f32[8,768]{1,0:T(8,128)S(1)}, f32[8,768]{1,0:T(8,128)S(1)}, u32[]{:S(2)}, u32[]{:S(2)}) collective-permute-start(f32[8,768]{1,0:T(8,128)S(1)} %copy-done.20), channel_id=1, source_target_pairs={{4,0},{5,1},{6,2},{7,3},{12,8},{13,9},{14,10},{15,11},{20,16},{21,... | collective-permute-start | bytes 73736 | tf_op jit(solution)/shard_map/ppermute | solution.py:540
  326.6 5.0 copy-start.7
  326.6 5.0 copy-start.18
  326.6 10.0 %slice-start = ((s8[6389760]{0:T(1024)(128)(4,1)}), s8[4194304]{0:T(1024)(128)(4,1)S(1)}, s32[]{:S(2)}) async-start(s8[6389760]{0:T(1024)(128)(4,1)} %bitcast.40), calls=%async_computation.16 | async-start | bytes 8388608
  331.6 5.1 slice-start.1
  331.6 5.0 copy-start.19
  331.7 5.0 copy-start.3
  342.0 153.0 %reduce-scatter.8.cloned.1.call-start = ((), (), s32[]{:S(2)}) async-start(), calls=%async_computation.10 | async-start | bytes 3932160 | tf_op jit(solution)/shard_map/reduce_scatter | solution.py:600
  348.6 203.5 %reduce-scatter.12.cloned.1.call-start = ((), (), s32[]{:S(2)}) async-start(), calls=%async_computation.12 | async-start | bytes 5308416 | tf_op jit(solution)/shard_map/reduce_scatter | solution.py:620
  357.3 1.0 copy-start.9
  357.3 1.0 copy-start.6
  357.3 75.1 %copy-start.1 = (bf16[256,1536]{1,0:T(8,128)(2,1)S(1)}, bf16[256,1536]{1,0:T(8,128)(2,1)}, u32[]{:S(2)}) copy-start(bf16[256,1536]{1,0:T(8,128)(2,1)} %param.16) | copy-start | bytes 2359300
  357.4 137.7 %copy-start.2 = (bf16[256,1536]{1,0:T(8,128)(2,1)S(1)}, bf16[256,1536]{1,0:T(8,128)(2,1)}, u32[]{:S(2)}) copy-start(bf16[256,1536]{1,0:T(8,128)(2,1)} %param.31) | copy-start | bytes 2359300
  357.4 232.6 %all-reduce.6.cloned.1.call-start = ((), (), s32[]{:S(2)}) async-start(), calls=%async_computation.14 | async-start | bytes 393216 | tf_op jit(solution)/shard_map/psum | solution.py:627
Sparse Core Ops, SparseCore 0:
  9.6 66.1 all-gather.6
  78.3 22.4 all-gather.10
  103.3 38.7 all-gather.8
  143.9 28.8 all-gather.14
  174.2 63.4 all-gather.12
  281.9 41.1 reduce-scatter.15
  326.5 42.5 reduce-scatter.13
  371.4 61.0 reduce-scatter.9
  434.8 60.2 reduce-scatter.7
  498.3 53.6 reduce-scatter.11
  555.0 34.9 all-reduce.5

commit v2 on v1

--- a/solution.py
+++ b/solution.py
@@ -42,8 +42,21 @@
     return jnp.maximum(v, 0.0) + jnp.log1p(jnp.exp(-jnp.abs(v)))
 
 
+def columns(row):
+    return jnp.broadcast_to(row, (128, row.shape[1])).T
+
+
+def segments(seg_row, prev_row, tail_row):
+    row = seg_row[0:1].astype(F32)
+    seg = columns(row)[:, 0:1]
+    length = row.shape[1]
+    prev = columns(prev_row[0:1].astype(F32))[length - 8 :, 0:1]
+    tail = tail_row[0:1, length - 1 :].astype(F32)
+    return row, seg, prev, tail
+
+
 def chunk_links(segc, halo):
-    ext = jnp.concatenate([halo[HALO - 8 :], segc], axis=0)
+    ext = jnp.concatenate([halo, segc], axis=0)
     length = segc.shape[0]
     return [(ext[8 - j : 8 - j + length] == segc).astype(F32) for j in range(1, 4)]
 
@@ -63,7 +76,7 @@
 
 
 def forward_kernel(
-    inner, inner_halo, shared, shared_halo, step_raw, segc, segc_halo, segr, taps, taps_s, heads,
+    inner, inner_halo, shared, shared_halo, step_raw, seg_row, seg_prev, seg_tail, taps, taps_s, heads,
     y_out, x_out, bc_out, dt_out, c_out, ct_out, dec_out, enter_out, final_out, state, total,
 ):
     k = pl.program_id(0)
@@ -76,12 +89,11 @@
         state[...] = jnp.zeros_like(state)
         total[...] = jnp.zeros_like(total)
 
-    seg = segc[...]
-    seg_halo = segc_halo[...]
+    segr, seg, seg_halo, tail_seg = segments(seg_row, seg_prev, seg_tail)
     links = chunk_links(seg, seg_halo)
     closing = (seg == seg[length - 1 :]).astype(F32)
-    entering = (seg == seg_halo[HALO - 1 :]).astype(F32)
-    kept = (seg[length - 1 :] == seg_halo[HALO - 1 :]).astype(F32)
+    entering = (seg == seg_halo[7:]).astype(F32)
+    kept = (seg[length - 1 :] == seg_halo[7:]).astype(F32)
     dt = softplus(step_raw[...] + heads[0:1])
     log_decay = -jnp.exp(heads[1:2]) * dt
     rows, cols = iota((length, length), 0), iota((length, length), 1)
@@ -92,7 +104,7 @@
     c_out[...] = c
     ct_out[...] = ct[: ct_out.shape[0]]
     whole = c + total[0:1]
-    dec_out[...] = jnp.exp(whole) * (seg == heads[7:8, 0:1].astype(jnp.int32)).astype(F32)
+    dec_out[...] = jnp.exp(whole) * (seg == tail_seg).astype(F32)
     total[0:1] = whole[length - 1 :]
     for half in range(2):
         sl = slice(half * state_dim, (half + 1) * state_dim)
@@ -100,7 +112,7 @@
         bc_out[:, sl] = (pre * sigmoid(pre)).astype(BF16)
     b = bc_out[:, :state_dim]
     cc = bc_out[:, state_dim:]
-    scores = jnp.where((rows >= cols) & (seg == segr[...]), nt(cc, b), 0.0)
+    scores = jnp.where((rows >= cols) & (seg == segr), nt(cc, b), 0.0)
     lo = iota((length, 128), 1) < 64
     enter_out[...] = state[...].astype(BF16)
     for p in range(pairs):
@@ -131,12 +143,20 @@
     return jnp.where(chunk == 0, chunks * (SPAN // HALO), chunk * (SPAN // HALO) - 1)
 
 
-def run_forward(both_ext, shared_ext, step_raw, segc_ext, segr, taps, taps_s, heads):
+def seg_specs(at, chunks):
+    return [
+        pl.BlockSpec((8, SPAN), lambda k: (at(k), 0)),
+        pl.BlockSpec((8, SPAN), lambda k: (jnp.where(at(k) == 0, chunks, at(k) - 1), 0)),
+        pl.BlockSpec((8, SPAN), lambda k: (chunks, 0)),
+    ]
+
+
+def run_forward(both_ext, shared_ext, step_raw, seg, taps, taps_s, heads):
     width = taps.shape[1]
     scols = taps_s.shape[1]
-    length = segr.shape[1]
-    chunks = length // SPAN
-    nrow = -(-heads.shape[1] // 8) * 0 + 16
+    chunks = seg.shape[0] // 8 - 1
+    length = chunks * SPAN
+    nrow = 16
     row = lambda k: (k, 0)
     halo = lambda col: (lambda k: (halo_index(k, chunks), col))
     fixed = lambda k: (0, 0)
@@ -150,9 +170,7 @@
             pl.BlockSpec((SPAN, scols), row),
             pl.BlockSpec((HALO, scols), halo(0)),
             pl.BlockSpec((SPAN, 128), row),
-            pl.BlockSpec((SPAN, 1), row),
-            pl.BlockSpec((HALO, 1), halo(0)),
-            pl.BlockSpec((1, SPAN), lambda k: (0, k)),
+            *seg_specs(lambda k: k, chunks),
             pl.BlockSpec(taps.shape, fixed),
             pl.BlockSpec(taps_s.shape, fixed),
             pl.BlockSpec(heads.shape, fixed),
@@ -181,7 +199,7 @@
         ],
         scratch_shapes=[pltpu.VMEM((scols // 2, width), F32), pltpu.VMEM((8, 128), F32)],
         name="scan_forward",
-    )(both_ext, both_ext, shared_ext, shared_ext, step_raw, segc_ext, segc_ext, segr, taps, taps_s, heads)
+    )(both_ext, both_ext, shared_ext, shared_ext, step_raw, seg, seg, seg, taps, taps_s, heads)
 
 
 def row_sums(value):
@@ -191,13 +209,16 @@
     return nt(ones, hi) + nt(ones, lo)
 
 
-def gate_kernel(y, x, bc, dec, start, gate, back, taps, ssd_out, sums_out):
+def first_rows(value):
+    return jnp.where(iota(value.shape, 0) == 0, value, 0.0)
+
+
+def gate_kernel(y, x, bc, dec, start, gate, taps, ssd_out, gated_out, sums_out):
     length, width = x.shape
     state_dim = start.shape[0]
     cc = bc[:, state_dim:]
     lo = iota((length, 128), 1) < 64
     squares = jnp.zeros((length, 128), F32)
-    inner = jnp.zeros((length, 128), F32)
     for p in range(width // 128):
         sl = slice(p * 128, (p + 1) * 128)
         corr = nn(cc, start[:, sl].astype(BF16)) * pick(lo, dec, 2 * p)
@@ -205,13 +226,12 @@
         ssd_out[:, sl] = ssd
         g = gate[:, sl].astype(F32)
         gated = ssd * (g * sigmoid(g))
+        gated_out[:, sl] = gated.astype(BF16)
         squares = squares + gated * gated
-        inner = inner + back[:, sl].astype(F32) * taps[5:6, sl] * gated
-    sums_out[0:8] = row_sums(squares)
-    sums_out[8:16] = row_sums(inner)
-
-
-def run_gate(y, x, bc, dec, start, both_ext, back, taps):
+    sums_out[...] = row_sums(squares)
+
+
+def run_gate(y, x, bc, dec, start, both_ext, taps):
     length, width = x.shape
     row = lambda k: (k, 0)
     fixed = lambda k: (0, 0)
@@ -226,22 +246,79 @@
             pl.BlockSpec((SPAN, 128), row),
             pl.BlockSpec(start.shape, fixed),
             pl.BlockSpec((SPAN, width), row),
-            pl.BlockSpec((SPAN, width), row),
             pl.BlockSpec(taps.shape, fixed),
         ],
-        out_specs=[pl.BlockSpec((SPAN, width), row), pl.BlockSpec((16, SPAN), lambda k: (0, k))],
-        out_shape=[S((length, width), F32), S((16, length), F32)],
+        out_specs=[
+            pl.BlockSpec((SPAN, width), row),
+            pl.BlockSpec((SPAN, width), row),
+            pl.BlockSpec((8, SPAN), lambda k: (0, k)),
+        ],
+        out_shape=[S((length, width), F32), S((length, width), BF16), S((8, length), F32)],
         name="gate_sums",
-    )(y, x, bc, dec, start, both_ext, back, taps)
-
-
-def columns(row):
-    return jnp.broadcast_to(row, (128, row.shape[1])).T
+    )(y, x, bc, dec, start, both_ext, taps)
+
+
+def project_kernel(full_width, gated, sums, taps, out_t, normed_out, proj_out):
+    rescale = columns(lax.rsqrt(sums[0:1] / full_width + EPS))
+    for p in range(gated.shape[1] // 128):
+        sl = slice(p * 128, (p + 1) * 128)
+        normed_out[:, sl] = (gated[:, sl].astype(F32) * rescale * taps[5:6, sl]).astype(BF16)
+    proj_out[...] = nt(normed_out[...], out_t[...]).astype(BF16)
+
+
+def run_project(full_width, gated, sums, taps, out_t):
+    length, width = gated.shape
+    row = lambda k: (k, 0)
+    fixed = lambda k: (0, 0)
+    S = jax.ShapeDtypeStruct
+    return pl.pallas_call(
+        functools.partial(project_kernel, full_width),
+        grid=(length // SPAN,),
+        in_specs=[
+            pl.BlockSpec((SPAN, width), row),
+            pl.BlockSpec((8, SPAN), lambda k: (0, k)),
+            pl.BlockSpec(taps.shape, fixed),
+            pl.BlockSpec(out_t.shape, fixed),
+        ],
+        out_specs=[pl.BlockSpec((SPAN, width), row), pl.BlockSpec((SPAN, out_t.shape[0]), row)],
+        out_shape=[S((length, width), BF16), S((length, out_t.shape[0]), BF16)],
+        name="project",
+    )(gated, sums, taps, out_t)
+
+
+def pull_kernel(cot, out_t, gated, taps, back_out, sums_out):
+    back = nn(cot[...], out_t[...])
+    back_out[...] = back.astype(BF16)
+    inner = jnp.zeros((cot.shape[0], 128), F32)
+    for p in range(back.shape[1] // 128):
+        sl = slice(p * 128, (p + 1) * 128)
+        inner = inner + back[:, sl] * taps[5:6, sl] * gated[:, sl].astype(F32)
+    sums_out[...] = row_sums(inner)
+
+
+def run_pull(cot, out_t, gated, taps):
+    length, width = gated.shape
+    row = lambda k: (k, 0)
+    fixed = lambda k: (0, 0)
+    S = jax.ShapeDtypeStruct
+    return pl.pallas_call(
+        pull_kernel,
+        grid=(length // SPAN,),
+        in_specs=[
+            pl.BlockSpec((SPAN, cot.shape[1]), row),
+            pl.BlockSpec(out_t.shape, fixed),
+            pl.BlockSpec((SPAN, width), row),
+            pl.BlockSpec(taps.shape, fixed),
+        ],
+        out_specs=[pl.BlockSpec((SPAN, width), row), pl.BlockSpec((8, SPAN), lambda k: (0, k))],
+        out_shape=[S((length, width), BF16), S((8, length), F32)],
+        name="pull_back",
+    )(cot, out_t, gated, taps)
 
 
 def back_kernel(
-    full_width, ssd, x, bc, dec, gate, back, sums, taps,
-    normed_out, dy_out, ggate_out, row_out, colsum_out, dstart_out,
+    full_width, ssd, x, bc, dec, gate, back, squares, inner, taps,
+    dy_out, ggate_out, row_out, colsum_out, dstart_out,
 ):
     length, width = x.shape
     state_dim = dstart_out.shape[0]
@@ -253,8 +330,8 @@
 
     cc = bc[:, state_dim:]
     lo = iota((length, 128), 1) < 64
-    rescale = columns(lax.rsqrt(sums[0:1] / full_width + EPS))
-    pull = columns(sums[1:2]) * (rescale * rescale * rescale / full_width)
+    rescale = columns(lax.rsqrt(squares[0:1] / full_width + EPS))
+    pull = columns(inner[0:1]) * (rescale * rescale * rescale / full_width)
     rowterm = jnp.zeros((length, 128), F32)
     for p in range(width // 128):
         sl = slice(p * 128, (p + 1) * 128)
@@ -265,14 +342,13 @@
         gated = s_ssd * (g * s)
         bk = back[:, sl].astype(F32)
         gain = taps[5:6, sl]
-        normed_out[:, sl] = (gated * rescale * gain).astype(BF16)
         gg = rescale * (bk * gain) - gated * pull
         dy = gg * (g * s)
         dyb = dy.astype(BF16)
         dy_out[:, sl] = dyb
         ggate_out[:, sl] = (gg * s_ssd * s * (1.0 + g * (1.0 - s))).astype(BF16)
-        colsum_out[0:1, sl] += jnp.sum(bk * gated * rescale, axis=0, keepdims=True)
-        colsum_out[1:2, sl] += jnp.sum(dy * xp, axis=0, keepdims=True)
+        colsum_out[5:6, sl] += jnp.sum(bk * gated * rescale, axis=0, keepdims=True)
+        colsum_out[6:7, sl] += jnp.sum(dy * xp, axis=0, keepdims=True)
         dstart_out[:, sl] += tn(cc, (dy * pick(lo, dec, 2 * p)).astype(BF16))
         rowterm = rowterm + split_dot(dyb.astype(F32) * (s_ssd - taps[6:7, sl] * xp), head_map(p))
     row_out[...] = rowterm
@@ -283,7 +359,7 @@
     return (head == 2 * p + lane // 64).astype(BF16)
 
 
-def run_back(full_width, ssd, x, bc, dec, both_ext, back, sums, taps):
+def run_back(full_width, ssd, x, bc, dec, both_ext, back, squares, inner, taps):
     length, width = x.shape
     row = lambda k: (k, 0)
     fixed = lambda k: (0, 0)
@@ -298,11 +374,11 @@
             pl.BlockSpec((SPAN, 128), row),
             pl.BlockSpec((SPAN, width), row),
             pl.BlockSpec((SPAN, width), row),
-            pl.BlockSpec((sums.shape[0], SPAN), lambda k: (0, k)),
+            pl.BlockSpec((8, SPAN), lambda k: (0, k)),
+            pl.BlockSpec((8, SPAN), lambda k: (0, k)),
             pl.BlockSpec(taps.shape, fixed),
         ],
         out_specs=[
-            pl.BlockSpec((SPAN, width), row),
             pl.BlockSpec((SPAN, width), row),
             pl.BlockSpec((SPAN, width), row),
             pl.BlockSpec((SPAN, 128), row),
@@ -310,7 +386,6 @@
             pl.BlockSpec((bc.shape[1] // 2, width), fixed),
         ],
         out_shape=[
-            S((length, width), BF16),
             S((length, width), BF16),
             S((length, width), BF16),
             S((length, 128), F32),
@@ -318,7 +393,7 @@
             S((bc.shape[1] // 2, width), F32),
         ],
         name="gated_back",
-    )(ssd, x, bc, dec, both_ext, back, sums, taps)
+    )(ssd, x, bc, dec, both_ext, back, squares, inner, taps)
 
 
 def conv_back(dout, pre, shifts, links, taps, sl, carry, carry_links, par_out):
@@ -343,8 +418,8 @@
 
 
 def backward_kernel(
-    inner, inner_halo, shared, shared_halo, step_raw, segc, segc_halo, segr, taps, taps_s, heads,
-    dy, x, bc, dt_in, c_in, ct_in, dec_halo, enter, start, row_in, dend,
+    inner, inner_halo, shared, shared_halo, step_raw, seg_row, seg_prev, seg_tail, taps, taps_s, heads,
+    dy, x, bc, dt_in, c_in, ct_in, dec_halo, enter, start, row_in, dend, colsum,
     ginner_out, gshared_out, gstep_out, par_out, par_s_out, par_h_out, edge_out, edge_s_out, last_out, last_s_out,
     dstate, carry, carry_s, carry_links, grads_bc,
 ):
@@ -359,16 +434,15 @@
         carry[...] = jnp.zeros_like(carry)
         carry_s[...] = jnp.zeros_like(carry_s)
         carry_links[...] = jnp.zeros_like(carry_links)
-        par_out[...] = jnp.zeros_like(par_out)
+        par_out[...] = colsum[...]
         par_s_out[...] = jnp.zeros_like(par_s_out)
         par_h_out[...] = jnp.zeros_like(par_h_out)
 
-    seg = segc[...]
-    seg_halo = segc_halo[...]
+    segr, seg, seg_halo, tail_seg = segments(seg_row, seg_prev, seg_tail)
     links = chunk_links(seg, seg_halo)
     closing = (seg == seg[length - 1 :]).astype(F32)
-    entering = (seg == seg_halo[HALO - 1 :]).astype(F32)
-    kept = (seg[length - 1 :] == seg_halo[HALO - 1 :]).astype(F32)
+    entering = (seg == seg_halo[7:]).astype(F32)
+    kept = (seg[length - 1 :] == seg_halo[7:]).astype(F32)
     next_links = carry_links[...]
     dt = dt_in[...]
     c = c_in[...]
@@ -378,7 +452,7 @@
     b = bc[:, :state_dim]
     cc = bc[:, state_dim:]
     rows, cols = iota((length, length), 0), iota((length, length), 1)
-    allowed = (rows <= cols) & (seg == segr[...])
+    allowed = (rows <= cols) & (seg == segr)
     scores = jnp.where(allowed, nt(b, cc), 0.0)
     lo = iota((length, 128), 1) < 64
     lo1 = lo[0:1]
@@ -460,8 +534,8 @@
 
 
 def run_backward(
-    both_ext, shared_ext, step_raw, segc_ext, segr, taps, taps_s, heads,
-    dy, x, bc, dt, c, ct, dec, enter, start, rowterm, dend,
+    both_ext, shared_ext, step_raw, seg, taps, taps_s, heads,
+    dy, x, bc, dt, c, ct, dec, enter, start, rowterm, dend, colsum,
 ):
     length, width = x.shape
     scols = bc.shape[1]
@@ -480,9 +554,7 @@
             pl.BlockSpec((SPAN, scols), row),
             pl.BlockSpec((HALO, scols), halo(0)),
             pl.BlockSpec((SPAN, 128), row),
-            pl.BlockSpec((SPAN, 1), row),
-            pl.BlockSpec((HALO, 1), halo(0)),
-            pl.BlockSpec((1, SPAN), lambda i: (0, at(i))),
+            *seg_specs(at, chunks),
             pl.BlockSpec(taps.shape, fixed),
             pl.BlockSpec(taps_s.shape, fixed),
             pl.BlockSpec(heads.shape, fixed),
@@ -497,6 +569,7 @@
             pl.BlockSpec(start.shape, fixed),
             pl.BlockSpec((SPAN, 128), row),
             pl.BlockSpec(dend.shape, fixed),
+            pl.BlockSpec(colsum.shape, fixed),
         ],
         out_specs=[
             pl.BlockSpec((SPAN, width), row),
@@ -530,8 +603,423 @@
             pltpu.VMEM((SPAN, scols), F32),
         ],
         name="scan_backward",
-    )(both_ext, both_ext, shared_ext, shared_ext, step_raw, segc_ext, segc_ext, segr, taps, taps_s, heads,
-      dy, x, bc, dt, c, ct, dec, enter, start, rowterm, dend)
+    )(both_ext, both_ext, shared_ext, shared_ext, step_raw, seg, seg, seg, taps, taps_s, heads,
+      dy, x, bc, dt, c, ct, dec, enter, start, rowterm, dend, colsum)
+
+
+def spread_kernel(ggate, ginner, gsmall, w_in, w_small, normed, part_out, gain_out):
+    width = ggate.shape[1]
+    part = nt(ggate[...], w_in[:, :width]) + nt(ginner[...], w_in[:, width:]) + nt(gsmall[...], w_small[...])
+    part_out[...] = part.astype(BF16)
+    gain_out[...] = first_rows(jnp.broadcast_to(
+        jnp.sum(part * normed[...].astype(F32), axis=0, keepdims=True), gain_out.shape))
+
+
+def run_spread(ggate, ginner, gsmall, w_in, w_small, normed_ext):
+    length = ggate.shape[0]
+    model = w_in.shape[0]
+    tile = 256
+    fixed = lambda n: (0, 0)
+    down = lambda n: (n, 0)
+    across = lambda n: (0, n)
+    S = jax.ShapeDtypeStruct
+    return pl.pallas_call(
+        spread_kernel,
+        grid=(model // tile,),
+        in_specs=[
+            pl.BlockSpec(ggate.shape, fixed),
+            pl.BlockSpec(ginner.shape, fixed),
+            pl.BlockSpec(gsmall.shape, fixed),
+            pl.BlockSpec((tile, w_in.shape[1]), down),
+            pl.BlockSpec((tile, w_small.shape[1]), down),
+            pl.BlockSpec((length, tile), across),
+        ],
+        out_specs=[pl.BlockSpec((length, tile), across), pl.BlockSpec((8, tile), across)],
+        out_shape=[S((length, model), BF16), S((8, model), F32)],
+        name="spread_back",
+    )(ggate, ginner, gsmall, w_in, w_small, normed_ext)
+
+
+MESH = pl.DeviceIdType.MESH
+ANY = pl.BlockSpec(memory_space=pl.ANY)
+
+
+def remote(src, dst, send, recv, **to):
+    return pltpu.make_async_remote_copy(
+        src_ref=src, dst_ref=dst, send_sem=send, recv_sem=recv, device_id=to, device_id_type=MESH
+    )
+
+
+def greet(barrier, when, **to):
+    @pl.when(when)
+    def _():
+        pl.semaphore_signal(barrier, inc=1, device_id=to, device_id_type=MESH)
+
+
+def gather_kernel(
+    ncol, ndp,
+    own, seg_own, w0, w1, w2, zero_tail, no_seg,
+    all_out, seg_out, w0_out, w1_out, w2_out,
+    z_send, z_recv, w_send, c_send, w_recv, t_send, t_recv, here,
+):
+    dp, row, z = lax.axis_index("dp"), lax.axis_index("row"), lax.axis_index("col")
+    other = 1 - row
+    last = ncol - 1
+    tokens, tail = own.shape[0], zero_tail.shape[0]
+    weights = ((w0, w0_out), (w1, w1_out), (w2, w2_out))
+    rows = w0.shape[0]
+    sends_tail = (row == 0) & (z == last)
+
+    barrier = pltpu.get_barrier_semaphore()
+    greet(barrier, z > 0, col=z - 1)
+    greet(barrier, z < last, col=z + 1)
+    greet(barrier, row >= 0, row=other)
+    for m in range(1, ndp):
+        greet(barrier, row >= 0, dp=dp ^ m)
+    greet(barrier, row == 1, row=0, col=last)
+    for c in range(ncol):
+        greet(barrier, sends_tail, row=1, col=c)
+    count = (z > 0).astype(jnp.int32) + (z < last).astype(jnp.int32) + ndp
+    count = count + row + jnp.where(sends_tail, ncol, 0)
+    pl.semaphore_wait(barrier, count)
+
+    def token_refs(s, mine):
+        if mine:
+            srcs = (own, seg_own)
+        else:
+            srcs = (all_out.at[pl.ds(s * tokens, tokens)], seg_out.at[pl.ds(s * 8, 8)])
+        return tuple(zip(srcs, (all_out.at[pl.ds(s * tokens, tokens)], seg_out.at[pl.ds(s * 8, 8)])))
+
+    def token_copies(s, mine, way):
+        target = z + 1 if way == 0 else z - 1
+        return [
+            remote(src, dst, z_send.at[way, s, i], z_recv.at[s, i], col=target)
+            for i, (src, dst) in enumerate(token_refs(s, mine))
+        ]
+
+    def weight_copies(j, mine, send, **to):
+        copies = []
+        for i, (src, dst) in enumerate(weights):
+            place = dst.at[pl.ds(j * rows, rows)]
+            copies.append(remote(src if mine else place, place, send.at[i], w_recv.at[j, i], **to))
+        return copies
+
+    def tail_copies(c):
+        return [
+            remote(own.at[pl.ds(tokens - tail, tail)], all_out.at[pl.ds(ncol * tokens, tail)],
+                   t_send.at[c, 0], t_recv.at[0], row=1, col=c),
+            remote(seg_own, seg_out.at[pl.ds(ncol * 8, 8)], t_send.at[c, 1], t_recv.at[1], row=1, col=c),
+        ]
+
+    def start(copies):
+        for copy in copies:
+            copy.start()
+
+    def guarded(when, action):
+        @pl.when(when)
+        def _():
+            action()
+
+    me = dp * 2 + row
+    guarded(z < last, lambda: start(token_copies(z, True, 0)))
+    guarded(z > 0, lambda: start(token_copies(z, True, 1)))
+    for m in range(1, ndp):
+        start(weight_copies(me, True, w_send.at[m], dp=dp ^ m))
+    start(weight_copies(me, True, c_send.at[0], row=other))
+    for c in range(ncol):
+        guarded(sends_tail, lambda c=c: start(tail_copies(c)))
+    local = [
+        pltpu.make_async_copy(own, all_out.at[pl.ds(z * tokens, tokens)], here.at[0]),
+        pltpu.make_async_copy(seg_own, seg_out.at[pl.ds(z * 8, 8)], here.at[1]),
+    ]
+    for i, (src, dst) in enumerate(weights):
+        local.append(pltpu.make_async_copy(src, dst.at[pl.ds(me * rows, rows)], here.at[2 + i]))
+    start(local)
+    fill = [
+        pltpu.make_async_copy(zero_tail, all_out.at[pl.ds(ncol * tokens, tail)], here.at[5]),
+        pltpu.make_async_copy(no_seg, seg_out.at[pl.ds(ncol * 8, 8)], here.at[6]),
+    ]
+    guarded(row == 0, lambda: start(fill))
+
+    def pass_tokens(s):
+        def from_below():
+            for copy in token_copies(z - s, False, 0):
+                copy.wait_recv()
+            guarded(z < last, lambda: start(token_copies(z - s, False, 0)))
+
+        def from_above():
+            for copy in token_copies(z + s, False, 1):
+                copy.wait_recv()
+            guarded(z > 0, lambda: start(token_copies(z + s, False, 1)))
+
+        guarded(z - s >= 0, from_below)
+        guarded(z + s <= last, from_above)
+
+    def pass_weights(m):
+        j = (dp ^ m) * 2 + row
+        for copy in weight_copies(j, False, w_send.at[m], dp=dp ^ m):
+            copy.wait_recv()
+        start(weight_copies(j, False, c_send.at[m], row=other))
+
+    done = 0
+    for s in range(1, ncol):
+        pass_tokens(s)
+        upto = (ndp - 1) * s // (ncol - 2) if s < ncol - 1 else ndp - 1
+        for m in range(done + 1, upto + 1):
+            pass_weights(m)
+        done = max(done, upto)
+    for m in range(ndp):
+        j = (dp ^ m) * 2 + other
+        for copy in weight_copies(j, False, c_send.at[m], row=other):
+            copy.wait_recv()
+    guarded(row == 1, lambda: [copy.wait_recv() for copy in tail_copies(0)])
+    for m in range(ndp):
+        if m:
+            for copy in weight_copies(me, True, w_send.at[m], dp=dp ^ m):
+                copy.wait_send()
+        for copy in weight_copies((dp ^ m) * 2 + row, m == 0, c_send.at[m], row=other):
+            copy.wait_send()
+    for s in range(ncol):
+        for way in range(2):
+            open_way = z < last if way == 0 else z > 0
+            mine = (z - s >= 0) if way == 0 else (z + s <= last)
+            src = z - s if way == 0 else z + s
+
+            def drain(way=way, src=src, s=s):
+                for copy in token_copies(src, s == 0, way):
+                    copy.wait_send()
+
+            guarded(open_way & mine, drain)
+    for c in range(ncol):
+        guarded(sends_tail, lambda c=c: [copy.wait_send() for copy in tail_copies(c)])
+    for copy in local:
+        copy.wait()
+    guarded(row == 0, lambda: [copy.wait() for copy in fill])
+
+
+def gather_inputs(own, seg_own, w0, w1, w2):
+    ncol, ndp = lax.axis_size("col"), lax.axis_size("dp")
+    tokens, width = own.shape
+    S = jax.ShapeDtypeStruct
+    shards = 2 * ndp
+    zero_tail = jnp.zeros((HALO, width), own.dtype)
+    no_seg = jnp.full((8, tokens), -1, jnp.int32)
+    dma = pltpu.SemaphoreType.DMA
+    sent = 2 * own.size * own.dtype.itemsize
+    return pl.pallas_call(
+        functools.partial(gather_kernel, ncol, ndp),
+        in_specs=[ANY] * 7,
+        out_specs=[ANY] * 5,
+        out_shape=[
+            S((ncol * tokens + HALO, width), own.dtype),
+            S(((ncol + 1) * 8, tokens), jnp.int32),
+        ] + [S((shards * w.shape[0], w.shape[1]), w.dtype) for w in (w0, w1, w2)],
+        scratch_shapes=[
+            dma((2, ncol, 2)), dma((ncol, 2)), dma((ndp, 3)), dma((ndp, 3)), dma((shards, 3)),
+            dma((ncol, 2)), dma((2,)), dma((7,)),
+        ],
+        compiler_params=pltpu.CompilerParams(collective_id=1, has_side_effects=True),
+        cost_estimate=pl.CostEstimate(flops=0, bytes_accessed=200_000_000, transcendentals=0),
+        name="gather_inputs",
+    )(own, seg_own, w0, w1, w2, zero_tail, no_seg)
+
+
+def sum_col_kernel(ncol, value, out, slots, send, recv):
+    z = lax.axis_index("col")
+    barrier = pltpu.get_barrier_semaphore()
+    for s in range(1, ncol):
+        pl.semaphore_signal(barrier, inc=1, device_id={"col": lax.rem(z + s, ncol)}, device_id_type=MESH)
+    pl.semaphore_wait(barrier, ncol - 1)
+    copies = [
+        remote(value, slots.at[z], send.at[s], recv.at[z], col=lax.rem(z + s, ncol)) for s in range(1, ncol)
+    ]
+    for copy in copies:
+        copy.start()
+    total = value[...]
+    for s in range(1, ncol):
+        source = lax.rem(z + s, ncol)
+        remote(value, slots.at[source], send.at[s], recv.at[source], col=source).wait_recv()
+        total = total + slots[source]
+    out[...] = total
+    for copy in copies:
+        copy.wait_send()
+
+
+def sum_col(value, collective_id):
+    ncol = lax.axis_size("col")
+    dma = pltpu.SemaphoreType.DMA
+    vmem = pl.BlockSpec(memory_space=pltpu.VMEM)
+    return pl.pallas_call(
+        functools.partial(sum_col_kernel, ncol),
+        in_specs=[vmem],
+        out_specs=vmem,
+        out_shape=jax.ShapeDtypeStruct(value.shape, F32),
+        scratch_shapes=[pltpu.VMEM((ncol,) + value.shape, F32), dma((ncol,)), dma((ncol,))],
+        compiler_params=pltpu.CompilerParams(collective_id=collective_id, has_side_effects=True),
+        name="sum_col",
+    )(value)
+
+
+def reduce_kernel(ncol, ndp, *refs):
+    g, vecs = refs[0:3], refs[3:7]
+    r, vec_outs = refs[7:10], refs[10:14]
+    own, near, sent, far = refs[14:17], refs[17:20], refs[20:23], refs[23:26]
+    vec_slots, col_slots, bc_slots = refs[26:30], refs[30:32], refs[32]
+    c_send, c_recv, p_send, p_recv, here, v_send, v_recv, u_send, u_recv, b_send, b_recv = refs[33:]
+    dp, row, z = lax.axis_index("dp"), lax.axis_index("row"), lax.axis_index("col")
+    other = 1 - row
+    me = dp * 2 + row
+    rows = [out.shape[0] for out in r]
+    barrier = pltpu.get_barrier_semaphore()
+    for q in range(1, 2 * ndp):
+        greet(barrier, row >= 0, dp=dp ^ (q >> 1), row=row ^ (q & 1))
+    for s in range(1, ncol):
+        greet(barrier, row >= 0, col=lax.rem(z + s, ncol))
+    pl.semaphore_wait(barrier, 2 * ndp + ncol - 2)
+
+    vec_copies = []
+    for q in range(1, 2 * ndp):
+        for i in range(4):
+            vec_copies.append(
+                remote(vecs[i], vec_slots[i].at[me], v_send.at[q, i], v_recv.at[me, i],
+                       dp=dp ^ (q >> 1), row=row ^ (q & 1))
+            )
+    for copy in vec_copies:
+        copy.start()
+
+    order = (1, 2, 0)
+
+    def core_copy(i, d):
+        return remote(g[i].at[pl.ds((d * 2 + other) * rows[i], rows[i])], near[i].at[d],
+                      c_send.at[i, d], c_recv.at[i, d], row=other)
+
+    def own_copy(i, d):
+        return pltpu.make_async_copy(g[i].at[pl.ds((d * 2 + row) * rows[i], rows[i])], own[i].at[d], here.at[i, d])
+
+    def peer_copy(i, m):
+        return remote(sent[i].at[m], far[i].at[m], p_send.at[i, m], p_recv.at[i, m], dp=dp ^ m)
+
+    turns = list(range(1, ndp)) + [0]
+    for i in order:
+        for m in turns:
+            core_copy(i, dp ^ m).start()
+            own_copy(i, dp ^ m).start()
+    waiting = []
+    for i in order:
+        for m in turns:
+            d = dp ^ m
+            core_copy(i, d).wait_recv()
+            own_copy(i, d).wait()
+            if m == 0:
+                continue
+
+            def add(step, carry, i=i, d=d, m=m):
+                at = pl.ds(pl.multiple_of(step * 16, 16), 16)
+                total = own[i][d, at].astype(F32) + near[i][d, at].astype(F32)
+                sent[i][m, at] = total.astype(BF16)
+                return carry
+
+            lax.fori_loop(0, rows[i] // 16, add, 0)
+            if waiting:
+                waiting.pop().start()
+            waiting.append(peer_copy(i, m))
+
+    def gather_vec():
+        for q in range(1, 2 * ndp):
+            j = me ^ q
+            for i in range(4):
+                remote(vecs[i], vec_slots[i].at[j], v_send.at[q, i], v_recv.at[j, i],
+                       dp=dp ^ (q >> 1), row=row ^ (q & 1)).wait_recv()
+        for i in range(4):
+            vec_slots[i][me] = vecs[i][...]
+            total = vec_slots[i][0]
+            for j in range(1, 2 * ndp):
+                total = total + vec_slots[i][j]
+            if i < 2:
+                vec_outs[i][...] = total
+            else:
+                col_slots[i - 2][z] = total
+
+    gather_vec()
+    waiting.pop().start()
+
+    def finish(i):
+        for m in range(1, ndp):
+            peer_copy(i, m).wait_recv()
+
+        def add(step, carry):
+            at = pl.ds(pl.multiple_of(step * 16, 16), 16)
+            total = own[i][dp, at].astype(F32) + near[i][dp, at].astype(F32)
+            for m in range(1, ndp):
+                total = total + far[i][m, at].astype(F32)
+            r[i][at] = total
+            if i == 1:
+                bc_slots[z, at] = total[:, : bc_slots.shape[2]].astype(BF16)
+            return carry
+
+        lax.fori_loop(0, rows[i] // 16, add, 0)
+
+    def col_copies(s, source):
+        to = lax.rem(z + s, ncol)
+        copies = [remote(col_slots[i].at[source], col_slots[i].at[source], u_send.at[s, i], u_recv.at[source, i], col=to)
+                  for i in range(2)]
+        return copies + [remote(bc_slots.at[source], bc_slots.at[source], b_send.at[s], b_recv.at[source], col=to)]
+
+    finish(1)
+    finish(2)
+    for s in range(1, ncol):
+        for copy in col_copies(s, z):
+            copy.start()
+    finish(0)
+    for s in range(1, ncol):
+        for copy in col_copies(s, lax.rem(z + s, ncol)):
+            copy.wait_recv()
+    for i in range(2):
+        total = col_slots[i][0]
+        for j in range(1, ncol):
+            total = total + col_slots[i][j]
+        vec_outs[2 + i][...] = total
+    total = bc_slots[0].astype(F32)
+    for j in range(1, ncol):
+        total = total + bc_slots[j].astype(F32)
+    r[1][:, : bc_slots.shape[2]] = total
+
+    for copy in vec_copies:
+        copy.wait_send()
+    for i in order:
+        for m in turns:
+            core_copy(i, dp ^ m).wait_send()
+            if m:
+                peer_copy(i, m).wait_send()
+    for s in range(1, ncol):
+        for copy in col_copies(s, z):
+            copy.wait_send()
+
+
+def reduce_grads(grads, vecs, scols):
+    ncol, ndp = lax.axis_size("col"), lax.axis_size("dp")
+    dma = pltpu.SemaphoreType.DMA
+    vmem = pl.BlockSpec(memory_space=pltpu.VMEM)
+    S = jax.ShapeDtypeStruct
+    blocks = [(g.shape[0] // (2 * ndp), g.shape[1]) for g in grads]
+    stack = [pltpu.VMEM((ndp,) + b, BF16) for b in blocks]
+    return pl.pallas_call(
+        functools.partial(reduce_kernel, ncol, ndp),
+        in_specs=[ANY] * 3 + [vmem] * 4,
+        out_specs=[vmem] * 7,
+        out_shape=[S(b, F32) for b in blocks] + [S(v.shape, F32) for v in vecs],
+        scratch_shapes=stack * 4
+        + [pltpu.VMEM((2 * ndp,) + v.shape, F32) for v in vecs]
+        + [pltpu.VMEM((ncol,) + v.shape, F32) for v in vecs[2:]]
+        + [pltpu.VMEM((ncol, blocks[1][0], scols), BF16)]
+        + [dma((3, ndp))] * 5
+        + [dma((2 * ndp, 4))] * 2
+        + [dma((ncol, 2))] * 2
+        + [dma((ncol,))] * 2,
+        compiler_params=pltpu.CompilerParams(collective_id=2, has_side_effects=True),
+        cost_estimate=pl.CostEstimate(flops=0, bytes_accessed=200_000_000, transcendentals=0),
+        name="reduce_grads",
+    )(*grads, *vecs)
 
 
 def pass_on(value, axis, by):
@@ -545,110 +1033,91 @@
     return jnp.concatenate(rows + [jnp.zeros((8 - used, width), F32)], axis=0)
 
 
+def normalized(tokens, gain):
+    wide = tokens.astype(F32)
+    scale = lax.rsqrt(jnp.mean(wide * wide, axis=1, keepdims=True) + EPS)
+    return wide, scale, (wide * scale * gain[None, :]).astype(BF16)
+
+
 def per_device(
     block_input, segment_ids, norm_gain, proj_zx, proj_bc, proj_dt, conv_inner, conv_inner_bias,
     conv_shared, conv_shared_bias, step_bias, rate_log, skip_gain, gated_gain, proj_out, cotangent,
 ):
-    model_dim = block_input.shape[1]
     width = proj_zx.shape[2]
     scols = proj_bc.shape[1]
     nheads = proj_dt.shape[1]
+    head_dim = width // nheads
     full_width = float(width * lax.axis_size("col"))
-    shards = ("dp", "row")
-    x_all = lax.all_gather(block_input, "col", axis=0, tiled=True)
-    cot_all = lax.all_gather(cotangent, "col", axis=0, tiled=True)
-    seg_all = lax.all_gather(segment_ids, "col", axis=0, tiled=True)
-    w_in = lax.all_gather(proj_zx.reshape(-1, 2 * width), shards, axis=0, tiled=True)
     small_own = jnp.concatenate(
         [proj_bc, proj_dt, jnp.zeros((proj_dt.shape[0], 128 - nheads), BF16)], axis=1
     )
-    w_small = lax.all_gather(small_own, shards, axis=0, tiled=True)
-    out_t = lax.all_gather(proj_out.T, shards, axis=0, tiled=True)
-
-    length = x_all.shape[0]
-    tail_x, tail_seg = pass_on((x_all[-HALO:], seg_all[-HALO:] + 1), "row", 1)
-    x_ext = jnp.concatenate([x_all, tail_x], axis=0)
-    seg_ext = jnp.concatenate([seg_all, tail_seg - 1], axis=0)
-    wide = x_ext.astype(F32)
-    scale = lax.rsqrt(jnp.mean(wide * wide, axis=1, keepdims=True) + EPS)
-    normed_ext = (wide * scale * norm_gain[None, :]).astype(BF16)
-    normed = normed_ext[:length]
-    both_ext = nn(normed_ext, w_in).astype(BF16)
-    small_ext = nn(normed_ext, w_small)
-    shared_ext = small_ext[:, :scols].astype(BF16)
-    step_ext = small_ext[:, scols:]
-
-    head_dim = width // nheads
+    wide, scale, normed_own = normalized(block_input, norm_gain)
+    seg_own = jnp.broadcast_to(segment_ids[None], (8, segment_ids.shape[0]))
     taps = pack_rows(
         [conv_inner, conv_inner_bias[None], gated_gain[None], jnp.repeat(skip_gain, head_dim)[None]], width
     )
     taps_s = pack_rows([conv_shared, conv_shared_bias[None]], scols)
     fill = (0, 128 - nheads)
-    heads = pack_rows([jnp.pad(step_bias, fill)[None], jnp.pad(rate_log, fill)[None], jnp.zeros((5, 128), F32)], 128)
-    heads = jnp.concatenate([heads[:7], jnp.full((1, 128), seg_ext[-1], F32)], axis=0)
-    common = (both_ext, shared_ext, step_ext, seg_ext[:, None], seg_all[None, :], taps, taps_s, heads)
+    heads = pack_rows([jnp.pad(step_bias, fill)[None], jnp.pad(rate_log, fill)[None]], 128)
+
+    normed_ext, seg, w_in, w_small, out_t = gather_inputs(
+        normed_own, seg_own, proj_zx.reshape(-1, 2 * width), small_own, proj_out.T
+    )
+    length = normed_ext.shape[0] - HALO
+    cot, normed_ext = lax.optimization_barrier((cotangent, normed_ext))
+    cot_all = lax.all_gather(cot, "col", axis=0, tiled=True)
+
+    both_ext = nn(normed_ext, w_in).astype(BF16)
+    small_ext = nn(normed_ext, w_small)
+    shared_ext = small_ext[:, :scols].astype(BF16)
+    step_ext = small_ext[:, scols:]
+    common = (both_ext, shared_ext, step_ext, seg, taps, taps_s, heads)
     y, x, bc, dt, c, ct, dec, enter, final = run_forward(*common)
     start = pass_on(final, "row", 1)
-    back = nn(cot_all, out_t).astype(BF16)
-    ssd, sums = run_gate(y, x, bc, dec, start, both_ext, back, taps)
-    sums = lax.psum(jnp.concatenate([sums[0:1], sums[8:9]], axis=0), "col")
-    sums = jnp.concatenate([sums, jnp.zeros((6, length), F32)], axis=0)
-    gated_normed, dy, ggate, rowterm, colsum, dstart = run_back(
-        full_width, ssd, x, bc, dec, both_ext, back, sums, taps
+    ssd, gated, squares = run_gate(y, x, bc, dec, start, both_ext, taps)
+    squares = sum_col(squares, 3)
+    gated_normed, projected = run_project(full_width, gated, squares, taps, out_t)
+    projected = lax.psum_scatter(projected, "col", scatter_dimension=0, tiled=True)
+    block_output = (wide + projected.astype(F32)).astype(BF16)
+    back, inner = run_pull(cot_all, out_t, gated, taps)
+    inner = sum_col(inner, 4)
+    dy, ggate, rowterm, colsum, dstart = run_back(
+        full_width, ssd, x, bc, dec, both_ext, back, squares, inner, taps
     )
     dend = pass_on(dstart, "row", -1)
-    projected = lax.psum_scatter(
-        nt(gated_normed, out_t).astype(BF16), "col", scatter_dimension=0, tiled=True
-    )
-    block_output = (block_input.astype(F32) + projected.astype(F32)).astype(BF16)
-    grad_out = lax.psum_scatter(
-        tn(cot_all, gated_normed).astype(BF16), shards, scatter_dimension=0, tiled=True
-    )
+    gout = tn(cot_all, gated_normed).astype(BF16)
     ginner, gshared, gstep, par, par_s, par_h, edge, edge_s, last, last_s = run_backward(
-        *common, dy, x, bc, dt, c, ct, dec, enter, start, rowterm, dend
+        *common, dy, x, bc, dt, c, ct, dec, enter, start, rowterm, dend, colsum
     )
     edge, edge_s = pass_on((edge, edge_s), "row", -1)
     ginner = lax.dynamic_update_slice(ginner, (last + edge).astype(BF16), (length - 8, 0))
     gshared = lax.dynamic_update_slice(gshared, (last_s + edge_s).astype(BF16), (length - 8, 0))
     gsmall = jnp.concatenate([gshared, gstep], axis=1)
-    part_normed = nt(ggate, w_in[:, :width]) + nt(ginner, w_in[:, width:]) + nt(gsmall, w_small)
-    grad_normed = lax.psum_scatter(
-        part_normed.astype(BF16), "col", scatter_dimension=0, tiled=True
-    ).astype(F32)
-    gain_part = jnp.sum(part_normed * (wide * scale)[:length], axis=0)
-    gboth = jnp.concatenate([ggate, ginner], axis=1)
-    gzx = lax.psum_scatter(tn(normed, gboth).astype(BF16), shards, scatter_dimension=0, tiled=True)
-    gsm = lax.psum_scatter(tn(normed, gsmall), shards, scatter_dimension=0, tiled=True)
-    rows_a = jnp.concatenate([par[:5], colsum[:2], jnp.zeros((1, width), F32)], axis=0)
-    vec_a = jnp.concatenate([rows_a.reshape(-1), par_h[:2].reshape(-1)])
-    vec_b = jnp.concatenate([par_s[:5].reshape(-1), gain_part])
-    vec_a = lax.psum(vec_a, shards)
-    vec_b = lax.psum(vec_b, shards)
-    vec_b, grad_bc = lax.psum((vec_b, gsm[:, :scols]), "col")
-    rows_a = vec_a[: 8 * width].reshape(8, width)
-    par_h = vec_a[8 * width :].reshape(2, 128)[:, :nheads]
-    rows_b = vec_b[: 5 * scols].reshape(5, scols)
-    own = block_input.astype(F32)
-    own_scale = lax.rsqrt(jnp.mean(own * own, axis=1, keepdims=True) + EPS)
+    part, gain_part = run_spread(ggate, ginner, gsmall, w_in, w_small, normed_ext)
+    grad_normed = lax.psum_scatter(part, "col", scatter_dimension=0, tiled=True).astype(F32)
+    normed = normed_ext[:length]
+    gzx = jnp.concatenate([tn(normed, ggate).astype(BF16), tn(normed, ginner).astype(BF16)], axis=1)
+    gsm = tn(normed, gsmall).astype(BF16)
+    gzx, gsm, gout, par, par_h, par_s, gain_sum = reduce_grads((gzx, gsm, gout), (par, par_h, par_s, gain_part), scols)
     pushed = grad_normed * norm_gain[None, :]
-    grad_wide = own_scale * pushed - own * own_scale**3 * jnp.mean(pushed * own, axis=1, keepdims=True)
+    grad_wide = scale * pushed - wide * scale**3 * jnp.mean(pushed * wide, axis=1, keepdims=True)
     grad_input = (cotangent.astype(F32) + grad_wide).astype(BF16)
     return (
         block_output,
         grad_input,
-        vec_b[5 * scols :],
-        gzx.astype(F32).reshape(-1, 2, width),
-        grad_bc,
+        gain_sum[0] / norm_gain,
+        gzx.reshape(-1, 2, width),
+        gsm[:, :scols],
         gsm[:, scols : scols + nheads],
-        rows_a[:4],
-        rows_a[4],
-        rows_b[:4],
-        rows_b[4],
-        par_h[0],
-        par_h[1],
-        jnp.sum(rows_a[6].reshape(nheads, head_dim), axis=1),
-        rows_a[5],
-        grad_out.astype(F32).T,
+        par[:4],
+        par[4],
+        par_s[:4],
+        par_s[4],
+        par_h[0, :nheads],
+        par_h[1, :nheads],
+        jnp.sum(par[6].reshape(nheads, head_dim), axis=1),
+        par[5],
+        gout.T,
     )
 
 

time: 608 us -> 356 us (0.59); the launches traced: 599 us -> 355 us
  waiting for transfers between devices: 339 us -> 37.3 us
  Pallas kernels: 60.2 us -> 228 us
  blocking collectives: 68.4 us -> 0 us
  matrix products: 59.6 us -> 28.1 us
    pallas_call x0 -> x7, Pallas kernels: none -> 168 us  [the longest x1 62.9 us: gather_inputs(): pl.pallas_call(functools.partial(gather_kernel, ncol, ndp), in_specs=[ANY...]
    all_gather x5 -> x1, waiting for transfers between devices: 165 us -> 12.9 us  [per_device(): cot_all = lax.all_gather(cot, 'col', axis=0, tiled=True)]
    reduce_scatter x4 -> x2, waiting for transfers between devices: 132 us -> 19.8 us  [the longest x1 19.8 us: per_device(): lax.psum_scatter(projected, 'col', scatter_dimension=0, tiled=True)]
    psum x3 -> x0, blocking collectives: 55.7 us -> none  [the longest x1 26.8 us: per_device(): vec_b = lax.psum(vec_b, shards)]
    psum x1 -> x0, waiting for transfers between devices: 35 us -> none  [per_device(): vec_b, grad_bc = lax.psum((vec_b, gsm[:, :scols]), 'col')]
    dot_general x4 -> x0, matrix products: 21.7 us -> none  [nt(): lax.dot_general(a, b, (((1,), (1,)), ((), ())), preferred_element_type=F32)]
    all_gather x1 -> x0, blocking collectives: 12.7 us -> none  [per_device(): seg_all = lax.all_gather(segment_ids, 'col', axis=0, tiled=True)]
    dot_general x3 -> x4, matrix products: 19.6 us -> 14.6 us  [tn(): lax.dot_general(a, b, (((0,), (0,)), ((), ())), preferred_element_type=F32)]
  transfers between devices with their start and end apart: 17 -> 7, of which waited for: 11 -> 5; matrix products, arithmetic and copies ran while one was open for 15% -> 15% of each run, Pallas kernels for 7% -> 28%
where the time goes in v2:
time: 356 us; the launch traced here: 355 us
  Pallas kernels  228 us (64%)
  waiting for transfers between devices  37.3 us (10%)
  matrix products  28.1 us (8%)
  local copies, waits for them, and re-layouts  24.9 us (7%)
  other arithmetic  16.9 us (5%)
  between operations  14.1 us (4%)
  starting transfers between devices  5.99 us (2%)
    pallas_call x1, Pallas kernels, gather_inputs(): pl.pallas_call(functools.partial(gather_kernel, ncol, ndp), in_specs=[ANY...  62.9 us
    pallas_call x1, Pallas kernels, reduce_grads(): pl.pallas_call(functools.partial(reduce_kernel, ncol, ndp), in_specs=[ANY...  61.5 us
    pallas_call x1, Pallas kernels, run_backward(): pl.pallas_call(backward_kernel, grid=(chunks,), in_specs=[pl.BlockSpec((S...  30.7 us
    reduce_scatter x1, waiting for transfers between devices, per_device(): lax.psum_scatter(projected, 'col', scatter_dimension=0, tiled=True)  19.8 us
    pallas_call x2, Pallas kernels, sum_col(): pl.pallas_call(functools.partial(sum_col_kernel, ncol), in_specs=[vmem],...  17.9 us
    dot_general x4, matrix products, tn(): lax.dot_general(a, b, (((0,), (0,)), ((), ())), preferred_element_type=F32)  14.6 us
    pallas_call x1, Pallas kernels, run_forward(): pl.pallas_call(forward_kernel, grid=(chunks,), in_specs=[pl.BlockSpec((SP...  13.7 us
    dot_general x2, matrix products, nn(): lax.dot_general(a, b, (((1,), (0,)), ((), ())), preferred_element_type=F32)  13.5 us
  transfers between devices with their start and end apart: 7, of which 5 were waited for; matrix products, arithmetic and copies ran while one was open for 15% of the time, Pallas kernels for 28%

profile of v2, /device:TPU:0, one launch (start us, length us, event | category | flops | bytes accessed | tf_op | source)
XLA Modules:
  0.0 355.0 jit_solution(11417569307641737884)
XLA Ops:
  7.2 1.4 fusion.3
  8.7 0.9 copy.31
  9.6 1.9 copy.37
  11.6 1.1 fusion.5.own
  15.2 62.9 %gather_inputs.1 = (bf16[1040,1536]{1,0:T(8,128)(2,1)}, s32[40,256]{1,0:T(8,128)}, bf16[1536,1536]{1,0:T(8,128)(2,1)}, bf16[1536,384]{1,0:T(8,128)(2,1)}, bf16[1536,768]{1,0:T(8,128)(2,1)}) custom-call(bf16[256,1536]{1,0:T(8,128)(2,1)} %fusion.5.own, s32[8,256]{1,0:T(8,128)} %broadcast_in_dim.46.seg_own, bf16[192,1536]{1,0:T(8,128)(2,1)} %bitcast.22, ...), custom_call_target="tpu_custom_call" | custom-call | bytes 200000000 | tf_op jit(solution)/shard_map/gather_inputs/pallas_call | solution.py:809
  78.2 4.1 %fusion.14 = f32[1040,384]{1,0:T(8,128)S(1)} fusion(bf16[1040,1536]{1,0:T(8,128)(2,1)} %get-tuple-element.63.normed, bf16[1536,384]{1,0:T(8,128)(2,1)} %get-tuple-element.65.w_small), kind=kOutput, calls=%fused_computation.44 | convolution fusion | flops 1226833920 | bytes 5971968 | tf_op jit(solution)/shard_map/dot_general | solution.py:16
  82.4 0.8 slice.58.step_raw
  83.2 0.8 slice.72.shared.shared_halo
  86.4 9.4 %convolution_convert_fusion.inner.inner_halo.gate = bf16[1040,1536]{1,0:T(8,128)(2,1)} fusion(bf16[1040,1536]{1,0:T(8,128)(2,1)} %get-tuple-element.63.normed, bf16[1536,1536]{1,0:T(8,128)(2,1)} %get-tuple-element.64.w_in), kind=kOutput, calls=%fused_computation | convolution fusion | flops 4908933120 | bytes 11108352 | tf_op jit(solution)/shard_map/dot_general | solution.py:16
  95.8 13.7 %scan_forward.1 = (f32[1024,768]{1,0:T(8,128)}, bf16[1024,768]{1,0:T(8,128)(2,1)}, bf16[1024,256]{1,0:T(8,128)(2,1)}, f32[1024,128]{1,0:T(8,128)}, f32[1024,128]...) custom-call(bf16[1040,1536]{1,0:T(8,128)(2,1)} %convolution_convert_, ...), custom_call_target="tpu_custom_call" | custom-call | tf_op jit(solution)/shard_map/scan_forward/pallas_call | solution.py:164
  109.6 1.6 collective-permute-start
  111.2 1.5 collective-permute-done.start
  113.4 6.9 %gate_sums.1 = (f32[1024,768]{1,0:T(8,128)}, bf16[1024,768]{1,0:T(8,128)(2,1)}, f32[8,1024]{1,0:T(8,128)}) custom-call(f32[1024,768]{1,0:T(8,128)} %get-tuple-element.67.y, bf16[1024,768]{1,0:T(8,128)(2,1)} %get-tuple-element.68.x, bf16[1024,256]{1,0:T(8,128)(2,1)} %get-tuple-element.69.bc, f32[1024,128]{1,0:T(8,128)} %get-tuple-element.70.dec.dec_halo, ...), custom_call_target="tpu_custom_call" | custom-call | tf_op jit(solution)/shard_map/gate_sums/pallas_call | solution.py:239
  120.4 10.6 %sum_col.2.sums.squares = f32[8,1024]{1,0:T(8,128)} custom-call(f32[8,1024]{1,0:T(8,128)} %get-tuple-element.73.value), custom_call_target="tpu_custom_call" | custom-call | tf_op jit(solution)/shard_map/sum_col/pallas_call | solution.py:852
  131.0 12.9 %all-gather.2.cloned.1.call-done.cot = bf16[1024,1536]{1,0:T(8,128)(2,1)} async-done(((bf16[256,1536]{1,0:T(8,128)(2,1)}), bf16[1024,1536]{1,0:T(8,128)(2,1)}) %all-gather.2.cloned.1.call-update) | async-done | bytes 3145744 | tf_op jit(solution)/shard_map/all_gather | solution.py:1068
  143.9 6.9 %pull_back.1 = (bf16[1024,768]{1,0:T(8,128)(2,1)}, f32[8,1024]{1,0:T(8,128)}) custom-call(bf16[1024,1536]{1,0:T(8,128)(2,1)} %all-gather.2.cloned.1.call-done.cot, bf16[1536,768]{1,0:T(8,128)(2,1)} %get-tuple-element.74.out_t, bf16[1024,768]{1,0:T(8,128)(2,1)} %get-tuple-element.72.gated, f32[8,768]{1,0:T(8,128)} %concatenate.19.taps), custom_call_target="tpu_custom_call" | custom-call | tf_op jit(solution)/shard_map/pull_back/pallas_call | solution.py:304
  150.8 7.2 %sum_col.3.inner = f32[8,1024]{1,0:T(8,128)} custom-call(f32[8,1024]{1,0:T(8,128)} %get-tuple-element.79.value), custom_call_target="tpu_custom_call" | custom-call | tf_op jit(solution)/shard_map/sum_col/pallas_call | solution.py:852
  158.0 8.6 %gated_back.1 = (bf16[1024,768]{1,0:T(8,128)(2,1)}, bf16[1024,768]{1,0:T(8,128)(2,1)}, f32[1024,128]{1,0:T(8,128)}, f32[8,768]{1,0:T(8,128)}, f32[128,768]{1,0:T(8,128)}) custom-call(f32[1024,768]{1,0:T(8,128)} %get-tuple-element.76.ssd, bf16[1024,768]{1,0:T(8,128)(2,1)} %get-tuple-element.68.x, bf16[1024,256]{1,0:T(8,128)(2,1)} %get-tuple-element.69.bc, ...), custom_call_target="tpu_custom_call" | custom-call | tf_op jit(solution)/shard_map/gated_back/pallas_call | solution.py:367
  166.7 1.5 collective-permute-start.1
  168.2 2.3 collective-permute-done.1.dend
  170.5 0.8 copy-done.10
  171.3 30.7 %scan_backward.1 = (bf16[1024,768]{1,0:T(8,128)(2,1)}, bf16[1024,256]{1,0:T(8,128)(2,1)}, bf16[1024,128]{1,0:T(8,128)(2,1)}, f32[8,768]{1,0:T(8,128)}, f32[8,256...) custom-call(bf16[1040,1536]{1,0:T(8,128)(2,1)} %convolution_convert_, ...), custom_call_target="tpu_custom_call" | custom-call | tf_op jit(solution)/shard_map/scan_backward/pallas_call | solution.py:548
  202.0 1.3 collective-permute-start.3
  203.3 1.3 collective-permute-start.2
  205.3 1.3 fusion.13
  206.6 2.1 pad_maximum_fusion.1.gsmall
  209.3 11.9 %spread_back.1 = (bf16[1024,1536]{1,0:T(8,128)(2,1)}, f32[8,1536]{1,0:T(8,128)}) custom-call(bf16[1024,768]{1,0:T(8,128)(2,1)} %get-tuple-element.80.ggate, bf16[1024,768]{1,0:T(8,128)(2,1)} %fusion.12.ginner, bf16[1024,384]{1,0:T(8,128)(2,1)} %pad_maximum_fusion.1.gsmall, bf16[1536,1536]{1,0:T(8,128)(2,1)} %get-tuple-element.64.w_in, ...), custom_call_target="tpu_custom_call" | custom-call | tf_op jit(solution)/shard_map/spread_back/pallas_call | solution.py:626
  221.4 6.7 %project.1 = (bf16[1024,768]{1,0:T(8,128)(2,1)}, bf16[1024,1536]{1,0:T(8,128)(2,1)}) custom-call(bf16[1024,768]{1,0:T(8,128)(2,1)} %get-tuple-element.72.gated, f32[8,1024]{1,0:T(8,128)} %sum_col.2.sums.squares, f32[8,768]{1,0:T(8,128)} %concatenate.19.taps, bf16[1536,768]{1,0:T(8,128)(2,1)} %get-tuple-element.74.out_t), custom_call_target="tpu_custom_call" | custom-call | tf_op jit(solution)/shard_map/project/pallas_call | solution.py:274
  228.2 1.4 copy-done.5
  229.6 4.7 %convolution_convert_fusion.3 = bf16[1536,768]{1,0:T(8,128)(2,1)S(1)} fusion(bf16[1024,768]{1,0:T(8,128)(2,1)S(1)} %copy-done.5, bf16[1040,1536]{1,0:T(8,128)(2,1)} %get-tuple-element.63.normed), kind=kOutput, calls=%fused_computation.4 | convolution fusion | flops 2417098752 | bytes 7077888 | tf_op jit(solution)/shard_map/dot_general | solution.py:24
  234.4 4.1 %convolution_convert_fusion.1.refs_2_ = bf16[1536,768]{1,0:T(8,128)(2,1)} fusion(bf16[1024,1536]{1,0:T(8,128)(2,1)S(1)} %copy-done.3, bf16[1024,768]{1,0:T(8,128)(2,1)S(1)} %copy-done.24), kind=kOutput, calls=%fused_computation.2 | convolution fusion | flops 2417098752 | bytes 7077888 | tf_op jit(solution)/shard_map/dot_general | solution.py:24
  238.4 2.9 convolution_convert_fusion.4.refs_1_
  241.3 2.9 convolution_convert_fusion.2
  244.3 2.5 pad_maximum_fusion.refs_0_
  246.8 61.5 %reduce_grads.1 = (f32[192,1536]{1,0:T(8,128)}, f32[192,384]{1,0:T(8,128)}, f32[192,768]{1,0:T(8,128)}, f32[8,768]{1,0:T(8,128)}, f32[8,128]{1,0:T(8,128)}, /*index=5*/f32[8,256]{1,0:T(8,128)}, f32[8,1536]{1,0:T(8,128)}) custom-call(bf16[1536,1536]{1,0:T(8,128)(2,1)} %pad_maximum_fusion.refs_0_, bf16[1536,384]{1,0:T(8,128)(2,1)} %convolution_convert_fusion.4.refs_1_, ...), custom_call_target="tpu_custom_call" | custom-call | bytes 200000000 | tf_op jit(solution)/shard_map/reduce_grads/pallas_call | solution.py:1006
  308.3 1.3 slice.52
  309.6 1.3 slice.51
  310.9 0.9 slice.48
  311.8 1.6 slice.47
  313.4 0.8 slice_reduce_fusion
  314.8 1.3 slice.49
  316.2 1.5 slice_reduce_fusion.1
  319.0 3.0 reshape.57
  322.0 1.3 slice_bitcast_fusion
  323.3 1.5 fusion.11
  324.9 19.8 %reduce-scatter.3.cloned.1.call-done = bf16[256,1536]{1,0:T(8,128)(2,1)} async-done(((bf16[1024,1536]{1,0:T(8,128)(2,1)}), bf16[256,1536]{1,0:T(8,128)(2,1)}) %reduce-scatter.3.cloned.1.call-update) | async-done | bytes 786448 | tf_op jit(solution)/shard_map/reduce_scatter | solution.py:1080
  344.7 3.0 fusion.10
  347.7 0.8 copy.41
  (83 shorter events, 9.4 us)
Async XLA Ops:
  7.2 4.4 %copy-start = (bf16[256,1536]{1,0:T(8,128)(2,1)S(1)}, bf16[256,1536]{1,0:T(8,128)(2,1)}, u32[]{:S(2)}) copy-start(bf16[256,1536]{1,0:T(8,128)(2,1)} %param.16) | copy-start | bytes 2359300
  7.2 4.4 %copy-start.12 = (f32[1536]{0:T(1024)S(1)}, f32[1536]{0:T(1024)}, u32[]{:S(2)}) copy-start(f32[1536]{0:T(1024)} %param.18) | copy-start | bytes 18436
  7.2 136.7 %all-gather.2.cloned.1.call-start = ((), (), s32[]{:S(2)}) async-start(), calls=%async_computation.3 | async-start | bytes 3932160 | tf_op jit(solution)/shard_map/all_gather | solution.py:1068
  8.7 4.0 %copy-start.13 = (bf16[192,256]{1,0:T(8,128)(2,1)S(1)}, bf16[192,256]{1,0:T(8,128)(2,1)}, u32[]{:S(2)}) copy-start(bf16[192,256]{1,0:T(8,128)(2,1)} %param.20) | copy-start | bytes 294916
  8.7 4.7 %copy-start.19 = (s32[256]{0:T(256)S(1)}, s32[256]{0:T(256)}, u32[]{:S(2)}) copy-start(s32[256]{0:T(256)} %param.17) | copy-start | bytes 3076
  78.2 245.1 %reduce-scatter.5.cloned.1.call-start = ((), (), s32[]{:S(2)}) async-start(), calls=%async_computation.4 | async-start | bytes 3932160 | tf_op jit(solution)/shard_map/reduce_scatter | solution.py:1097
  82.3 1.9 copy-start.17
  82.3 1.9 copy-start.18
  82.3 1.9 copy-start.21
  82.3 2.1 copy-start.15
  82.3 2.7 copy-start.22
  82.3 2.7 copy-start.23
  82.4 3.4 copy-start.16
  82.4 3.4 copy-start.20
  109.6 3.1 collective-permute-start
  112.7 0.8 copy-start.7
  166.7 3.8 %collective-permute-start.1 = (f32[128,768]{1,0:T(8,128)}, f32[128,768]{1,0:T(8,128)S(1)}, u32[]{:S(2)}, u32[]{:S(2)}) collective-permute-start(f32[128,768]{1,0:T(8,128)} %get-tuple-element.87), channel_id=1, source_target_pairs={{4,0},{5,1},{6,2},{7,3},{12,8},{13,9},{14,10},{15,11},{20,16},{21,... | collective-permute-start | bytes 1179656 | tf_op jit(solution)/shard_map/ppermute | solution.py:1028
  170.5 0.8 copy-start.10
  202.0 6.7 %copy-start.14 = (f32[8,768]{1,0:T(8,128)S(1)}, f32[8,768]{1,0:T(8,128)}, u32[]{:S(2)}) copy-start(f32[8,768]{1,0:T(8,128)} %get-tuple-element.90) | copy-start | bytes 73732
  202.0 3.3 collective-permute-start.3
  203.3 5.4 %collective-permute-start.2 = (f32[8,768]{1,0:T(8,128)}, f32[8,768]{1,0:T(8,128)S(1)}, u32[]{:S(2)}, u32[]{:S(2)}) collective-permute-start(f32[8,768]{1,0:T(8,128)} %get-tuple-element.91), channel_id=1, source_target_pairs={{4,0},{5,1},{6,2},{7,3},{12,8},{13,9},{14,10},{15,11},{20,16},{21,... | collective-permute-start | bytes 73736 | tf_op jit(solution)/shard_map/ppermute | solution.py:1028
  221.2 123.5 %reduce-scatter.3.cloned.1.call-start = ((), (), s32[]{:S(2)}) async-start(), calls=%async_computation.2 | async-start | bytes 3932160 | tf_op jit(solution)/shard_map/reduce_scatter | solution.py:1080
  228.2 1.4 copy-start.5
  229.6 4.7 %copy-start.3 = (bf16[1024,1536]{1,0:T(8,128)(2,1)S(1)}, bf16[1024,1536]{1,0:T(8,128)(2,1)}, u32[]{:S(2)}) copy-start(bf16[1024,1536]{1,0:T(8,128)(2,1)} %all-gather.2.cloned.1.call-done.cot) | copy-start | bytes 9437188
  229.6 4.7 %copy-start.24 = (bf16[1024,768]{1,0:T(8,128)(2,1)S(1)}, bf16[1024,768]{1,0:T(8,128)(2,1)}, u32[]{:S(2)}) copy-start(bf16[1024,768]{1,0:T(8,128)(2,1)} %get-tuple-element.97) | copy-start | bytes 4718596
  234.3 4.1 %copy-start.1 = (bf16[1040,1536]{1,0:T(8,128)(2,1)S(1)}, bf16[1040,1536]{1,0:T(8,128)(2,1)}, u32[]{:S(2)}) copy-start(bf16[1040,1536]{1,0:T(8,128)(2,1)} %get-tuple-element.63.normed) | copy-start | bytes 9584644
  234.3 4.1 %copy-start.9 = (bf16[1024,256]{1,0:T(8,128)(2,1)S(1)}, bf16[1024,256]{1,0:T(8,128)(2,1)}, u32[]{:S(2)}) copy-start(bf16[1024,256]{1,0:T(8,128)(2,1)} %fusion.13) | copy-start | bytes 1572868
  234.4 4.1 %copy-start.11 = (bf16[1024,128]{1,0:T(8,128)(2,1)S(1)}, bf16[1024,128]{1,0:T(8,128)(2,1)}, u32[]{:S(2)}) copy-start(bf16[1024,128]{1,0:T(8,128)(2,1)} %get-tuple-element.95) | copy-start | bytes 786436
  238.4 2.9 copy-start.6
  319.0 25.7 %copy-start.2 = (bf16[256,1536]{1,0:T(8,128)(2,1)S(1)}, bf16[256,1536]{1,0:T(8,128)(2,1)}, u32[]{:S(2)}) copy-start(bf16[256,1536]{1,0:T(8,128)(2,1)} %param.31) | copy-start | bytes 2359300
  323.3 21.4 %copy-start.4 = (bf16[256,1536]{1,0:T(8,128)(2,1)S(1)}, bf16[256,1536]{1,0:T(8,128)(2,1)}, u32[]{:S(2)}) copy-start(bf16[256,1536]{1,0:T(8,128)(2,1)} %reduce-scatter.5.cloned.1.call-done) | copy-start | bytes 2359300
  344.7 3.0 copy-start.8
Sparse Core Ops, SparseCore 0:
  78.3 65.5 all-gather.1
  221.3 60.1 reduce-scatter.4
  283.8 60.8 reduce-scatter.2

commit v3 on v2

--- a/solution.py
+++ b/solution.py
@@ -420,7 +420,7 @@
 def backward_kernel(
     inner, inner_halo, shared, shared_halo, step_raw, seg_row, seg_prev, seg_tail, taps, taps_s, heads,
     dy, x, bc, dt_in, c_in, ct_in, dec_halo, enter, start, row_in, dend, colsum,
-    ginner_out, gshared_out, gstep_out, par_out, par_s_out, par_h_out, edge_out, edge_s_out, last_out, last_s_out,
+    ginner_out, gsmall_out, par_out, par_s_out, par_h_out, edge_out, last_out,
     dstate, carry, carry_s, carry_links, grads_bc,
 ):
     i = pl.program_id(0)
@@ -514,12 +514,13 @@
         sl = slice(half * state_dim, (half + 1) * state_dim)
         pre, shifts = conv_tile(shared, shared_halo, links, taps_s, sl)
         grad, above = conv_back(grads_bc[:, sl], pre, shifts, links, taps_s, sl, carry_s, next_links, par_s_out)
-        gshared_out[:, sl] = grad.astype(BF16)
-        edge_s_out[:, sl] = above
+        gsmall_out[:, sl] = grad.astype(BF16)
+        at = slice(width + half * state_dim, width + (half + 1) * state_dim)
+        edge_out[:, at] = above
 
         @pl.when(i == 0)
         def _():
-            last_s_out[:, sl] = grad[length - 8 :]
+            last_out[:, at] = grad[length - 8 :]
 
     for j in range(3):
         carry_links[:, j : j + 1] = links[j][0:8]
@@ -528,7 +529,7 @@
     dlog = jnp.dot(upper, dcum, precision=HIGH, preferred_element_type=F32) + closing_term
     rate = -jnp.exp(heads[1:2])
     dstep = (direct + dlog * rate) * sigmoid(step_raw[...] + heads[0:1])
-    gstep_out[...] = dstep.astype(BF16)
+    gsmall_out[:, 2 * state_dim :] = dstep.astype(BF16)
     par_h_out[0:1] += jnp.sum(dstep, axis=0, keepdims=True)
     par_h_out[1:2] += jnp.sum(dlog * (rate * dt), axis=0, keepdims=True)
 
@@ -573,27 +574,21 @@
         ],
         out_specs=[
             pl.BlockSpec((SPAN, width), row),
-            pl.BlockSpec((SPAN, scols), row),
-            pl.BlockSpec((SPAN, 128), row),
+            pl.BlockSpec((SPAN, scols + 128), row),
             pl.BlockSpec((8, width), fixed),
             pl.BlockSpec((8, scols), fixed),
             pl.BlockSpec((8, 128), fixed),
-            pl.BlockSpec((8, width), fixed),
-            pl.BlockSpec((8, scols), fixed),
-            pl.BlockSpec((8, width), fixed),
-            pl.BlockSpec((8, scols), fixed),
+            pl.BlockSpec((8, width + scols), fixed),
+            pl.BlockSpec((8, width + scols), fixed),
         ],
         out_shape=[
             S((length, width), BF16),
-            S((length, scols), BF16),
-            S((length, 128), BF16),
+            S((length, scols + 128), BF16),
             S((8, width), F32),
             S((8, scols), F32),
             S((8, 128), F32),
-            S((8, width), F32),
-            S((8, scols), F32),
-            S((8, width), F32),
-            S((8, scols), F32),
+            S((8, width + scols), F32),
+            S((8, width + scols), F32),
         ],
         scratch_shapes=[
             pltpu.VMEM((scols // 2, width), F32),
@@ -656,16 +651,19 @@
         pl.semaphore_signal(barrier, inc=1, device_id=to, device_id_type=MESH)
 
 
+PIECES = 2
+
+
 def gather_kernel(
     ncol, ndp,
-    own, seg_own, w0, w1, w2, zero_tail, no_seg,
+    tokens_in, gain, seg_in, w0, w1, w2,
     all_out, seg_out, w0_out, w1_out, w2_out,
-    z_send, z_recv, w_send, c_send, w_recv, t_send, t_recv, here,
+    z_send, z_recv, w_send, c_send, w_recv, t_send, t_recv, here, own, seg_own, zero_tail, no_seg,
 ):
     dp, row, z = lax.axis_index("dp"), lax.axis_index("row"), lax.axis_index("col")
     other = 1 - row
     last = ncol - 1
-    tokens, tail = own.shape[0], zero_tail.shape[0]
+    tokens, tail, part = own.shape[0], zero_tail.shape[0], own.shape[0] // PIECES
     weights = ((w0, w0_out), (w1, w1_out), (w2, w2_out))
     rows = w0.shape[0]
     sends_tail = (row == 0) & (z == last)
@@ -681,21 +679,32 @@
         greet(barrier, sends_tail, row=1, col=c)
     count = (z > 0).astype(jnp.int32) + (z < last).astype(jnp.int32) + ndp
     count = count + row + jnp.where(sends_tail, ncol, 0)
+    seg_own[...] = jnp.broadcast_to(seg_in[...], seg_own.shape)
+    no_seg[...] = jnp.full(no_seg.shape, -1, jnp.int32)
+    zero_tail[...] = jnp.zeros_like(zero_tail)
+
+    def normalize(step, carry):
+        at = pl.ds(pl.multiple_of(step * 32, 32), 32)
+        wide = tokens_in[at].astype(F32)
+        scale = lax.rsqrt(jnp.sum(wide * wide, axis=1, keepdims=True) / wide.shape[1] + EPS)
+        own[at] = (wide * scale * gain[...]).astype(BF16)
+        return carry
+
+    lax.fori_loop(0, tokens // 32, normalize, 0)
     pl.semaphore_wait(barrier, count)
 
-    def token_refs(s, mine):
-        if mine:
-            srcs = (own, seg_own)
-        else:
-            srcs = (all_out.at[pl.ds(s * tokens, tokens)], seg_out.at[pl.ds(s * 8, 8)])
-        return tuple(zip(srcs, (all_out.at[pl.ds(s * tokens, tokens)], seg_out.at[pl.ds(s * 8, 8)])))
-
-    def token_copies(s, mine, way):
+    def token_copies(s, mine, way, which=None):
         target = z + 1 if way == 0 else z - 1
-        return [
-            remote(src, dst, z_send.at[way, s, i], z_recv.at[s, i], col=target)
-            for i, (src, dst) in enumerate(token_refs(s, mine))
-        ]
+        copies = []
+        for i in range(PIECES + 1) if which is None else which:
+            if i < PIECES:
+                dst = all_out.at[pl.ds(s * tokens + i * part, part)]
+                src = own.at[pl.ds(i * part, part)] if mine else dst
+            else:
+                dst = seg_out.at[pl.ds(s * 8, 8)]
+                src = seg_own if mine else dst
+            copies.append(remote(src, dst, z_send.at[way, s, i], z_recv.at[s, i], col=target))
+        return copies
 
     def weight_copies(j, mine, send, **to):
         copies = []
@@ -742,18 +751,20 @@
     guarded(row == 0, lambda: start(fill))
 
     def pass_tokens(s):
-        def from_below():
-            for copy in token_copies(z - s, False, 0):
-                copy.wait_recv()
-            guarded(z < last, lambda: start(token_copies(z - s, False, 0)))
-
-        def from_above():
-            for copy in token_copies(z + s, False, 1):
-                copy.wait_recv()
-            guarded(z > 0, lambda: start(token_copies(z + s, False, 1)))
-
-        guarded(z - s >= 0, from_below)
-        guarded(z + s <= last, from_above)
+        for which in [(i,) for i in range(PIECES - 1)] + [(PIECES - 1, PIECES)]:
+
+            def from_below(which=which):
+                for copy in token_copies(z - s, False, 0, which):
+                    copy.wait_recv()
+                guarded(z < last, lambda: start(token_copies(z - s, False, 0, which)))
+
+            def from_above(which=which):
+                for copy in token_copies(z + s, False, 1, which):
+                    copy.wait_recv()
+                guarded(z > 0, lambda: start(token_copies(z + s, False, 1, which)))
+
+            guarded(z - s >= 0, from_below)
+            guarded(z + s <= last, from_above)
 
     def pass_weights(m):
         j = (dp ^ m) * 2 + row
@@ -797,31 +808,31 @@
     guarded(row == 0, lambda: [copy.wait() for copy in fill])
 
 
-def gather_inputs(own, seg_own, w0, w1, w2):
+def gather_inputs(tokens_in, gain, seg, w0, w1, w2):
     ncol, ndp = lax.axis_size("col"), lax.axis_size("dp")
-    tokens, width = own.shape
+    tokens, width = tokens_in.shape
     S = jax.ShapeDtypeStruct
     shards = 2 * ndp
-    zero_tail = jnp.zeros((HALO, width), own.dtype)
-    no_seg = jnp.full((8, tokens), -1, jnp.int32)
     dma = pltpu.SemaphoreType.DMA
-    sent = 2 * own.size * own.dtype.itemsize
+    vmem = pl.BlockSpec(memory_space=pltpu.VMEM)
     return pl.pallas_call(
         functools.partial(gather_kernel, ncol, ndp),
-        in_specs=[ANY] * 7,
+        in_specs=[vmem] * 3 + [ANY] * 3,
         out_specs=[ANY] * 5,
         out_shape=[
-            S((ncol * tokens + HALO, width), own.dtype),
+            S((ncol * tokens + HALO, width), BF16),
             S(((ncol + 1) * 8, tokens), jnp.int32),
         ] + [S((shards * w.shape[0], w.shape[1]), w.dtype) for w in (w0, w1, w2)],
         scratch_shapes=[
-            dma((2, ncol, 2)), dma((ncol, 2)), dma((ndp, 3)), dma((ndp, 3)), dma((shards, 3)),
+            dma((2, ncol, PIECES + 1)), dma((ncol, PIECES + 1)), dma((ndp, 3)), dma((ndp, 3)), dma((shards, 3)),
             dma((ncol, 2)), dma((2,)), dma((7,)),
+            pltpu.VMEM((tokens, width), BF16), pltpu.VMEM((8, tokens), jnp.int32),
+            pltpu.VMEM((HALO, width), BF16), pltpu.VMEM((8, tokens), jnp.int32),
         ],
         compiler_params=pltpu.CompilerParams(collective_id=1, has_side_effects=True),
         cost_estimate=pl.CostEstimate(flops=0, bytes_accessed=200_000_000, transcendentals=0),
         name="gather_inputs",
-    )(own, seg_own, w0, w1, w2, zero_tail, no_seg)
+    )(tokens_in, gain[None], seg[None], w0, w1, w2)
 
 
 def sum_col_kernel(ncol, value, out, slots, send, recv):
@@ -861,11 +872,19 @@
 
 
 def reduce_kernel(ncol, ndp, *refs):
-    g, vecs = refs[0:3], refs[3:7]
-    r, vec_outs = refs[7:10], refs[10:14]
-    own, near, sent, far = refs[14:17], refs[17:20], refs[20:23], refs[23:26]
-    vec_slots, col_slots, bc_slots = refs[26:30], refs[30:32], refs[32]
-    c_send, c_recv, p_send, p_recv, here, v_send, v_recv, u_send, u_recv, b_send, b_recv = refs[33:]
+    count = 4
+    refs = list(refs)
+
+    def take(number):
+        taken = refs[:number]
+        del refs[:number]
+        return taken
+
+    g, vecs = take(count), take(4)
+    r, vec_outs = take(count), take(4)
+    own, near, sent, far = take(count), take(count), take(count), take(count)
+    vec_slots, col_slots = take(4), take(2)
+    bc_slots, c_send, c_recv, p_send, p_recv, here, v_send, v_recv, u_send, u_recv, b_send, b_recv = refs
     dp, row, z = lax.axis_index("dp"), lax.axis_index("row"), lax.axis_index("col")
     other = 1 - row
     me = dp * 2 + row
@@ -877,17 +896,8 @@
         greet(barrier, row >= 0, col=lax.rem(z + s, ncol))
     pl.semaphore_wait(barrier, 2 * ndp + ncol - 2)
 
-    vec_copies = []
-    for q in range(1, 2 * ndp):
-        for i in range(4):
-            vec_copies.append(
-                remote(vecs[i], vec_slots[i].at[me], v_send.at[q, i], v_recv.at[me, i],
-                       dp=dp ^ (q >> 1), row=row ^ (q & 1))
-            )
-    for copy in vec_copies:
-        copy.start()
-
-    order = (1, 2, 0)
+    order = (0, 1, 2, 3)
+    turns = [3, 1, 2, 0] if ndp == 4 else list(range(1, ndp)) + [0]
 
     def core_copy(i, d):
         return remote(g[i].at[pl.ds((d * 2 + other) * rows[i], rows[i])], near[i].at[d],
@@ -896,68 +906,136 @@
     def own_copy(i, d):
         return pltpu.make_async_copy(g[i].at[pl.ds((d * 2 + row) * rows[i], rows[i])], own[i].at[d], here.at[i, d])
 
-    def peer_copy(i, m):
-        return remote(sent[i].at[m], far[i].at[m], p_send.at[i, m], p_recv.at[i, m], dp=dp ^ m)
-
-    turns = list(range(1, ndp)) + [0]
+    def vec_copy(q, i, j):
+        return remote(vecs[i], vec_slots[i].at[j], v_send.at[q, i], v_recv.at[j, i],
+                      dp=dp ^ (q >> 1), row=row ^ (q & 1))
+
     for i in order:
         for m in turns:
             core_copy(i, dp ^ m).start()
             own_copy(i, dp ^ m).start()
+    for q in range(1, 2 * ndp):
+        for i in range(4):
+            vec_copy(q, i, me).start()
+
     waiting = []
+
+    def later(copy):
+        if waiting:
+            waiting.pop().start()
+        if copy is not None:
+            waiting.append(copy)
+
+    def accumulate(i, first, number, terms, store):
+        def step(k, carry):
+            at = first + pl.multiple_of(k * 16, 16)
+            total = terms[0](at)
+            for term in terms[1:]:
+                total = total + term(at)
+            store(at, total)
+            return carry
+
+        lax.fori_loop(0, number // 16, step, 0)
+
+    def read(ref, index, shift=0):
+        return lambda at: ref[index, pl.ds(at - shift, 16)].astype(F32)
+
+    def write(ref, index, shift):
+        def store(at, total):
+            ref[index, pl.ds(at - shift, 16)] = total.astype(BF16)
+
+        return store
+
+    def arrived(i, d):
+        core_copy(i, d).wait_recv()
+        own_copy(i, d).wait()
+
+    if ndp == 4:
+        halves = ((0, 1, 2), (1, 2, 1))
+
+        def leg(i, slot, m):
+            return remote(sent[i].at[slot], far[i].at[slot], p_send.at[i, slot], p_recv.at[i, slot], dp=dp ^ m)
+
+        for i in order:
+            half = rows[i] // 2
+            arrived(i, dp ^ 3)
+            for h, m1, m2 in halves:
+                accumulate(i, h * half, half, [read(own[i], dp ^ 3), read(near[i], dp ^ 3)],
+                           write(sent[i], 3 * h + 1, h * half))
+                later(leg(i, 3 * h + 1, m1))
+            for h, m1, m2 in halves:
+                arrived(i, dp ^ m1)
+                accumulate(i, h * half, half, [read(own[i], dp ^ m1), read(near[i], dp ^ m1)],
+                           write(sent[i], 3 * h, h * half))
+                later(leg(i, 3 * h, m1))
+        later(None)
+
+        def relay(i):
+            half = rows[i] // 2
+            for h, m1, m2 in halves:
+                leg(i, 3 * h + 1, m1).wait_recv()
+                accumulate(i, h * half, half,
+                           [read(own[i], dp ^ m2), read(near[i], dp ^ m2), read(far[i], 3 * h + 1, h * half)],
+                           write(sent[i], 3 * h + 2, h * half))
+                later(leg(i, 3 * h + 2, m2))
+
+        def finish(i, store):
+            half = rows[i] // 2
+            for h, m1, m2 in halves:
+                leg(i, 3 * h, m1).wait_recv()
+                leg(i, 3 * h + 2, m2).wait_recv()
+                accumulate(i, h * half, half,
+                           [read(own[i], dp), read(near[i], dp), read(far[i], 3 * h, h * half),
+                            read(far[i], 3 * h + 2, h * half)], store)
+
+        sends = [leg(i, 3 * h + k, m2 if k == 2 else m1) for i in order for h, m1, m2 in halves for k in range(3)]
+    else:
+
+        def peer(i, m):
+            return remote(sent[i].at[m], far[i].at[m], p_send.at[i, m], p_recv.at[i, m], dp=dp ^ m)
+
+        for i in order:
+            for m in turns[:-1]:
+                arrived(i, dp ^ m)
+                accumulate(i, 0, rows[i], [read(own[i], dp ^ m), read(near[i], dp ^ m)], write(sent[i], m, 0))
+                later(peer(i, m))
+        later(None)
+
+        def relay(i):
+            pass
+
+        def finish(i, store):
+            for m in range(1, ndp):
+                peer(i, m).wait_recv()
+            accumulate(i, 0, rows[i],
+                       [read(own[i], dp), read(near[i], dp)] + [read(far[i], m) for m in range(1, ndp)], store)
+
+        sends = [peer(i, m) for i in order for m in range(1, ndp)]
+
     for i in order:
-        for m in turns:
-            d = dp ^ m
-            core_copy(i, d).wait_recv()
-            own_copy(i, d).wait()
-            if m == 0:
-                continue
-
-            def add(step, carry, i=i, d=d, m=m):
-                at = pl.ds(pl.multiple_of(step * 16, 16), 16)
-                total = own[i][d, at].astype(F32) + near[i][d, at].astype(F32)
-                sent[i][m, at] = total.astype(BF16)
-                return carry
-
-            lax.fori_loop(0, rows[i] // 16, add, 0)
-            if waiting:
-                waiting.pop().start()
-            waiting.append(peer_copy(i, m))
-
-    def gather_vec():
-        for q in range(1, 2 * ndp):
-            j = me ^ q
-            for i in range(4):
-                remote(vecs[i], vec_slots[i].at[j], v_send.at[q, i], v_recv.at[j, i],
-                       dp=dp ^ (q >> 1), row=row ^ (q & 1)).wait_recv()
+        arrived(i, dp)
+    for q in range(1, 2 * ndp):
         for i in range(4):
-            vec_slots[i][me] = vecs[i][...]
-            total = vec_slots[i][0]
-            for j in range(1, 2 * ndp):
-                total = total + vec_slots[i][j]
-            if i < 2:
-                vec_outs[i][...] = total
-            else:
-                col_slots[i - 2][z] = total
-
-    gather_vec()
-    waiting.pop().start()
-
-    def finish(i):
-        for m in range(1, ndp):
-            peer_copy(i, m).wait_recv()
-
-        def add(step, carry):
-            at = pl.ds(pl.multiple_of(step * 16, 16), 16)
-            total = own[i][dp, at].astype(F32) + near[i][dp, at].astype(F32)
-            for m in range(1, ndp):
-                total = total + far[i][m, at].astype(F32)
-            r[i][at] = total
-            if i == 1:
-                bc_slots[z, at] = total[:, : bc_slots.shape[2]].astype(BF16)
-            return carry
-
-        lax.fori_loop(0, rows[i] // 16, add, 0)
+            vec_copy(q, i, me ^ q).wait_recv()
+    for i in range(4):
+        vec_slots[i][me] = vecs[i][...]
+        total = vec_slots[i][0]
+        for j in range(1, 2 * ndp):
+            total = total + vec_slots[i][j]
+        if i < 2:
+            vec_outs[i][...] = total
+        else:
+            col_slots[i - 2][z] = total
+
+    def plain(i):
+        def store(at, total):
+            r[i][pl.ds(at, 16)] = total
+
+        return store
+
+    def shared_rows(at, total):
+        r[0][pl.ds(at, 16)] = total
+        bc_slots[z, pl.ds(at, 16)] = total[:, : bc_slots.shape[2]].astype(BF16)
 
     def col_copies(s, source):
         to = lax.rem(z + s, ncol)
@@ -965,12 +1043,18 @@
                   for i in range(2)]
         return copies + [remote(bc_slots.at[source], bc_slots.at[source], b_send.at[s], b_recv.at[source], col=to)]
 
-    finish(1)
-    finish(2)
+    relay(0)
+    relay(1)
+    relay(2)
+    finish(0, shared_rows)
+    relay(3)
+    later(None)
     for s in range(1, ncol):
         for copy in col_copies(s, z):
             copy.start()
-    finish(0)
+    finish(1, plain(1))
+    finish(2, plain(2))
+    finish(3, plain(3))
     for s in range(1, ncol):
         for copy in col_copies(s, lax.rem(z + s, ncol)):
             copy.wait_recv()
@@ -982,15 +1066,16 @@
     total = bc_slots[0].astype(F32)
     for j in range(1, ncol):
         total = total + bc_slots[j].astype(F32)
-    r[1][:, : bc_slots.shape[2]] = total
-
-    for copy in vec_copies:
-        copy.wait_send()
+    r[0][:, : bc_slots.shape[2]] = total
+
+    for q in range(1, 2 * ndp):
+        for i in range(4):
+            vec_copy(q, i, me).wait_send()
     for i in order:
         for m in turns:
             core_copy(i, dp ^ m).wait_send()
-            if m:
-                peer_copy(i, m).wait_send()
+    for copy in sends:
+        copy.wait_send()
     for s in range(1, ncol):
         for copy in col_copies(s, z):
             copy.wait_send()
@@ -1001,18 +1086,23 @@
     dma = pltpu.SemaphoreType.DMA
     vmem = pl.BlockSpec(memory_space=pltpu.VMEM)
     S = jax.ShapeDtypeStruct
+    count = len(grads)
     blocks = [(g.shape[0] // (2 * ndp), g.shape[1]) for g in grads]
     stack = [pltpu.VMEM((ndp,) + b, BF16) for b in blocks]
+    slots = 6 if ndp == 4 else ndp
+    legs = [pltpu.VMEM((6, b[0] // 2, b[1]) if ndp == 4 else (ndp,) + b, BF16) for b in blocks]
     return pl.pallas_call(
         functools.partial(reduce_kernel, ncol, ndp),
-        in_specs=[ANY] * 3 + [vmem] * 4,
-        out_specs=[vmem] * 7,
+        in_specs=[ANY] * count + [vmem] * 4,
+        out_specs=[vmem] * (count + 4),
         out_shape=[S(b, F32) for b in blocks] + [S(v.shape, F32) for v in vecs],
-        scratch_shapes=stack * 4
+        scratch_shapes=stack * 2 + legs * 2
         + [pltpu.VMEM((2 * ndp,) + v.shape, F32) for v in vecs]
         + [pltpu.VMEM((ncol,) + v.shape, F32) for v in vecs[2:]]
-        + [pltpu.VMEM((ncol, blocks[1][0], scols), BF16)]
-        + [dma((3, ndp))] * 5
+        + [pltpu.VMEM((ncol, blocks[0][0], scols), BF16)]
+        + [dma((count, ndp))] * 2
+        + [dma((count, slots))] * 2
+        + [dma((count, ndp))]
         + [dma((2 * ndp, 4))] * 2
         + [dma((ncol, 2))] * 2
         + [dma((ncol,))] * 2,
@@ -1022,6 +1112,59 @@
     )(*grads, *vecs)
 
 
+def finish_kernel(
+    nheads, small, gate, inner, out, par, par_h, par_s, gain_sum, gain, tokens, cot, gnormed,
+    zx_out, bc_out, dt_out, out_out, ci_out, cib_out, cs_out, csb_out, sb_out, rl_out, sg_out, gg_out, ng_out, gin_out,
+):
+    width = par.shape[1]
+    scols = par_s.shape[1]
+    zx_out[:, 0, :] = gate[...]
+    zx_out[:, 1, :] = inner[...]
+    bc_out[...] = small[:, :scols]
+    dt_out[...] = small[:, scols:].T[:nheads]
+    out_out[...] = out[...]
+    ci_out[...] = par[0:4]
+    cib_out[...] = par[4:5]
+    gg_out[...] = par[5:6]
+    cs_out[...] = par_s[0:4]
+    csb_out[...] = par_s[4:5]
+    sb_out[...] = par_h[0:1, :nheads]
+    rl_out[...] = par_h[1:2, :nheads]
+    skip = jnp.zeros((8, 128), F32)
+    for p in range(width // 128):
+        skip = skip + split_dot(jnp.broadcast_to(par[6:7, p * 128 : (p + 1) * 128], (8, 128)), head_map(p))
+    sg_out[...] = skip[0:1, :nheads]
+    ng_out[...] = gain_sum[0:1] / gain[...]
+
+    def rows(step, carry):
+        at = pl.ds(pl.multiple_of(step * 32, 32), 32)
+        wide = tokens[at].astype(F32)
+        scale = lax.rsqrt(jnp.sum(wide * wide, axis=1, keepdims=True) / wide.shape[1] + EPS)
+        pushed = gnormed[at].astype(F32) * gain[...]
+        mean = jnp.sum(pushed * wide, axis=1, keepdims=True) / wide.shape[1]
+        grad = scale * pushed - wide * (scale * scale * scale * mean)
+        gin_out[at] = (cot[at].astype(F32) + grad).astype(BF16)
+        return carry
+
+    lax.fori_loop(0, tokens.shape[0] // 32, rows, 0)
+
+
+def run_finish(nheads, small, gate, inner, out, par, par_h, par_s, gain_sum, gain, tokens, cot, gnormed):
+    rows, width = gate.shape
+    scols = par_s.shape[1]
+    model = gain.shape[0]
+    S = jax.ShapeDtypeStruct
+    shapes = [
+        (rows, 2, width), (rows, scols), (nheads, rows), (rows, width), (4, width), (1, width), (4, scols), (1, scols),
+        (1, nheads), (1, nheads), (1, nheads), (1, width), (1, model),
+    ]
+    return pl.pallas_call(
+        functools.partial(finish_kernel, nheads),
+        out_shape=[S(shape, F32) for shape in shapes] + [S(tokens.shape, BF16)],
+        name="finish",
+    )(small, gate, inner, out, par, par_h, par_s, gain_sum, gain[None], tokens, cot, gnormed)
+
+
 def pass_on(value, axis, by):
     count = lax.axis_size(axis)
     pairs = [(i, i + by) for i in range(count) if 0 <= i + by < count]
@@ -1031,12 +1174,6 @@
 def pack_rows(rows, width):
     used = sum(r.shape[0] for r in rows)
     return jnp.concatenate(rows + [jnp.zeros((8 - used, width), F32)], axis=0)
-
-
-def normalized(tokens, gain):
-    wide = tokens.astype(F32)
-    scale = lax.rsqrt(jnp.mean(wide * wide, axis=1, keepdims=True) + EPS)
-    return wide, scale, (wide * scale * gain[None, :]).astype(BF16)
 
 
 def per_device(
@@ -1048,24 +1185,22 @@
     nheads = proj_dt.shape[1]
     head_dim = width // nheads
     full_width = float(width * lax.axis_size("col"))
-    small_own = jnp.concatenate(
-        [proj_bc, proj_dt, jnp.zeros((proj_dt.shape[0], 128 - nheads), BF16)], axis=1
+    fill = (0, 128 - nheads)
+    small_own = jnp.concatenate([proj_bc, jnp.pad(proj_dt, ((0, 0), fill))], axis=1)
+    normed_ext, seg, w_in, w_small, out_t = gather_inputs(
+        block_input, norm_gain, segment_ids, proj_zx.reshape(-1, 2 * width), small_own, proj_out.T
     )
-    wide, scale, normed_own = normalized(block_input, norm_gain)
-    seg_own = jnp.broadcast_to(segment_ids[None], (8, segment_ids.shape[0]))
+    length = normed_ext.shape[0] - HALO
+    (cot, normed_ext, conv_inner, conv_inner_bias, conv_shared, conv_shared_bias, step_bias, rate_log, skip_gain,
+     gated_gain) = lax.optimization_barrier((
+        cotangent, normed_ext, conv_inner, conv_inner_bias, conv_shared, conv_shared_bias, step_bias, rate_log,
+        skip_gain, gated_gain))
+    cot_all = lax.all_gather(cot, "col", axis=0, tiled=True)
     taps = pack_rows(
         [conv_inner, conv_inner_bias[None], gated_gain[None], jnp.repeat(skip_gain, head_dim)[None]], width
     )
     taps_s = pack_rows([conv_shared, conv_shared_bias[None]], scols)
-    fill = (0, 128 - nheads)
     heads = pack_rows([jnp.pad(step_bias, fill)[None], jnp.pad(rate_log, fill)[None]], 128)
-
-    normed_ext, seg, w_in, w_small, out_t = gather_inputs(
-        normed_own, seg_own, proj_zx.reshape(-1, 2 * width), small_own, proj_out.T
-    )
-    length = normed_ext.shape[0] - HALO
-    cot, normed_ext = lax.optimization_barrier((cotangent, normed_ext))
-    cot_all = lax.all_gather(cot, "col", axis=0, tiled=True)
 
     both_ext = nn(normed_ext, w_in).astype(BF16)
     small_ext = nn(normed_ext, w_small)
@@ -1077,47 +1212,37 @@
     ssd, gated, squares = run_gate(y, x, bc, dec, start, both_ext, taps)
     squares = sum_col(squares, 3)
     gated_normed, projected = run_project(full_width, gated, squares, taps, out_t)
+    cot_all, projected = lax.optimization_barrier((cot_all, projected))
     projected = lax.psum_scatter(projected, "col", scatter_dimension=0, tiled=True)
-    block_output = (wide + projected.astype(F32)).astype(BF16)
+    block_output = (block_input.astype(F32) + projected.astype(F32)).astype(BF16)
     back, inner = run_pull(cot_all, out_t, gated, taps)
     inner = sum_col(inner, 4)
     dy, ggate, rowterm, colsum, dstart = run_back(
         full_width, ssd, x, bc, dec, both_ext, back, squares, inner, taps
     )
     dend = pass_on(dstart, "row", -1)
-    gout = tn(cot_all, gated_normed).astype(BF16)
-    ginner, gshared, gstep, par, par_s, par_h, edge, edge_s, last, last_s = run_backward(
+    ginner, gsmall, par, par_s, par_h, edge, last = run_backward(
         *common, dy, x, bc, dt, c, ct, dec, enter, start, rowterm, dend, colsum
     )
-    edge, edge_s = pass_on((edge, edge_s), "row", -1)
-    ginner = lax.dynamic_update_slice(ginner, (last + edge).astype(BF16), (length - 8, 0))
-    gshared = lax.dynamic_update_slice(gshared, (last_s + edge_s).astype(BF16), (length - 8, 0))
-    gsmall = jnp.concatenate([gshared, gstep], axis=1)
+    edge = pass_on(edge, "row", -1)
+    fixed = (last + edge).astype(BF16)
+    ginner = lax.dynamic_update_slice(ginner, fixed[:, :width], (length - 8, 0))
+    gsmall = lax.dynamic_update_slice(gsmall, fixed[:, width:], (length - 8, 0))
     part, gain_part = run_spread(ggate, ginner, gsmall, w_in, w_small, normed_ext)
-    grad_normed = lax.psum_scatter(part, "col", scatter_dimension=0, tiled=True).astype(F32)
+    grad_normed = lax.psum_scatter(part, "col", scatter_dimension=0, tiled=True)
     normed = normed_ext[:length]
-    gzx = jnp.concatenate([tn(normed, ggate).astype(BF16), tn(normed, ginner).astype(BF16)], axis=1)
-    gsm = tn(normed, gsmall).astype(BF16)
-    gzx, gsm, gout, par, par_h, par_s, gain_sum = reduce_grads((gzx, gsm, gout), (par, par_h, par_s, gain_part), scols)
-    pushed = grad_normed * norm_gain[None, :]
-    grad_wide = scale * pushed - wide * scale**3 * jnp.mean(pushed * wide, axis=1, keepdims=True)
-    grad_input = (cotangent.astype(F32) + grad_wide).astype(BF16)
+    grads = (
+        tn(normed, gsmall).astype(BF16),
+        tn(normed, ggate).astype(BF16),
+        tn(cot_all, gated_normed).astype(BF16),
+        tn(normed, ginner).astype(BF16),
+    )
+    gsm, gz, gout, gx, par, par_h, par_s, gain_sum = reduce_grads(grads, (par, par_h, par_s, gain_part), scols)
+    zx, gbc, gdt, gout, ci, cib, cs, csb, sb, rl, sg, gg, ng, grad_input = run_finish(
+        nheads, gsm, gz, gx, gout, par, par_h, par_s, gain_sum, norm_gain, block_input, cotangent, grad_normed
+    )
     return (
-        block_output,
-        grad_input,
-        gain_sum[0] / norm_gain,
-        gzx.reshape(-1, 2, width),
-        gsm[:, :scols],
-        gsm[:, scols : scols + nheads],
-        par[:4],
-        par[4],
-        par_s[:4],
-        par_s[4],
-        par_h[0, :nheads],
-        par_h[1, :nheads],
-        jnp.sum(par[6].reshape(nheads, head_dim), axis=1),
-        par[5],
-        gout.T,
+        block_output, grad_input, ng[0], zx, gbc, gdt.T, ci, cib[0], cs, csb[0], sb[0], rl[0], sg[0], gg[0], gout.T,
     )
 
 

time: 356 us -> 310 us (0.87)
  waiting for transfers between devices: 37.3 us -> 12.8 us
  local copies, waits for them, and re-layouts: 24.9 us -> 9.45 us
  other arithmetic: 16.9 us -> 9.75 us
    reduce_scatter x1, waiting for transfers between devices: 19.8 us -> 0.02 us  [per_device(): lax.psum_scatter(projected, 'col', scatter_dimension=0, tiled=True)]
    slice x7 -> x0, local copies, waits for them, and re-layouts: 8.7 us -> none  [the longest x1 1.62 us: per_device(): gsm[:, :scols]]
    all_gather x1, waiting for transfers between devices: 12.9 us -> 7.08 us  [per_device(): cot_all = lax.all_gather(cot, 'col', axis=0, tiled=True)]
    pallas_call x0 -> x3, other arithmetic: none -> 3.88 us  [run_finish(): pl.pallas_call(functools.partial(finish_kernel, nheads), out_shape=[S(sha...]
    concatenate x3 -> x1, other arithmetic: 5.29 us -> 1.57 us  [per_device(): jnp.concatenate([proj_bc, jnp.pad(proj_dt, ((0, 0), fill))], axis=1)]
    reduce_sum x3 -> x0, other arithmetic: 3.6 us -> none  [the longest x1 1.54 us: per_device(): jnp.mean(pushed * wide, axis=1, keepdims=True)]
    pallas_call x1 -> x2, Pallas kernels: 62.9 us -> 65.9 us  [the longest x1 60.6 us: gather_inputs(): pl.pallas_call(functools.partial(gather_kernel, ncol, ndp), in_specs=[vme...]
    unnamed x54 -> x36, local copies, waits for them, and re-layouts: 7.32 us -> 4.34 us
  transfers between devices with their start and end apart: 7 -> 6, of which waited for: 5 -> 4; matrix products, arithmetic and copies ran while one was open for 15% -> 12% of each run, Pallas kernels for 28% -> 53%
where the time goes in v3:
time: 310 us; the launch traced here: 308 us
  Pallas kernels  228 us (74%)
  matrix products  29.3 us (9%)
  between operations  14 us (5%)
  waiting for transfers between devices  12.8 us (4%)
  other arithmetic  9.75 us (3%)
  local copies, waits for them, and re-layouts  9.45 us (3%)
  starting transfers between devices  4.77 us (2%)
    pallas_call x1, Pallas kernels, gather_inputs(): pl.pallas_call(functools.partial(gather_kernel, ncol, ndp), in_specs=[vme...  60.6 us
    pallas_call x1, Pallas kernels, reduce_grads(): pl.pallas_call(functools.partial(reduce_kernel, ncol, ndp), in_specs=[ANY...  58.2 us
    pallas_call x1, Pallas kernels, run_backward(): pl.pallas_call(backward_kernel, grid=(chunks,), in_specs=[pl.BlockSpec((S...  30.8 us
    pallas_call x2, Pallas kernels, sum_col(): pl.pallas_call(functools.partial(sum_col_kernel, ncol), in_specs=[vmem],...  18.5 us
    dot_general x4, matrix products, tn(): lax.dot_general(a, b, (((0,), (0,)), ((), ())), preferred_element_type=F32)  16.3 us
    pallas_call x1, Pallas kernels, run_forward(): pl.pallas_call(forward_kernel, grid=(chunks,), in_specs=[pl.BlockSpec((SP...  13.7 us
    dot_general x2, matrix products, nn(): lax.dot_general(a, b, (((1,), (0,)), ((), ())), preferred_element_type=F32)  13 us
    pallas_call x1, Pallas kernels, run_spread(): pl.pallas_call(spread_kernel, grid=(model // tile,), in_specs=[pl.BlockSp...  12 us
  transfers between devices with their start and end apart: 6, of which 4 were waited for; matrix products, arithmetic and copies ran while one was open for 12% of the time, Pallas kernels for 53%

profile of v3, /device:TPU:0, one launch (start us, length us, event | category | flops | bytes accessed | tf_op | source)
XLA Modules:
  0.0 308.4 jit_solution(17443768988198042313)
XLA Ops:
  7.2 1.3 broadcast_in_dim.34.gain
  8.5 1.9 copy.32
  10.5 0.8 copy.31
  11.3 1.6 fusion.4.w1
  12.8 60.6 %gather_inputs.1 = (bf16[1040,1536]{1,0:T(8,128)(2,1)}, s32[40,256]{1,0:T(8,128)}, bf16[1536,1536]{1,0:T(8,128)(2,1)}, bf16[1536,384]{1,0:T(8,128)(2,1)}, bf16[1536,768]{1,0:T(8,128)(2,1)}) custom-call(bf16[256,1536]{1,0:T(8,128)(2,1)} %tokens.1, f32[1,1536]{1,0:T(1,128)} %broadcast_in_dim.34.gain, s32[1,256]{1,0:T(1,128)} %bitcast.27, ...), custom_call_target="tpu_custom_call" | custom-call | bytes 200000000 | tf_op jit(solution)/shard_map/gather_inputs/pallas_call | solution.py:818
  73.4 0.0 reduce-scatter.3.cloned.1.call-start
  73.6 4.2 %fusion.5 = f32[1040,384]{1,0:T(8,128)S(1)} fusion(bf16[1040,1536]{1,0:T(8,128)(2,1)} %get-tuple-element.86.normed, bf16[1536,384]{1,0:T(8,128)(2,1)} %get-tuple-element.88.w_small), kind=kOutput, calls=%fused_computation.20 | convolution fusion | flops 1226833920 | bytes 5971968 | tf_op jit(solution)/shard_map/dot_general | solution.py:16
  77.8 0.9 slice.34.shared.shared_halo
  78.6 0.8 slice.22.step_raw
  79.5 0.1 broadcast_in_dim.38
  79.6 0.1 broadcast_in_dim_reshape.3
  79.7 0.1 pad.19.clone
  79.7 0.1 pad.16.clone
  79.8 0.6 concatenate.13.taps
  80.5 0.7 maximum_maximum_fusion.1.heads
  81.1 0.7 maximum_maximum_fusion.taps_s
  81.8 8.8 %convolution_convert_fusion.inner.inner_halo.gate = bf16[1040,1536]{1,0:T(8,128)(2,1)} fusion(bf16[1040,1536]{1,0:T(8,128)(2,1)S(1)} %copy-done.1, bf16[1536,1536]{1,0:T(8,128)(2,1)} %get-tuple-element.87.w_in), kind=kOutput, calls=%fused_computation | convolution fusion | flops 4908933120 | bytes 11108352 | tf_op jit(solution)/shard_map/dot_general | solution.py:16
  90.6 13.7 %scan_forward.1 = (f32[1024,768]{1,0:T(8,128)}, bf16[1024,768]{1,0:T(8,128)(2,1)}, bf16[1024,256]{1,0:T(8,128)(2,1)}, f32[1024,128]{1,0:T(8,128)}, f32[1024,128]...) custom-call(bf16[1040,1536]{1,0:T(8,128)(2,1)} %convolution_convert_, ...), custom_call_target="tpu_custom_call" | custom-call | tf_op jit(solution)/shard_map/scan_forward/pallas_call | solution.py:164
  104.4 1.7 collective-permute-start
  106.0 1.5 collective-permute-done.start
  107.6 0.7 copy-done.5
  108.3 6.9 %gate_sums.1 = (f32[1024,768]{1,0:T(8,128)}, bf16[1024,768]{1,0:T(8,128)(2,1)}, f32[8,1024]{1,0:T(8,128)}) custom-call(f32[1024,768]{1,0:T(8,128)} %get-tuple-element.98.y, bf16[1024,768]{1,0:T(8,128)(2,1)} %get-tuple-element.99.x, bf16[1024,256]{1,0:T(8,128)(2,1)} %get-tuple-element.100.bc, f32[1024,128]{1,0:T(8,128)} %get-tuple-element.101.dec.dec_halo, ...), custom_call_target="tpu_custom_call" | custom-call | tf_op jit(solution)/shard_map/gate_sums/pallas_call | solution.py:239
  115.2 9.2 %sum_col.2.sums.squares = f32[8,1024]{1,0:T(8,128)} custom-call(f32[8,1024]{1,0:T(8,128)} %get-tuple-element.104.value), custom_call_target="tpu_custom_call" | custom-call | tf_op jit(solution)/shard_map/sum_col/pallas_call | solution.py:863
  124.4 6.7 %project.1 = (bf16[1024,768]{1,0:T(8,128)(2,1)}, bf16[1024,1536]{1,0:T(8,128)(2,1)}) custom-call(bf16[1024,768]{1,0:T(8,128)(2,1)} %get-tuple-element.103.gated, f32[8,1024]{1,0:T(8,128)} %sum_col.2.sums.squares, f32[8,768]{1,0:T(8,128)} %concatenate.13.taps, bf16[1536,768]{1,0:T(8,128)(2,1)} %get-tuple-element.105.out_t), custom_call_target="tpu_custom_call" | custom-call | tf_op jit(solution)/shard_map/project/pallas_call | solution.py:274
  131.2 7.1 %all-gather.2.cloned.1.call-done.cot = bf16[1024,1536]{1,0:T(8,128)(2,1)} async-done(((bf16[256,1536]{1,0:T(8,128)(2,1)}), bf16[1024,1536]{1,0:T(8,128)(2,1)}) %all-gather.2.cloned.1.call-update) | async-done | bytes 3145744 | tf_op jit(solution)/shard_map/all_gather | solution.py:1198
  138.3 6.9 %pull_back.1 = (bf16[1024,768]{1,0:T(8,128)(2,1)}, f32[8,1024]{1,0:T(8,128)}) custom-call(bf16[1024,1536]{1,0:T(8,128)(2,1)} %all-gather.2.cloned.1.call-done.cot, bf16[1536,768]{1,0:T(8,128)(2,1)} %get-tuple-element.105.out_t, bf16[1024,768]{1,0:T(8,128)(2,1)} %get-tuple-element.103.gated, f32[8,768]{1,0:T(8,128)} %concatenate.13.taps), custom_call_target="tpu_custom_call" | custom-call | tf_op jit(solution)/shard_map/pull_back/pallas_call | solution.py:304
  145.2 9.3 %sum_col.3.inner = f32[8,1024]{1,0:T(8,128)} custom-call(f32[8,1024]{1,0:T(8,128)} %get-tuple-element.111.value), custom_call_target="tpu_custom_call" | custom-call | tf_op jit(solution)/shard_map/sum_col/pallas_call | solution.py:863
  154.5 8.7 %gated_back.1 = (bf16[1024,768]{1,0:T(8,128)(2,1)}, bf16[1024,768]{1,0:T(8,128)(2,1)}, f32[1024,128]{1,0:T(8,128)}, f32[8,768]{1,0:T(8,128)}, f32[128,768]{1,0:T(8,128)}) custom-call(f32[1024,768]{1,0:T(8,128)} %get-tuple-element.108.ssd, bf16[1024,768]{1,0:T(8,128)(2,1)} %get-tuple-element.99.x, bf16[1024,256]{1,0:T(8,128)(2,1)} %get-tuple-element.100.bc, ...), custom_call_target="tpu_custom_call" | custom-call | tf_op jit(solution)/shard_map/gated_back/pallas_call | solution.py:367
  163.2 1.5 collective-permute-start.1
  164.7 2.3 collective-permute-done.1.dend
  167.0 0.7 copy-done.7
  167.8 30.8 %scan_backward.1 = (bf16[1024,768]{1,0:T(8,128)(2,1)}, bf16[1024,384]{1,0:T(8,128)(2,1)}, f32[8,768]{1,0:T(8,128)}, f32[8,256]{1,0:T(8,128)}, f32[8,128]{1,0:T(8...) custom-call(bf16[1040,1536]{1,0:T(8,128)(2,1)} %convolution_convert_fusion.inner.inner_halo.gate, ...), custom_call_target="tpu_custom_call" | custom-call | tf_op jit(solution)/shard_map/scan_backward/pallas_call | solution.py:549
  198.6 1.5 collective-permute-start.2
  200.1 1.8 collective-permute-done.2
  201.9 0.8 add_convert_fusion.1
  202.6 0.6 slice_dynamic-update-slice_fusion.1.gsmall
  203.2 0.6 slice_dynamic-update-slice_fusion.ginner
  203.8 12.0 %spread_back.1 = (bf16[1024,1536]{1,0:T(8,128)(2,1)}, f32[8,1536]{1,0:T(8,128)}) custom-call(bf16[1024,768]{1,0:T(8,128)(2,1)} %get-tuple-element.123.ggate, bf16[1024,768]{1,0:T(8,128)(2,1)} %slice_dynamic-update-slice_fusion.ginner, bf16[1024,384]{1,0:T(8,128)(2,1)} %slice_dynamic-update-slice_fusion.1.gsmall, bf16[1536,1536]{1,0:T(8,128)(2,1)} %get-tuple-element.87.w_in, ...), custom_call_target="tpu_custom_call" | custom-call | tf_op jit(solution)/shard_map/spread_back/pallas_call | solution.py:621
  215.9 5.5 %convolution_convert_fusion.3.refs_1_ = bf16[1536,768]{1,0:T(8,128)(2,1)} fusion(bf16[1024,768]{1,0:T(8,128)(2,1)} %get-tuple-element.123.ggate, bf16[1040,1536]{1,0:T(8,128)(2,1)S(1)} %copy-done.2), kind=kOutput, calls=%fused_computation.3 | convolution fusion | flops 2417098752 | bytes 7077888 | tf_op jit(solution)/shard_map/dot_general | solution.py:24
  221.4 4.0 %convolution_convert_fusion.2.refs_2_ = bf16[1536,768]{1,0:T(8,128)(2,1)} fusion(bf16[1024,1536]{1,0:T(8,128)(2,1)S(1)} %copy-done.3, bf16[1024,768]{1,0:T(8,128)(2,1)S(1)} %copy-done.16), kind=kOutput, calls=%fused_computation.2 | convolution fusion | flops 2417098752 | bytes 7077888 | tf_op jit(solution)/shard_map/dot_general | solution.py:24
  225.4 2.9 convolution_convert_fusion.4.refs_0_
  228.3 4.0 %convolution_convert_fusion.1.refs_3_ = bf16[1536,768]{1,0:T(8,128)(2,1)} fusion(bf16[1024,768]{1,0:T(8,128)(2,1)S(1)} %copy-done.4, bf16[1040,1536]{1,0:T(8,128)(2,1)S(1)} %copy-done.2), kind=kOutput, calls=%fused_computation.1 | convolution fusion | flops 2417098752 | bytes 7077888 | tf_op jit(solution)/shard_map/dot_general | solution.py:24
  232.2 58.2 %reduce_grads.1 = (f32[192,384]{1,0:T(8,128)}, f32[192,768]{1,0:T(8,128)}, f32[192,768]{1,0:T(8,128)}, f32[192,768]{1,0:T(8,128)}, f32[8,768]{1,0:T(8,128)}, /*i...) custom-call(bf16[1536,384]{1,0:T(8,128)(2,1)} %convolution_convert_fusion.4.refs_0_, ...), custom_call_target="tpu_custom_call" | custom-call | bytes 200000000 | tf_op jit(solution)/shard_map/reduce_grads/pallas_call | solution.py:1094
  290.4 2.2 add_convert_fusion
  292.6 5.3 %finish.1 = (f32[192,2,768]{2,1,0:T(2,128)}, f32[192,256]{1,0:T(8,128)}, f32[12,192]{1,0:T(8,128)}, f32[192,768]{1,0:T(8,128)}, f32[4,768]{1,0:T(4,128)}, /*inde...) custom-call(f32[192,384]{1,0:T(8,128)} %get-tuple-element.130.small,, ...), custom_call_target="tpu_custom_call" | custom-call | tf_op jit(solution)/shard_map/finish/pallas_call | solution.py:1161
  298.0 1.3 reduce
  299.3 1.3 reduce.1
  300.6 1.3 reduce.2
  (45 shorter events, 0.2 us)
Async XLA Ops:
  7.2 131.1 %all-gather.2.cloned.1.call-start = ((), (), s32[]{:S(2)}) async-start(), calls=%async_computation.2 | async-start | bytes 3932160 | tf_op jit(solution)/shard_map/all_gather | solution.py:1198
  73.4 217.0 %reduce-scatter.3.cloned.1.call-start = ((), (), s32[]{:S(2)}) async-start(), calls=%async_computation.3 | async-start | bytes 3932160 | tf_op jit(solution)/shard_map/reduce_scatter | solution.py:1216
  73.5 6.0 %copy-start.10 = (f32[768]{0:T(1024)S(1)}, f32[768]{0:T(1024)}, u32[]{:S(2)}) copy-start(f32[768]{0:T(1024)} %param.23) | copy-start | bytes 9220
  73.5 6.0 %copy-start.11 = (f32[768]{0:T(1024)S(1)}, f32[768]{0:T(1024)}, u32[]{:S(2)}) copy-start(f32[768]{0:T(1024)} %param.29) | copy-start | bytes 9220
  73.5 6.0 %copy-start.13 = (f32[12]{0:T(128)S(1)}, f32[12]{0:T(128)}, u32[]{:S(2)}) copy-start(f32[12]{0:T(128)} %param.28) | copy-start | bytes 148
  73.5 6.3 %copy-start.8 = (f32[4,768]{1,0:T(4,128)S(1)}, f32[4,768]{1,0:T(4,128)}, u32[]{:S(2)}) copy-start(f32[4,768]{1,0:T(4,128)} %param.22) | copy-start | bytes 36868
  73.5 6.9 %copy-start.14 = (f32[12]{0:T(128)S(1)}, f32[12]{0:T(128)}, u32[]{:S(2)}) copy-start(f32[12]{0:T(128)} %param.27) | copy-start | bytes 148
  73.5 6.9 %copy-start.15 = (f32[12]{0:T(128)S(1)}, f32[12]{0:T(128)}, u32[]{:S(2)}) copy-start(f32[12]{0:T(128)} %param.26) | copy-start | bytes 148
  73.6 7.6 %copy-start.9 = (f32[4,256]{1,0:T(4,128)S(1)}, f32[4,256]{1,0:T(4,128)}, u32[]{:S(2)}) copy-start(f32[4,256]{1,0:T(4,128)} %param.24) | copy-start | bytes 12292
  73.6 7.6 %copy-start.12 = (f32[256]{0:T(256)S(1)}, f32[256]{0:T(256)}, u32[]{:S(2)}) copy-start(f32[256]{0:T(256)} %param.25) | copy-start | bytes 3076
  73.6 8.2 %copy-start.1 = (bf16[1040,1536]{1,0:T(8,128)(2,1)S(1)}, bf16[1040,1536]{1,0:T(8,128)(2,1)}, u32[]{:S(2)}) copy-start(bf16[1040,1536]{1,0:T(8,128)(2,1)} %get-tuple-element.86.normed) | copy-start | bytes 9584644
  104.4 3.2 %collective-permute-start = (f32[128,768]{1,0:T(8,128)}, f32[128,768]{1,0:T(8,128)S(1)}, u32[]{:S(2)}, u32[]{:S(2)}) collective-permute-start(f32[128,768]{1,0:T(8,128)} %get-tuple-element.102), channel_id=1, source_target_pairs={{0,4},{1,5},{2,6},{3,7},{8,12},{9,13},{10,14},{11,15},{16,20},{17,... | collective-permute-start | bytes 1179656 | tf_op jit(solution)/shard_map/ppermute | solution.py:1171
  107.6 0.8 copy-start.5
  138.3 154.4 %reduce-scatter.5.cloned.1.call-start = ((), (), s32[]{:S(2)}) async-start(), calls=%async_computation.4 | async-start | bytes 3932160 | tf_op jit(solution)/shard_map/reduce_scatter | solution.py:1232
  163.2 3.8 %collective-permute-start.1 = (f32[128,768]{1,0:T(8,128)}, f32[128,768]{1,0:T(8,128)S(1)}, u32[]{:S(2)}, u32[]{:S(2)}) collective-permute-start(f32[128,768]{1,0:T(8,128)} %get-tuple-element.118), channel_id=1, source_target_pairs={{4,0},{5,1},{6,2},{7,3},{12,8},{13,9},{14,10},{15,11},{20,16},{21,... | collective-permute-start | bytes 1179656 | tf_op jit(solution)/shard_map/ppermute | solution.py:1171
  167.0 0.7 copy-start.7
  198.6 3.3 %collective-permute-start.2 = (f32[8,1024]{1,0:T(8,128)}, f32[8,1024]{1,0:T(8,128)S(1)}, u32[]{:S(2)}, u32[]{:S(2)}) collective-permute-start(f32[8,1024]{1,0:T(8,128)} %get-tuple-element.122), channel_id=1, source_target_pairs={{4,0},{5,1},{6,2},{7,3},{12,8},{13,9},{14,10},{15,11},{20,16},{21,... | collective-permute-start | bytes 98312 | tf_op jit(solution)/shard_map/ppermute | solution.py:1171
  203.8 12.0 %copy-start.2 = (bf16[1040,1536]{1,0:T(8,128)(2,1)S(1)}, bf16[1040,1536]{1,0:T(8,128)(2,1)}, u32[]{:S(2)}) copy-start(bf16[1040,1536]{1,0:T(8,128)(2,1)} %get-tuple-element.86.normed) | copy-start | bytes 9584644
  215.9 5.5 %copy-start.3 = (bf16[1024,1536]{1,0:T(8,128)(2,1)S(1)}, bf16[1024,1536]{1,0:T(8,128)(2,1)}, u32[]{:S(2)}) copy-start(bf16[1024,1536]{1,0:T(8,128)(2,1)} %all-gather.2.cloned.1.call-done.cot) | copy-start | bytes 9437188
  215.9 5.5 %copy-start.16 = (bf16[1024,768]{1,0:T(8,128)(2,1)S(1)}, bf16[1024,768]{1,0:T(8,128)(2,1)}, u32[]{:S(2)}) copy-start(bf16[1024,768]{1,0:T(8,128)(2,1)} %get-tuple-element.124) | copy-start | bytes 4718596
  221.4 4.0 %copy-start.6 = (bf16[1024,384]{1,0:T(8,128)(2,1)S(1)}, bf16[1024,384]{1,0:T(8,128)(2,1)}, u32[]{:S(2)}) copy-start(bf16[1024,384]{1,0:T(8,128)(2,1)} %slice_dynamic-update-slice_fusion.1.gsmall) | copy-start | bytes 2359300
  225.4 2.9 copy-start.4
  232.2 58.2 %copy-start = (bf16[256,1536]{1,0:T(8,128)(2,1)S(1)}, bf16[256,1536]{1,0:T(8,128)(2,1)}, u32[]{:S(2)}) copy-start(bf16[256,1536]{1,0:T(8,128)(2,1)} %tokens.1) | copy-start | bytes 2359300
Sparse Core Ops, SparseCore 0:
  73.6 64.6 all-gather.1
  140.5 61.1 reduce-scatter.2
  216.0 67.8 reduce-scatter.4

commit v4 on v3

--- a/solution.py
+++ b/solution.py
@@ -871,7 +871,106 @@
     )(value)
 
 
-def reduce_kernel(ncol, ndp, *refs):
+class LineReduce:
+    def __init__(self, ncol, z, source, local, inbox, send, recv):
+        self.ncol, self.z, self.last = ncol, z, ncol - 1
+        self.source, self.local, self.inbox = source, local, inbox
+        self.send, self.recv = send, recv
+        self.tokens = local.shape[0] // ncol
+        self.part = self.tokens // PIECES
+
+    def rows(self, way, t, p):
+        d = self.last - t if way == 0 else t
+        return pl.multiple_of(d * self.tokens + p * self.part, self.part)
+
+    def copy(self, way, t, p, first):
+        src = self.source.at[pl.ds(self.rows(way, t, p), self.part)] if first else self.inbox.at[way, t, p]
+        to = self.z + 1 if way == 0 else self.z - 1
+        return remote(src, self.inbox.at[way, t, p], self.send.at[way, t, p], self.recv.at[way, t, p], col=to)
+
+    def edge(self, way):
+        return self.z == (0 if way == 0 else self.last)
+
+    def depth(self, way):
+        return self.z if way == 0 else self.last - self.z
+
+    def start(self):
+        for way in range(2):
+
+            @pl.when(self.edge(way))
+            def _(way=way):
+                for t in range(self.last):
+                    for p in range(PIECES):
+                        self.copy(way, t, p, True).start()
+
+    ticks = property(lambda self: self.last * PIECES)
+
+    def tick(self, tau):
+        for stage in range(2):
+            for way in range(2):
+                depth = self.depth(way)
+                index = tau - depth
+                t, p = index // PIECES, lax.rem(index, PIECES)
+
+                @pl.when((depth > 0) & (index >= 0) & (index < (self.ncol - depth) * PIECES))
+                def _(way=way, depth=depth, t=t, p=p, stage=stage):
+                    onward = t < self.last - depth
+                    if stage == 0:
+                        self.copy(way, t, p, False).wait_recv()
+
+                        @pl.when(onward)
+                        def _():
+                            base = self.rows(way, t, p)
+
+                            def add(k, carry):
+                                at = pl.multiple_of(k * 16, 16)
+                                mine = self.local[pl.ds(pl.multiple_of(base + at, 16), 16)].astype(F32)
+                                here = pl.ds(at, 16)
+                                self.inbox[way, t, p, here] = (self.inbox[way, t, p, here].astype(F32) + mine).astype(BF16)
+                                return carry
+
+                            lax.fori_loop(0, self.part // 16, add, 0)
+                    else:
+
+                        @pl.when(onward)
+                        def _():
+                            self.copy(way, t, p, False).start()
+
+    def total(self, store):
+        z, last = self.z, self.last
+        for p in range(PIECES):
+
+            def add(k, carry, p=p):
+                at = pl.multiple_of(k * 16, 16)
+                here = pl.ds(at, 16)
+                row = p * self.part + at
+                value = self.local[pl.ds(pl.multiple_of(z * self.tokens + row, 16), 16)].astype(F32)
+                low = self.inbox[0, jnp.minimum(last - z, last - 1), p, here].astype(F32)
+                high = self.inbox[1, jnp.minimum(z, last - 1), p, here].astype(F32)
+                value = value + jnp.where(z > 0, low, 0.0) + jnp.where(z < last, high, 0.0)
+                store(row, value)
+                return carry
+
+            lax.fori_loop(0, self.part // 16, add, 0)
+
+    def drain(self):
+        for way in range(2):
+            depth = self.depth(way)
+            for t in range(self.last):
+
+                @pl.when((depth < self.last) & (t < self.last - depth))
+                def _(way=way, t=t):
+                    for p in range(PIECES):
+                        self.copy(way, t, p, False).wait_send()
+
+
+def line_scratch(ncol, tokens, width):
+    shape = (2, ncol - 1, PIECES)
+    dma = pltpu.SemaphoreType.DMA
+    return [pltpu.VMEM(shape + (tokens // PIECES, width), BF16), dma(shape), dma(shape)]
+
+
+def reduce_kernel(ncol, ndp, scols, *refs):
     count = 4
     refs = list(refs)
 
@@ -880,11 +979,14 @@
         del refs[:number]
         return taken
 
-    g, vecs = take(count), take(4)
-    r, vec_outs = take(count), take(4)
-    own, near, sent, far = take(count), take(count), take(count), take(count)
+    sources = take(7)
+    vecs = take(4)
+    r, vec_outs, gsum_out = take(count), take(4), refs.pop(0)
+    held = take(7)
+    (line_box, line_send, line_recv) = take(3)
+    g, near, sent, far = take(count), take(count), take(count), take(count)
     vec_slots, col_slots = take(4), take(2)
-    bc_slots, c_send, c_recv, p_send, p_recv, here, v_send, v_recv, u_send, u_recv, b_send, b_recv = refs
+    bc_slots, load, c_send, c_recv, p_send, p_recv, v_send, v_recv, u_send, u_recv, b_send, b_recv = refs
     dp, row, z = lax.axis_index("dp"), lax.axis_index("row"), lax.axis_index("col")
     other = 1 - row
     me = dp * 2 + row
@@ -894,7 +996,15 @@
         greet(barrier, row >= 0, dp=dp ^ (q >> 1), row=row ^ (q & 1))
     for s in range(1, ncol):
         greet(barrier, row >= 0, col=lax.rem(z + s, ncol))
+    loads = []
+    for i, (src, dst) in enumerate(zip(sources, held)):
+        src = src.at[pl.ds(0, dst.shape[0])]
+        loads.append(pltpu.make_async_copy(src, dst, load.at[i]))
+        loads[-1].start()
+    normed, gsmall, ggate, cot, gnorm, ginner, part = held
     pl.semaphore_wait(barrier, 2 * ndp + ncol - 2)
+    line = LineReduce(ncol, z, sources[6], part, line_box, line_send, line_recv)
+    line.start()
 
     order = (0, 1, 2, 3)
     turns = [3, 1, 2, 0] if ndp == 4 else list(range(1, ndp)) + [0]
@@ -903,17 +1013,10 @@
         return remote(g[i].at[pl.ds((d * 2 + other) * rows[i], rows[i])], near[i].at[d],
                       c_send.at[i, d], c_recv.at[i, d], row=other)
 
-    def own_copy(i, d):
-        return pltpu.make_async_copy(g[i].at[pl.ds((d * 2 + row) * rows[i], rows[i])], own[i].at[d], here.at[i, d])
-
     def vec_copy(q, i, j):
         return remote(vecs[i], vec_slots[i].at[j], v_send.at[q, i], v_recv.at[j, i],
                       dp=dp ^ (q >> 1), row=row ^ (q & 1))
 
-    for i in order:
-        for m in turns:
-            core_copy(i, dp ^ m).start()
-            own_copy(i, dp ^ m).start()
     for q in range(1, 2 * ndp):
         for i in range(4):
             vec_copy(q, i, me).start()
@@ -940,6 +1043,9 @@
     def read(ref, index, shift=0):
         return lambda at: ref[index, pl.ds(at - shift, 16)].astype(F32)
 
+    def mine(i, d):
+        return lambda at: g[i][pl.ds(pl.multiple_of((d * 2 + row) * rows[i] + at, 16), 16)].astype(F32)
+
     def write(ref, index, shift):
         def store(at, total):
             ref[index, pl.ds(at - shift, 16)] = total.astype(BF16)
@@ -948,7 +1054,38 @@
 
     def arrived(i, d):
         core_copy(i, d).wait_recv()
-        own_copy(i, d).wait()
+
+    model = normed.shape[1]
+    block = model // 4
+    ends = [[] for _ in range(4)]
+    products = ((normed, gsmall), (normed, ggate), (cot, gnorm), (normed, ginner))
+    ready = {0: (0, 1), 1: (2,), 2: (3, 4), 3: (5,)}
+    ticks = list(range(1, line.ticks + 1))
+    loaded = [False]
+    for i in order:
+        for at in ready[i]:
+            loads[at].wait()
+        left, right = products[i]
+        for m in ([3, 1, 2, 0] if ndp == 4 else range(4)):
+            b = dp ^ m if ndp == 4 else m
+            first = pl.multiple_of(b * block, 128)
+            g[i][pl.ds(pl.multiple_of(b * block, 16), block)] = tn(left[:, pl.ds(first, block)], right[...]).astype(BF16)
+            if ndp == 4:
+                later(core_copy(i, b))
+        if i == 1:
+            loads[6].wait()
+            line.tick(ticks.pop(0))
+        if i == 3 and ticks:
+            line.tick(ticks.pop(0))
+    later(None)
+    if ndp != 4:
+        for i in order:
+            for m in turns:
+                core_copy(i, dp ^ m).start()
+
+    def tick():
+        if ticks:
+            line.tick(ticks.pop(0))
 
     if ndp == 4:
         halves = ((0, 1, 2), (1, 2, 1))
@@ -960,12 +1097,12 @@
             half = rows[i] // 2
             arrived(i, dp ^ 3)
             for h, m1, m2 in halves:
-                accumulate(i, h * half, half, [read(own[i], dp ^ 3), read(near[i], dp ^ 3)],
+                accumulate(i, h * half, half, [mine(i, dp ^ 3), read(near[i], dp ^ 3)],
                            write(sent[i], 3 * h + 1, h * half))
                 later(leg(i, 3 * h + 1, m1))
             for h, m1, m2 in halves:
                 arrived(i, dp ^ m1)
-                accumulate(i, h * half, half, [read(own[i], dp ^ m1), read(near[i], dp ^ m1)],
+                accumulate(i, h * half, half, [mine(i, dp ^ m1), read(near[i], dp ^ m1)],
                            write(sent[i], 3 * h, h * half))
                 later(leg(i, 3 * h, m1))
         later(None)
@@ -975,7 +1112,7 @@
             for h, m1, m2 in halves:
                 leg(i, 3 * h + 1, m1).wait_recv()
                 accumulate(i, h * half, half,
-                           [read(own[i], dp ^ m2), read(near[i], dp ^ m2), read(far[i], 3 * h + 1, h * half)],
+                           [mine(i, dp ^ m2), read(near[i], dp ^ m2), read(far[i], 3 * h + 1, h * half)],
                            write(sent[i], 3 * h + 2, h * half))
                 later(leg(i, 3 * h + 2, m2))
 
@@ -985,7 +1122,7 @@
                 leg(i, 3 * h, m1).wait_recv()
                 leg(i, 3 * h + 2, m2).wait_recv()
                 accumulate(i, h * half, half,
-                           [read(own[i], dp), read(near[i], dp), read(far[i], 3 * h, h * half),
+                           [mine(i, dp), read(near[i], dp), read(far[i], 3 * h, h * half),
                             read(far[i], 3 * h + 2, h * half)], store)
 
         sends = [leg(i, 3 * h + k, m2 if k == 2 else m1) for i in order for h, m1, m2 in halves for k in range(3)]
@@ -997,7 +1134,7 @@
         for i in order:
             for m in turns[:-1]:
                 arrived(i, dp ^ m)
-                accumulate(i, 0, rows[i], [read(own[i], dp ^ m), read(near[i], dp ^ m)], write(sent[i], m, 0))
+                accumulate(i, 0, rows[i], [mine(i, dp ^ m), read(near[i], dp ^ m)], write(sent[i], m, 0))
                 later(peer(i, m))
         later(None)
 
@@ -1008,12 +1145,13 @@
             for m in range(1, ndp):
                 peer(i, m).wait_recv()
             accumulate(i, 0, rows[i],
-                       [read(own[i], dp), read(near[i], dp)] + [read(far[i], m) for m in range(1, ndp)], store)
+                       [mine(i, dp), read(near[i], dp)] + [read(far[i], m) for m in range(1, ndp)], store)
 
         sends = [peer(i, m) for i in order for m in range(1, ndp)]
 
     for i in order:
         arrived(i, dp)
+    tick()
     for q in range(1, 2 * ndp):
         for i in range(4):
             vec_copy(q, i, me ^ q).wait_recv()
@@ -1045,16 +1183,26 @@
 
     relay(0)
     relay(1)
+    tick()
     relay(2)
-    finish(0, shared_rows)
     relay(3)
     later(None)
+    finish(0, shared_rows)
     for s in range(1, ncol):
         for copy in col_copies(s, z):
             copy.start()
+    while len(ticks) > 1:
+        tick()
     finish(1, plain(1))
     finish(2, plain(2))
     finish(3, plain(3))
+    while ticks:
+        tick()
+
+    def keep(at, value):
+        gsum_out[pl.ds(pl.multiple_of(at, 16), 16)] = value.astype(BF16)
+
+    line.total(keep)
     for s in range(1, ncol):
         for copy in col_copies(s, lax.rem(z + s, ncol)):
             copy.wait_recv()
@@ -1079,37 +1227,47 @@
     for s in range(1, ncol):
         for copy in col_copies(s, z):
             copy.wait_send()
-
-
-def reduce_grads(grads, vecs, scols):
+    line.drain()
+
+
+def reduce_grads(sources, vecs, scols):
     ncol, ndp = lax.axis_size("col"), lax.axis_size("dp")
     dma = pltpu.SemaphoreType.DMA
     vmem = pl.BlockSpec(memory_space=pltpu.VMEM)
     S = jax.ShapeDtypeStruct
-    count = len(grads)
-    blocks = [(g.shape[0] // (2 * ndp), g.shape[1]) for g in grads]
-    stack = [pltpu.VMEM((ndp,) + b, BF16) for b in blocks]
+    length = sources[1].shape[0]
+    model = sources[0].shape[1]
+    widths = [sources[1].shape[1], sources[2].shape[1], sources[4].shape[1], sources[5].shape[1]]
+    count = len(widths)
+    blocks = [(model // (2 * ndp), w) for w in widths]
+    near = [pltpu.VMEM((ndp,) + b, BF16) for b in blocks]
     slots = 6 if ndp == 4 else ndp
     legs = [pltpu.VMEM((6, b[0] // 2, b[1]) if ndp == 4 else (ndp,) + b, BF16) for b in blocks]
+    tokens = length // ncol
     return pl.pallas_call(
-        functools.partial(reduce_kernel, ncol, ndp),
-        in_specs=[ANY] * count + [vmem] * 4,
-        out_specs=[vmem] * (count + 4),
-        out_shape=[S(b, F32) for b in blocks] + [S(v.shape, F32) for v in vecs],
-        scratch_shapes=stack * 2 + legs * 2
+        functools.partial(reduce_kernel, ncol, ndp, scols),
+        in_specs=[ANY] * 7 + [vmem] * 4,
+        out_specs=[vmem] * (count + 5),
+        out_shape=[S(b, F32) for b in blocks] + [S(v.shape, F32) for v in vecs] + [S((tokens, model), BF16)],
+        scratch_shapes=[pltpu.VMEM((length, s.shape[1]), BF16) for s in sources]
+        + line_scratch(ncol, tokens, model)
+        + [pltpu.VMEM((model, w), BF16) for w in widths]
+        + near + legs * 2
         + [pltpu.VMEM((2 * ndp,) + v.shape, F32) for v in vecs]
         + [pltpu.VMEM((ncol,) + v.shape, F32) for v in vecs[2:]]
         + [pltpu.VMEM((ncol, blocks[0][0], scols), BF16)]
+        + [dma((7,))]
         + [dma((count, ndp))] * 2
         + [dma((count, slots))] * 2
-        + [dma((count, ndp))]
         + [dma((2 * ndp, 4))] * 2
         + [dma((ncol, 2))] * 2
         + [dma((ncol,))] * 2,
-        compiler_params=pltpu.CompilerParams(collective_id=2, has_side_effects=True),
+        compiler_params=pltpu.CompilerParams(
+            collective_id=2, has_side_effects=True, vmem_limit_bytes=60 * 1024 * 1024
+        ),
         cost_estimate=pl.CostEstimate(flops=0, bytes_accessed=200_000_000, transcendentals=0),
         name="reduce_grads",
-    )(*grads, *vecs)
+    )(*sources, *vecs)
 
 
 def finish_kernel(
@@ -1229,15 +1387,9 @@
     ginner = lax.dynamic_update_slice(ginner, fixed[:, :width], (length - 8, 0))
     gsmall = lax.dynamic_update_slice(gsmall, fixed[:, width:], (length - 8, 0))
     part, gain_part = run_spread(ggate, ginner, gsmall, w_in, w_small, normed_ext)
-    grad_normed = lax.psum_scatter(part, "col", scatter_dimension=0, tiled=True)
-    normed = normed_ext[:length]
-    grads = (
-        tn(normed, gsmall).astype(BF16),
-        tn(normed, ggate).astype(BF16),
-        tn(cot_all, gated_normed).astype(BF16),
-        tn(normed, ginner).astype(BF16),
+    gsm, gz, gout, gx, par, par_h, par_s, gain_sum, grad_normed = reduce_grads(
+        (normed_ext, gsmall, ggate, cot_all, gated_normed, ginner, part), (par, par_h, par_s, gain_part), scols
     )
-    gsm, gz, gout, gx, par, par_h, par_s, gain_sum = reduce_grads(grads, (par, par_h, par_s, gain_part), scols)
     zx, gbc, gdt, gout, ci, cib, cs, csb, sb, rl, sg, gg, ng, grad_input = run_finish(
         nheads, gsm, gz, gx, gout, par, par_h, par_s, gain_sum, norm_gain, block_input, cotangent, grad_normed
     )

time: 310 us -> 304 us (0.981)
  matrix products: 29.3 us -> 13 us
  Pallas kernels: 228 us -> 239 us
    dot_general x4 -> x0, matrix products: 16.3 us -> none  [tn(): lax.dot_general(a, b, (((0,), (0,)), ((), ())), preferred_element_type=F32)]
    pallas_call x1, Pallas kernels: 58.2 us -> 68.9 us  [reduce_grads(): pl.pallas_call(functools.partial(reduce_kernel, ncol, ndp, scols), in_spe...]
  transfers between devices with their start and end apart: 6 -> 5, of which waited for: 4 -> 4; matrix products, arithmetic and copies ran while one was open for 12% -> 8% of each run, Pallas kernels for 53% -> 59%
where the time goes in v4:
time: 304 us; the launch traced here: 303 us
  Pallas kernels  239 us (79%)
  between operations  14.3 us (5%)
  waiting for transfers between devices  13 us (4%)
  matrix products  13 us (4%)
  other arithmetic  9.74 us (3%)
  local copies, waits for them, and re-layouts  9.47 us (3%)
  starting transfers between devices  4.52 us (1%)
    pallas_call x1, Pallas kernels, reduce_grads(): pl.pallas_call(functools.partial(reduce_kernel, ncol, ndp, scols), in_spe...  68.9 us
    pallas_call x1, Pallas kernels, gather_inputs(): pl.pallas_call(functools.partial(gather_kernel, ncol, ndp), in_specs=[vme...  60.6 us
    pallas_call x1, Pallas kernels, run_backward(): pl.pallas_call(backward_kernel, grid=(chunks,), in_specs=[pl.BlockSpec((S...  30.8 us
    pallas_call x2, Pallas kernels, sum_col(): pl.pallas_call(functools.partial(sum_col_kernel, ncol), in_specs=[vmem],...  18.5 us
    pallas_call x1, Pallas kernels, run_forward(): pl.pallas_call(forward_kernel, grid=(chunks,), in_specs=[pl.BlockSpec((SP...  13.8 us
    dot_general x2, matrix products, nn(): lax.dot_general(a, b, (((1,), (0,)), ((), ())), preferred_element_type=F32)  13 us
    pallas_call x1, Pallas kernels, run_spread(): pl.pallas_call(spread_kernel, grid=(model // tile,), in_specs=[pl.BlockSp...  11.9 us
    pallas_call x1, Pallas kernels, run_back(): pl.pallas_call(functools.partial(back_kernel, full_width), grid=(length /...  8.69 us
  transfers between devices with their start and end apart: 5, of which 4 were waited for; matrix products, arithmetic and copies ran while one was open for 8% of the time, Pallas kernels for 59%

profile of v4, /device:TPU:0, one launch (start us, length us, event | category | flops | bytes accessed | tf_op | source)
XLA Modules:
  0.0 303.0 jit_solution(966614054314448993)
XLA Ops:
  7.2 0.0 all-gather.2.cloned.1.call-start
  7.2 1.3 broadcast_in_dim.34.gain
  8.5 1.9 copy.32
  10.5 0.8 copy.31
  11.3 1.6 fusion.1.w1
  12.9 60.6 %gather_inputs.1 = (bf16[1040,1536]{1,0:T(8,128)(2,1)}, s32[40,256]{1,0:T(8,128)}, bf16[1536,1536]{1,0:T(8,128)(2,1)}, bf16[1536,384]{1,0:T(8,128)(2,1)}, bf16[1536,768]{1,0:T(8,128)(2,1)}) custom-call(bf16[256,1536]{1,0:T(8,128)(2,1)} %tokens.1, f32[1,1536]{1,0:T(1,128)} %broadcast_in_dim.34.gain, s32[1,256]{1,0:T(1,128)} %bitcast.22, ...), custom_call_target="tpu_custom_call" | custom-call | bytes 200000000 | tf_op jit(solution)/shard_map/gather_inputs/pallas_call | solution.py:818
  73.4 0.0 all-gather.2.cloned.1.call-update
  73.4 0.0 reduce-scatter.2.cloned.1.call-start
  73.5 0.0 copy-start.9
  73.6 4.2 %fusion.2 = f32[1040,384]{1,0:T(8,128)S(1)} fusion(bf16[1040,1536]{1,0:T(8,128)(2,1)} %get-tuple-element.87.normed.refs_0_, bf16[1536,384]{1,0:T(8,128)(2,1)} %get-tuple-element.89.w_small), kind=kOutput, calls=%fused_computation.13 | convolution fusion | flops 1226833920 | bytes 5971968 | tf_op jit(solution)/shard_map/dot_general | solution.py:16
  77.8 0.9 slice.24.shared.shared_halo
  78.7 0.8 slice.18.step_raw
  79.5 0.1 broadcast_in_dim.38
  79.6 0.1 broadcast_in_dim_reshape.3
  79.7 0.1 pad.19.clone
  79.7 0.1 pad.16.clone
  79.8 0.6 concatenate.13.taps
  80.5 0.7 maximum_maximum_fusion.1.heads
  81.1 0.7 maximum_maximum_fusion.taps_s
  81.8 8.8 %convolution_convert_fusion.inner.inner_halo.gate = bf16[1040,1536]{1,0:T(8,128)(2,1)} fusion(bf16[1040,1536]{1,0:T(8,128)(2,1)S(1)} %copy-done, bf16[1536,1536]{1,0:T(8,128)(2,1)} %get-tuple-element.88.w_in), kind=kOutput, calls=%fused_computation | convolution fusion | flops 4908933120 | bytes 11108352 | tf_op jit(solution)/shard_map/dot_general | solution.py:16
  90.6 13.8 %scan_forward.1 = (f32[1024,768]{1,0:T(8,128)}, bf16[1024,768]{1,0:T(8,128)(2,1)}, bf16[1024,256]{1,0:T(8,128)(2,1)}, f32[1024,128]{1,0:T(8,128)}, f32[1024,128]...) custom-call(bf16[1040,1536]{1,0:T(8,128)(2,1)} %convolution_convert_, ...), custom_call_target="tpu_custom_call" | custom-call | tf_op jit(solution)/shard_map/scan_forward/pallas_call | solution.py:164
  104.4 1.7 collective-permute-start
  106.1 1.5 collective-permute-done.start
  107.6 0.8 copy-done.2
  108.4 6.9 %gate_sums.1 = (f32[1024,768]{1,0:T(8,128)}, bf16[1024,768]{1,0:T(8,128)(2,1)}, f32[8,1024]{1,0:T(8,128)}) custom-call(f32[1024,768]{1,0:T(8,128)} %get-tuple-element.99.y, bf16[1024,768]{1,0:T(8,128)(2,1)} %get-tuple-element.100.x, bf16[1024,256]{1,0:T(8,128)(2,1)} %get-tuple-element.101.bc, f32[1024,128]{1,0:T(8,128)} %get-tuple-element.102.dec.dec_halo, ...), custom_call_target="tpu_custom_call" | custom-call | tf_op jit(solution)/shard_map/gate_sums/pallas_call | solution.py:239
  115.3 9.1 %sum_col.2.sums.squares = f32[8,1024]{1,0:T(8,128)} custom-call(f32[8,1024]{1,0:T(8,128)} %get-tuple-element.105.value), custom_call_target="tpu_custom_call" | custom-call | tf_op jit(solution)/shard_map/sum_col/pallas_call | solution.py:863
  124.4 6.7 %project.1 = (bf16[1024,768]{1,0:T(8,128)(2,1)}, bf16[1024,1536]{1,0:T(8,128)(2,1)}) custom-call(bf16[1024,768]{1,0:T(8,128)(2,1)} %get-tuple-element.104.gated, f32[8,1024]{1,0:T(8,128)} %sum_col.2.sums.squares, f32[8,768]{1,0:T(8,128)} %concatenate.13.taps, bf16[1536,768]{1,0:T(8,128)(2,1)} %get-tuple-element.106.out_t), custom_call_target="tpu_custom_call" | custom-call | tf_op jit(solution)/shard_map/project/pallas_call | solution.py:274
  131.1 7.1 %all-gather.2.cloned.1.call-done.cot.refs_3_ = bf16[1024,1536]{1,0:T(8,128)(2,1)} async-done(((bf16[256,1536]{1,0:T(8,128)(2,1)}), bf16[1024,1536]{1,0:T(8,128)(2,1)}) %all-gather.2.cloned.1.call-update) | async-done | bytes 3145744 | tf_op jit(solution)/shard_map/all_gather | solution.py:1356
  138.3 0.0 reduce-scatter.2.cloned.1.call-update
  138.3 6.9 %pull_back.1 = (bf16[1024,768]{1,0:T(8,128)(2,1)}, f32[8,1024]{1,0:T(8,128)}) custom-call(bf16[1024,1536]{1,0:T(8,128)(2,1)} %all-gather.2.cloned.1.call-done.cot.refs_3_, bf16[1536,768]{1,0:T(8,128)(2,1)} %get-tuple-element.106.out_t, bf16[1024,768]{1,0:T(8,128)(2,1)} %get-tuple-element.104.gated, f32[8,768]{1,0:T(8,128)} %concatenate.13.taps), custom_call_target="tpu_custom_call" | custom-call | tf_op jit(solution)/shard_map/pull_back/pallas_call | solution.py:304
  145.2 9.3 %sum_col.3.inner = f32[8,1024]{1,0:T(8,128)} custom-call(f32[8,1024]{1,0:T(8,128)} %get-tuple-element.112.value), custom_call_target="tpu_custom_call" | custom-call | tf_op jit(solution)/shard_map/sum_col/pallas_call | solution.py:863
  154.5 8.7 %gated_back.1 = (bf16[1024,768]{1,0:T(8,128)(2,1)}, bf16[1024,768]{1,0:T(8,128)(2,1)}, f32[1024,128]{1,0:T(8,128)}, f32[8,768]{1,0:T(8,128)}, f32[128,768]{1,0:T(8,128)}) custom-call(f32[1024,768]{1,0:T(8,128)} %get-tuple-element.109.ssd, bf16[1024,768]{1,0:T(8,128)(2,1)} %get-tuple-element.100.x, bf16[1024,256]{1,0:T(8,128)(2,1)} %get-tuple-element.101.bc, ...), custom_call_target="tpu_custom_call" | custom-call | tf_op jit(solution)/shard_map/gated_back/pallas_call | solution.py:367
  163.2 1.5 collective-permute-start.1
  164.7 2.3 collective-permute-done.1.dend
  167.1 0.8 copy-done.3
  167.8 30.8 %scan_backward.1 = (bf16[1024,768]{1,0:T(8,128)(2,1)}, bf16[1024,384]{1,0:T(8,128)(2,1)}, f32[8,768]{1,0:T(8,128)}, f32[8,256]{1,0:T(8,128)}, f32[8,128]{1,0:T(8...) custom-call(bf16[1040,1536]{1,0:T(8,128)(2,1)} %convolution_convert_fusion.inner.inner_halo.gate, ...), custom_call_target="tpu_custom_call" | custom-call | tf_op jit(solution)/shard_map/scan_backward/pallas_call | solution.py:549
  198.6 1.3 collective-permute-start.2
  199.9 2.0 collective-permute-done.2
  201.9 0.8 add_convert_fusion.1
  202.7 0.6 slice_dynamic-update-slice_fusion.1.gsmall.refs_1_
  203.3 0.6 slice_dynamic-update-slice_fusion.ginner.refs_5_
  203.9 11.9 %spread_back.1 = (bf16[1024,1536]{1,0:T(8,128)(2,1)}, f32[8,1536]{1,0:T(8,128)}) custom-call(bf16[1024,768]{1,0:T(8,128)(2,1)} %get-tuple-element.124.ggate.refs_2_, bf16[1024,768]{1,0:T(8,128)(2,1)} %slice_dynamic-update-slice_fusion.ginner.refs_5_, bf16[1024,384]{1,0:T(8,128)(2,1)} %slice_dynamic-update-slice_fusion.1.gsmall.refs_1_, ...), custom_call_target="tpu_custom_call" | custom-call | tf_op jit(solution)/shard_map/spread_back/pallas_call | solution.py:621
  215.8 68.9 %reduce_grads.1 = (f32[192,384]{1,0:T(8,128)}, f32[192,768]{1,0:T(8,128)}, f32[192,768]{1,0:T(8,128)}, f32[192,768]{1,0:T(8,128)}, f32[8,768]{1,0:T(8,128)}, /*i...) custom-call(bf16[1040,1536]{1,0:T(8,128)(2,1)} %get-tuple-element.87.normed.refs_0_, ...), custom_call_target="tpu_custom_call" | custom-call | bytes 200000000 | tf_op jit(solution)/shard_map/reduce_grads/pallas_call | solution.py:1247
  284.7 5.4 %finish.1 = (f32[192,2,768]{2,1,0:T(2,128)}, f32[192,256]{1,0:T(8,128)}, f32[12,192]{1,0:T(8,128)}, f32[192,768]{1,0:T(8,128)}, f32[4,768]{1,0:T(4,128)}, /*inde...) custom-call(f32[192,384]{1,0:T(8,128)} %get-tuple-element.132.small,, ...), custom_call_target="tpu_custom_call" | custom-call | tf_op jit(solution)/shard_map/finish/pallas_call | solution.py:1319
  290.1 1.3 reduce
  291.4 1.3 reduce.1
  292.7 1.3 reduce.2
  294.0 2.2 add_convert_fusion
  (28 shorter events, 0.1 us)
Async XLA Ops:
  7.2 131.1 %all-gather.2.cloned.1.call-start = ((), (), s32[]{:S(2)}) async-start(), calls=%async_computation.1 | async-start | bytes 3932160 | tf_op jit(solution)/shard_map/all_gather | solution.py:1356
  73.4 220.5 %reduce-scatter.2.cloned.1.call-start = ((), (), s32[]{:S(2)}) async-start(), calls=%async_computation.2 | async-start | bytes 3932160 | tf_op jit(solution)/shard_map/reduce_scatter | solution.py:1374
  73.5 6.0 %copy-start.6 = (f32[768]{0:T(1024)S(1)}, f32[768]{0:T(1024)}, u32[]{:S(2)}) copy-start(f32[768]{0:T(1024)} %param.23) | copy-start | bytes 9220
  73.5 6.0 %copy-start.7 = (f32[768]{0:T(1024)S(1)}, f32[768]{0:T(1024)}, u32[]{:S(2)}) copy-start(f32[768]{0:T(1024)} %param.29) | copy-start | bytes 9220
  73.5 6.0 %copy-start.9 = (f32[12]{0:T(128)S(1)}, f32[12]{0:T(128)}, u32[]{:S(2)}) copy-start(f32[12]{0:T(128)} %param.28) | copy-start | bytes 148
  73.5 6.3 %copy-start.4 = (f32[4,768]{1,0:T(4,128)S(1)}, f32[4,768]{1,0:T(4,128)}, u32[]{:S(2)}) copy-start(f32[4,768]{1,0:T(4,128)} %param.22) | copy-start | bytes 36868
  73.5 6.9 %copy-start.10 = (f32[12]{0:T(128)S(1)}, f32[12]{0:T(128)}, u32[]{:S(2)}) copy-start(f32[12]{0:T(128)} %param.27) | copy-start | bytes 148
  73.6 6.9 %copy-start.11 = (f32[12]{0:T(128)S(1)}, f32[12]{0:T(128)}, u32[]{:S(2)}) copy-start(f32[12]{0:T(128)} %param.26) | copy-start | bytes 148
  73.6 7.6 %copy-start.5 = (f32[4,256]{1,0:T(4,128)S(1)}, f32[4,256]{1,0:T(4,128)}, u32[]{:S(2)}) copy-start(f32[4,256]{1,0:T(4,128)} %param.24) | copy-start | bytes 12292
  73.6 7.6 %copy-start.8 = (f32[256]{0:T(256)S(1)}, f32[256]{0:T(256)}, u32[]{:S(2)}) copy-start(f32[256]{0:T(256)} %param.25) | copy-start | bytes 3076
  73.6 8.2 %copy-start = (bf16[1040,1536]{1,0:T(8,128)(2,1)S(1)}, bf16[1040,1536]{1,0:T(8,128)(2,1)}, u32[]{:S(2)}) copy-start(bf16[1040,1536]{1,0:T(8,128)(2,1)} %get-tuple-element.87.normed.refs_0_) | copy-start | bytes 9584644
  104.4 3.2 %collective-permute-start = (f32[128,768]{1,0:T(8,128)}, f32[128,768]{1,0:T(8,128)S(1)}, u32[]{:S(2)}, u32[]{:S(2)}) collective-permute-start(f32[128,768]{1,0:T(8,128)} %get-tuple-element.103), channel_id=1, source_target_pairs={{0,4},{1,5},{2,6},{3,7},{8,12},{9,13},{10,14},{11,15},{16,20},{17,... | collective-permute-start | bytes 1179656 | tf_op jit(solution)/shard_map/ppermute | solution.py:1329
  107.6 0.8 copy-start.2
  163.2 3.8 %collective-permute-start.1 = (f32[128,768]{1,0:T(8,128)}, f32[128,768]{1,0:T(8,128)S(1)}, u32[]{:S(2)}, u32[]{:S(2)}) collective-permute-start(f32[128,768]{1,0:T(8,128)} %get-tuple-element.119), channel_id=1, source_target_pairs={{4,0},{5,1},{6,2},{7,3},{12,8},{13,9},{14,10},{15,11},{20,16},{21,... | collective-permute-start | bytes 1179656 | tf_op jit(solution)/shard_map/ppermute | solution.py:1329
  167.1 0.8 copy-start.3
  198.6 3.3 %collective-permute-start.2 = (f32[8,1024]{1,0:T(8,128)}, f32[8,1024]{1,0:T(8,128)S(1)}, u32[]{:S(2)}, u32[]{:S(2)}) collective-permute-start(f32[8,1024]{1,0:T(8,128)} %get-tuple-element.123), channel_id=1, source_target_pairs={{4,0},{5,1},{6,2},{7,3},{12,8},{13,9},{14,10},{15,11},{20,16},{21,... | collective-permute-start | bytes 98312 | tf_op jit(solution)/shard_map/ppermute | solution.py:1329
  284.7 9.3 %copy-start.1 = (bf16[256,1536]{1,0:T(8,128)(2,1)S(1)}, bf16[256,1536]{1,0:T(8,128)(2,1)}, u32[]{:S(2)}) copy-start(bf16[256,1536]{1,0:T(8,128)(2,1)} %tokens.1) | copy-start | bytes 2359300
Sparse Core Ops, SparseCore 0:
  73.6 64.6 all-gather.1
  140.6 61.0 reduce-scatter.1

commit v5 on v4

--- a/solution.py
+++ b/solution.py
@@ -75,19 +75,13 @@
     return jnp.where(lo, cols[:, h : h + 1], cols[:, h + 1 : h + 2])
 
 
-def forward_kernel(
+def forward_body(
     inner, inner_halo, shared, shared_halo, step_raw, seg_row, seg_prev, seg_tail, taps, taps_s, heads,
-    y_out, x_out, bc_out, dt_out, c_out, ct_out, dec_out, enter_out, final_out, state, total,
+    y_out, x_out, bc_out, dt_out, c_out, ct_out, dec_out, enter_out, state, total,
 ):
-    k = pl.program_id(0)
     length, width = inner.shape
     pairs = width // 128
     state_dim = state.shape[0]
-
-    @pl.when(k == 0)
-    def _():
-        state[...] = jnp.zeros_like(state)
-        total[...] = jnp.zeros_like(total)
 
     segr, seg, seg_halo, tail_seg = segments(seg_row, seg_prev, seg_tail)
     links = chunk_links(seg, seg_halo)
@@ -134,73 +128,6 @@
         leaving = jnp.exp(last - cb) * closing * xdt
         state[:, sl] = state[:, sl] * (jnp.exp(last) * kept) + tn(b, leaving.astype(BF16))
 
-    @pl.when(k == pl.num_programs(0) - 1)
-    def _():
-        final_out[...] = state[...]
-
-
-def halo_index(chunk, chunks):
-    return jnp.where(chunk == 0, chunks * (SPAN // HALO), chunk * (SPAN // HALO) - 1)
-
-
-def seg_specs(at, chunks):
-    return [
-        pl.BlockSpec((8, SPAN), lambda k: (at(k), 0)),
-        pl.BlockSpec((8, SPAN), lambda k: (jnp.where(at(k) == 0, chunks, at(k) - 1), 0)),
-        pl.BlockSpec((8, SPAN), lambda k: (chunks, 0)),
-    ]
-
-
-def run_forward(both_ext, shared_ext, step_raw, seg, taps, taps_s, heads):
-    width = taps.shape[1]
-    scols = taps_s.shape[1]
-    chunks = seg.shape[0] // 8 - 1
-    length = chunks * SPAN
-    nrow = 16
-    row = lambda k: (k, 0)
-    halo = lambda col: (lambda k: (halo_index(k, chunks), col))
-    fixed = lambda k: (0, 0)
-    S = jax.ShapeDtypeStruct
-    return pl.pallas_call(
-        forward_kernel,
-        grid=(chunks,),
-        in_specs=[
-            pl.BlockSpec((SPAN, width), lambda k: (k, 1)),
-            pl.BlockSpec((HALO, width), halo(1)),
-            pl.BlockSpec((SPAN, scols), row),
-            pl.BlockSpec((HALO, scols), halo(0)),
-            pl.BlockSpec((SPAN, 128), row),
-            *seg_specs(lambda k: k, chunks),
-            pl.BlockSpec(taps.shape, fixed),
-            pl.BlockSpec(taps_s.shape, fixed),
-            pl.BlockSpec(heads.shape, fixed),
-        ],
-        out_specs=[
-            pl.BlockSpec((SPAN, width), row),
-            pl.BlockSpec((SPAN, width), row),
-            pl.BlockSpec((SPAN, scols), row),
-            pl.BlockSpec((SPAN, 128), row),
-            pl.BlockSpec((SPAN, 128), row),
-            pl.BlockSpec((nrow, SPAN), lambda k: (0, k)),
-            pl.BlockSpec((SPAN, 128), row),
-            pl.BlockSpec((None, scols // 2, width), lambda k: (k, 0, 0)),
-            pl.BlockSpec((scols // 2, width), fixed),
-        ],
-        out_shape=[
-            S((length, width), F32),
-            S((length, width), BF16),
-            S((length, scols), BF16),
-            S((length, 128), F32),
-            S((length, 128), F32),
-            S((nrow, length), F32),
-            S((length, 128), F32),
-            S((chunks, scols // 2, width), BF16),
-            S((scols // 2, width), F32),
-        ],
-        scratch_shapes=[pltpu.VMEM((scols // 2, width), F32), pltpu.VMEM((8, 128), F32)],
-        name="scan_forward",
-    )(both_ext, both_ext, shared_ext, shared_ext, step_raw, seg, seg, seg, taps, taps_s, heads)
-
 
 def row_sums(value):
     hi = value.astype(BF16)
@@ -213,7 +140,12 @@
     return jnp.where(iota(value.shape, 0) == 0, value, 0.0)
 
 
-def gate_kernel(y, x, bc, dec, start, gate, taps, ssd_out, gated_out, sums_out):
+def head_map(p):
+    lane, head = iota((128, 128), 0), iota((128, 128), 1)
+    return (head == 2 * p + lane // 64).astype(BF16)
+
+
+def gate_body(y, x, bc, dec, start, gate, taps, ssd_out, gated_out, sums_out):
     length, width = x.shape
     state_dim = start.shape[0]
     cc = bc[:, state_dim:]
@@ -231,34 +163,7 @@
     sums_out[...] = row_sums(squares)
 
 
-def run_gate(y, x, bc, dec, start, both_ext, taps):
-    length, width = x.shape
-    row = lambda k: (k, 0)
-    fixed = lambda k: (0, 0)
-    S = jax.ShapeDtypeStruct
-    return pl.pallas_call(
-        gate_kernel,
-        grid=(length // SPAN,),
-        in_specs=[
-            pl.BlockSpec((SPAN, width), row),
-            pl.BlockSpec((SPAN, width), row),
-            pl.BlockSpec((SPAN, bc.shape[1]), row),
-            pl.BlockSpec((SPAN, 128), row),
-            pl.BlockSpec(start.shape, fixed),
-            pl.BlockSpec((SPAN, width), row),
-            pl.BlockSpec(taps.shape, fixed),
-        ],
-        out_specs=[
-            pl.BlockSpec((SPAN, width), row),
-            pl.BlockSpec((SPAN, width), row),
-            pl.BlockSpec((8, SPAN), lambda k: (0, k)),
-        ],
-        out_shape=[S((length, width), F32), S((length, width), BF16), S((8, length), F32)],
-        name="gate_sums",
-    )(y, x, bc, dec, start, both_ext, taps)
-
-
-def project_kernel(full_width, gated, sums, taps, out_t, normed_out, proj_out):
+def project_body(full_width, gated, sums, taps, out_t, normed_out, proj_out):
     rescale = columns(lax.rsqrt(sums[0:1] / full_width + EPS))
     for p in range(gated.shape[1] // 128):
         sl = slice(p * 128, (p + 1) * 128)
@@ -266,27 +171,7 @@
     proj_out[...] = nt(normed_out[...], out_t[...]).astype(BF16)
 
 
-def run_project(full_width, gated, sums, taps, out_t):
-    length, width = gated.shape
-    row = lambda k: (k, 0)
-    fixed = lambda k: (0, 0)
-    S = jax.ShapeDtypeStruct
-    return pl.pallas_call(
-        functools.partial(project_kernel, full_width),
-        grid=(length // SPAN,),
-        in_specs=[
-            pl.BlockSpec((SPAN, width), row),
-            pl.BlockSpec((8, SPAN), lambda k: (0, k)),
-            pl.BlockSpec(taps.shape, fixed),
-            pl.BlockSpec(out_t.shape, fixed),
-        ],
-        out_specs=[pl.BlockSpec((SPAN, width), row), pl.BlockSpec((SPAN, out_t.shape[0]), row)],
-        out_shape=[S((length, width), BF16), S((length, out_t.shape[0]), BF16)],
-        name="project",
-    )(gated, sums, taps, out_t)
-
-
-def pull_kernel(cot, out_t, gated, taps, back_out, sums_out):
+def pull_body(cot, out_t, gated, taps, back_out, sums_out):
     back = nn(cot[...], out_t[...])
     back_out[...] = back.astype(BF16)
     inner = jnp.zeros((cot.shape[0], 128), F32)
@@ -296,37 +181,12 @@
     sums_out[...] = row_sums(inner)
 
 
-def run_pull(cot, out_t, gated, taps):
-    length, width = gated.shape
-    row = lambda k: (k, 0)
-    fixed = lambda k: (0, 0)
-    S = jax.ShapeDtypeStruct
-    return pl.pallas_call(
-        pull_kernel,
-        grid=(length // SPAN,),
-        in_specs=[
-            pl.BlockSpec((SPAN, cot.shape[1]), row),
-            pl.BlockSpec(out_t.shape, fixed),
-            pl.BlockSpec((SPAN, width), row),
-            pl.BlockSpec(taps.shape, fixed),
-        ],
-        out_specs=[pl.BlockSpec((SPAN, width), row), pl.BlockSpec((8, SPAN), lambda k: (0, k))],
-        out_shape=[S((length, width), BF16), S((8, length), F32)],
-        name="pull_back",
-    )(cot, out_t, gated, taps)
-
-
-def back_kernel(
+def back_body(
     full_width, ssd, x, bc, dec, gate, back, squares, inner, taps,
     dy_out, ggate_out, row_out, colsum_out, dstart_out,
 ):
     length, width = x.shape
     state_dim = dstart_out.shape[0]
-
-    @pl.when(pl.program_id(0) == 0)
-    def _():
-        colsum_out[...] = jnp.zeros_like(colsum_out)
-        dstart_out[...] = jnp.zeros_like(dstart_out)
 
     cc = bc[:, state_dim:]
     lo = iota((length, 128), 1) < 64
@@ -354,48 +214,6 @@
     row_out[...] = rowterm
 
 
-def head_map(p):
-    lane, head = iota((128, 128), 0), iota((128, 128), 1)
-    return (head == 2 * p + lane // 64).astype(BF16)
-
-
-def run_back(full_width, ssd, x, bc, dec, both_ext, back, squares, inner, taps):
-    length, width = x.shape
-    row = lambda k: (k, 0)
-    fixed = lambda k: (0, 0)
-    S = jax.ShapeDtypeStruct
-    return pl.pallas_call(
-        functools.partial(back_kernel, full_width),
-        grid=(length // SPAN,),
-        in_specs=[
-            pl.BlockSpec((SPAN, width), row),
-            pl.BlockSpec((SPAN, width), row),
-            pl.BlockSpec((SPAN, bc.shape[1]), row),
-            pl.BlockSpec((SPAN, 128), row),
-            pl.BlockSpec((SPAN, width), row),
-            pl.BlockSpec((SPAN, width), row),
-            pl.BlockSpec((8, SPAN), lambda k: (0, k)),
-            pl.BlockSpec((8, SPAN), lambda k: (0, k)),
-            pl.BlockSpec(taps.shape, fixed),
-        ],
-        out_specs=[
-            pl.BlockSpec((SPAN, width), row),
-            pl.BlockSpec((SPAN, width), row),
-            pl.BlockSpec((SPAN, 128), row),
-            pl.BlockSpec((8, width), fixed),
-            pl.BlockSpec((bc.shape[1] // 2, width), fixed),
-        ],
-        out_shape=[
-            S((length, width), BF16),
-            S((length, width), BF16),
-            S((length, 128), F32),
-            S((8, width), F32),
-            S((bc.shape[1] // 2, width), F32),
-        ],
-        name="gated_back",
-    )(ssd, x, bc, dec, both_ext, back, squares, inner, taps)
-
-
 def conv_back(dout, pre, shifts, links, taps, sl, carry, carry_links, par_out):
     length = dout.shape[0]
     s = sigmoid(pre)
@@ -417,26 +235,15 @@
     return grad, above
 
 
-def backward_kernel(
+def backward_body(
+    k, chunks,
     inner, inner_halo, shared, shared_halo, step_raw, seg_row, seg_prev, seg_tail, taps, taps_s, heads,
-    dy, x, bc, dt_in, c_in, ct_in, dec_halo, enter, start, row_in, dend, colsum,
+    dy, x, bc, dt_in, c_in, ct_in, dec_halo, enter, start, row_in,
     ginner_out, gsmall_out, par_out, par_s_out, par_h_out, edge_out, last_out,
     dstate, carry, carry_s, carry_links, grads_bc,
 ):
-    i = pl.program_id(0)
-    k = pl.num_programs(0) - 1 - i
     length, width = x.shape
     state_dim = dstate.shape[0]
-
-    @pl.when(i == 0)
-    def _():
-        dstate[...] = dend[...]
-        carry[...] = jnp.zeros_like(carry)
-        carry_s[...] = jnp.zeros_like(carry_s)
-        carry_links[...] = jnp.zeros_like(carry_links)
-        par_out[...] = colsum[...]
-        par_s_out[...] = jnp.zeros_like(par_s_out)
-        par_h_out[...] = jnp.zeros_like(par_h_out)
 
     segr, seg, seg_halo, tail_seg = segments(seg_row, seg_prev, seg_tail)
     links = chunk_links(seg, seg_halo)
@@ -447,7 +254,7 @@
     dt = dt_in[...]
     c = c_in[...]
     ct = ct_in[...]
-    first = (k == 0).astype(F32)
+    first = jnp.where(k == 0, 1.0, 0.0)
     reach = dec_halo[7:8] * (1.0 - first) + first
     b = bc[:, :state_dim]
     cc = bc[:, state_dim:]
@@ -503,7 +310,7 @@
         ginner_out[:, sl] = grad.astype(BF16)
         edge_out[:, sl] = above
 
-        @pl.when(i == 0)
+        @pl.when(k == chunks - 1)
         def _():
             last_out[:, sl] = grad[length - 8 :]
 
@@ -518,7 +325,7 @@
         at = slice(width + half * state_dim, width + (half + 1) * state_dim)
         edge_out[:, at] = above
 
-        @pl.when(i == 0)
+        @pl.when(k == chunks - 1)
         def _():
             last_out[:, at] = grad[length - 8 :]
 
@@ -534,75 +341,7 @@
     par_h_out[1:2] += jnp.sum(dlog * (rate * dt), axis=0, keepdims=True)
 
 
-def run_backward(
-    both_ext, shared_ext, step_raw, seg, taps, taps_s, heads,
-    dy, x, bc, dt, c, ct, dec, enter, start, rowterm, dend, colsum,
-):
-    length, width = x.shape
-    scols = bc.shape[1]
-    chunks = length // SPAN
-    at = lambda i: chunks - 1 - i
-    row = lambda i: (at(i), 0)
-    halo = lambda col: (lambda i: (halo_index(at(i), chunks), col))
-    fixed = lambda i: (0, 0)
-    S = jax.ShapeDtypeStruct
-    return pl.pallas_call(
-        backward_kernel,
-        grid=(chunks,),
-        in_specs=[
-            pl.BlockSpec((SPAN, width), lambda i: (at(i), 1)),
-            pl.BlockSpec((HALO, width), halo(1)),
-            pl.BlockSpec((SPAN, scols), row),
-            pl.BlockSpec((HALO, scols), halo(0)),
-            pl.BlockSpec((SPAN, 128), row),
-            *seg_specs(at, chunks),
-            pl.BlockSpec(taps.shape, fixed),
-            pl.BlockSpec(taps_s.shape, fixed),
-            pl.BlockSpec(heads.shape, fixed),
-            pl.BlockSpec((SPAN, width), row),
-            pl.BlockSpec((SPAN, width), row),
-            pl.BlockSpec((SPAN, scols), row),
-            pl.BlockSpec((SPAN, 128), row),
-            pl.BlockSpec((SPAN, 128), row),
-            pl.BlockSpec((ct.shape[0], SPAN), lambda i: (0, at(i))),
-            pl.BlockSpec((8, 128), lambda i: (jnp.maximum(at(i) * (SPAN // 8) - 1, 0), 0)),
-            pl.BlockSpec((None, scols // 2, width), lambda i: (at(i), 0, 0)),
-            pl.BlockSpec(start.shape, fixed),
-            pl.BlockSpec((SPAN, 128), row),
-            pl.BlockSpec(dend.shape, fixed),
-            pl.BlockSpec(colsum.shape, fixed),
-        ],
-        out_specs=[
-            pl.BlockSpec((SPAN, width), row),
-            pl.BlockSpec((SPAN, scols + 128), row),
-            pl.BlockSpec((8, width), fixed),
-            pl.BlockSpec((8, scols), fixed),
-            pl.BlockSpec((8, 128), fixed),
-            pl.BlockSpec((8, width + scols), fixed),
-            pl.BlockSpec((8, width + scols), fixed),
-        ],
-        out_shape=[
-            S((length, width), BF16),
-            S((length, scols + 128), BF16),
-            S((8, width), F32),
-            S((8, scols), F32),
-            S((8, 128), F32),
-            S((8, width + scols), F32),
-            S((8, width + scols), F32),
-        ],
-        scratch_shapes=[
-            pltpu.VMEM((scols // 2, width), F32),
-            pltpu.VMEM((8, width), F32),
-            pltpu.VMEM((8, scols), F32),
-            pltpu.VMEM((8, 128), F32),
-            pltpu.VMEM((SPAN, scols), F32),
-        ],
-        name="scan_backward",
-    )(both_ext, both_ext, shared_ext, shared_ext, step_raw, seg, seg, seg, taps, taps_s, heads,
-      dy, x, bc, dt, c, ct, dec, enter, start, rowterm, dend, colsum)
-
-
-def spread_kernel(ggate, ginner, gsmall, w_in, w_small, normed, part_out, gain_out):
+def spread_body(ggate, ginner, gsmall, w_in, w_small, normed, part_out, gain_out):
     width = ggate.shape[1]
     part = nt(ggate[...], w_in[:, :width]) + nt(ginner[...], w_in[:, width:]) + nt(gsmall[...], w_small[...])
     part_out[...] = part.astype(BF16)
@@ -610,31 +349,7 @@
         jnp.sum(part * normed[...].astype(F32), axis=0, keepdims=True), gain_out.shape))
 
 
-def run_spread(ggate, ginner, gsmall, w_in, w_small, normed_ext):
-    length = ggate.shape[0]
-    model = w_in.shape[0]
-    tile = 256
-    fixed = lambda n: (0, 0)
-    down = lambda n: (n, 0)
-    across = lambda n: (0, n)
-    S = jax.ShapeDtypeStruct
-    return pl.pallas_call(
-        spread_kernel,
-        grid=(model // tile,),
-        in_specs=[
-            pl.BlockSpec(ggate.shape, fixed),
-            pl.BlockSpec(ginner.shape, fixed),
-            pl.BlockSpec(gsmall.shape, fixed),
-            pl.BlockSpec((tile, w_in.shape[1]), down),
-            pl.BlockSpec((tile, w_small.shape[1]), down),
-            pl.BlockSpec((length, tile), across),
-        ],
-        out_specs=[pl.BlockSpec((length, tile), across), pl.BlockSpec((8, tile), across)],
-        out_shape=[S((length, model), BF16), S((8, model), F32)],
-        name="spread_back",
-    )(ggate, ginner, gsmall, w_in, w_small, normed_ext)
-
-
+PIECES = 2
 MESH = pl.DeviceIdType.MESH
 ANY = pl.BlockSpec(memory_space=pl.ANY)
 
@@ -651,120 +366,203 @@
         pl.semaphore_signal(barrier, inc=1, device_id=to, device_id_type=MESH)
 
 
-PIECES = 2
-
-
-def gather_kernel(
-    ncol, ndp,
-    tokens_in, gain, seg_in, w0, w1, w2,
-    all_out, seg_out, w0_out, w1_out, w2_out,
-    z_send, z_recv, w_send, c_send, w_recv, t_send, t_recv, here, own, seg_own, zero_tail, no_seg,
-):
+def start(copies):
+    for copy in copies:
+        copy.start()
+
+
+def guarded(when, action):
+    @pl.when(when)
+    def _():
+        action()
+
+
+class LineGather:
+    def __init__(self, ncol, z, first, second, extra, sems):
+        self.ncol, self.z, self.last = ncol, z, ncol - 1
+        self.parts = (first, second)
+        self.extra = extra
+        self.sems = sems
+        self.tokens = second[1].shape[0] // ncol
+        self.part = self.tokens // PIECES
+
+    def copies(self, kind, s, way, pieces, mine=False):
+        source, dest = self.parts[kind]
+        send, recv = self.sems[2 * kind : 2 * kind + 2]
+        to = self.z + 1 if way == 0 else self.z - 1
+        made = []
+        for p in pieces:
+            at = pl.ds(pl.multiple_of(s * self.tokens + p * self.part, self.part), self.part)
+            src = source.at[pl.ds(p * self.part, self.part)] if mine and source is not None else dest.at[at]
+            made.append(remote(src, dest.at[at], send.at[way, s, p], recv.at[s, p], col=to))
+            if kind == 0 and p == PIECES - 1:
+                place = self.extra.at[pl.ds(pl.multiple_of(s * 8, 8), 8)]
+                made.append(remote(place, place, send.at[way, s, PIECES], recv.at[s, PIECES], col=to))
+        return made
+
+    def exit(self, way):
+        return self.z < self.last if way == 0 else self.z > 0
+
+    def depth(self, way):
+        return self.z if way == 0 else self.last - self.z
+
+    def begin(self):
+        every = range(PIECES)
+        for way in range(2):
+            guarded(self.exit(way), lambda way=way: start(self.copies(0, self.z, way, every, True)))
+        for way in range(2):
+            guarded(self.depth(way) == 0, lambda way=way: start(self.copies(1, self.z, way, every, True)))
+
+    ticks = property(lambda self: 2 * self.last * PIECES)
+
+    def tick(self, tau):
+        j, p = (tau - 1) // PIECES, (tau - 1) % PIECES
+        for way in range(2):
+            depth = self.depth(way)
+            sign = -1 if way == 0 else 1
+
+            def relay(kind, s, way=way, depth=depth):
+                for copy in self.copies(kind, s, way, (p,)):
+                    copy.wait_recv()
+                guarded(self.exit(way), lambda: start(self.copies(kind, s, way, (p,))))
+                if kind == 0 and p == PIECES - 1:
+                    guarded(self.exit(way) & (j == depth - 1),
+                            lambda: start(self.copies(1, self.z, way, range(PIECES), True)))
+
+            guarded(j < depth, lambda s=self.z + sign * (j + 1), relay=relay: relay(0, s))
+            guarded((j >= depth) & (j < 2 * depth),
+                    lambda s=self.z + sign * (j - depth + 1), relay=relay: relay(1, s))
+
+    def drain(self):
+        for kind in range(2):
+            for way in range(2):
+                sign = -1 if way == 0 else 1
+                for s in range(self.ncol):
+
+                    def wait(kind=kind, way=way, s=s, sign=sign):
+                        for copy in self.copies(kind, self.z + sign * s, way, range(PIECES)):
+                            copy.wait_send()
+
+                    guarded(self.exit(way) & (s <= self.depth(way)), wait)
+
+
+def mixer_kernel(ncol, ndp, full_width, *refs):
+    refs = list(refs)
+
+    def take(number):
+        taken = refs[:number]
+        del refs[:number]
+        return taken
+
+    tokens_in, gain, seg_in, ci, cib, gg, cs, csb, sb, rl, sg = take(11)
+    w0, w1, w2, cot_in = take(4)
+    normed_hbm, gsmall_hbm, ggate_hbm, cot_hbm, gnorm_hbm, ginner_hbm, part_hbm = take(7)
+    par, par_s, par_h, gain_out, total_out = take(5)
+    normed, seg, w_in, w_small, out_t, cot = take(6)
+    taps, taps_s, heads = take(3)
+    both, shared, step = take(3)
+    ssd, x, bc, dt, c, ct, dec, enter, state, start_state, total = take(11)
+    gated, gnorm, projected, back, dy, ggate, rowterm, dstart, dend = take(9)
+    ginner, gsmall, part, edge, edge_in, last_rows = take(6)
+    dstate, carry, carry_s, carry_links, grads_bc = take(5)
+    squares, squares_all, inner, inner_all, slots = take(5)
+    line_box, line_send, line_recv = take(3)
+    xs_send, xs_recv, cs_send, cs_recv, w_send, c_send, w_recv, t_send, t_recv = take(9)
+    sum_send, sum_recv, row_send, row_recv, here = take(5)
+
     dp, row, z = lax.axis_index("dp"), lax.axis_index("row"), lax.axis_index("col")
     other = 1 - row
     last = ncol - 1
-    tokens, tail, part = own.shape[0], zero_tail.shape[0], own.shape[0] // PIECES
-    weights = ((w0, w0_out), (w1, w1_out), (w2, w2_out))
+    tokens = tokens_in.shape[0]
+    tail = HALO
+    length = ncol * tokens
+    width = taps.shape[1]
+    scols = taps_s.shape[1]
+    state_dim = scols // 2
+    chunks = length // SPAN
     rows = w0.shape[0]
+    me = dp * 2 + row
     sends_tail = (row == 0) & (z == last)
 
     barrier = pltpu.get_barrier_semaphore()
-    greet(barrier, z > 0, col=z - 1)
-    greet(barrier, z < last, col=z + 1)
+    for s in range(1, ncol):
+        greet(barrier, row >= 0, col=lax.rem(z + s, ncol))
     greet(barrier, row >= 0, row=other)
     for m in range(1, ndp):
         greet(barrier, row >= 0, dp=dp ^ m)
     greet(barrier, row == 1, row=0, col=last)
-    for c in range(ncol):
-        greet(barrier, sends_tail, row=1, col=c)
-    count = (z > 0).astype(jnp.int32) + (z < last).astype(jnp.int32) + ndp
-    count = count + row + jnp.where(sends_tail, ncol, 0)
-    seg_own[...] = jnp.broadcast_to(seg_in[...], seg_own.shape)
-    no_seg[...] = jnp.full(no_seg.shape, -1, jnp.int32)
-    zero_tail[...] = jnp.zeros_like(zero_tail)
-
-    def normalize(step, carry):
-        at = pl.ds(pl.multiple_of(step * 32, 32), 32)
-        wide = tokens_in[at].astype(F32)
+    for s in range(ncol):
+        greet(barrier, sends_tail, row=1, col=s)
+
+    seg[pl.ds(pl.multiple_of(z * 8, 8), 8)] = jnp.broadcast_to(seg_in[...], (8, tokens))
+    base = pl.multiple_of(z * tokens, 32)
+
+    def normalize(n, carried):
+        at = pl.multiple_of(n * 32, 32)
+        wide = tokens_in[pl.ds(at, 32)].astype(F32)
         scale = lax.rsqrt(jnp.sum(wide * wide, axis=1, keepdims=True) / wide.shape[1] + EPS)
-        own[at] = (wide * scale * gain[...]).astype(BF16)
-        return carry
+        normed[pl.ds(pl.multiple_of(base + at, 32), 32)] = (wide * scale * gain[...]).astype(BF16)
+        return carried
 
     lax.fori_loop(0, tokens // 32, normalize, 0)
+
+    @pl.when(row == 0)
+    def _():
+        seg[pl.ds(ncol * 8, 8)] = jnp.full((8, tokens), -1, jnp.int32)
+        normed[pl.ds(length, tail)] = jnp.zeros((tail, normed.shape[1]), BF16)
+        start_state[...] = jnp.zeros_like(start_state)
+
+    @pl.when(row == 1)
+    def _():
+        dend[...] = jnp.zeros_like(dend)
+        edge_in[...] = jnp.zeros_like(edge_in)
+
+    taps[0:4] = ci[...]
+    taps[4:5] = cib[...]
+    taps[5:6] = gg[...]
+    lo1 = iota((1, 128), 1) < 64
+    for p in range(width // 128):
+        taps[6:7, p * 128 : (p + 1) * 128] = pick(lo1, sg, 2 * p)
+    taps_s[0:4] = cs[...]
+    taps_s[4:5] = csb[...]
+    heads[...] = jnp.zeros_like(heads)
+    heads[0:1, : sb.shape[1]] = sb[...]
+    heads[1:2, : rl.shape[1]] = rl[...]
+    for ref in (state, total, dstart, carry, carry_s, carry_links, par, par_s, par_h):
+        ref[...] = jnp.zeros_like(ref)
+
+    count = ncol - 1 + ndp + row + jnp.where(sends_tail, ncol, 0)
     pl.semaphore_wait(barrier, count)
 
-    def token_copies(s, mine, way, which=None):
-        target = z + 1 if way == 0 else z - 1
-        copies = []
-        for i in range(PIECES + 1) if which is None else which:
-            if i < PIECES:
-                dst = all_out.at[pl.ds(s * tokens + i * part, part)]
-                src = own.at[pl.ds(i * part, part)] if mine else dst
-            else:
-                dst = seg_out.at[pl.ds(s * 8, 8)]
-                src = seg_own if mine else dst
-            copies.append(remote(src, dst, z_send.at[way, s, i], z_recv.at[s, i], col=target))
-        return copies
+    weights = ((w0, w_in), (w1, w_small), (w2, out_t))
 
     def weight_copies(j, mine, send, **to):
         copies = []
         for i, (src, dst) in enumerate(weights):
-            place = dst.at[pl.ds(j * rows, rows)]
+            place = dst.at[pl.ds(pl.multiple_of(j * rows, 16), rows)]
             copies.append(remote(src if mine else place, place, send.at[i], w_recv.at[j, i], **to))
         return copies
 
-    def tail_copies(c):
+    def tail_copies(s):
+        place = seg.at[pl.ds(pl.multiple_of(z * 8, 8), 8)]
+        end = pl.multiple_of(z * tokens + tokens - tail, 16)
         return [
-            remote(own.at[pl.ds(tokens - tail, tail)], all_out.at[pl.ds(ncol * tokens, tail)],
-                   t_send.at[c, 0], t_recv.at[0], row=1, col=c),
-            remote(seg_own, seg_out.at[pl.ds(ncol * 8, 8)], t_send.at[c, 1], t_recv.at[1], row=1, col=c),
+            remote(normed.at[pl.ds(end, tail)], normed.at[pl.ds(length, tail)],
+                   t_send.at[s, 0], t_recv.at[0], row=1, col=s),
+            remote(place, seg.at[pl.ds(ncol * 8, 8)], t_send.at[s, 1], t_recv.at[1], row=1, col=s),
         ]
 
-    def start(copies):
-        for copy in copies:
-            copy.start()
-
-    def guarded(when, action):
-        @pl.when(when)
-        def _():
-            action()
-
-    me = dp * 2 + row
-    guarded(z < last, lambda: start(token_copies(z, True, 0)))
-    guarded(z > 0, lambda: start(token_copies(z, True, 1)))
+    for s in range(ncol):
+        guarded(sends_tail, lambda s=s: start(tail_copies(s)))
+    gather = LineGather(ncol, z, (None, normed), (cot_in, cot), seg, (xs_send, xs_recv, cs_send, cs_recv))
+    gather.begin()
     for m in range(1, ndp):
         start(weight_copies(me, True, w_send.at[m], dp=dp ^ m))
     start(weight_copies(me, True, c_send.at[0], row=other))
-    for c in range(ncol):
-        guarded(sends_tail, lambda c=c: start(tail_copies(c)))
-    local = [
-        pltpu.make_async_copy(own, all_out.at[pl.ds(z * tokens, tokens)], here.at[0]),
-        pltpu.make_async_copy(seg_own, seg_out.at[pl.ds(z * 8, 8)], here.at[1]),
-    ]
+    local = [pltpu.make_async_copy(cot_in, cot.at[pl.ds(base, tokens)], here.at[0])]
     for i, (src, dst) in enumerate(weights):
-        local.append(pltpu.make_async_copy(src, dst.at[pl.ds(me * rows, rows)], here.at[2 + i]))
+        local.append(pltpu.make_async_copy(src, dst.at[pl.ds(pl.multiple_of(me * rows, 16), rows)], here.at[1 + i]))
     start(local)
-    fill = [
-        pltpu.make_async_copy(zero_tail, all_out.at[pl.ds(ncol * tokens, tail)], here.at[5]),
-        pltpu.make_async_copy(no_seg, seg_out.at[pl.ds(ncol * 8, 8)], here.at[6]),
-    ]
-    guarded(row == 0, lambda: start(fill))
-
-    def pass_tokens(s):
-        for which in [(i,) for i in range(PIECES - 1)] + [(PIECES - 1, PIECES)]:
-
-            def from_below(which=which):
-                for copy in token_copies(z - s, False, 0, which):
-                    copy.wait_recv()
-                guarded(z < last, lambda: start(token_copies(z - s, False, 0, which)))
-
-            def from_above(which=which):
-                for copy in token_copies(z + s, False, 1, which):
-                    copy.wait_recv()
-                guarded(z > 0, lambda: start(token_copies(z + s, False, 1, which)))
-
-            guarded(z - s >= 0, from_below)
-            guarded(z + s <= last, from_above)
 
     def pass_weights(m):
         j = (dp ^ m) * 2 + row
@@ -772,18 +570,204 @@
             copy.wait_recv()
         start(weight_copies(j, False, c_send.at[m], row=other))
 
-    done = 0
-    for s in range(1, ncol):
-        pass_tokens(s)
-        upto = (ndp - 1) * s // (ncol - 2) if s < ncol - 1 else ndp - 1
-        for m in range(done + 1, upto + 1):
+    half = gather.ticks // 2
+    due = {tau: [] for tau in range(1, half + 1)}
+    for m in range(1, ndp):
+        due[min(half - 1, 2 + (3 * (m - 1)) // (ndp - 1) * (half - 3) // 2)].append(m)
+    for tau in range(1, half):
+        gather.tick(tau)
+        for m in due[tau]:
             pass_weights(m)
-        done = max(done, upto)
     for m in range(ndp):
-        j = (dp ^ m) * 2 + other
-        for copy in weight_copies(j, False, c_send.at[m], row=other):
+        for copy in weight_copies((dp ^ m) * 2 + other, False, c_send.at[m], row=other):
             copy.wait_recv()
     guarded(row == 1, lambda: [copy.wait_recv() for copy in tail_copies(0)])
+    for copy in local:
+        copy.wait()
+
+    def nth(n):
+        return pl.multiple_of(jnp.where(z * 2 < ncol, n, last - n) * tokens, tokens)
+
+    def put(at, size, value, small):
+        both[pl.ds(at, size)] = value.astype(BF16)
+        shared[pl.ds(at, size)] = small[:, :scols].astype(BF16)
+        step[pl.ds(at, size)] = small[:, scols:]
+
+    def project_tokens(n, with_tail):
+        at = nth(n)
+        lhs = normed[pl.ds(at, tokens)]
+        if with_tail:
+            lhs = jnp.concatenate([lhs, normed[pl.ds(length, tail)]], axis=0)
+        value, small = nn(lhs, w_in[...]), nn(lhs, w_small[...])
+        put(at, tokens, value[:tokens], small[:tokens])
+        if with_tail:
+            put(length, tail, value[tokens:], small[tokens:])
+
+    for n in range(ncol - 1):
+        project_tokens(n, n == 0)
+    gather.tick(half)
+    project_tokens(ncol - 1, False)
+    outs = [pltpu.make_async_copy(normed, normed_hbm, here.at[4])]
+    outs[0].start()
+
+    def at_rows(k):
+        return pl.ds(pl.multiple_of(k * SPAN, SPAN), SPAN)
+
+    def common(k):
+        this = at_rows(k)
+        above = pl.ds(pl.multiple_of(jnp.where(k == 0, length, k * SPAN - HALO), HALO), HALO)
+        prev = pl.ds(pl.multiple_of(jnp.where(k == 0, chunks, k - 1) * 8, 8), 8)
+        side = pl.ds(width, width)
+        return (
+            both.at[this, side], both.at[above, side], shared.at[this], shared.at[above], step.at[this],
+            seg.at[pl.ds(pl.multiple_of(k * 8, 8), 8)], seg.at[prev], seg.at[pl.ds(chunks * 8, 8)], taps, taps_s, heads,
+        )
+
+    later = list(range(half + 1, gather.ticks + 1))
+
+    def forward(k, carried):
+        this = at_rows(k)
+        forward_body(*common(k), ssd.at[this], x.at[this], bc.at[this], dt.at[this], c.at[this],
+                     ct.at[:, this], dec.at[this], enter.at[k], state, total)
+        guarded(k == chunks // 2, lambda: gather.tick(half + 1))
+        return carried
+
+    lax.fori_loop(0, chunks, forward, 0)
+    later.pop(0)
+
+    def row_copy(n, src, dst):
+        return remote(src, dst, row_send.at[n], row_recv.at[n], row=other)
+
+    guarded(row == 0, lambda: row_copy(0, state, start_state).start())
+    gather.tick(later.pop(0))
+    guarded(row == 1, lambda: row_copy(0, state, start_state).wait_recv())
+
+    def gating(k, carried):
+        this = at_rows(k)
+        gate_body(ssd.at[this], x.at[this], bc.at[this], dec.at[this], start_state, both.at[this, pl.ds(0, width)],
+                  taps, ssd.at[this], gated.at[this], squares.at[:, this])
+        return carried
+
+    lax.fori_loop(0, chunks, gating, 0)
+
+    def sum_copy(n, value, s, source):
+        return remote(value, slots.at[n, source], sum_send.at[n, s], sum_recv.at[n, source],
+                      col=lax.rem(z + s, ncol))
+
+    def sum_begin(n, value):
+        for s in range(1, ncol):
+            sum_copy(n, value, s, z).start()
+
+    def sum_end(n, value, out):
+        result = value[...]
+        for s in range(1, ncol):
+            source = lax.rem(z + s, ncol)
+            sum_copy(n, value, s, source).wait_recv()
+            result = result + slots[n, source]
+        out[...] = result
+
+    sum_begin(0, squares)
+    gather.tick(later.pop(0))
+    sum_end(0, squares, squares_all)
+
+    def projecting(k, carried):
+        this = at_rows(k)
+        project_body(full_width, gated.at[this], squares_all.at[:, this], taps, out_t, gnorm.at[this], projected.at[this])
+        return carried
+
+    lax.fori_loop(0, chunks, projecting, 0)
+    line = LineReduce(ncol, z, projected, projected, line_box, line_send, line_recv)
+    while len(later) > 2:
+        gather.tick(later.pop(0))
+
+    def pulling(n):
+        this = pl.ds(nth(n), tokens)
+        pull_body(cot.at[this], out_t, gated.at[this], taps, back.at[this], inner.at[:, this])
+
+    for n in range(ncol - 1):
+        pulling(n)
+        if n == 0:
+            gather.tick(later.pop(0))
+    gather.tick(later.pop(0))
+    ticks = list(range(1, line.ticks + 1))
+    pulling(ncol - 1)
+    outs.append(pltpu.make_async_copy(cot, cot_hbm, here.at[5]))
+    outs.append(pltpu.make_async_copy(gnorm, gnorm_hbm, here.at[6]))
+    start(outs[1:])
+    sum_begin(1, inner)
+    sum_end(1, inner, inner_all)
+    line.start()
+
+    def pull_gate(k, carried):
+        this = at_rows(k)
+        back_body(full_width, ssd.at[this], x.at[this], bc.at[this], dec.at[this], both.at[this, pl.ds(0, width)],
+                  back.at[this], squares_all.at[:, this], inner_all.at[:, this], taps,
+                  dy.at[this], ggate.at[this], rowterm.at[this], par, dstart)
+        return carried
+
+    lax.fori_loop(0, chunks, pull_gate, 0)
+    guarded(row == 1, lambda: row_copy(1, dstart, dend).start())
+    outs.append(pltpu.make_async_copy(ggate, ggate_hbm, here.at[7]))
+    outs[-1].start()
+    line.tick(ticks.pop(0))
+    guarded(row == 0, lambda: row_copy(1, dstart, dend).wait_recv())
+    dstate[...] = dend[...]
+
+    spaced = {n: [tau] for n, tau in enumerate(ticks[:chunks])}
+    ticks = ticks[chunks:]
+
+    def backward(n, carried):
+        k = chunks - 1 - n
+        this = at_rows(k)
+        before = pl.ds(pl.multiple_of(jnp.maximum(k * SPAN - 8, 0), 8), 8)
+        backward_body(k, chunks, *common(k), dy.at[this], x.at[this], bc.at[this], dt.at[this], c.at[this],
+                      ct.at[:, this], dec.at[before], enter.at[k], start_state, rowterm.at[this],
+                      ginner.at[this], gsmall.at[this], par, par_s, par_h, edge, last_rows,
+                      dstate, carry, carry_s, carry_links, grads_bc)
+        for turn, taus in spaced.items():
+            if turn < chunks - 1:
+                for tau in taus:
+                    guarded(n == turn, lambda tau=tau: line.tick(tau))
+        return carried
+
+    lax.fori_loop(0, chunks, backward, 0)
+    guarded(row == 1, lambda: row_copy(2, edge, edge_in).start())
+    for tau in spaced.get(chunks - 1, []):
+        line.tick(tau)
+    guarded(row == 0, lambda: row_copy(2, edge, edge_in).wait_recv())
+    fixed = (last_rows[...] + edge_in[...]).astype(BF16)
+    ginner[length - 8 :] = fixed[:, :width]
+    gsmall[length - 8 :, : fixed.shape[1] - width] = fixed[:, width:]
+    outs.append(pltpu.make_async_copy(ginner, ginner_hbm, here.at[8]))
+    outs.append(pltpu.make_async_copy(gsmall, gsmall_hbm, here.at[9]))
+    start(outs[-2:])
+
+    tile = 256
+    tiles = part.shape[1] // tile
+
+    def part_copy(n):
+        at = pl.ds(pl.multiple_of(n * tile, tile), tile)
+        return pltpu.make_async_copy(part.at[:, at], part_hbm.at[:, at], here.at[10 + n])
+
+    def spreading(n, carried):
+        at = pl.ds(pl.multiple_of(n * tile, tile), tile)
+        spread_body(ggate, ginner, gsmall, w_in.at[at], w_small.at[at], normed.at[pl.ds(0, length), at],
+                    part.at[:, at], gain_out.at[:, at])
+        guarded(n > 0, lambda: part_copy(jnp.maximum(n - 1, 0)).start())
+        for tau in ticks:
+            guarded(n == tiles // 2, lambda tau=tau: line.tick(tau))
+        return carried
+
+    lax.fori_loop(0, tiles, spreading, 0)
+    part_copy(tiles - 1).start()
+
+    def keep(at, value):
+        total_out[pl.ds(pl.multiple_of(at, 16), 16)] = value.astype(BF16)
+
+    line.total(keep)
+
+    gather.drain()
+    line.drain()
     for m in range(ndp):
         if m:
             for copy in weight_copies(me, True, w_send.at[m], dp=dp ^ m):
@@ -791,86 +775,68 @@
         for copy in weight_copies((dp ^ m) * 2 + row, m == 0, c_send.at[m], row=other):
             copy.wait_send()
     for s in range(ncol):
-        for way in range(2):
-            open_way = z < last if way == 0 else z > 0
-            mine = (z - s >= 0) if way == 0 else (z + s <= last)
-            src = z - s if way == 0 else z + s
-
-            def drain(way=way, src=src, s=s):
-                for copy in token_copies(src, s == 0, way):
-                    copy.wait_send()
-
-            guarded(open_way & mine, drain)
-    for c in range(ncol):
-        guarded(sends_tail, lambda c=c: [copy.wait_send() for copy in tail_copies(c)])
-    for copy in local:
+        guarded(sends_tail, lambda s=s: [copy.wait_send() for copy in tail_copies(s)])
+    for n, value in ((0, squares), (1, inner)):
+        for s in range(1, ncol):
+            sum_copy(n, value, s, z).wait_send()
+    guarded(row == 0, lambda: row_copy(0, state, start_state).wait_send())
+    guarded(row == 1, lambda: row_copy(1, dstart, dend).wait_send())
+    guarded(row == 1, lambda: row_copy(2, edge, edge_in).wait_send())
+    for copy in outs:
         copy.wait()
-    guarded(row == 0, lambda: [copy.wait() for copy in fill])
-
-
-def gather_inputs(tokens_in, gain, seg, w0, w1, w2):
+    for n in range(tiles):
+        part_copy(n).wait()
+
+
+def run_mixer(full_width, tokens_in, gain, seg, ci, cib, gg, cs, csb, sb, rl, sg, w0, w1, w2, cot):
     ncol, ndp = lax.axis_size("col"), lax.axis_size("dp")
-    tokens, width = tokens_in.shape
+    tokens, model = tokens_in.shape
+    width, scols = ci.shape[1], cs.shape[1]
+    length = ncol * tokens
+    chunks = length // SPAN
+    state_dim = scols // 2
+    small = w1.shape[1]
+    shards = 2 * ndp
     S = jax.ShapeDtypeStruct
-    shards = 2 * ndp
+    V = pltpu.VMEM
     dma = pltpu.SemaphoreType.DMA
-    vmem = pl.BlockSpec(memory_space=pltpu.VMEM)
+    vmem = pl.BlockSpec(memory_space=V)
     return pl.pallas_call(
-        functools.partial(gather_kernel, ncol, ndp),
-        in_specs=[vmem] * 3 + [ANY] * 3,
-        out_specs=[ANY] * 5,
+        functools.partial(mixer_kernel, ncol, ndp, full_width),
+        in_specs=[vmem] * 11 + [ANY] * 4,
+        out_specs=[ANY] * 7 + [vmem] * 5,
         out_shape=[
-            S((ncol * tokens + HALO, width), BF16),
-            S(((ncol + 1) * 8, tokens), jnp.int32),
-        ] + [S((shards * w.shape[0], w.shape[1]), w.dtype) for w in (w0, w1, w2)],
+            S((length + HALO, model), BF16), S((length, small), BF16), S((length, width), BF16), S((length, model), BF16),
+            S((length, width), BF16), S((length, width), BF16), S((length, model), BF16),
+            S((8, width), F32), S((8, scols), F32), S((8, 128), F32), S((8, model), F32), S((tokens, model), BF16),
+        ],
         scratch_shapes=[
-            dma((2, ncol, PIECES + 1)), dma((ncol, PIECES + 1)), dma((ndp, 3)), dma((ndp, 3)), dma((shards, 3)),
-            dma((ncol, 2)), dma((2,)), dma((7,)),
-            pltpu.VMEM((tokens, width), BF16), pltpu.VMEM((8, tokens), jnp.int32),
-            pltpu.VMEM((HALO, width), BF16), pltpu.VMEM((8, tokens), jnp.int32),
+            V((length + HALO, model), BF16), V(((ncol + 1) * 8, tokens), jnp.int32), V((model, 2 * width), BF16),
+            V((model, small), BF16), V((model, width), BF16), V((length, model), BF16),
+            V((8, width), F32), V((8, scols), F32), V((8, 128), F32),
+            V((length + HALO, 2 * width), BF16), V((length + HALO, scols), BF16), V((length + HALO, 128), F32),
+            V((length, width), F32), V((length, width), BF16), V((length, scols), BF16), V((length, 128), F32),
+            V((length, 128), F32), V((16, length), F32), V((length, 128), F32), V((chunks, state_dim, width), BF16),
+            V((state_dim, width), F32), V((state_dim, width), F32), V((8, 128), F32),
+            V((length, width), BF16), V((length, width), BF16), V((length, model), BF16), V((length, width), BF16),
+            V((length, width), BF16), V((length, width), BF16), V((length, 128), F32), V((state_dim, width), F32),
+            V((state_dim, width), F32),
+            V((length, width), BF16), V((length, small), BF16), V((length, model), BF16),
+            V((8, width + scols), F32), V((8, width + scols), F32), V((8, width + scols), F32),
+            V((state_dim, width), F32), V((8, width), F32), V((8, scols), F32), V((8, 128), F32), V((SPAN, scols), F32),
+            V((8, length), F32), V((8, length), F32), V((8, length), F32), V((8, length), F32),
+            V((2, ncol, 8, length), F32),
+            *line_scratch(ncol, tokens, model),
+            dma((2, ncol, PIECES + 1)), dma((ncol, PIECES + 1)), dma((2, ncol, PIECES)), dma((ncol, PIECES)),
+            dma((ndp, 3)), dma((ndp, 3)), dma((shards, 3)), dma((ncol, 2)), dma((2,)),
+            dma((2, ncol)), dma((2, ncol)), dma((3,)), dma((3,)), dma((10 + model // 256,)),
         ],
-        compiler_params=pltpu.CompilerParams(collective_id=1, has_side_effects=True),
-        cost_estimate=pl.CostEstimate(flops=0, bytes_accessed=200_000_000, transcendentals=0),
-        name="gather_inputs",
-    )(tokens_in, gain[None], seg[None], w0, w1, w2)
-
-
-def sum_col_kernel(ncol, value, out, slots, send, recv):
-    z = lax.axis_index("col")
-    barrier = pltpu.get_barrier_semaphore()
-    for s in range(1, ncol):
-        pl.semaphore_signal(barrier, inc=1, device_id={"col": lax.rem(z + s, ncol)}, device_id_type=MESH)
-    pl.semaphore_wait(barrier, ncol - 1)
-    copies = [
-        remote(value, slots.at[z], send.at[s], recv.at[z], col=lax.rem(z + s, ncol)) for s in range(1, ncol)
-    ]
-    for copy in copies:
-        copy.start()
-    total = value[...]
-    for s in range(1, ncol):
-        source = lax.rem(z + s, ncol)
-        remote(value, slots.at[source], send.at[s], recv.at[source], col=source).wait_recv()
-        total = total + slots[source]
-    out[...] = total
-    for copy in copies:
-        copy.wait_send()
-
-
-def sum_col(value, collective_id):
-    ncol = lax.axis_size("col")
-    dma = pltpu.SemaphoreType.DMA
-    vmem = pl.BlockSpec(memory_space=pltpu.VMEM)
-    return pl.pallas_call(
-        functools.partial(sum_col_kernel, ncol),
-        in_specs=[vmem],
-        out_specs=vmem,
-        out_shape=jax.ShapeDtypeStruct(value.shape, F32),
-        scratch_shapes=[pltpu.VMEM((ncol,) + value.shape, F32), dma((ncol,)), dma((ncol,))],
-        compiler_params=pltpu.CompilerParams(collective_id=collective_id, has_side_effects=True),
-        name="sum_col",
-    )(value)
-
-
+        compiler_params=pltpu.CompilerParams(
+            collective_id=1, has_side_effects=True, vmem_limit_bytes=63 * 1024 * 1024
+        ),
+        cost_estimate=pl.CostEstimate(flops=0, bytes_accessed=500_000_000, transcendentals=0),
+        name="mixer",
+    )(tokens_in, gain[None], seg[None], ci, cib[None], gg[None], cs, csb[None], sb[None], rl[None], sg[None], w0, w1, w2, cot)
 class LineReduce:
     def __init__(self, ncol, z, source, local, inbox, send, recv):
         self.ncol, self.z, self.last = ncol, z, ncol - 1
@@ -1271,8 +1237,8 @@
 
 
 def finish_kernel(
-    nheads, small, gate, inner, out, par, par_h, par_s, gain_sum, gain, tokens, cot, gnormed,
-    zx_out, bc_out, dt_out, out_out, ci_out, cib_out, cs_out, csb_out, sb_out, rl_out, sg_out, gg_out, ng_out, gin_out,
+    nheads, small, gate, inner, out, par, par_h, par_s, gain_sum, gain, tokens, cot, gnormed, projected,
+    zx_out, bc_out, dt_out, out_out, ci_out, cib_out, cs_out, csb_out, sb_out, rl_out, sg_out, gg_out, ng_out, gin_out, block_out,
 ):
     width = par.shape[1]
     scols = par_s.shape[1]
@@ -1302,12 +1268,13 @@
         mean = jnp.sum(pushed * wide, axis=1, keepdims=True) / wide.shape[1]
         grad = scale * pushed - wide * (scale * scale * scale * mean)
         gin_out[at] = (cot[at].astype(F32) + grad).astype(BF16)
+        block_out[at] = (wide + projected[at].astype(F32)).astype(BF16)
         return carry
 
     lax.fori_loop(0, tokens.shape[0] // 32, rows, 0)
 
 
-def run_finish(nheads, small, gate, inner, out, par, par_h, par_s, gain_sum, gain, tokens, cot, gnormed):
+def run_finish(nheads, small, gate, inner, out, par, par_h, par_s, gain_sum, gain, tokens, cot, gnormed, projected):
     rows, width = gate.shape
     scols = par_s.shape[1]
     model = gain.shape[0]
@@ -1318,20 +1285,9 @@
     ]
     return pl.pallas_call(
         functools.partial(finish_kernel, nheads),
-        out_shape=[S(shape, F32) for shape in shapes] + [S(tokens.shape, BF16)],
+        out_shape=[S(shape, F32) for shape in shapes] + [S(tokens.shape, BF16)] * 2,
         name="finish",
-    )(small, gate, inner, out, par, par_h, par_s, gain_sum, gain[None], tokens, cot, gnormed)
-
-
-def pass_on(value, axis, by):
-    count = lax.axis_size(axis)
-    pairs = [(i, i + by) for i in range(count) if 0 <= i + by < count]
-    return lax.ppermute(value, axis, pairs)
-
-
-def pack_rows(rows, width):
-    used = sum(r.shape[0] for r in rows)
-    return jnp.concatenate(rows + [jnp.zeros((8 - used, width), F32)], axis=0)
+    )(small, gate, inner, out, par, par_h, par_s, gain_sum, gain[None], tokens, cot, gnormed, projected)
 
 
 def per_device(
@@ -1341,57 +1297,17 @@
     width = proj_zx.shape[2]
     scols = proj_bc.shape[1]
     nheads = proj_dt.shape[1]
-    head_dim = width // nheads
     full_width = float(width * lax.axis_size("col"))
-    fill = (0, 128 - nheads)
-    small_own = jnp.concatenate([proj_bc, jnp.pad(proj_dt, ((0, 0), fill))], axis=1)
-    normed_ext, seg, w_in, w_small, out_t = gather_inputs(
-        block_input, norm_gain, segment_ids, proj_zx.reshape(-1, 2 * width), small_own, proj_out.T
+    small_own = jnp.concatenate([proj_bc, jnp.pad(proj_dt, ((0, 0), (0, 128 - nheads)))], axis=1)
+    (normed, gsmall, ggate, cot_all, gated_normed, ginner, part, par, par_s, par_h, gain_part, projected) = run_mixer(
+        full_width, block_input, norm_gain, segment_ids, conv_inner, conv_inner_bias, gated_gain, conv_shared,
+        conv_shared_bias, step_bias, rate_log, skip_gain, proj_zx.reshape(-1, 2 * width), small_own, proj_out.T, cotangent,
     )
-    length = normed_ext.shape[0] - HALO
-    (cot, normed_ext, conv_inner, conv_inner_bias, conv_shared, conv_shared_bias, step_bias, rate_log, skip_gain,
-     gated_gain) = lax.optimization_barrier((
-        cotangent, normed_ext, conv_inner, conv_inner_bias, conv_shared, conv_shared_bias, step_bias, rate_log,
-        skip_gain, gated_gain))
-    cot_all = lax.all_gather(cot, "col", axis=0, tiled=True)
-    taps = pack_rows(
-        [conv_inner, conv_inner_bias[None], gated_gain[None], jnp.repeat(skip_gain, head_dim)[None]], width
+    gsm, gz, gout, gx, par, par_h, par_s, gain_sum, grad_normed = reduce_grads(
+        (normed, gsmall, ggate, cot_all, gated_normed, ginner, part), (par, par_h, par_s, gain_part), scols
     )
-    taps_s = pack_rows([conv_shared, conv_shared_bias[None]], scols)
-    heads = pack_rows([jnp.pad(step_bias, fill)[None], jnp.pad(rate_log, fill)[None]], 128)
-
-    both_ext = nn(normed_ext, w_in).astype(BF16)
-    small_ext = nn(normed_ext, w_small)
-    shared_ext = small_ext[:, :scols].astype(BF16)
-    step_ext = small_ext[:, scols:]
-    common = (both_ext, shared_ext, step_ext, seg, taps, taps_s, heads)
-    y, x, bc, dt, c, ct, dec, enter, final = run_forward(*common)
-    start = pass_on(final, "row", 1)
-    ssd, gated, squares = run_gate(y, x, bc, dec, start, both_ext, taps)
-    squares = sum_col(squares, 3)
-    gated_normed, projected = run_project(full_width, gated, squares, taps, out_t)
-    cot_all, projected = lax.optimization_barrier((cot_all, projected))
-    projected = lax.psum_scatter(projected, "col", scatter_dimension=0, tiled=True)
-    block_output = (block_input.astype(F32) + projected.astype(F32)).astype(BF16)
-    back, inner = run_pull(cot_all, out_t, gated, taps)
-    inner = sum_col(inner, 4)
-    dy, ggate, rowterm, colsum, dstart = run_back(
-        full_width, ssd, x, bc, dec, both_ext, back, squares, inner, taps
-    )
-    dend = pass_on(dstart, "row", -1)
-    ginner, gsmall, par, par_s, par_h, edge, last = run_backward(
-        *common, dy, x, bc, dt, c, ct, dec, enter, start, rowterm, dend, colsum
-    )
-    edge = pass_on(edge, "row", -1)
-    fixed = (last + edge).astype(BF16)
-    ginner = lax.dynamic_update_slice(ginner, fixed[:, :width], (length - 8, 0))
-    gsmall = lax.dynamic_update_slice(gsmall, fixed[:, width:], (length - 8, 0))
-    part, gain_part = run_spread(ggate, ginner, gsmall, w_in, w_small, normed_ext)
-    gsm, gz, gout, gx, par, par_h, par_s, gain_sum, grad_normed = reduce_grads(
-        (normed_ext, gsmall, ggate, cot_all, gated_normed, ginner, part), (par, par_h, par_s, gain_part), scols
-    )
-    zx, gbc, gdt, gout, ci, cib, cs, csb, sb, rl, sg, gg, ng, grad_input = run_finish(
-        nheads, gsm, gz, gx, gout, par, par_h, par_s, gain_sum, norm_gain, block_input, cotangent, grad_normed
+    zx, gbc, gdt, gout, ci, cib, cs, csb, sb, rl, sg, gg, ng, grad_input, block_output = run_finish(
+        nheads, gsm, gz, gx, gout, par, par_h, par_s, gain_sum, norm_gain, block_input, cotangent, grad_normed, projected
     )
     return (
         block_output, grad_input, ng[0], zx, gbc, gdt.T, ci, cib[0], cs, csb[0], sb[0], rl[0], sg[0], gg[0], gout.T,

time: 304 us -> 269 us (0.88)
  Pallas kernels: 239 us -> 256 us
  between operations: 14.3 us -> 0.67 us
  matrix products: 13 us -> 0 us
  waiting for transfers between devices: 13 us -> 0 us
  starting transfers between devices: 4.52 us -> 0 us
  other arithmetic: 9.74 us -> 5.44 us
    pallas_call x10 -> x1, Pallas kernels: 165 us -> 184 us  [run_mixer(): pl.pallas_call(functools.partial(mixer_kernel, ncol, ndp, full_width), in...]
    dot_general x2 -> x0, matrix products: 13 us -> none  [nn(): lax.dot_general(a, b, (((1,), (0,)), ((), ())), preferred_element_type=F32)]
    all_gather x1 -> x0, waiting for transfers between devices: 7.13 us -> none  [per_device(): cot_all = lax.all_gather(cot, 'col', axis=0, tiled=True)]
    ppermute x3 -> x0, waiting for transfers between devices: 5.88 us -> none  [pass_on(): return lax.ppermute(value, axis, pairs)]
    ppermute x3 -> x0, starting transfers between devices: 4.44 us -> none  [pass_on(): return lax.ppermute(value, axis, pairs)]
  transfers between devices with their start and end apart: 5 -> 0, of which waited for: 4 -> 0; matrix products, arithmetic and copies ran while one was open for 8% -> 0% of each run, Pallas kernels for 59% -> 0%
where the time goes in v5:
time: 269 us
  Pallas kernels  256 us (95%)
  local copies, waits for them, and re-layouts  6.59 us (2%)
  other arithmetic  5.44 us (2%)
    pallas_call x1, Pallas kernels, run_mixer(): pl.pallas_call(functools.partial(mixer_kernel, ncol, ndp, full_width), in...  184 us
    pallas_call x1, Pallas kernels, reduce_grads(): pl.pallas_call(functools.partial(reduce_kernel, ncol, ndp, scols), in_spe...  66.6 us
    pallas_call x1, Pallas kernels, run_finish(): pl.pallas_call(functools.partial(finish_kernel, nheads), out_shape=[S(sha...  5.95 us

profile of v5, /device:TPU:0, one launch (start us, length us, event | category | flops | bytes accessed | tf_op | source)
XLA Modules:
  0.0 268.9 jit_solution(6268924527489992069)
XLA Ops:
  0.6 1.3 broadcast_in_dim.27.refs_4_
  1.9 1.3 broadcast_in_dim.28.refs_5_
  3.2 1.3 broadcast_in_dim.25.refs_1_.gain
  4.5 0.8 copy.31
  5.3 1.6 fusion.1.refs_12_
  6.9 1.9 copy.32
  8.8 183.7 %mixer.1 = (bf16[1040,1536]{1,0:T(8,128)(2,1)}, bf16[1024,384]{1,0:T(8,128)(2,1)}, bf16[1024,768]{1,0:T(8,128)(2,1)}, bf16[1024,1536]{1,0:T(8,128)(2,1)}, bf16[1...) custom-call(bf16[256,1536]{1,0:T(8,128)(2,1)} %tokens.1, ...), custom_call_target="tpu_custom_call" | custom-call | bytes 500000000 | tf_op jit(solution)/shard_map/mixer/pallas_call | solution.py:804
  192.5 66.6 %reduce_grads.1 = (f32[192,384]{1,0:T(8,128)}, f32[192,768]{1,0:T(8,128)}, f32[192,768]{1,0:T(8,128)}, f32[192,768]{1,0:T(8,128)}, f32[8,768]{1,0:T(8,128)}, /*i...) custom-call(bf16[1040,1536]{1,0:T(8,128)(2,1)} %get-tuple-element.51.refs_0_, ...), custom_call_target="tpu_custom_call" | custom-call | bytes 200000000 | tf_op jit(solution)/shard_map/reduce_grads/pallas_call | solution.py:1213
  259.1 6.0 %finish.1 = (f32[192,2,768]{2,1,0:T(2,128)}, f32[192,256]{1,0:T(8,128)}, f32[12,192]{1,0:T(8,128)}, f32[192,768]{1,0:T(8,128)}, f32[4,768]{1,0:T(4,128)}, /*inde...) custom-call(f32[192,384]{1,0:T(8,128)} %get-tuple-element.62.small, ...), custom_call_target="tpu_custom_call" | custom-call | tf_op jit(solution)/shard_map/finish/pallas_call | solution.py:1286
  265.1 1.3 reduce.1
  266.4 1.3 reduce.2
  267.6 1.3 reduce

commit v6 on v5

--- a/solution.py
+++ b/solution.py
@@ -35,7 +35,7 @@
 
 
 def sigmoid(v):
-    return 1.0 / (1.0 + jnp.exp(-v))
+    return 0.5 * jnp.tanh(0.5 * v) + 0.5
 
 
 def softplus(v):
@@ -64,11 +64,16 @@
 def conv_tile(cur, halo, links, taps, sl):
     v = jnp.concatenate([halo[HALO - 8 :, sl].astype(F32), cur[:, sl].astype(F32)], axis=0)
     length = cur.shape[0]
-    shifted = [v[8 - j : 8 - j + length] * links[j - 1] for j in range(1, 4)]
     pre = taps[4:5, sl] + taps[3:4, sl] * v[8:]
     for j in range(1, 4):
-        pre = pre + taps[3 - j : 4 - j, sl] * shifted[j - 1]
-    return pre, [v[8:]] + shifted
+        pre = pre + taps[3 - j : 4 - j, sl] * (v[8 - j : 8 - j + length] * links[j - 1])
+    return pre
+
+
+def silu_and_slope(pre):
+    s = sigmoid(pre)
+    value = pre * s
+    return value, s + value * (1.0 - s)
 
 
 def pick(lo, cols, h):
@@ -77,7 +82,7 @@
 
 def forward_body(
     inner, inner_halo, shared, shared_halo, step_raw, seg_row, seg_prev, seg_tail, taps, taps_s, heads,
-    y_out, x_out, bc_out, dt_out, c_out, ct_out, dec_out, enter_out, state, total,
+    y_out, x_out, bc_out, dt_out, c_out, ct_out, dec_out, enter_out, slope_out, slope_s_out, state, total,
 ):
     length, width = inner.shape
     pairs = width // 128
@@ -102,31 +107,35 @@
     total[0:1] = whole[length - 1 :]
     for half in range(2):
         sl = slice(half * state_dim, (half + 1) * state_dim)
-        pre, _ = conv_tile(shared, shared_halo, links, taps_s, sl)
-        bc_out[:, sl] = (pre * sigmoid(pre)).astype(BF16)
+        value, slope = silu_and_slope(conv_tile(shared, shared_halo, links, taps_s, sl))
+        bc_out[:, sl] = value.astype(BF16)
+        slope_s_out[:, sl] = slope.astype(BF16)
     b = bc_out[:, :state_dim]
     cc = bc_out[:, state_dim:]
     scores = jnp.where((rows >= cols) & (seg == segr), nt(cc, b), 0.0)
     lo = iota((length, 128), 1) < 64
+    lo1 = lo[0:1]
+    sides = [jnp.where(lo, 1.0, 0.0).astype(BF16), jnp.where(lo, 0.0, 1.0).astype(BF16)]
+    arriving = jnp.exp(c) * entering
+    leaving = jnp.exp(c[length - 1 :] - c) * closing
+    held = jnp.exp(c[length - 1 :]) * kept
     enter_out[...] = state[...].astype(BF16)
     for p in range(pairs):
         sl = slice(p * 128, (p + 1) * 128)
-        pre, _ = conv_tile(inner, inner_halo, links, taps, sl)
-        xp = pre * sigmoid(pre)
+        xp, slope = silu_and_slope(conv_tile(inner, inner_halo, links, taps, sl))
         xb = xp.astype(BF16)
         x_out[:, sl] = xb
+        slope_out[:, sl] = slope.astype(BF16)
         xdt = xb.astype(F32) * pick(lo, dt, 2 * p)
-        cb = pick(lo, c, 2 * p)
-        acc = nn(cc, state[:, sl].astype(BF16)) * (jnp.exp(cb) * entering)
+        xdtb = xdt.astype(BF16)
+        acc = nn(cc, state[:, sl].astype(BF16)) * pick(lo, arriving, 2 * p)
         for a in range(2):
             h = 2 * p + a
             weights = jnp.exp(jnp.minimum(c[:, h : h + 1] - ct[h : h + 1], 0.0)) * scores
-            mine = lo if a == 0 else ~lo
-            acc = acc + nn(weights.astype(BF16), jnp.where(mine, xdt, 0.0).astype(BF16))
+            acc = acc + nn(weights.astype(BF16), xdtb * sides[a])
         y_out[:, sl] = acc
-        last = cb[length - 1 :]
-        leaving = jnp.exp(last - cb) * closing * xdt
-        state[:, sl] = state[:, sl] * (jnp.exp(last) * kept) + tn(b, leaving.astype(BF16))
+        moved = pick(lo, leaving, 2 * p) * xdt
+        state[:, sl] = state[:, sl] * pick(lo1, held, 2 * p) + tn(b, moved.astype(BF16))
 
 
 def row_sums(value):
@@ -214,23 +223,26 @@
     row_out[...] = rowterm
 
 
-def conv_back(dout, pre, shifts, links, taps, sl, carry, carry_links, par_out):
+def conv_back(dout, slope, cur, halo, links, taps, sl, carry, carry_links, par_out, first):
     length = dout.shape[0]
-    s = sigmoid(pre)
-    dconv = dout * (s * (1.0 + pre * (1.0 - s)))
+    dconv = dout * slope[:, sl].astype(F32)
+    v = cur[:, sl].astype(F32)
+    v_above = halo[HALO - 8 :, sl].astype(F32) * first
     nxt = carry[:, sl]
     grad = taps[3:4, sl] * dconv
     above = jnp.zeros((8, dout.shape[1]), F32)
-    par_out[3:4, sl] += jnp.sum(dconv * shifts[0], axis=0, keepdims=True)
+    par_out[3:4, sl] += jnp.sum(dconv * v, axis=0, keepdims=True)
     par_out[4:5, sl] += jnp.sum(dconv, axis=0, keepdims=True)
     for j in range(1, 4):
         z = dconv * links[j - 1]
         w = taps[3 - j : 4 - j, sl]
-        low = jnp.concatenate([z, nxt * carry_links[:, j - 1 : j]], axis=0)
-        grad = grad + w * low[j : j + length]
-        high = jnp.concatenate([above * 0.0, z[0:8]], axis=0)
-        above = above + w * high[j : j + 8]
-        par_out[3 - j : 4 - j, sl] += jnp.sum(dconv * shifts[j], axis=0, keepdims=True)
+        low = jnp.concatenate([z, nxt * carry_links[:, j - 1 : j]], axis=0)[j : j + length]
+        high = jnp.concatenate([jnp.zeros_like(nxt), z[0:8]], axis=0)[j : j + 8]
+        grad = grad + w * low
+        above = above + w * high
+        par_out[3 - j : 4 - j, sl] += jnp.sum(low * v, axis=0, keepdims=True) + jnp.sum(
+            high * v_above, axis=0, keepdims=True
+        )
     carry[:, sl] = dconv[0:8]
     return grad, above
 
@@ -238,7 +250,7 @@
 def backward_body(
     k, chunks,
     inner, inner_halo, shared, shared_halo, step_raw, seg_row, seg_prev, seg_tail, taps, taps_s, heads,
-    dy, x, bc, dt_in, c_in, ct_in, dec_halo, enter, start, row_in,
+    dy, x, bc, dt_in, c_in, ct_in, dec_halo, enter, slope, slope_s, start, row_in,
     ginner_out, gsmall_out, par_out, par_s_out, par_h_out, edge_out, last_out,
     dstate, carry, carry_s, carry_links, grads_bc,
 ):
@@ -263,6 +275,10 @@
     scores = jnp.where(allowed, nt(b, cc), 0.0)
     lo = iota((length, 128), 1) < 64
     lo1 = lo[0:1]
+    sides = [jnp.where(lo, 1.0, 0.0).astype(BF16), jnp.where(lo, 0.0, 1.0).astype(BF16)]
+    arriving = jnp.exp(c) * entering
+    leaving_all = jnp.exp(c[length - 1 :] - c) * closing
+    held_all = jnp.exp(c[length - 1 :]) * kept
     dscores = jnp.zeros((length, length), F32)
     db = jnp.zeros((length, state_dim), F32)
     dc_mat = jnp.zeros((length, state_dim), F32)
@@ -271,42 +287,39 @@
     closing_term = jnp.zeros((1, 128), F32)
     for p in range(width // 128):
         sl = slice(p * 128, (p + 1) * 128)
-        pre, shifts = conv_tile(inner, inner_halo, links, taps, sl)
         dyb = dy[:, sl]
         dyf = dyb.astype(F32)
         xp = x[:, sl].astype(F32)
         dtb = pick(lo, dt, 2 * p)
         xdt = xp * dtb
-        cb = pick(lo, c, 2 * p)
+        xdtb = xdt.astype(BF16)
         hm = head_map(p)
-        last = cb[length - 1 :]
         entry = enter[:, sl].astype(F32) + start[:, sl] * pick(lo1, reach, 2 * p)
         entryb = entry.astype(BF16)
         ds = dstate[:, sl]
         dsb = ds.astype(BF16)
-        leaving = jnp.exp(last - cb) * closing
+        leaving = pick(lo, leaving_all, 2 * p)
         bds = nn(b, dsb)
         dxdt = jnp.zeros((length, 128), F32)
         for a in range(2):
             h = 2 * p + a
-            mine = lo if a == 0 else ~lo
             decay = jnp.exp(jnp.minimum(ct[h : h + 1] - c[:, h : h + 1], 0.0))
-            dscores = dscores + decay * nt(jnp.where(mine, xdt, 0.0).astype(BF16), dyb)
-            dxdt = dxdt + nn((decay * scores).astype(BF16), jnp.where(mine, dyf, 0.0).astype(BF16))
+            dscores = dscores + decay * nt(xdtb * sides[a], dyb)
+            dxdt = dxdt + nn((decay * scores).astype(BF16), dyb * sides[a])
         spread = leaving * xdt
         moved = spread * bds
-        matched = matched + split_dot(xdt.astype(BF16).astype(F32) * dxdt + moved, hm)
+        matched = matched + split_dot(xdtb.astype(F32) * dxdt + moved, hm)
         dxdt = dxdt + leaving * bds
-        held = jnp.exp(last) * kept
+        held = pick(lo1, held_all, 2 * p)
         col = jnp.sum(moved, axis=0, keepdims=True) + held * jnp.sum(entry * ds, axis=0, keepdims=True)
         closing_term = closing_term + split_dot(jnp.broadcast_to(col, (8, 128)), hm)[0:1]
-        direct = direct + split_dot(xp * dxdt, hm)
-        edy = (jnp.exp(cb) * entering * dyf).astype(BF16)
+        direct = direct + nn((xp * dxdt).astype(BF16), hm)
+        edy = (pick(lo, arriving, 2 * p) * dyf).astype(BF16)
         db = db + nt(spread.astype(BF16), dsb)
         dc_mat = dc_mat + nt(edy, entryb)
         dstate[:, sl] = ds * held + tn(cc, edy)
         dx = dtb * dxdt + taps[6:7, sl] * dyf
-        grad, above = conv_back(dx, pre, shifts, links, taps, sl, carry, next_links, par_out)
+        grad, above = conv_back(dx, slope, inner, inner_halo, links, taps, sl, carry, next_links, par_out, first)
         ginner_out[:, sl] = grad.astype(BF16)
         edge_out[:, sl] = above
 
@@ -319,8 +332,9 @@
     grads_bc[:, state_dim:] = dc_mat + tn(dsc, b)
     for half in range(2):
         sl = slice(half * state_dim, (half + 1) * state_dim)
-        pre, shifts = conv_tile(shared, shared_halo, links, taps_s, sl)
-        grad, above = conv_back(grads_bc[:, sl], pre, shifts, links, taps_s, sl, carry_s, next_links, par_s_out)
+        grad, above = conv_back(
+            grads_bc[:, sl], slope_s, shared, shared_halo, links, taps_s, sl, carry_s, next_links, par_s_out, first
+        )
         gsmall_out[:, sl] = grad.astype(BF16)
         at = slice(width + half * state_dim, width + (half + 1) * state_dim)
         edge_out[:, at] = above
@@ -345,8 +359,7 @@
     width = ggate.shape[1]
     part = nt(ggate[...], w_in[:, :width]) + nt(ginner[...], w_in[:, width:]) + nt(gsmall[...], w_small[...])
     part_out[...] = part.astype(BF16)
-    gain_out[...] = first_rows(jnp.broadcast_to(
-        jnp.sum(part * normed[...].astype(F32), axis=0, keepdims=True), gain_out.shape))
+    gain_out[...] = jnp.sum(part * normed[...].astype(F32), axis=0, keepdims=True)
 
 
 PIECES = 2
@@ -364,6 +377,10 @@
     @pl.when(when)
     def _():
         pl.semaphore_signal(barrier, inc=1, device_id=to, device_id_type=MESH)
+
+
+def line_of(ref):
+    return ref[...].reshape(1, ref.shape[0])
 
 
 def start(copies):
@@ -455,13 +472,13 @@
         return taken
 
     tokens_in, gain, seg_in, ci, cib, gg, cs, csb, sb, rl, sg = take(11)
-    w0, w1, w2, cot_in = take(4)
+    zx, bc_in, dt_in, w2, cot_in = take(5)
     normed_hbm, gsmall_hbm, ggate_hbm, cot_hbm, gnorm_hbm, ginner_hbm, part_hbm = take(7)
     par, par_s, par_h, gain_out, total_out = take(5)
     normed, seg, w_in, w_small, out_t, cot = take(6)
     taps, taps_s, heads = take(3)
     both, shared, step = take(3)
-    ssd, x, bc, dt, c, ct, dec, enter, state, start_state, total = take(11)
+    ssd, x, bc, dt, c, ct, dec, enter, slope, slope_s, state, start_state, total = take(13)
     gated, gnorm, projected, back, dy, ggate, rowterm, dstart, dend = take(9)
     ginner, gsmall, part, edge, edge_in, last_rows = take(6)
     dstate, carry, carry_s, carry_links, grads_bc = take(5)
@@ -480,7 +497,7 @@
     scols = taps_s.shape[1]
     state_dim = scols // 2
     chunks = length // SPAN
-    rows = w0.shape[0]
+    rows = bc_in.shape[0]
     me = dp * 2 + row
     sends_tail = (row == 0) & (z == last)
 
@@ -494,14 +511,15 @@
     for s in range(ncol):
         greet(barrier, sends_tail, row=1, col=s)
 
-    seg[pl.ds(pl.multiple_of(z * 8, 8), 8)] = jnp.broadcast_to(seg_in[...], (8, tokens))
+    seg[pl.ds(pl.multiple_of(z * 8, 8), 8)] = jnp.broadcast_to(line_of(seg_in), (8, tokens))
     base = pl.multiple_of(z * tokens, 32)
+    gain_row = line_of(gain)
 
     def normalize(n, carried):
         at = pl.multiple_of(n * 32, 32)
         wide = tokens_in[pl.ds(at, 32)].astype(F32)
         scale = lax.rsqrt(jnp.sum(wide * wide, axis=1, keepdims=True) / wide.shape[1] + EPS)
-        normed[pl.ds(pl.multiple_of(base + at, 32), 32)] = (wide * scale * gain[...]).astype(BF16)
+        normed[pl.ds(pl.multiple_of(base + at, 32), 32)] = (wide * scale * gain_row).astype(BF16)
         return carried
 
     lax.fori_loop(0, tokens // 32, normalize, 0)
@@ -517,30 +535,20 @@
         dend[...] = jnp.zeros_like(dend)
         edge_in[...] = jnp.zeros_like(edge_in)
 
-    taps[0:4] = ci[...]
-    taps[4:5] = cib[...]
-    taps[5:6] = gg[...]
-    lo1 = iota((1, 128), 1) < 64
-    for p in range(width // 128):
-        taps[6:7, p * 128 : (p + 1) * 128] = pick(lo1, sg, 2 * p)
-    taps_s[0:4] = cs[...]
-    taps_s[4:5] = csb[...]
-    heads[...] = jnp.zeros_like(heads)
-    heads[0:1, : sb.shape[1]] = sb[...]
-    heads[1:2, : rl.shape[1]] = rl[...]
-    for ref in (state, total, dstart, carry, carry_s, carry_links, par, par_s, par_h):
-        ref[...] = jnp.zeros_like(ref)
-
     count = ncol - 1 + ndp + row + jnp.where(sends_tail, ncol, 0)
     pl.semaphore_wait(barrier, count)
 
-    weights = ((w0, w_in), (w1, w_small), (w2, out_t))
+    weights = ((None, w_in), (None, w_small), (w2, out_t))
+
+    def weight_rows(j):
+        return pl.ds(pl.multiple_of(j * rows, 16), rows)
 
     def weight_copies(j, mine, send, **to):
         copies = []
         for i, (src, dst) in enumerate(weights):
-            place = dst.at[pl.ds(pl.multiple_of(j * rows, 16), rows)]
-            copies.append(remote(src if mine else place, place, send.at[i], w_recv.at[j, i], **to))
+            place = dst.at[weight_rows(j)]
+            from_input = mine and src is not None
+            copies.append(remote(src if from_input else place, place, send.at[i], w_recv.at[j, i], **to))
         return copies
 
     def tail_copies(s):
@@ -556,13 +564,34 @@
         guarded(sends_tail, lambda s=s: start(tail_copies(s)))
     gather = LineGather(ncol, z, (None, normed), (cot_in, cot), seg, (xs_send, xs_recv, cs_send, cs_recv))
     gather.begin()
+    w_in[weight_rows(me), 0:width] = zx[:, 0, :]
+    w_in[weight_rows(me), width : 2 * width] = zx[:, 1, :]
+    w_small[weight_rows(me), 0:scols] = bc_in[...]
+    dt_rows = jnp.concatenate([dt_in[...].astype(F32), jnp.zeros((128 - dt_in.shape[0], rows), F32)], axis=0)
+    w_small[weight_rows(me), scols : scols + 128] = dt_rows.T.astype(BF16)
+    local = [
+        pltpu.make_async_copy(cot_in, cot.at[pl.ds(base, tokens)], here.at[0]),
+        pltpu.make_async_copy(w2, out_t.at[weight_rows(me)], here.at[1]),
+    ]
+    start(local)
+    taps[0:4] = ci[...]
+    taps[4:5] = line_of(cib)
+    taps[5:6] = line_of(gg)
+    sg_row = line_of(sg)
+    lo1 = iota((1, 128), 1) < 64
+    for p in range(width // 128):
+        taps[6:7, p * 128 : (p + 1) * 128] = pick(lo1, sg_row, 2 * p)
+    taps_s[0:4] = cs[...]
+    taps_s[4:5] = line_of(csb)
+    heads[...] = jnp.zeros_like(heads)
+    heads[0:1, : sb.shape[0]] = line_of(sb)
+    heads[1:2, : rl.shape[0]] = line_of(rl)
+    for ref in (state, total, dstart, carry, carry_s, carry_links, par, par_s, par_h):
+        ref[...] = jnp.zeros_like(ref)
+
     for m in range(1, ndp):
         start(weight_copies(me, True, w_send.at[m], dp=dp ^ m))
     start(weight_copies(me, True, c_send.at[0], row=other))
-    local = [pltpu.make_async_copy(cot_in, cot.at[pl.ds(base, tokens)], here.at[0])]
-    for i, (src, dst) in enumerate(weights):
-        local.append(pltpu.make_async_copy(src, dst.at[pl.ds(pl.multiple_of(me * rows, 16), rows)], here.at[1 + i]))
-    start(local)
 
     def pass_weights(m):
         j = (dp ^ m) * 2 + row
@@ -628,7 +657,7 @@
     def forward(k, carried):
         this = at_rows(k)
         forward_body(*common(k), ssd.at[this], x.at[this], bc.at[this], dt.at[this], c.at[this],
-                     ct.at[:, this], dec.at[this], enter.at[k], state, total)
+                     ct.at[:, this], dec.at[this], enter.at[k], slope.at[this], slope_s.at[this], state, total)
         guarded(k == chunks // 2, lambda: gather.tick(half + 1))
         return carried
 
@@ -676,7 +705,7 @@
         return carried
 
     lax.fori_loop(0, chunks, projecting, 0)
-    line = LineReduce(ncol, z, projected, projected, line_box, line_send, line_recv)
+    line = LineReduce(ncol, z, projected, projected, line_box, line_send, line_recv, False)
     while len(later) > 2:
         gather.tick(later.pop(0))
 
@@ -696,7 +725,7 @@
     start(outs[1:])
     sum_begin(1, inner)
     sum_end(1, inner, inner_all)
-    line.start()
+    line.start(0, line.ticks)
 
     def pull_gate(k, carried):
         this = at_rows(k)
@@ -709,7 +738,6 @@
     guarded(row == 1, lambda: row_copy(1, dstart, dend).start())
     outs.append(pltpu.make_async_copy(ggate, ggate_hbm, here.at[7]))
     outs[-1].start()
-    line.tick(ticks.pop(0))
     guarded(row == 0, lambda: row_copy(1, dstart, dend).wait_recv())
     dstate[...] = dend[...]
 
@@ -721,7 +749,7 @@
         this = at_rows(k)
         before = pl.ds(pl.multiple_of(jnp.maximum(k * SPAN - 8, 0), 8), 8)
         backward_body(k, chunks, *common(k), dy.at[this], x.at[this], bc.at[this], dt.at[this], c.at[this],
-                      ct.at[:, this], dec.at[before], enter.at[k], start_state, rowterm.at[this],
+                      ct.at[:, this], dec.at[before], enter.at[k], slope.at[this], slope_s.at[this], start_state, rowterm.at[this],
                       ginner.at[this], gsmall.at[this], par, par_s, par_h, edge, last_rows,
                       dstate, carry, carry_s, carry_links, grads_bc)
         for turn, taus in spaced.items():
@@ -754,12 +782,14 @@
         spread_body(ggate, ginner, gsmall, w_in.at[at], w_small.at[at], normed.at[pl.ds(0, length), at],
                     part.at[:, at], gain_out.at[:, at])
         guarded(n > 0, lambda: part_copy(jnp.maximum(n - 1, 0)).start())
-        for tau in ticks:
+        for tau in ticks[:-1]:
             guarded(n == tiles // 2, lambda tau=tau: line.tick(tau))
         return carried
 
     lax.fori_loop(0, tiles, spreading, 0)
     part_copy(tiles - 1).start()
+    for tau in ticks[-1:]:
+        line.tick(tau)
 
     def keep(at, value):
         total_out[pl.ds(pl.multiple_of(at, 16), 16)] = value.astype(BF16)
@@ -788,14 +818,14 @@
         part_copy(n).wait()
 
 
-def run_mixer(full_width, tokens_in, gain, seg, ci, cib, gg, cs, csb, sb, rl, sg, w0, w1, w2, cot):
+def run_mixer(full_width, tokens_in, gain, seg, ci, cib, gg, cs, csb, sb, rl, sg, zx, bc, dt, w2, cot):
     ncol, ndp = lax.axis_size("col"), lax.axis_size("dp")
     tokens, model = tokens_in.shape
     width, scols = ci.shape[1], cs.shape[1]
     length = ncol * tokens
     chunks = length // SPAN
     state_dim = scols // 2
-    small = w1.shape[1]
+    small = scols + 128
     shards = 2 * ndp
     S = jax.ShapeDtypeStruct
     V = pltpu.VMEM
@@ -803,12 +833,12 @@
     vmem = pl.BlockSpec(memory_space=V)
     return pl.pallas_call(
         functools.partial(mixer_kernel, ncol, ndp, full_width),
-        in_specs=[vmem] * 11 + [ANY] * 4,
+        in_specs=[vmem] * 14 + [ANY] * 2,
         out_specs=[ANY] * 7 + [vmem] * 5,
         out_shape=[
             S((length + HALO, model), BF16), S((length, small), BF16), S((length, width), BF16), S((length, model), BF16),
             S((length, width), BF16), S((length, width), BF16), S((length, model), BF16),
-            S((8, width), F32), S((8, scols), F32), S((8, 128), F32), S((8, model), F32), S((tokens, model), BF16),
+            S((8, width), F32), S((8, scols), F32), S((8, 128), F32), S((1, model), F32), S((tokens, model), BF16),
         ],
         scratch_shapes=[
             V((length + HALO, model), BF16), V(((ncol + 1) * 8, tokens), jnp.int32), V((model, 2 * width), BF16),
@@ -817,6 +847,7 @@
             V((length + HALO, 2 * width), BF16), V((length + HALO, scols), BF16), V((length + HALO, 128), F32),
             V((length, width), F32), V((length, width), BF16), V((length, scols), BF16), V((length, 128), F32),
             V((length, 128), F32), V((16, length), F32), V((length, 128), F32), V((chunks, state_dim, width), BF16),
+            V((length, width), BF16), V((length, scols), BF16),
             V((state_dim, width), F32), V((state_dim, width), F32), V((8, 128), F32),
             V((length, width), BF16), V((length, width), BF16), V((length, model), BF16), V((length, width), BF16),
             V((length, width), BF16), V((length, width), BF16), V((length, 128), F32), V((state_dim, width), F32),
@@ -836,9 +867,10 @@
         ),
         cost_estimate=pl.CostEstimate(flops=0, bytes_accessed=500_000_000, transcendentals=0),
         name="mixer",
-    )(tokens_in, gain[None], seg[None], ci, cib[None], gg[None], cs, csb[None], sb[None], rl[None], sg[None], w0, w1, w2, cot)
+    )(tokens_in, gain, seg, ci, cib, gg, cs, csb, sb, rl, sg, zx, bc, dt, w2, cot)
 class LineReduce:
-    def __init__(self, ncol, z, source, local, inbox, send, recv):
+    def __init__(self, ncol, z, source, local, inbox, send, recv, paced):
+        self.paced = paced
         self.ncol, self.z, self.last = ncol, z, ncol - 1
         self.source, self.local, self.inbox = source, local, inbox
         self.send, self.recv = send, recv
@@ -860,22 +892,28 @@
     def depth(self, way):
         return self.z if way == 0 else self.last - self.z
 
-    def start(self):
+    def start(self, first=0, stop=2):
         for way in range(2):
 
             @pl.when(self.edge(way))
             def _(way=way):
-                for t in range(self.last):
-                    for p in range(PIECES):
-                        self.copy(way, t, p, True).start()
+                for i in range(first, min(stop, self.ticks)):
+                    self.copy(way, i // PIECES, i % PIECES, True).start()
 
     ticks = property(lambda self: self.last * PIECES)
 
     def tick(self, tau):
+        for way in range(2):
+
+            @pl.when(self.edge(way) & (self.paced and tau + 1 < self.ticks))
+            def _(way=way):
+                self.copy(way, (tau - 1) // PIECES, (tau - 1) % PIECES, True).wait_send()
+                self.copy(way, (tau + 1) // PIECES, (tau + 1) % PIECES, True).start()
+
         for stage in range(2):
             for way in range(2):
                 depth = self.depth(way)
-                index = tau - depth
+                index = tau - (2 * depth - 1)
                 t, p = index // PIECES, lax.rem(index, PIECES)
 
                 @pl.when((depth > 0) & (index >= 0) & (index < (self.ncol - depth) * PIECES))
@@ -922,9 +960,15 @@
     def drain(self):
         for way in range(2):
             depth = self.depth(way)
+
+            @pl.when(self.edge(way))
+            def _(way=way):
+                for i in range(self.ticks - 2 if self.paced else 0, self.ticks):
+                    self.copy(way, i // PIECES, i % PIECES, True).wait_send()
+
             for t in range(self.last):
 
-                @pl.when((depth < self.last) & (t < self.last - depth))
+                @pl.when((depth > 0) & (t < self.last - depth))
                 def _(way=way, t=t):
                     for p in range(PIECES):
                         self.copy(way, t, p, False).wait_send()
@@ -952,7 +996,8 @@
     (line_box, line_send, line_recv) = take(3)
     g, near, sent, far = take(count), take(count), take(count), take(count)
     vec_slots, col_slots = take(4), take(2)
-    bc_slots, load, c_send, c_recv, p_send, p_recv, v_send, v_recv, u_send, u_recv, b_send, b_recv = refs
+    col_sums = take(2)
+    bc_slots, bc_sum, load, c_send, c_recv, p_send, p_recv, v_send, v_recv, u_send, u_recv, b_send, b_recv = refs
     dp, row, z = lax.axis_index("dp"), lax.axis_index("row"), lax.axis_index("col")
     other = 1 - row
     me = dp * 2 + row
@@ -969,7 +1014,7 @@
         loads[-1].start()
     normed, gsmall, ggate, cot, gnorm, ginner, part = held
     pl.semaphore_wait(barrier, 2 * ndp + ncol - 2)
-    line = LineReduce(ncol, z, sources[6], part, line_box, line_send, line_recv)
+    line = LineReduce(ncol, z, sources[6], part, line_box, line_send, line_recv, True)
     line.start()
 
     order = (0, 1, 2, 3)
@@ -1021,34 +1066,6 @@
     def arrived(i, d):
         core_copy(i, d).wait_recv()
 
-    model = normed.shape[1]
-    block = model // 4
-    ends = [[] for _ in range(4)]
-    products = ((normed, gsmall), (normed, ggate), (cot, gnorm), (normed, ginner))
-    ready = {0: (0, 1), 1: (2,), 2: (3, 4), 3: (5,)}
-    ticks = list(range(1, line.ticks + 1))
-    loaded = [False]
-    for i in order:
-        for at in ready[i]:
-            loads[at].wait()
-        left, right = products[i]
-        for m in ([3, 1, 2, 0] if ndp == 4 else range(4)):
-            b = dp ^ m if ndp == 4 else m
-            first = pl.multiple_of(b * block, 128)
-            g[i][pl.ds(pl.multiple_of(b * block, 16), block)] = tn(left[:, pl.ds(first, block)], right[...]).astype(BF16)
-            if ndp == 4:
-                later(core_copy(i, b))
-        if i == 1:
-            loads[6].wait()
-            line.tick(ticks.pop(0))
-        if i == 3 and ticks:
-            line.tick(ticks.pop(0))
-    later(None)
-    if ndp != 4:
-        for i in order:
-            for m in turns:
-                core_copy(i, dp ^ m).start()
-
     def tick():
         if ticks:
             line.tick(ticks.pop(0))
@@ -1059,7 +1076,7 @@
         def leg(i, slot, m):
             return remote(sent[i].at[slot], far[i].at[slot], p_send.at[i, slot], p_recv.at[i, slot], dp=dp ^ m)
 
-        for i in order:
+        def step_one(i):
             half = rows[i] // 2
             arrived(i, dp ^ 3)
             for h, m1, m2 in halves:
@@ -1071,7 +1088,8 @@
                 accumulate(i, h * half, half, [mine(i, dp ^ m1), read(near[i], dp ^ m1)],
                            write(sent[i], 3 * h, h * half))
                 later(leg(i, 3 * h, m1))
-        later(None)
+            later(None)
+            arrived(i, dp)
 
         def relay(i):
             half = rows[i] // 2
@@ -1081,6 +1099,7 @@
                            [mine(i, dp ^ m2), read(near[i], dp ^ m2), read(far[i], 3 * h + 1, h * half)],
                            write(sent[i], 3 * h + 2, h * half))
                 later(leg(i, 3 * h + 2, m2))
+            later(None)
 
         def finish(i, store):
             half = rows[i] // 2
@@ -1097,12 +1116,13 @@
         def peer(i, m):
             return remote(sent[i].at[m], far[i].at[m], p_send.at[i, m], p_recv.at[i, m], dp=dp ^ m)
 
-        for i in order:
+        def step_one(i):
             for m in turns[:-1]:
                 arrived(i, dp ^ m)
                 accumulate(i, 0, rows[i], [mine(i, dp ^ m), read(near[i], dp ^ m)], write(sent[i], m, 0))
                 later(peer(i, m))
-        later(None)
+            later(None)
+            arrived(i, dp)
 
         def relay(i):
             pass
@@ -1115,9 +1135,80 @@
 
         sends = [peer(i, m) for i in order for m in range(1, ndp)]
 
+    def plain(i):
+        def store(at, total):
+            r[i][pl.ds(at, 16)] = total
+
+        return store
+
+    def shared_rows(at, total):
+        r[0][pl.ds(at, 16)] = total
+        bc_slots[z, pl.ds(at, 16)] = total[:, : bc_slots.shape[2]].astype(BF16)
+
+    root = ncol // 2
+    at_root = z == root
+
+    def to_root(source):
+        pairs = [(col_slots[i].at[source], u_send.at[0, i], u_recv.at[source, i]) for i in range(2)]
+        pairs.append((bc_slots.at[source], b_send.at[0], b_recv.at[source]))
+        return [remote(ref, ref, send, recv, col=root) for ref, send, recv in pairs]
+
+    def from_root(target):
+        pairs = [(col_sums[i], u_send.at[target, i], u_recv.at[root, i]) for i in range(2)]
+        pairs.append((bc_sum, b_send.at[target], b_recv.at[root]))
+        return [remote(ref, ref, send, recv, col=target) for ref, send, recv in pairs]
+
+    others = [s for s in range(ncol) if s != root]
+
+    def sum_at_root():
+        @pl.when(at_root)
+        def _():
+            for s in others:
+                for copy in to_root(s):
+                    copy.wait_recv()
+            for i in range(2):
+                total = col_slots[i][0]
+                for j in range(1, ncol):
+                    total = total + col_slots[i][j]
+                col_sums[i][...] = total
+            total = bc_slots[0].astype(F32)
+            for j in range(1, ncol):
+                total = total + bc_slots[j].astype(F32)
+            bc_sum[...] = total.astype(BF16)
+            for s in others:
+                for copy in from_root(s):
+                    copy.start()
+
+    model = normed.shape[1]
+    block = model // 4
+    products = ((normed, gsmall), (normed, ggate), (cot, gnorm), (normed, ginner))
+    ready = {0: (0, 1), 1: (2,), 2: (3, 4), 3: (5,)}
+    ticks = list(range(1, line.ticks + 1))
     for i in order:
-        arrived(i, dp)
-    tick()
+        for at in ready[i]:
+            loads[at].wait()
+        left, right = products[i]
+        for n, m in enumerate([3, 1, 2, 0] if ndp == 4 else range(4)):
+            b = dp ^ m if ndp == 4 else m
+            first = pl.multiple_of(b * block, 128)
+            g[i][pl.ds(pl.multiple_of(b * block, 16), block)] = tn(left[:, pl.ds(first, block)], right[...]).astype(BF16)
+            if ndp == 4:
+                later(core_copy(i, b))
+        if ndp != 4:
+            for m in turns:
+                later(core_copy(i, dp ^ m))
+        if i == 1:
+            loads[6].wait()
+        if i > 0:
+            step_one(i - 1)
+        if i > 1:
+            relay(i - 2)
+        if i % 2:
+            tick()
+    later(None)
+    step_one(3)
+    relay(2)
+    finish(0, shared_rows)
     for q in range(1, 2 * ndp):
         for i in range(4):
             vec_copy(q, i, me ^ q).wait_recv()
@@ -1131,34 +1222,16 @@
         else:
             col_slots[i - 2][z] = total
 
-    def plain(i):
-        def store(at, total):
-            r[i][pl.ds(at, 16)] = total
-
-        return store
-
-    def shared_rows(at, total):
-        r[0][pl.ds(at, 16)] = total
-        bc_slots[z, pl.ds(at, 16)] = total[:, : bc_slots.shape[2]].astype(BF16)
-
-    def col_copies(s, source):
-        to = lax.rem(z + s, ncol)
-        copies = [remote(col_slots[i].at[source], col_slots[i].at[source], u_send.at[s, i], u_recv.at[source, i], col=to)
-                  for i in range(2)]
-        return copies + [remote(bc_slots.at[source], bc_slots.at[source], b_send.at[s], b_recv.at[source], col=to)]
-
-    relay(0)
-    relay(1)
+    @pl.when(~at_root)
+    def _():
+        for copy in to_root(z):
+            copy.start()
+
     tick()
-    relay(2)
     relay(3)
-    later(None)
-    finish(0, shared_rows)
-    for s in range(1, ncol):
-        for copy in col_copies(s, z):
-            copy.start()
     while len(ticks) > 1:
         tick()
+    sum_at_root()
     finish(1, plain(1))
     finish(2, plain(2))
     finish(3, plain(3))
@@ -1169,18 +1242,14 @@
         gsum_out[pl.ds(pl.multiple_of(at, 16), 16)] = value.astype(BF16)
 
     line.total(keep)
-    for s in range(1, ncol):
-        for copy in col_copies(s, lax.rem(z + s, ncol)):
+    @pl.when(~at_root)
+    def _():
+        for copy in from_root(z):
             copy.wait_recv()
+
     for i in range(2):
-        total = col_slots[i][0]
-        for j in range(1, ncol):
-            total = total + col_slots[i][j]
-        vec_outs[2 + i][...] = total
-    total = bc_slots[0].astype(F32)
-    for j in range(1, ncol):
-        total = total + bc_slots[j].astype(F32)
-    r[0][:, : bc_slots.shape[2]] = total
+        vec_outs[2 + i][...] = col_sums[i][...]
+    r[0][:, : bc_slots.shape[2]] = bc_sum[...].astype(F32)
 
     for q in range(1, 2 * ndp):
         for i in range(4):
@@ -1190,9 +1259,17 @@
             core_copy(i, dp ^ m).wait_send()
     for copy in sends:
         copy.wait_send()
-    for s in range(1, ncol):
-        for copy in col_copies(s, z):
+    @pl.when(~at_root)
+    def _():
+        for copy in to_root(z):
             copy.wait_send()
+
+    @pl.when(at_root)
+    def _():
+        for s in others:
+            for copy in from_root(s):
+                copy.wait_send()
+
     line.drain()
 
 
@@ -1221,7 +1298,8 @@
         + near + legs * 2
         + [pltpu.VMEM((2 * ndp,) + v.shape, F32) for v in vecs]
         + [pltpu.VMEM((ncol,) + v.shape, F32) for v in vecs[2:]]
-        + [pltpu.VMEM((ncol, blocks[0][0], scols), BF16)]
+        + [pltpu.VMEM(v.shape, F32) for v in vecs[2:]]
+        + [pltpu.VMEM((ncol, blocks[0][0], scols), BF16), pltpu.VMEM((blocks[0][0], scols), BF16)]
         + [dma((7,))]
         + [dma((count, ndp))] * 2
         + [dma((count, slots))] * 2
@@ -1242,29 +1320,30 @@
 ):
     width = par.shape[1]
     scols = par_s.shape[1]
+    gain_row = gain[...].reshape(1, gain.shape[0])
     zx_out[:, 0, :] = gate[...]
     zx_out[:, 1, :] = inner[...]
     bc_out[...] = small[:, :scols]
     dt_out[...] = small[:, scols:].T[:nheads]
     out_out[...] = out[...]
     ci_out[...] = par[0:4]
-    cib_out[...] = par[4:5]
-    gg_out[...] = par[5:6]
+    cib_out[...] = par[4:5].reshape(width)
+    gg_out[...] = par[5:6].reshape(width)
     cs_out[...] = par_s[0:4]
-    csb_out[...] = par_s[4:5]
-    sb_out[...] = par_h[0:1, :nheads]
-    rl_out[...] = par_h[1:2, :nheads]
+    csb_out[...] = par_s[4:5].reshape(scols)
+    sb_out[...] = par_h[0:1, :nheads].reshape(nheads)
+    rl_out[...] = par_h[1:2, :nheads].reshape(nheads)
     skip = jnp.zeros((8, 128), F32)
     for p in range(width // 128):
         skip = skip + split_dot(jnp.broadcast_to(par[6:7, p * 128 : (p + 1) * 128], (8, 128)), head_map(p))
-    sg_out[...] = skip[0:1, :nheads]
-    ng_out[...] = gain_sum[0:1] / gain[...]
+    sg_out[...] = skip[0:1, :nheads].reshape(nheads)
+    ng_out[...] = (gain_sum[0:1] / gain_row).reshape(gain.shape[0])
 
     def rows(step, carry):
         at = pl.ds(pl.multiple_of(step * 32, 32), 32)
         wide = tokens[at].astype(F32)
         scale = lax.rsqrt(jnp.sum(wide * wide, axis=1, keepdims=True) / wide.shape[1] + EPS)
-        pushed = gnormed[at].astype(F32) * gain[...]
+        pushed = gnormed[at].astype(F32) * gain_row
         mean = jnp.sum(pushed * wide, axis=1, keepdims=True) / wide.shape[1]
         grad = scale * pushed - wide * (scale * scale * scale * mean)
         gin_out[at] = (cot[at].astype(F32) + grad).astype(BF16)
@@ -1280,14 +1359,14 @@
     model = gain.shape[0]
     S = jax.ShapeDtypeStruct
     shapes = [
-        (rows, 2, width), (rows, scols), (nheads, rows), (rows, width), (4, width), (1, width), (4, scols), (1, scols),
-        (1, nheads), (1, nheads), (1, nheads), (1, width), (1, model),
+        (rows, 2, width), (rows, scols), (nheads, rows), (rows, width), (4, width), (width,), (4, scols), (scols,),
+        (nheads,), (nheads,), (nheads,), (width,), (model,),
     ]
     return pl.pallas_call(
         functools.partial(finish_kernel, nheads),
         out_shape=[S(shape, F32) for shape in shapes] + [S(tokens.shape, BF16)] * 2,
         name="finish",
-    )(small, gate, inner, out, par, par_h, par_s, gain_sum, gain[None], tokens, cot, gnormed, projected)
+    )(small, gate, inner, out, par, par_h, par_s, gain_sum, gain, tokens, cot, gnormed, projected)
 
 
 def per_device(
@@ -1298,10 +1377,9 @@
     scols = proj_bc.shape[1]
     nheads = proj_dt.shape[1]
     full_width = float(width * lax.axis_size("col"))
-    small_own = jnp.concatenate([proj_bc, jnp.pad(proj_dt, ((0, 0), (0, 128 - nheads)))], axis=1)
     (normed, gsmall, ggate, cot_all, gated_normed, ginner, part, par, par_s, par_h, gain_part, projected) = run_mixer(
         full_width, block_input, norm_gain, segment_ids, conv_inner, conv_inner_bias, gated_gain, conv_shared,
-        conv_shared_bias, step_bias, rate_log, skip_gain, proj_zx.reshape(-1, 2 * width), small_own, proj_out.T, cotangent,
+        conv_shared_bias, step_bias, rate_log, skip_gain, proj_zx, proj_bc, proj_dt.T, proj_out.T, cotangent,
     )
     gsm, gz, gout, gx, par, par_h, par_s, gain_sum, grad_normed = reduce_grads(
         (normed, gsmall, ggate, cot_all, gated_normed, ginner, part), (par, par_h, par_s, gain_part), scols
@@ -1310,7 +1388,7 @@
         nheads, gsm, gz, gx, gout, par, par_h, par_s, gain_sum, norm_gain, block_input, cotangent, grad_normed, projected
     )
     return (
-        block_output, grad_input, ng[0], zx, gbc, gdt.T, ci, cib[0], cs, csb[0], sb[0], rl[0], sg[0], gg[0], gout.T,
+        block_output, grad_input, ng, zx, gbc, gdt.T, ci, cib, cs, csb, sb, rl, sg, gg, gout.T,
     )
 
 

time: 269 us -> 245 us (0.911)
  Pallas kernels: 256 us -> 243 us
  local copies, waits for them, and re-layouts: 6.59 us -> 0 us
  other arithmetic: 5.44 us -> 0 us
    pallas_call x1, Pallas kernels: 184 us -> 177 us  [run_mixer(): pl.pallas_call(functools.partial(mixer_kernel, ncol, ndp, full_width), in...]
    pallas_call x1, Pallas kernels: 66.6 us -> 60.4 us  [reduce_grads(): pl.pallas_call(functools.partial(reduce_kernel, ncol, ndp, scols), in_spe...]
    pallas_call x3 -> x0, other arithmetic: 3.87 us -> none  [run_finish(): pl.pallas_call(functools.partial(finish_kernel, nheads), out_shape=[S(sha...]
    broadcast_in_dim x3 -> x0, local copies, waits for them, and re-layouts: 3.83 us -> none  [the longest x1 1.29 us: run_mixer(): gain[None]]
    unnamed x2 -> x0, local copies, waits for them, and re-layouts: 2.76 us -> none
where the time goes in v6:
time: 245 us; the launch traced here: 244 us
  Pallas kernels  243 us (99%)
    pallas_call x1, Pallas kernels, run_mixer(): pl.pallas_call(functools.partial(mixer_kernel, ncol, ndp, full_width), in...  177 us
    pallas_call x1, Pallas kernels, reduce_grads(): pl.pallas_call(functools.partial(reduce_kernel, ncol, ndp, scols), in_spe...  60.4 us
    pallas_call x1, Pallas kernels, run_finish(): pl.pallas_call(functools.partial(finish_kernel, nheads), out_shape=[S(sha...  5.97 us

profile of v6, /device:TPU:0, one launch (start us, length us, event | category | flops | bytes accessed | tf_op | source)
XLA Modules:
  0.0 244.1 jit_solution(6898141621258601805)
XLA Ops:
  0.7 176.9 %mixer.1 = (bf16[1040,1536]{1,0:T(8,128)(2,1)}, bf16[1024,384]{1,0:T(8,128)(2,1)}, bf16[1024,768]{1,0:T(8,128)(2,1)}, bf16[1024,1536]{1,0:T(8,128)(2,1)}, bf16[1...) custom-call(bf16[256,1536]{1,0:T(8,128)(2,1)} %tokens.1, ...), custom_call_target="tpu_custom_call" | custom-call | bytes 500000000 | tf_op jit(solution)/shard_map/mixer/pallas_call | solution.py:834
  177.6 60.4 %reduce_grads.1 = (f32[192,384]{1,0:T(8,128)}, f32[192,768]{1,0:T(8,128)}, f32[192,768]{1,0:T(8,128)}, f32[192,768]{1,0:T(8,128)}, f32[8,768]{1,0:T(8,128)}, /*i...) custom-call(bf16[1040,1536]{1,0:T(8,128)(2,1)} %get-tuple-element.51.refs_0_, ...), custom_call_target="tpu_custom_call" | custom-call | bytes 200000000 | tf_op jit(solution)/shard_map/reduce_grads/pallas_call | solution.py:1290
  238.0 6.0 %finish.1 = (f32[192,2,768]{2,1,0:T(2,128)}, f32[192,256]{1,0:T(8,128)}, f32[12,192]{1,0:T(8,128)}, f32[192,768]{1,0:T(8,128)}, f32[4,768]{1,0:T(4,128)}, /*inde...) custom-call(f32[192,384]{1,0:T(8,128)} %get-tuple-element.62.small, ...), custom_call_target="tpu_custom_call" | custom-call | tf_op jit(solution)/shard_map/finish/pallas_call | solution.py:1365

commit v7 on v6

--- a/solution.py
+++ b/solution.py
@@ -154,7 +154,7 @@
     return (head == 2 * p + lane // 64).astype(BF16)
 
 
-def gate_body(y, x, bc, dec, start, gate, taps, ssd_out, gated_out, sums_out):
+def gate_body(y, x, bc, dec, start, gate, taps, ssd_out, gained_out, sums_out):
     length, width = x.shape
     state_dim = start.shape[0]
     cc = bc[:, state_dim:]
@@ -167,40 +167,32 @@
         ssd_out[:, sl] = ssd
         g = gate[:, sl].astype(F32)
         gated = ssd * (g * sigmoid(g))
-        gated_out[:, sl] = gated.astype(BF16)
+        gained_out[:, sl] = (gated * taps[5:6, sl]).astype(BF16)
         squares = squares + gated * gated
-    sums_out[...] = row_sums(squares)
-
-
-def project_body(full_width, gated, sums, taps, out_t, normed_out, proj_out):
-    rescale = columns(lax.rsqrt(sums[0:1] / full_width + EPS))
-    for p in range(gated.shape[1] // 128):
-        sl = slice(p * 128, (p + 1) * 128)
-        normed_out[:, sl] = (gated[:, sl].astype(F32) * rescale * taps[5:6, sl]).astype(BF16)
-    proj_out[...] = nt(normed_out[...], out_t[...]).astype(BF16)
-
-
-def pull_body(cot, out_t, gated, taps, back_out, sums_out):
+    sums_out[0:1] = row_sums(squares)[0:1]
+
+
+def pull_body(cot, out_t, gained, back_out, sums_out):
     back = nn(cot[...], out_t[...])
     back_out[...] = back.astype(BF16)
     inner = jnp.zeros((cot.shape[0], 128), F32)
     for p in range(back.shape[1] // 128):
         sl = slice(p * 128, (p + 1) * 128)
-        inner = inner + back[:, sl] * taps[5:6, sl] * gated[:, sl].astype(F32)
-    sums_out[...] = row_sums(inner)
+        inner = inner + back[:, sl] * gained[:, sl].astype(F32)
+    sums_out[1:2] = row_sums(inner)[0:1]
 
 
 def back_body(
-    full_width, ssd, x, bc, dec, gate, back, squares, inner, taps,
-    dy_out, ggate_out, row_out, colsum_out, dstart_out,
+    full_width, ssd, x, bc, dec, gate, back, sums, taps,
+    normed_out, dy_out, ggate_out, row_out, colsum_out, dstart_out,
 ):
     length, width = x.shape
     state_dim = dstart_out.shape[0]
 
     cc = bc[:, state_dim:]
     lo = iota((length, 128), 1) < 64
-    rescale = columns(lax.rsqrt(squares[0:1] / full_width + EPS))
-    pull = columns(inner[0:1]) * (rescale * rescale * rescale / full_width)
+    rescale = columns(lax.rsqrt(sums[0:1] / full_width + EPS))
+    pull = columns(sums[1:2]) * (rescale * rescale * rescale / full_width)
     rowterm = jnp.zeros((length, 128), F32)
     for p in range(width // 128):
         sl = slice(p * 128, (p + 1) * 128)
@@ -211,6 +203,7 @@
         gated = s_ssd * (g * s)
         bk = back[:, sl].astype(F32)
         gain = taps[5:6, sl]
+        normed_out[:, sl] = (gated * rescale * gain).astype(BF16)
         gg = rescale * (bk * gain) - gated * pull
         dy = gg * (g * s)
         dyb = dy.astype(BF16)
@@ -479,10 +472,10 @@
     taps, taps_s, heads = take(3)
     both, shared, step = take(3)
     ssd, x, bc, dt, c, ct, dec, enter, slope, slope_s, state, start_state, total = take(13)
-    gated, gnorm, projected, back, dy, ggate, rowterm, dstart, dend = take(9)
+    gained, gnorm, projected, back, dy, ggate, rowterm, dstart, dend = take(9)
     ginner, gsmall, part, edge, edge_in, last_rows = take(6)
     dstate, carry, carry_s, carry_links, grads_bc = take(5)
-    squares, squares_all, inner, inner_all, slots = take(5)
+    sums, sums_all, own_scale, slots = take(4)
     line_box, line_send, line_recv = take(3)
     xs_send, xs_recv, cs_send, cs_recv, w_send, c_send, w_recv, t_send, t_recv = take(9)
     sum_send, sum_recv, row_send, row_recv, here = take(5)
@@ -586,7 +579,7 @@
     heads[...] = jnp.zeros_like(heads)
     heads[0:1, : sb.shape[0]] = line_of(sb)
     heads[1:2, : rl.shape[0]] = line_of(rl)
-    for ref in (state, total, dstart, carry, carry_s, carry_links, par, par_s, par_h):
+    for ref in (state, total, dstart, carry, carry_s, carry_links, par, par_s, par_h, sums):
         ref[...] = jnp.zeros_like(ref)
 
     for m in range(1, ndp):
@@ -674,44 +667,38 @@
     def gating(k, carried):
         this = at_rows(k)
         gate_body(ssd.at[this], x.at[this], bc.at[this], dec.at[this], start_state, both.at[this, pl.ds(0, width)],
-                  taps, ssd.at[this], gated.at[this], squares.at[:, this])
+                  taps, ssd.at[this], gained.at[this], sums.at[:, this])
         return carried
 
     lax.fori_loop(0, chunks, gating, 0)
 
-    def sum_copy(n, value, s, source):
-        return remote(value, slots.at[n, source], sum_send.at[n, s], sum_recv.at[n, source],
-                      col=lax.rem(z + s, ncol))
-
-    def sum_begin(n, value):
-        for s in range(1, ncol):
-            sum_copy(n, value, s, z).start()
-
-    def sum_end(n, value, out):
-        result = value[...]
+    def sum_copy(s, source):
+        return remote(sums, slots.at[source], sum_send.at[s], sum_recv.at[source], col=lax.rem(z + s, ncol))
+
+    def sum_end():
+        result = sums[...]
         for s in range(1, ncol):
             source = lax.rem(z + s, ncol)
-            sum_copy(n, value, s, source).wait_recv()
-            result = result + slots[n, source]
-        out[...] = result
-
-    sum_begin(0, squares)
+            sum_copy(s, source).wait_recv()
+            result = result + slots[source]
+        sums_all[...] = result
+
     gather.tick(later.pop(0))
-    sum_end(0, squares, squares_all)
 
     def projecting(k, carried):
         this = at_rows(k)
-        project_body(full_width, gated.at[this], squares_all.at[:, this], taps, out_t, gnorm.at[this], projected.at[this])
+        projected[this] = nt(gained[this], out_t[...]).astype(BF16)
         return carried
 
     lax.fori_loop(0, chunks, projecting, 0)
     line = LineReduce(ncol, z, projected, projected, line_box, line_send, line_recv, False)
+    line.start()
     while len(later) > 2:
         gather.tick(later.pop(0))
 
     def pulling(n):
         this = pl.ds(nth(n), tokens)
-        pull_body(cot.at[this], out_t, gated.at[this], taps, back.at[this], inner.at[:, this])
+        pull_body(cot.at[this], out_t, gained.at[this], back.at[this], sums.at[:, this])
 
     for n in range(ncol - 1):
         pulling(n)
@@ -721,23 +708,27 @@
     ticks = list(range(1, line.ticks + 1))
     pulling(ncol - 1)
     outs.append(pltpu.make_async_copy(cot, cot_hbm, here.at[5]))
-    outs.append(pltpu.make_async_copy(gnorm, gnorm_hbm, here.at[6]))
-    start(outs[1:])
-    sum_begin(1, inner)
-    sum_end(1, inner, inner_all)
-    line.start(0, line.ticks)
+    outs[-1].start()
+    for s in range(1, ncol):
+        sum_copy(s, z).start()
+    line.start(2, line.ticks)
+    line.tick(ticks.pop(0))
+    sum_end()
+    own_scale[...] = columns(lax.rsqrt(sums_all[0:1, pl.ds(pl.multiple_of(z * tokens, tokens), tokens)] / full_width + EPS))
 
     def pull_gate(k, carried):
         this = at_rows(k)
         back_body(full_width, ssd.at[this], x.at[this], bc.at[this], dec.at[this], both.at[this, pl.ds(0, width)],
-                  back.at[this], squares_all.at[:, this], inner_all.at[:, this], taps,
-                  dy.at[this], ggate.at[this], rowterm.at[this], par, dstart)
+                  back.at[this], sums_all.at[:, this], taps,
+                  gnorm.at[this], dy.at[this], ggate.at[this], rowterm.at[this], par, dstart)
         return carried
 
     lax.fori_loop(0, chunks, pull_gate, 0)
     guarded(row == 1, lambda: row_copy(1, dstart, dend).start())
     outs.append(pltpu.make_async_copy(ggate, ggate_hbm, here.at[7]))
-    outs[-1].start()
+    outs.append(pltpu.make_async_copy(gnorm, gnorm_hbm, here.at[6]))
+    start(outs[-2:])
+    line.tick(ticks.pop(0))
     guarded(row == 0, lambda: row_copy(1, dstart, dend).wait_recv())
     dstate[...] = dend[...]
 
@@ -792,7 +783,8 @@
         line.tick(tau)
 
     def keep(at, value):
-        total_out[pl.ds(pl.multiple_of(at, 16), 16)] = value.astype(BF16)
+        here_rows = pl.ds(pl.multiple_of(at, 16), 16)
+        total_out[here_rows] = (value * own_scale[here_rows, 0:1]).astype(BF16)
 
     line.total(keep)
 
@@ -806,9 +798,8 @@
             copy.wait_send()
     for s in range(ncol):
         guarded(sends_tail, lambda s=s: [copy.wait_send() for copy in tail_copies(s)])
-    for n, value in ((0, squares), (1, inner)):
-        for s in range(1, ncol):
-            sum_copy(n, value, s, z).wait_send()
+    for s in range(1, ncol):
+        sum_copy(s, z).wait_send()
     guarded(row == 0, lambda: row_copy(0, state, start_state).wait_send())
     guarded(row == 1, lambda: row_copy(1, dstart, dend).wait_send())
     guarded(row == 1, lambda: row_copy(2, edge, edge_in).wait_send())
@@ -855,12 +846,11 @@
             V((length, width), BF16), V((length, small), BF16), V((length, model), BF16),
             V((8, width + scols), F32), V((8, width + scols), F32), V((8, width + scols), F32),
             V((state_dim, width), F32), V((8, width), F32), V((8, scols), F32), V((8, 128), F32), V((SPAN, scols), F32),
-            V((8, length), F32), V((8, length), F32), V((8, length), F32), V((8, length), F32),
-            V((2, ncol, 8, length), F32),
+            V((8, length), F32), V((8, length), F32), V((tokens, 128), F32), V((ncol, 8, length), F32),
             *line_scratch(ncol, tokens, model),
             dma((2, ncol, PIECES + 1)), dma((ncol, PIECES + 1)), dma((2, ncol, PIECES)), dma((ncol, PIECES)),
             dma((ndp, 3)), dma((ndp, 3)), dma((shards, 3)), dma((ncol, 2)), dma((2,)),
-            dma((2, ncol)), dma((2, ncol)), dma((3,)), dma((3,)), dma((10 + model // 256,)),
+            dma((ncol,)), dma((ncol,)), dma((3,)), dma((3,)), dma((10 + model // 256,)),
         ],
         compiler_params=pltpu.CompilerParams(
             collective_id=1, has_side_effects=True, vmem_limit_bytes=63 * 1024 * 1024
@@ -1314,18 +1304,14 @@
     )(*sources, *vecs)
 
 
-def finish_kernel(
-    nheads, small, gate, inner, out, par, par_h, par_s, gain_sum, gain, tokens, cot, gnormed, projected,
-    zx_out, bc_out, dt_out, out_out, ci_out, cib_out, cs_out, csb_out, sb_out, rl_out, sg_out, gg_out, ng_out, gin_out, block_out,
+def finish_small(
+    nheads, small, par, par_h, par_s, gain_sum, gain_row, bc_out, dt_out, ci_out, cib_out, cs_out,
+    csb_out, sb_out, rl_out, sg_out, gg_out, ng_out,
 ):
     width = par.shape[1]
     scols = par_s.shape[1]
-    gain_row = gain[...].reshape(1, gain.shape[0])
-    zx_out[:, 0, :] = gate[...]
-    zx_out[:, 1, :] = inner[...]
     bc_out[...] = small[:, :scols]
     dt_out[...] = small[:, scols:].T[:nheads]
-    out_out[...] = out[...]
     ci_out[...] = par[0:4]
     cib_out[...] = par[4:5].reshape(width)
     gg_out[...] = par[5:6].reshape(width)
@@ -1337,7 +1323,22 @@
     for p in range(width // 128):
         skip = skip + split_dot(jnp.broadcast_to(par[6:7, p * 128 : (p + 1) * 128], (8, 128)), head_map(p))
     sg_out[...] = skip[0:1, :nheads].reshape(nheads)
-    ng_out[...] = (gain_sum[0:1] / gain_row).reshape(gain.shape[0])
+    ng_out[...] = (gain_sum[0:1] / gain_row).reshape(gain_row.shape[1])
+
+
+def finish_kernel(
+    nheads, small, gate, inner, out, par, par_h, par_s, gain_sum, gain, tokens, cot, gnormed, projected,
+    zx_out, bc_out, dt_out, out_out, ci_out, cib_out, cs_out, csb_out, sb_out, rl_out, sg_out, gg_out, ng_out, gin_out, block_out,
+):
+    gain_row = gain[...].reshape(1, gain.shape[0])
+    zx_out[:, 0, :] = gate[...]
+    zx_out[:, 1, :] = inner[...]
+    out_out[...] = out[...]
+
+    @pl.when(pl.program_id(0) == 0)
+    def _():
+        finish_small(nheads, small, par, par_h, par_s, gain_sum, gain_row, bc_out, dt_out, ci_out, cib_out, cs_out,
+                     csb_out, sb_out, rl_out, sg_out, gg_out, ng_out)
 
     def rows(step, carry):
         at = pl.ds(pl.multiple_of(step * 32, 32), 32)
@@ -1362,8 +1363,20 @@
         (rows, 2, width), (rows, scols), (nheads, rows), (rows, width), (4, width), (width,), (4, scols), (scols,),
         (nheads,), (nheads,), (nheads,), (width,), (model,),
     ]
+    steps = 4 if rows % 32 == 0 else 2
+    block = rows // steps
+    some = tokens.shape[0] // steps
+    down = lambda n: (n, 0)
+    whole = lambda shape: pl.BlockSpec(shape, lambda n: (0,) * len(shape))
+    wide_spec = pl.BlockSpec((block, width), down)
+    token_spec = pl.BlockSpec((some, model), down)
     return pl.pallas_call(
         functools.partial(finish_kernel, nheads),
+        grid=(steps,),
+        in_specs=[whole(small.shape), wide_spec, wide_spec, wide_spec, whole(par.shape), whole(par_h.shape),
+                  whole(par_s.shape), whole(gain_sum.shape), whole(gain.shape)] + [token_spec] * 4,
+        out_specs=[pl.BlockSpec((block, 2, width), lambda n: (n, 0, 0)), whole(shapes[1]), whole(shapes[2]), wide_spec]
+        + [whole(shape) for shape in shapes[4:]] + [token_spec] * 2,
         out_shape=[S(shape, F32) for shape in shapes] + [S(tokens.shape, BF16)] * 2,
         name="finish",
     )(small, gate, inner, out, par, par_h, par_s, gain_sum, gain, tokens, cot, gnormed, projected)

time: 245 us -> 230 us (0.939)
  Pallas kernels: 243 us -> 228 us
    pallas_call x1, Pallas kernels: 177 us -> 160 us  [run_mixer(): pl.pallas_call(functools.partial(mixer_kernel, ncol, ndp, full_width), in...]
where the time goes in v7:
time: 230 us; the launch traced here: 229 us
  Pallas kernels  228 us (99%)
    pallas_call x1, Pallas kernels, run_mixer(): pl.pallas_call(functools.partial(mixer_kernel, ncol, ndp, full_width), in...  160 us
    pallas_call x1, Pallas kernels, reduce_grads(): pl.pallas_call(functools.partial(reduce_kernel, ncol, ndp, scols), in_spe...  61.2 us
    pallas_call x1, Pallas kernels, run_finish(): pl.pallas_call(functools.partial(finish_kernel, nheads), grid=(steps,), i...  6.17 us

profile of v7, /device:TPU:0, one launch (start us, length us, event | category | flops | bytes accessed | tf_op | source)
XLA Modules:
  0.0 228.7 jit_solution(4401154919283701106)
XLA Ops:
  0.7 160.4 %mixer.1 = (bf16[1040,1536]{1,0:T(8,128)(2,1)}, bf16[1024,384]{1,0:T(8,128)(2,1)}, bf16[1024,768]{1,0:T(8,128)(2,1)}, bf16[1024,1536]{1,0:T(8,128)(2,1)}, bf16[1...) custom-call(bf16[256,1536]{1,0:T(8,128)(2,1)} %tokens.1, ...), custom_call_target="tpu_custom_call" | custom-call | bytes 500000000 | tf_op jit(solution)/shard_map/mixer/pallas_call | solution.py:825
  161.1 61.2 %reduce_grads.1 = (f32[192,384]{1,0:T(8,128)}, f32[192,768]{1,0:T(8,128)}, f32[192,768]{1,0:T(8,128)}, f32[192,768]{1,0:T(8,128)}, f32[8,768]{1,0:T(8,128)}, /*i...) custom-call(bf16[1040,1536]{1,0:T(8,128)(2,1)} %get-tuple-element.51.refs_0_, ...), custom_call_target="tpu_custom_call" | custom-call | bytes 200000000 | tf_op jit(solution)/shard_map/reduce_grads/pallas_call | solution.py:1280
  222.3 6.2 %finish.1 = (f32[192,2,768]{2,1,0:T(2,128)}, f32[192,256]{1,0:T(8,128)}, f32[12,192]{1,0:T(8,128)}, f32[192,768]{1,0:T(8,128)}, f32[4,768]{1,0:T(4,128)}, /*inde...) custom-call(f32[192,384]{1,0:T(8,128)} %get-tuple-element.62.small, ...), custom_call_target="tpu_custom_call" | custom-call | tf_op jit(solution)/shard_map/finish/pallas_call | solution.py:1373

commit v8 on v7

--- a/solution.py
+++ b/solution.py
@@ -272,7 +272,10 @@
     arriving = jnp.exp(c) * entering
     leaving_all = jnp.exp(c[length - 1 :] - c) * closing
     held_all = jnp.exp(c[length - 1 :]) * kept
-    dscores = jnp.zeros((length, length), F32)
+    half = length // 2
+    scores_top, scores_low = scores[:half], scores[half:, half:]
+    top = jnp.zeros((half, length), F32)
+    low = jnp.zeros((half, half), F32)
     db = jnp.zeros((length, state_dim), F32)
     dc_mat = jnp.zeros((length, state_dim), F32)
     direct = jnp.zeros((length, 128), F32)
@@ -293,12 +296,18 @@
         dsb = ds.astype(BF16)
         leaving = pick(lo, leaving_all, 2 * p)
         bds = nn(b, dsb)
-        dxdt = jnp.zeros((length, 128), F32)
+        dx_top = jnp.zeros((half, 128), F32)
+        dx_low = jnp.zeros((half, 128), F32)
         for a in range(2):
             h = 2 * p + a
-            decay = jnp.exp(jnp.minimum(ct[h : h + 1] - c[:, h : h + 1], 0.0))
-            dscores = dscores + decay * nt(xdtb * sides[a], dyb)
-            dxdt = dxdt + nn((decay * scores).astype(BF16), dyb * sides[a])
+            mine = dyb * sides[a]
+            decay = jnp.exp(jnp.minimum(ct[h : h + 1] - c[:half, h : h + 1], 0.0))
+            top = top + decay * nt(xdtb[:half], mine)
+            dx_top = dx_top + nn((decay * scores_top).astype(BF16), mine)
+            decay = jnp.exp(jnp.minimum(ct[h : h + 1, half:] - c[half:, h : h + 1], 0.0))
+            low = low + decay * nt(xdtb[half:], mine[half:])
+            dx_low = dx_low + nn((decay * scores_low).astype(BF16), mine[half:])
+        dxdt = jnp.concatenate([dx_top, dx_low], axis=0)
         spread = leaving * xdt
         moved = spread * bds
         matched = matched + split_dot(xdtb.astype(F32) * dxdt + moved, hm)
@@ -320,7 +329,8 @@
         def _():
             last_out[:, sl] = grad[length - 8 :]
 
-    dsc = jnp.where(allowed, dscores, 0.0).astype(BF16)
+    low = jnp.concatenate([jnp.zeros((half, half), F32), low], axis=1)
+    dsc = jnp.where(allowed, jnp.concatenate([top, low], axis=0), 0.0).astype(BF16)
     grads_bc[:, :state_dim] = db + nn(dsc, cc)
     grads_bc[:, state_dim:] = dc_mat + tn(dsc, b)
     for half in range(2):

time: 230 us -> 228 us (level)
  no operation moved by 1% of the time
where the time goes in v8:
time: 228 us; the launch traced here: 227 us
  Pallas kernels  226 us (99%)
    pallas_call x1, Pallas kernels, run_mixer(): pl.pallas_call(functools.partial(mixer_kernel, ncol, ndp, full_width), in...  159 us
    pallas_call x1, Pallas kernels, reduce_grads(): pl.pallas_call(functools.partial(reduce_kernel, ncol, ndp, scols), in_spe...  61.2 us
    pallas_call x1, Pallas kernels, run_finish(): pl.pallas_call(functools.partial(finish_kernel, nheads), grid=(steps,), i...  6.17 us

profile of v8, /device:TPU:0, one launch (start us, length us, event | category | flops | bytes accessed | tf_op | source)
XLA Modules:
  0.0 227.2 jit_solution(7376133662001361741)
XLA Ops:
  0.7 159.0 %mixer.1 = (bf16[1040,1536]{1,0:T(8,128)(2,1)}, bf16[1024,384]{1,0:T(8,128)(2,1)}, bf16[1024,768]{1,0:T(8,128)(2,1)}, bf16[1024,1536]{1,0:T(8,128)(2,1)}, bf16[1...) custom-call(bf16[256,1536]{1,0:T(8,128)(2,1)} %tokens.1, ...), custom_call_target="tpu_custom_call" | custom-call | bytes 500000000 | tf_op jit(solution)/shard_map/mixer/pallas_call | solution.py:835
  159.7 61.2 %reduce_grads.1 = (f32[192,384]{1,0:T(8,128)}, f32[192,768]{1,0:T(8,128)}, f32[192,768]{1,0:T(8,128)}, f32[192,768]{1,0:T(8,128)}, f32[8,768]{1,0:T(8,128)}, /*i...) custom-call(bf16[1040,1536]{1,0:T(8,128)(2,1)} %get-tuple-element.51.refs_0_, ...), custom_call_target="tpu_custom_call" | custom-call | bytes 200000000 | tf_op jit(solution)/shard_map/reduce_grads/pallas_call | solution.py:1290
  220.9 6.2 %finish.1 = (f32[192,2,768]{2,1,0:T(2,128)}, f32[192,256]{1,0:T(8,128)}, f32[12,192]{1,0:T(8,128)}, f32[192,768]{1,0:T(8,128)}, f32[4,768]{1,0:T(4,128)}, /*inde...) custom-call(f32[192,384]{1,0:T(8,128)} %get-tuple-element.62.small, ...), custom_call_target="tpu_custom_call" | custom-call | tf_op jit(solution)/shard_map/finish/pallas_call | solution.py:1383

commit v9 on v8

--- a/solution.py
+++ b/solution.py
@@ -856,7 +856,7 @@
             V((length, width), BF16), V((length, small), BF16), V((length, model), BF16),
             V((8, width + scols), F32), V((8, width + scols), F32), V((8, width + scols), F32),
             V((state_dim, width), F32), V((8, width), F32), V((8, scols), F32), V((8, 128), F32), V((SPAN, scols), F32),
-            V((8, length), F32), V((8, length), F32), V((tokens, 128), F32), V((ncol, 8, length), F32),
+            V((2, length), F32), V((2, length), F32), V((tokens, 128), F32), V((ncol, 2, length), F32),
             *line_scratch(ncol, tokens, model),
             dma((2, ncol, PIECES + 1)), dma((ncol, PIECES + 1)), dma((2, ncol, PIECES)), dma((ncol, PIECES)),
             dma((ndp, 3)), dma((ndp, 3)), dma((shards, 3)), dma((ncol, 2)), dma((2,)),

time: 228 us -> 226 us (level)
  no operation moved by 1% of the time
where the time goes in v9:
time: 226 us; the launch traced here: 225 us
  Pallas kernels  224 us (99%)
    pallas_call x1, Pallas kernels, run_mixer(): pl.pallas_call(functools.partial(mixer_kernel, ncol, ndp, full_width), in...  158 us
    pallas_call x1, Pallas kernels, reduce_grads(): pl.pallas_call(functools.partial(reduce_kernel, ncol, ndp, scols), in_spe...  60.1 us
    pallas_call x1, Pallas kernels, run_finish(): pl.pallas_call(functools.partial(finish_kernel, nheads), grid=(steps,), i...  6.17 us

profile of v9, /device:TPU:0, one launch (start us, length us, event | category | flops | bytes accessed | tf_op | source)
XLA Modules:
  0.0 224.9 jit_solution(15661997973986717142)
XLA Ops:
  0.7 157.7 %mixer.1 = (bf16[1040,1536]{1,0:T(8,128)(2,1)}, bf16[1024,384]{1,0:T(8,128)(2,1)}, bf16[1024,768]{1,0:T(8,128)(2,1)}, bf16[1024,1536]{1,0:T(8,128)(2,1)}, bf16[1...) custom-call(bf16[256,1536]{1,0:T(8,128)(2,1)} %tokens.1, ...), custom_call_target="tpu_custom_call" | custom-call | bytes 500000000 | tf_op jit(solution)/shard_map/mixer/pallas_call | solution.py:835
  158.4 60.1 %reduce_grads.1 = (f32[192,384]{1,0:T(8,128)}, f32[192,768]{1,0:T(8,128)}, f32[192,768]{1,0:T(8,128)}, f32[192,768]{1,0:T(8,128)}, f32[8,768]{1,0:T(8,128)}, /*i...) custom-call(bf16[1040,1536]{1,0:T(8,128)(2,1)} %get-tuple-element.51.refs_0_, ...), custom_call_target="tpu_custom_call" | custom-call | bytes 200000000 | tf_op jit(solution)/shard_map/reduce_grads/pallas_call | solution.py:1290
  218.5 6.2 %finish.1 = (f32[192,2,768]{2,1,0:T(2,128)}, f32[192,256]{1,0:T(8,128)}, f32[12,192]{1,0:T(8,128)}, f32[192,768]{1,0:T(8,128)}, f32[4,768]{1,0:T(4,128)}, /*inde...) custom-call(f32[192,384]{1,0:T(8,128)} %get-tuple-element.62.small, ...), custom_call_target="tpu_custom_call" | custom-call | tf_op jit(solution)/shard_map/finish/pallas_call | solution.py:1383
